TPU v7x, 32 devices: a whole 2x2x4 slice. The times are simulated.
32 devices in a mesh: group: 2 (over x), expert: 4 (over z), shard: 4 (over y, core).
Axes of the slice: x: 2, y: 2, z: 4, core: 2. Of those that a mesh axis runs over, the one named last changes fastest.
Arguments:
- hidden_in: bfloat16 [6144, 768], P(('group', 'expert', 'shard')), may hold values from -6 to 6
- segment_ids: int32 [2, 3072], P('group'), may hold values from 0 to 8, never falling along the last dimension, each value on 1 to 1536 neighbouring positions
- routes: int32 [6144, 2], P(('group', 'expert', 'shard')), may hold values from 0 to 7, all different within a row; in each aligned block of 192 rows (0 to 191, 192 to 383, ...) at most 48 rows name the same one
- attn_gain: float32 [768], replicated, may hold values from 0.5 to 1.5
- w_query: bfloat16 [768, 768], P('shard'), may hold values from -0.21875 to 0.21875
- w_key: bfloat16 [768, 768], P('shard'), may hold values from -0.21875 to 0.21875
- w_value: bfloat16 [768, 768], P('shard'), may hold values from -0.21875 to 0.21875
- w_out: bfloat16 [768, 768], P('shard'), may hold values from -2.5 to 2.5
- moe_gain: float32 [768], replicated, may hold values from 0.5 to 1.5
- w_router: float32 [768, 8], replicated, may hold values from -0.15625 to 0.15625
- const_mix: float32 [768, 4], replicated, may hold values from -0.21875 to 0.21875
- const_vec: float32 [2, 768], replicated, may hold values from -6 to 6
- w_gate: bfloat16 [4, 768, 2048], P('expert'), may hold values from -0.21875 to 0.21875
- w_up: bfloat16 [4, 768, 2048], P('expert'), may hold values from -0.21875 to 0.21875
- w_down: bfloat16 [4, 2048, 768], P('expert'), may hold values from -0.1875 to 0.1875
- out_grad: bfloat16 [6144, 768], P(('group', 'expert', 'shard')), may hold values from -6 to 6
Outputs:
- layer_out: bfloat16 [6144, 768], P(('group', 'expert', 'shard'))
- input_grad: float32 [6144, 768], P(('group', 'expert', 'shard'))
- attn_gain_grad: float32 [768], replicated
- query_grad: float32 [768, 768], P(('expert', 'shard'))
- key_grad: float32 [768, 768], P(('expert', 'shard'))
- value_grad: float32 [768, 768], P(('expert', 'shard'))
- out_proj_grad: float32 [768, 768], P(('expert', 'shard'))
- moe_gain_grad: float32 [768], replicated
- router_grad: float32 [768, 8], replicated
- mix_grad: float32 [768, 4], replicated
- vec_grad: float32 [2, 768], replicated
- gate_grad: float32 [4, 768, 2048], P('expert', 'shard')
- up_grad: float32 [4, 768, 2048], P('expert', 'shard')
- down_grad: float32 [4, 2048, 768], P('expert', 'shard')
Inputs may be any that keep to these rules, and one draw needn't show every extreme that they name: Each row names two different ids; ids below 4 are feed-forward experts, 4 is the zero expert, 5 the copy expert, 6 and 7 the constant experts. Among the routes of the 192 tokens of one device no id is named more than 48 times, a bound that some block reaches. `segment_ids`: each row numbers the documents of one group in order, never falling, starting at 0; document 0 is the prompt that every later document of the row attends; each of the 9 documents has at least one position and one has exactly 1536.
All inputs are finite; a program needn't handle non-finite values.
Results may differ from a plain program's by a relative error of at most 0.02.
Values may be sent and summed in bfloat16 or wider, within the bound.
A program may use at most 192 MiB of HBM per device.

v0:
```python
import jax
import jax.numpy as jnp
from jax import lax
from jax.sharding import PartitionSpec as P

HEADS = 12
HEAD_DIM = 64
CAP = 48


neg_fill = -1e30
norm_eps = 1e-05


def dense32(left_side, right_side):
    return jnp.dot(left_side, right_side, precision=lax.Precision.HIGHEST)


def allowed_mask(query_pos, query_seg, key_pos, key_seg):
    same_doc = (key_seg[None, :] == query_seg[:, None]) | (key_seg[None, :] == 0)
    return same_doc & (key_pos[None, :] <= query_pos[:, None])


def rms_back(inputs, inverse, gain_vec, upstream):
    scaled = upstream * gain_vec
    return inverse * scaled - inputs * inverse**3 * jnp.mean(scaled * inputs, axis=1, keepdims=True)


def block_scores(query_blk, keys_blk, score_scale):
    return (
        jnp.einsum("qhd,khd->hqk", query_blk, keys_blk, preferred_element_type=jnp.float32)
        * score_scale
    )


def grad_pieces(
    query_blk, back_blk, keys_blk, values_blk, norm_blk, delta_blk, key_mask, score_scale
):
    scores = block_scores(query_blk, keys_blk, score_scale)
    prob_rows = jnp.where(key_mask[None], jnp.exp(scores - norm_blk[:, :, None]), 0.0)
    prob_grad = jnp.einsum("qhd,khd->hqk", back_blk, values_blk, preferred_element_type=jnp.float32)
    score_low = (prob_rows * (prob_grad - delta_blk[:, :, None])).astype(jnp.bfloat16)
    return (prob_rows.astype(jnp.bfloat16), score_low)


def shards(
    hidden_in,
    segment_ids,
    routes,
    attn_gain,
    w_query,
    w_key,
    w_value,
    w_out,
    moe_gain,
    w_router,
    const_mix,
    const_vec,
    w_gate,
    w_up,
    w_down,
    out_grad,
):
    tok_rows, model_width = hidden_in.shape
    score_scale = HEAD_DIM ** (-0.5)
    inner_rank = lax.axis_index(("expert", "shard"))
    seg_group = segment_ids[0]
    group_len = seg_group.shape[0]
    key_block = min(512, group_len)
    num_blocks = group_len // key_block
    row_start = inner_rank * tok_rows
    own_pos = row_start + jnp.arange(tok_rows, dtype=jnp.int32)
    own_seg = lax.dynamic_slice_in_dim(seg_group, row_start, tok_rows)
    wq_full, wk_full, wv_full, wo_full = (
        lax.all_gather(w_query, "shard", axis=0, tiled=True),
        lax.all_gather(w_key, "shard", axis=0, tiled=True),
        lax.all_gather(w_value, "shard", axis=0, tiled=True),
        lax.all_gather(w_out, "shard", axis=0, tiled=True),
    )
    inputs = hidden_in.astype(jnp.float32)
    inv_one = lax.rsqrt(jnp.mean(inputs * inputs, axis=1, keepdims=True) + norm_eps)
    normed_one = inputs * inv_one
    attn_in = (normed_one * attn_gain).astype(jnp.bfloat16)
    queries = jnp.dot(attn_in, wq_full, preferred_element_type=jnp.float32).astype(jnp.bfloat16)
    keys_own = jnp.dot(attn_in, wk_full, preferred_element_type=jnp.float32).astype(jnp.bfloat16)
    values_own = jnp.dot(attn_in, wv_full, preferred_element_type=jnp.float32).astype(jnp.bfloat16)
    keys_all, values_all = (
        lax.all_gather(keys_own, ("expert", "shard"), axis=0, tiled=True),
        lax.all_gather(values_own, ("expert", "shard"), axis=0, tiled=True),
    )
    query_heads = queries.reshape(tok_rows, HEADS, HEAD_DIM)

    def fetch_block(source, block_index):
        return lax.dynamic_slice_in_dim(source, block_index * key_block, key_block).reshape(
            key_block, HEADS, HEAD_DIM
        )

    def block_mask(block_index):
        key_pos = block_index * key_block + jnp.arange(key_block, dtype=jnp.int32)
        key_seg = lax.dynamic_slice_in_dim(seg_group, block_index * key_block, key_block)
        return allowed_mask(own_pos, own_seg, key_pos, key_seg)

    def stats_step(carry_now, block_index):
        key_mask = block_mask(block_index)

        def stats_live_block(carry_in):
            row_max, row_sum = carry_in
            scores = jnp.where(
                key_mask[None],
                block_scores(query_heads, fetch_block(keys_all, block_index), score_scale),
                neg_fill,
            )
            new_max = jnp.maximum(row_max, jnp.max(scores, axis=2))
            weights = jnp.where(key_mask[None], jnp.exp(scores - new_max[:, :, None]), 0.0)
            return (new_max, row_sum * jnp.exp(row_max - new_max) + jnp.sum(weights, axis=2))

        return (
            lax.cond(jnp.any(key_mask), stats_live_block, lambda carry_in: carry_in, carry_now),
            None,
        )

    start_max = jnp.full((HEADS, tok_rows), neg_fill, jnp.float32)
    row_max, row_sum = lax.scan(
        stats_step, (start_max, jnp.zeros_like(start_max)), jnp.arange(num_blocks)
    )[0]
    log_norm = row_max + jnp.log(row_sum)

    def output_step(running, block_index):
        key_mask = block_mask(block_index)

        def output_live_block(carry_in):
            scores = block_scores(query_heads, fetch_block(keys_all, block_index), score_scale)
            prob_rows = jnp.where(
                key_mask[None], jnp.exp(scores - log_norm[:, :, None]), 0.0
            ).astype(jnp.bfloat16)
            return carry_in + jnp.einsum(
                "hqk,khd->qhd",
                prob_rows,
                fetch_block(values_all, block_index),
                preferred_element_type=jnp.float32,
            )

        return (
            lax.cond(jnp.any(key_mask), output_live_block, lambda carry_in: carry_in, running),
            None,
        )

    zero_heads = jnp.zeros((tok_rows, HEADS, HEAD_DIM), jnp.float32)
    attn_sum = lax.scan(output_step, zero_heads, jnp.arange(num_blocks))[0]
    attn_low = attn_sum.reshape(tok_rows, model_width).astype(jnp.bfloat16)
    resid_one = inputs + jnp.dot(attn_low, wo_full, preferred_element_type=jnp.float32)
    inv_two = lax.rsqrt(jnp.mean(resid_one * resid_one, axis=1, keepdims=True) + norm_eps)
    normed_two = resid_one * inv_two
    moe_in = normed_two * moe_gain
    moe_low = moe_in.astype(jnp.bfloat16)
    n_ids = w_router.shape[1]
    local_experts = w_gate.shape[0]
    owners = lax.axis_size("expert")
    ffn_count = local_experts * owners
    id_table = jnp.arange(n_ids, dtype=jnp.int32)
    route_hot = (routes[:, :, None] == id_table).astype(jnp.float32)
    logits = dense32(moe_in, w_router)
    chosen = jnp.einsum("rkn,rn->rk", route_hot, logits, precision=lax.Precision.HIGHEST)
    gate_probs = jax.nn.softmax(chosen, axis=1)
    mix_alpha = jax.nn.softmax(dense32(moe_in, const_mix).reshape(tok_rows, 2, 2), axis=2)
    const_rows = mix_alpha[:, :, 0:1] * moe_in[:, None, :] + mix_alpha[:, :, 1:2] * const_vec[None]
    ffn_mask = (routes < ffn_count).astype(jnp.float32)
    copy_mask = (routes == ffn_count + 1).astype(jnp.float32)
    const_mask = (routes[:, :, None] == ffn_count + 2 + jnp.arange(2, dtype=jnp.int32)).astype(
        jnp.float32
    )
    copy_gate = jnp.sum(gate_probs * copy_mask, axis=1)
    const_gate = jnp.sum(gate_probs[:, :, None] * const_mask, axis=1)
    ffn_gate = gate_probs * ffn_mask
    flat_ids = routes.reshape(-1)
    id_hot = (flat_ids[:, None] == id_table).astype(jnp.int32)
    earlier = jnp.cumsum(id_hot, axis=0, dtype=jnp.int32) - id_hot
    slot_num = jnp.sum(earlier * id_hot, axis=1, dtype=jnp.int32)
    slot_total = ffn_count * CAP
    slot_of_route = jnp.where(flat_ids < ffn_count, flat_ids * CAP + slot_num, slot_total)
    route_count = flat_ids.shape[0]
    route_of_slot = (
        jnp.zeros(slot_total + 1, jnp.int32)
        .at[slot_of_route]
        .set(jnp.arange(route_count, dtype=jnp.int32))[:slot_total]
    )
    slot_used = jnp.zeros(slot_total + 1, jnp.bool_).at[slot_of_route].set(True)[:slot_total]
    send_rows = jnp.where(
        slot_used[:, None], moe_low[route_of_slot // 2], jnp.zeros((), jnp.bfloat16)
    )
    recv_rows = lax.all_to_all(
        send_rows.reshape(owners, local_experts * CAP, model_width),
        "expert",
        split_axis=0,
        concat_axis=0,
        tiled=True,
    )
    expert_in = recv_rows.reshape(owners, local_experts, CAP, model_width)
    gate_pre = jnp.einsum("sjcd,jdf->sjcf", expert_in, w_gate, preferred_element_type=jnp.float32)
    up_pre = jnp.einsum("sjcd,jdf->sjcf", expert_in, w_up, preferred_element_type=jnp.float32)
    gate_sigmoid = jax.nn.sigmoid(gate_pre)
    hidden_act = (gate_pre * gate_sigmoid * up_pre).astype(jnp.bfloat16)
    expert_out = jnp.einsum(
        "sjcf,jfd->sjcd", hidden_act, w_down, preferred_element_type=jnp.float32
    ).astype(jnp.bfloat16)
    returned = lax.all_to_all(
        expert_out.reshape(owners, local_experts * CAP, model_width),
        "expert",
        split_axis=0,
        concat_axis=0,
        tiled=True,
    )
    padded_out = jnp.concatenate(
        [returned.reshape(slot_total, model_width), jnp.zeros((1, model_width), jnp.bfloat16)],
        axis=0,
    )
    route_out = padded_out[slot_of_route].astype(jnp.float32).reshape(tok_rows, 2, model_width)
    moe_sum = (
        jnp.sum(ffn_gate[:, :, None] * route_out, axis=1)
        + copy_gate[:, None] * moe_in
        + jnp.sum(const_gate[:, :, None] * const_rows, axis=1)
    )
    layer_out = (resid_one + moe_sum).astype(jnp.bfloat16)
    upstream = out_grad.astype(jnp.float32)
    route_dot = jnp.sum(upstream[:, None, :] * route_out, axis=2)
    copy_dot = jnp.sum(upstream * moe_in, axis=1)
    const_dot = jnp.sum(upstream[:, None, :] * const_rows, axis=2)
    gate_back_r = (
        ffn_mask * route_dot
        + copy_mask * copy_dot[:, None]
        + jnp.sum(const_mask * const_dot[:, None, :], axis=2)
    )
    chosen_grad = gate_probs * (
        gate_back_r - jnp.sum(gate_probs * gate_back_r, axis=1, keepdims=True)
    )
    logit_grad = jnp.einsum("rk,rkn->rn", chosen_grad, route_hot, precision=lax.Precision.HIGHEST)
    const_up = const_gate[:, :, None] * upstream[:, None, :]
    alpha_grad = jnp.stack(
        [
            jnp.sum(const_up * moe_in[:, None, :], axis=2),
            jnp.sum(const_up * const_vec[None], axis=2),
        ],
        axis=2,
    )
    mix_back = (
        mix_alpha * (alpha_grad - jnp.sum(mix_alpha * alpha_grad, axis=2, keepdims=True))
    ).reshape(tok_rows, 4)
    vec_grad = jnp.sum(mix_alpha[:, :, 1:2] * const_up, axis=0)
    route_weight = ffn_gate.reshape(-1)
    grad_send = (route_weight[route_of_slot][:, None] * upstream[route_of_slot // 2]).astype(
        jnp.bfloat16
    )
    grad_send = jnp.where(slot_used[:, None], grad_send, jnp.zeros((), jnp.bfloat16))
    grad_recv = lax.all_to_all(
        grad_send.reshape(owners, local_experts * CAP, model_width),
        "expert",
        split_axis=0,
        concat_axis=0,
        tiled=True,
    )
    grad_recv = grad_recv.reshape(owners, local_experts, CAP, model_width)
    hidden_grad = jnp.einsum(
        "sjcd,jfd->sjcf", grad_recv, w_down, preferred_element_type=jnp.float32
    )
    down_term = jnp.einsum(
        "sjcf,sjcd->jfd", hidden_act, grad_recv, preferred_element_type=jnp.float32
    )
    gate_back = (
        hidden_grad * up_pre * gate_sigmoid * (1.0 + gate_pre * (1.0 - gate_sigmoid))
    ).astype(jnp.bfloat16)
    up_back = (hidden_grad * gate_pre * gate_sigmoid).astype(jnp.bfloat16)
    gate_term = jnp.einsum(
        "sjcd,sjcf->jdf", expert_in, gate_back, preferred_element_type=jnp.float32
    )
    up_term = jnp.einsum("sjcd,sjcf->jdf", expert_in, up_back, preferred_element_type=jnp.float32)
    input_back = (
        jnp.einsum("sjcf,jdf->sjcd", gate_back, w_gate, preferred_element_type=jnp.float32)
        + jnp.einsum("sjcf,jdf->sjcd", up_back, w_up, preferred_element_type=jnp.float32)
    ).astype(jnp.bfloat16)
    input_ret = lax.all_to_all(
        input_back.reshape(owners, local_experts * CAP, model_width),
        "expert",
        split_axis=0,
        concat_axis=0,
        tiled=True,
    )
    padded_in = jnp.concatenate(
        [input_ret.reshape(slot_total, model_width), jnp.zeros((1, model_width), jnp.bfloat16)],
        axis=0,
    )
    ffn_in_grad = jnp.sum(
        padded_in[slot_of_route].astype(jnp.float32).reshape(tok_rows, 2, model_width), axis=1
    )
    moe_in_grad = (
        ffn_in_grad
        + copy_gate[:, None] * upstream
        + jnp.sum(mix_alpha[:, :, 0:1] * const_up, axis=1)
        + dense32(mix_back, const_mix.T)
        + dense32(logit_grad, w_router.T)
    )
    moe_gain_grad = jnp.sum(moe_in_grad * normed_two, axis=0)
    router_grad = dense32(moe_in.T, logit_grad)
    mix_grad = dense32(moe_in.T, mix_back)
    resid_grad = upstream + rms_back(resid_one, inv_two, moe_gain, moe_in_grad)
    branch_low = resid_grad.astype(jnp.bfloat16)
    out_proj_term = jnp.dot(attn_low.T, branch_low, preferred_element_type=jnp.float32)
    attn_back = jnp.dot(branch_low, wo_full.T, preferred_element_type=jnp.float32).astype(
        jnp.bfloat16
    )
    back_heads = attn_back.reshape(tok_rows, HEADS, HEAD_DIM)
    row_delta = jnp.sum(back_heads.astype(jnp.float32) * attn_sum, axis=2).T

    def back_step(query_acc, block_index):
        key_mask = block_mask(block_index)
        keys_blk = fetch_block(keys_all, block_index)
        values_blk = fetch_block(values_all, block_index)

        def back_live_block(running):
            prob_low, score_low = grad_pieces(
                query_heads,
                back_heads,
                keys_blk,
                values_blk,
                log_norm,
                row_delta,
                key_mask,
                score_scale,
            )
            value_part = jnp.einsum(
                "hqk,qhd->khd", prob_low, back_heads, preferred_element_type=jnp.float32
            )
            key_part = (
                jnp.einsum(
                    "hqk,qhd->khd", score_low, query_heads, preferred_element_type=jnp.float32
                )
                * score_scale
            )
            running = (
                running
                + jnp.einsum(
                    "hqk,khd->qhd", score_low, keys_blk, preferred_element_type=jnp.float32
                )
                * score_scale
            )
            return (
                running,
                (
                    key_part.reshape(key_block, model_width),
                    value_part.reshape(key_block, model_width),
                ),
            )

        def dead_block(running):
            empty_rows = jnp.zeros((key_block, model_width), jnp.float32)
            return (running, (empty_rows, empty_rows))

        return lax.cond(jnp.any(key_mask), back_live_block, dead_block, query_acc)

    query_grad32, key_terms = lax.scan(back_step, zero_heads, jnp.arange(num_blocks))
    key_grad32, value_grad32 = (
        lax.psum_scatter(
            key_terms[0].reshape(group_len, model_width).astype(jnp.bfloat16),
            ("expert", "shard"),
            scatter_dimension=0,
            tiled=True,
        ).astype(jnp.float32),
        lax.psum_scatter(
            key_terms[1].reshape(group_len, model_width).astype(jnp.bfloat16),
            ("expert", "shard"),
            scatter_dimension=0,
            tiled=True,
        ).astype(jnp.float32),
    )
    query_low = query_grad32.reshape(tok_rows, model_width).astype(jnp.bfloat16)
    key_low = key_grad32.astype(jnp.bfloat16)
    value_low = value_grad32.astype(jnp.bfloat16)
    query_term = jnp.dot(attn_in.T, query_low, preferred_element_type=jnp.float32)
    key_term = jnp.dot(attn_in.T, key_low, preferred_element_type=jnp.float32)
    value_term = jnp.dot(attn_in.T, value_low, preferred_element_type=jnp.float32)
    attn_in_grad = (
        jnp.dot(query_low, wq_full.T, preferred_element_type=jnp.float32)
        + jnp.dot(key_low, wk_full.T, preferred_element_type=jnp.float32)
        + jnp.dot(value_low, wv_full.T, preferred_element_type=jnp.float32)
    )
    attn_gain_grad = jnp.sum(attn_in_grad * normed_one, axis=0)
    input_grad = resid_grad + rms_back(inputs, inv_one, attn_gain, attn_in_grad)
    query_part, key_part_w, value_part_w, out_part = (
        lax.psum_scatter(
            query_term.astype(jnp.bfloat16), ("expert", "shard"), scatter_dimension=0, tiled=True
        ).astype(jnp.float32),
        lax.psum_scatter(
            key_term.astype(jnp.bfloat16), ("expert", "shard"), scatter_dimension=0, tiled=True
        ).astype(jnp.float32),
        lax.psum_scatter(
            value_term.astype(jnp.bfloat16), ("expert", "shard"), scatter_dimension=0, tiled=True
        ).astype(jnp.float32),
        lax.psum_scatter(
            out_proj_term.astype(jnp.bfloat16), ("expert", "shard"), scatter_dimension=0, tiled=True
        ).astype(jnp.float32),
    )
    gate_part, up_part, down_part = (
        lax.psum_scatter(
            gate_term.astype(jnp.bfloat16), "shard", scatter_dimension=1, tiled=True
        ).astype(jnp.float32),
        lax.psum_scatter(
            up_term.astype(jnp.bfloat16), "shard", scatter_dimension=1, tiled=True
        ).astype(jnp.float32),
        lax.psum_scatter(
            down_term.astype(jnp.bfloat16), "shard", scatter_dimension=1, tiled=True
        ).astype(jnp.float32),
    )
    summed = (
        lax.psum(query_part.astype(jnp.bfloat16), "group").astype(jnp.float32),
        lax.psum(key_part_w.astype(jnp.bfloat16), "group").astype(jnp.float32),
        lax.psum(value_part_w.astype(jnp.bfloat16), "group").astype(jnp.float32),
        lax.psum(out_part.astype(jnp.bfloat16), "group").astype(jnp.float32),
        lax.psum(gate_part.astype(jnp.bfloat16), "group").astype(jnp.float32),
        lax.psum(up_part.astype(jnp.bfloat16), "group").astype(jnp.float32),
        lax.psum(down_part.astype(jnp.bfloat16), "group").astype(jnp.float32),
    )
    small_sums = lax.psum(
        (attn_gain_grad, moe_gain_grad, router_grad, mix_grad, vec_grad),
        ("group", "expert", "shard"),
    )
    return (
        layer_out,
        input_grad,
        small_sums[0],
        summed[0],
        summed[1],
        summed[2],
        summed[3],
        small_sums[1],
        small_sums[2],
        small_sums[3],
        small_sums[4],
        summed[4],
        summed[5],
        summed[6],
    )


def solution(mesh):
    placed = (
        P(("group", "expert", "shard"), None),
        P("group", None),
        P(("group", "expert", "shard"), None),
        P(),
        P("shard", None),
        P("shard", None),
        P("shard", None),
        P("shard", None),
        P(),
        P(),
        P(),
        P(),
        P("expert", None, None),
        P("expert", None, None),
        P("expert", None, None),
        P(("group", "expert", "shard"), None),
    )
    return jax.shard_map(
        shards,
        mesh=mesh,
        in_specs=placed,
        out_specs=(
            P(("group", "expert", "shard"), None),
            P(("group", "expert", "shard"), None),
            P(),
            P(("expert", "shard"), None),
            P(("expert", "shard"), None),
            P(("expert", "shard"), None),
            P(("expert", "shard"), None),
            P(),
            P(),
            P(),
            P(),
            P("expert", "shard", None),
            P("expert", "shard", None),
            P("expert", "shard", None),
        ),
        check_vma=False,
    )
```

profile of v0, /device:TPU:0, one launch (start us, length us, event | category | flops | bytes accessed | tf_op | source)
XLA Modules:
  0.0 1070.2 jit_solution(17542057378038829399)
XLA Ops:
  11.2 18.6 %all-gather.11.cloned.1.call-done = bf16[768,768]{1,0:T(8,128)(2,1)} async-done(((bf16[192,768]{1,0:T(8,128)(2,1)}), bf16[768,768]{1,0:T(8,128)(2,1)}) %all-gather.11.cloned.1.call-update) | async-done | bytes 1179664 | tf_op jit(solution)/shard_map/all_gather | solution.py:76
  29.8 2.5 convolution_convert_fusion.6
  32.4 16.4 %all-gather.7.cloned.1.call-done = bf16[768,768]{1,0:T(8,128)(2,1)} async-done(((bf16[192,768]{1,0:T(8,128)(2,1)}), bf16[768,768]{1,0:T(8,128)(2,1)}) %all-gather.7.cloned.1.call-update) | async-done | bytes 1179664 | tf_op jit(solution)/shard_map/all_gather | solution.py:77
  48.8 2.4 convolution_convert_fusion.7
  65.9 3.5 scatter_custom_fusion.1
  69.4 2.1 scatter_custom_fusion
  76.5 3.1 gather_fusion.3
  79.7 2.4 convolution_convert_fusion.5
  83.3 40.4 %all-gather.13.cloned.1.call-done = bf16[3072,768]{1,0:T(8,128)(2,1)} async-done(((bf16[192,768]{1,0:T(8,128)(2,1)}), bf16[3072,768]{1,0:T(8,128)(2,1)}) %all-gather.13.cloned.1.call-update) | async-done | bytes 4718608 | tf_op jit(solution)/shard_map/all_gather | solution.py:88
  123.7 6.6 copy.179
  131.5 39.2 %while.45 = (s32[]{:T(128)}, f32[12,192]{1,0:T(8,128)S(1)}, f32[12,192]{1,0:T(8,128)}, s32[6]{0:T(128)}, s32[3072]{0:T(1024)}, /*index=5*/s32[192]{0:T(256)}, bf...) while((s32[]{:T(128)}, f32[12,192]{1,0:T(8,128)S(1)}, ...), condition=%wide.region_7.8_spmd.clone, body=%wide.region_1.7_spmd.clone.sunk | while | flops 160929472 | bytes 12987055 | solution.py:123
  134.1 2.1 fusion.174
  136.9 6.1 conditional.9
  138.8 2.0 fusion.6
  145.8 2.1 fusion.174
  151.3 2.1 fusion.174
  156.8 2.1 fusion.174
  162.3 2.1 fusion.174
  167.8 2.1 fusion.174
  172.0 6.2 all-gather.9.cloned.1.call-done
  178.1 6.7 copy.178
  185.8 32.8 %while.46 = (s32[]{:T(128)}, f32[192,12,64]{0,2,1:T(8,128)}, s32[6]{0:T(128)S(1)}, s32[3072]{0:T(1024)}, s32[192]{0:T(256)S(1)}, /*index=5*/bf16[3072,768]{0,1:T...) while((s32[]{:T(128)}, f32[192,12,64]{0,2,1:T(8,128)}, ...), condition=%wide.region_12.13_spmd.clone, body=%wide.region_8.12_spmd.clone.sunk | while | flops 307348672 | bytes 6412875 | solution.py:149
  189.9 7.8 conditional.10
  190.6 2.6 constant_dynamic-slice_fusion.1
  193.2 4.5 fusion.19
  218.6 1.9 convert_element_type.207
  220.6 2.0 multiply_reduce_fusion.8
  233.8 2.3 gather_fusion.2
  237.4 3.0 gather_fusion
  240.5 2.1 fusion.88
  242.5 38.5 %all-to-all-start = ((bf16[4,48,768]{2,1,0:T(8,128)(2,1)}), bf16[4,48,768]{2,1,0:T(8,128)(2,1)}, u32[]{:S(2)}, u32[]{:S(2)}) async-start(bf16[4,48,768]{2,1,0:T(8,128)(2,1)} %get-tuple-element.772), calls=%async_computation | async-start | bytes 589824 | tf_op jit(solution)/shard_map/all_to_all | solution.py:191
  281.0 2.3 fusion.116
  288.1 4.4 all-to-all-start.2
  304.7 3.9 fusion.54
  308.6 3.3 fusion.57
  311.9 3.7 multiply_convert_fusion.1
  318.0 5.1 all-to-all-start.1
  323.1 3.4 fusion.40
  330.3 4.1 all-to-all-start.3
  335.4 2.4 gather_fusion.1
  338.6 10.5 multiply_reduce_fusion.1
  351.7 2.2 gather_fusion.4
  354.5 2.3 reduce_sum.246
  357.0 2.0 convolution_add_fusion.4
  363.9 44.8 %while.47 = (s32[]{:T(128)}, f32[192,12,64]{0,2,1:T(8,128)S(1)}, bf16[6,512,768]{2,1,0:T(8,128)(2,1)}, bf16[6,512,768]{2,1,0:T(8,128)(2,1)}, s32[6]{0:T(128)S(1)...) while((s32[]{:T(128)}, f32[192,12,64]{0,2,1:T(8,128)S(1)}, ...), condition=%wide.region_43.44_spmd.clone, body=%wide.region_39.43_spmd.clone.sunk | while | flops 768345280 | bytes 38945488 | solution.py:359
  368.5 7.8 conditional.11
  368.5 2.2 constant_dynamic-slice_fusion.3
  413.3 3.6 fusion.50
  418.1 3.7 fusion.48
  422.9 3.7 fusion.49
  426.7 103.1 %reduce-scatter.12.cloned.1.call-done = bf16[192,768]{1,0:T(8,128)(2,1)} async-done(((bf16[3072,768]{1,0:T(8,128)(2,1)}), bf16[192,768]{1,0:T(8,128)(2,1)}) %reduce-scatter.12.cloned.1.call-update) | async-done | bytes 294928 | tf_op jit(solution)/shard_map/reduce_scatter | solution.py:367
  529.8 2.6 convolution_convert_fusion.1
  532.4 76.0 %reduce-scatter.10.cloned.1.call-done = bf16[192,768]{1,0:T(8,128)(2,1)} async-done(((bf16[3072,768]{1,0:T(8,128)(2,1)}), bf16[192,768]{1,0:T(8,128)(2,1)}) %reduce-scatter.10.cloned.1.call-update) | async-done | bytes 294928 | tf_op jit(solution)/shard_map/reduce_scatter | solution.py:361
  608.4 2.6 convolution_convert_fusion.2
  611.3 58.2 %reduce-scatter.20.cloned.1.call-done = bf16[48,768]{1,0:T(8,128)(2,1)} async-done(((bf16[768,768]{1,0:T(8,128)(2,1)}), bf16[48,768]{1,0:T(8,128)(2,1)}) %reduce-scatter.20.cloned.1.call-update) | async-done | bytes 73744 | tf_op jit(solution)/shard_map/reduce_scatter | solution.py:397
  669.5 61.2 %reduce-scatter.14.cloned.1.call-done = bf16[48,768]{1,0:T(8,128)(2,1)} async-done(((bf16[768,768]{1,0:T(8,128)(2,1)}), bf16[48,768]{1,0:T(8,128)(2,1)}) %reduce-scatter.14.cloned.1.call-update) | async-done | bytes 73744 | tf_op jit(solution)/shard_map/reduce_scatter | solution.py:388
  730.6 39.5 %reduce-scatter.26.cloned.1.call-done = bf16[1,512,768]{2,1,0:T(8,128)(2,1)} async-done(((bf16[1,2048,768]{2,1,0:T(8,128)(2,1)}), bf16[1,512,768]{2,1,0:T(8,128)(2,1)}) %reduce-scatter.26.cloned.1.call-update) | async-done | bytes 786448 | tf_op jit(solution)/shard_map/reduce_scatter | solution.py:408
  770.2 40.3 %reduce-scatter.22.cloned.1.call-done = bf16[1,192,2048]{2,1,0:T(8,128)(2,1)} async-done(((bf16[1,768,2048]{2,1,0:T(8,128)(2,1)}), bf16[1,192,2048]{2,1,0:T(8,128)(2,1)}) %reduce-scatter.22.cloned.1.call-update) | async-done | bytes 786448 | tf_op jit(solution)/shard_map/reduce_scatter | solution.py:402
  810.5 40.5 %reduce-scatter.24.cloned.1.call-done = bf16[1,192,2048]{2,1,0:T(8,128)(2,1)} async-done(((bf16[1,768,2048]{2,1,0:T(8,128)(2,1)}), bf16[1,192,2048]{2,1,0:T(8,128)(2,1)}) %reduce-scatter.24.cloned.1.call-update) | async-done | bytes 786448 | tf_op jit(solution)/shard_map/reduce_scatter | solution.py:405
  850.9 62.2 %reduce-scatter.18.cloned.1.call-done = bf16[48,768]{1,0:T(8,128)(2,1)} async-done(((bf16[768,768]{1,0:T(8,128)(2,1)}), bf16[48,768]{1,0:T(8,128)(2,1)}) %reduce-scatter.18.cloned.1.call-update) | async-done | bytes 73744 | tf_op jit(solution)/shard_map/reduce_scatter | solution.py:394
  913.2 61.3 %reduce-scatter.16.cloned.1.call-done = bf16[48,768]{1,0:T(8,128)(2,1)} async-done(((bf16[768,768]{1,0:T(8,128)(2,1)}), bf16[48,768]{1,0:T(8,128)(2,1)}) %reduce-scatter.16.cloned.1.call-update) | async-done | bytes 73744 | tf_op jit(solution)/shard_map/reduce_scatter | solution.py:391
  978.9 42.0 %all-reduce.2 = (f32[768]{0:T(1024)}, f32[768]{0:T(1024)}, f32[768,8]{0,1:T(8,128)}, f32[768,4]{0,1:T(4,128)}, f32[2,768]{1,0:T(2,128)}) all-reduce(f32[768]{0:T(1024)S(1)} %get-tuple-element.641, f32[768]{0:T(1024)S(1)} %copy-done.66, ...), channel_id=1, replica_groups=mesh['group'=2,'expert'=4,'shard'=4] {'group','expert','shard'}, use_global_device_ids=true, to_apply=%region_48.49 | all-reduce | flops 12288 | bytes 98304 | tf_op jit(solution)/shard_map/psum | solution.py:421
  1021.9 30.1 %all-reduce.6.cloned.1.call-done = (bf16[48,768]{1,0:T(8,128)(2,1)}, bf16[48,768]{1,0:T(8,128)(2,1)}, bf16[48,768]{1,0:T(8,128)(2,1)}, bf16[48,768]{1,0:T(8,128)...) async-done(((bf16[48,768]{1,0:T(8,128)(2,1)}, bf16[48,768]{1,0:T(8,128)(2,1)}, bf16[48,768]{1,0:T(8,128)(2,1)}, ...) | async-done | bytes 2654224 | tf_op jit(solution)/shard_map/psum | solution.py:413
  1058.3 2.5 convert_element_type.243
  (433 shorter events, 161.8 us)
Async XLA Ops:
  7.2 304.7 %copy-start = (bf16[1,768,2048]{2,1,0:T(8,128)(2,1)S(1)}, bf16[1,768,2048]{2,1,0:T(8,128)(2,1)}, u32[]{:S(2)}) copy-start(bf16[1,768,2048]{2,1,0:T(8,128)(2,1)} %param.40) | copy-start | bytes 9437188
  7.2 41.6 %copy-start.7 = (bf16[192,768]{1,0:T(8,128)(2,1)S(1)}, bf16[192,768]{1,0:T(8,128)(2,1)}, u32[]{:S(2)}) copy-start(bf16[192,768]{1,0:T(8,128)(2,1)} %param.28) | copy-start | bytes 884740
  7.2 41.6 %copy-start.43 = (f32[768]{0:T(1024)S(1)}, f32[768]{0:T(1024)}, u32[]{:S(2)}) copy-start(f32[768]{0:T(1024)} %param.31) | copy-start | bytes 9220
  7.2 22.6 %all-gather.11.cloned.1.call-start = ((), (), s32[]{:S(2)}) async-start(), calls=%async_computation.15 | async-start | bytes 1474560 | tf_op jit(solution)/shard_map/all_gather | solution.py:76
  8.0 40.9 %all-gather.7.cloned.1.call-start = ((), (), s32[]{:S(2)}) async-start(), calls=%async_computation.13 | async-start | bytes 1474560 | tf_op jit(solution)/shard_map/all_gather | solution.py:77
  8.7 71.0 %all-gather.15.cloned.1.call-start = ((), (), s32[]{:S(2)}) async-start(), calls=%async_computation.17 | async-start | bytes 1474560 | tf_op jit(solution)/shard_map/all_gather | solution.py:75
  9.4 42.9 %copy-start.45 = (s32[192,2]{0,1:T(2,128)S(1)}, s32[192,2]{0,1:T(2,128)}, u32[]{:S(2)}) copy-start(s32[192,2]{0,1:T(2,128)} %param.30) | copy-start | bytes 4612
  9.4 114.2 %all-gather.13.cloned.1.call-start = ((), (), s32[]{:S(2)}) async-start(), calls=%async_computation.16 | async-start | bytes 5013504 | tf_op jit(solution)/shard_map/all_gather | solution.py:88
  11.2 42.0 %copy-start.54 = (f32[192]{0:T(256)}, f32[192]{0:T(256)S(1)}, u32[]{:S(2)}) copy-start(f32[192]{0:T(256)S(1)} %get-tuple-element.766) | copy-start | bytes 2308
  32.4 145.8 %all-gather.9.cloned.1.call-start = ((), (), s32[]{:S(2)}) async-start(), calls=%async_computation.14 | async-start | bytes 5013504 | tf_op jit(solution)/shard_map/all_gather | solution.py:89
  51.3 169.3 %all-gather.17.cloned.1.call-start = ((), (), s32[]{:S(2)}) async-start(), calls=%async_computation.18 | async-start | bytes 1474560 | tf_op jit(solution)/shard_map/all_gather | solution.py:78
  53.1 26.6 %copy-start.22 = (s32[192,2]{1,0:T(8,128)}, s32[192,2]{1,0:T(8,128)S(1)}, u32[]{:S(2)}) copy-start(s32[192,2]{1,0:T(8,128)S(1)} %copy.180) | copy-start | bytes 4612
  76.5 3.1 copy-start.70
  76.5 3.1 copy-start.55
  172.0 13.8 %copy-start.41 = (s32[192]{0:T(256)S(1)}, s32[192]{0:T(256)}, u32[]{:S(2)}) copy-start(s32[192]{0:T(256)} %get-tuple-element.1258) | copy-start | bytes 2308
  218.6 4.7 copy-start.42
  220.5 4.4 copy-start.47
  220.5 5.1 copy-start.23
  220.5 9.5 copy-start.46
  237.4 43.6 %copy-start.50 = (f32[192]{0:T(256)S(1)}, f32[192]{0:T(256)}, u32[]{:S(2)}) copy-start(f32[192]{0:T(256)} %copy-done.49) | copy-start | bytes 2308
  242.5 45.6 %all-to-all-start = ((bf16[4,48,768]{2,1,0:T(8,128)(2,1)}), bf16[4,48,768]{2,1,0:T(8,128)(2,1)}, u32[]{:S(2)}, u32[]{:S(2)}) async-start(bf16[4,48,768]{2,1,0:T(8,128)(2,1)} %get-tuple-element.772), calls=%async_computation | async-start | bytes 589824 | tf_op jit(solution)/shard_map/all_to_all | solution.py:191
  288.1 20.5 %all-to-all-start.2 = ((bf16[4,48,768]{2,1,0:T(8,128)(2,1)}), bf16[4,48,768]{2,1,0:T(8,128)(2,1)}, u32[]{:S(2)}, u32[]{:S(2)}) async-start(bf16[4,48,768]{2,1,0:T(8,128)(2,1)} %get-tuple-element.771), calls=%async_computation.2 | async-start | bytes 589824 | tf_op jit(solution)/shard_map/all_to_all | solution.py:254
  308.6 3.3 copy-start.21
  311.9 4.6 copy-start.16
  318.0 12.2 %all-to-all-start.1 = ((bf16[4,48,768]{2,1,0:T(8,128)(2,1)}), bf16[4,48,768]{2,1,0:T(8,128)(2,1)}, u32[]{:S(2)}, u32[]{:S(2)}) async-start(bf16[4,48,768]{2,1,0:T(8,128)(2,1)} %fusion.63), calls=%async_computation.1 | async-start | bytes 589824 | tf_op jit(solution)/shard_map/all_to_all | solution.py:206
  323.1 3.4 copy-start.34
  330.3 20.4 %all-to-all-start.3 = ((bf16[4,48,768]{2,1,0:T(8,128)(2,1)}), bf16[4,48,768]{2,1,0:T(8,128)(2,1)}, u32[]{:S(2)}, u32[]{:S(2)}) async-start(bf16[4,48,768]{2,1,0:T(8,128)(2,1)} %fusion.66), calls=%async_computation.3 | async-start | bytes 589824 | tf_op jit(solution)/shard_map/all_to_all | solution.py:280
  334.4 195.4 %reduce-scatter.12.cloned.1.call-start = ((), (), s32[]{:S(2)}) async-start(), calls=%async_computation.20 | async-start | bytes 5013504 | tf_op jit(solution)/shard_map/reduce_scatter | solution.py:367
  335.4 3.1 copy-start.2
  335.4 3.1 copy-start.20
  335.4 3.1 copy-start.31
  338.5 10.8 %copy-start.52 = (f32[192,2]{0,1:T(2,128)S(1)}, f32[192,2]{0,1:T(2,128)}, u32[]{:S(2)}) copy-start(f32[192,2]{0,1:T(2,128)} %reduce_max.28) | copy-start | bytes 4612
  338.5 10.8 %copy-start.62 = (f32[192,2]{0,1:T(2,128)S(1)}, f32[192,2]{0,1:T(2,128)}, u32[]{:S(2)}) copy-start(f32[192,2]{0,1:T(2,128)} %copy-done.61) | copy-start | bytes 4612
  338.5 11.0 %copy-start.75 = (s32[2]{0:T(128)S(1)}, s32[2]{0:T(128)}, u32[]{:S(2)}) copy-start(s32[2]{0:T(128)} %iota_add_fusion.6) | copy-start | bytes 28
  338.5 11.1 %copy-start.60 = (f32[192,2]{0,1:T(2,128)S(1)}, f32[192,2]{0,1:T(2,128)}, u32[]{:S(2)}) copy-start(f32[192,2]{0,1:T(2,128)} %get-tuple-element.746) | copy-start | bytes 4612
  338.5 11.1 %copy-start.74 = (f32[192]{0:T(256)S(1)}, f32[192]{0:T(256)}, u32[]{:S(2)}) copy-start(f32[192]{0:T(256)} %get-tuple-element.760) | copy-start | bytes 2308
  338.5 11.2 %copy-start.24 = (s32[192,2]{1,0:T(8,128)S(1)}, s32[192,2]{1,0:T(8,128)}, u32[]{:S(2)}) copy-start(s32[192,2]{1,0:T(8,128)} %copy-done.22) | copy-start | bytes 4612
  349.6 7.3 copy-start.71
  350.7 8.4 copy-start.39
  353.9 3.1 copy-start.13
  353.9 3.1 copy-start.53
  354.5 4.5 copy-start.4
  354.5 4.5 copy-start.48
  354.5 4.5 copy-start.51
  356.9 3.6 copy-start.18
  356.9 3.6 copy-start.19
  356.9 3.6 copy-start.73
  356.9 3.5 copy-start.58
  359.1 3.3 copy-start.14
  408.7 199.7 %reduce-scatter.10.cloned.1.call-start = ((), (), s32[]{:S(2)}) async-start(), calls=%async_computation.19 | async-start | bytes 5013504 | tf_op jit(solution)/shard_map/reduce_scatter | solution.py:361
  409.5 260.0 %reduce-scatter.20.cloned.1.call-start = ((), (), s32[]{:S(2)}) async-start(), calls=%async_computation.24 | async-start | bytes 1253376 | tf_op jit(solution)/shard_map/reduce_scatter | solution.py:397
  411.5 319.2 %reduce-scatter.14.cloned.1.call-start = ((), (), s32[]{:S(2)}) async-start(), calls=%async_computation.21 | async-start | bytes 1253376 | tf_op jit(solution)/shard_map/reduce_scatter | solution.py:388
  413.3 356.9 %reduce-scatter.26.cloned.1.call-start = ((), (), s32[]{:S(2)}) async-start(), calls=%async_computation.27 | async-start | bytes 3932160 | tf_op jit(solution)/shard_map/reduce_scatter | solution.py:408
  417.0 393.5 %reduce-scatter.22.cloned.1.call-start = ((), (), s32[]{:S(2)}) async-start(), calls=%async_computation.25 | async-start | bytes 3932160 | tf_op jit(solution)/shard_map/reduce_scatter | solution.py:402
  421.8 429.1 %reduce-scatter.24.cloned.1.call-start = ((), (), s32[]{:S(2)}) async-start(), calls=%async_computation.26 | async-start | bytes 3932160 | tf_op jit(solution)/shard_map/reduce_scatter | solution.py:405
  426.6 486.6 %reduce-scatter.18.cloned.1.call-start = ((), (), s32[]{:S(2)}) async-start(), calls=%async_computation.23 | async-start | bytes 1253376 | tf_op jit(solution)/shard_map/reduce_scatter | solution.py:394
  532.4 442.1 %reduce-scatter.16.cloned.1.call-start = ((), (), s32[]{:S(2)}) async-start(), calls=%async_computation.22 | async-start | bytes 1253376 | tf_op jit(solution)/shard_map/reduce_scatter | solution.py:391
  611.0 363.4 %copy-start.5 = (f32[192,768]{1,0:T(8,128)S(1)}, f32[192,768]{1,0:T(8,128)}, u32[]{:S(2)}) copy-start(f32[192,768]{1,0:T(8,128)} %copy-done.3) | copy-start | bytes 1769476
  611.0 363.4 %copy-start.59 = (f32[192,4]{0,1:T(4,128)S(1)}, f32[192,4]{0,1:T(4,128)}, u32[]{:S(2)}) copy-start(f32[192,4]{0,1:T(4,128)} %copy-done.58) | copy-start | bytes 9220
  611.0 364.0 %copy-start.40 = (f32[192,1,8]{2,1,0:T(1,128)S(1)}, f32[192,1,8]{2,1,0:T(1,128)}, u32[]{:S(2)}) copy-start(f32[192,1,8]{2,1,0:T(1,128)} %copy-done.39) | copy-start | bytes 18436
  611.1 441.0 %all-reduce.6.cloned.1.call-start = ((), (), s32[]{:S(2)}) async-start(), calls=%async_computation.28 | async-start | bytes 5308416 | tf_op jit(solution)/shard_map/psum | solution.py:413
  977.5 43.3 %copy-start.72 = (f32[192]{0:T(256)S(1)}, f32[192]{0:T(256)}, u32[]{:S(2)}) copy-start(f32[192]{0:T(256)} %get-tuple-element.765) | copy-start | bytes 2308
  1052.0 8.8 copy-start.37
  1058.3 3.9 copy-start.36
  (34 other events, 63.0 us)
Sparse Core Ops, SparseCore 0:
  9.6 20.1 all-gather.10
  31.3 17.4 all-gather.6
  50.4 17.4 all-gather.14
  70.5 53.1 all-gather.12
  126.4 51.6 all-gather.8
  179.5 15.9 all-gather.16
  408.9 120.8 reduce-scatter.11
  533.6 74.7 reduce-scatter.9
  612.1 57.3 reduce-scatter.19
  673.5 57.0 reduce-scatter.13
  733.2 36.9 reduce-scatter.25
  772.6 37.8 reduce-scatter.21
  813.0 37.8 reduce-scatter.23
  855.0 58.1 reduce-scatter.17
  917.2 57.1 reduce-scatter.15
  977.0 74.9 all-reduce.5
where the time goes:
time: 1080 us; the launch traced here: 1070 us
  waiting for transfers between devices  660 us (61%)
  other arithmetic  102 us (9%)
  local copies, waits for them, and re-layouts  101 us (9%)
  matrix products  70.3 us (7%)
  starting transfers between devices  52.9 us (5%)
  blocking collectives  42 us (4%)
  loops' own time  26.4 us (2%)
  between operations  15.1 us (1%)
    reduce_scatter x1, waiting for transfers between devices, shards(): lax.psum_scatter(key_terms[1].reshape(group_len, model_width).astype(jnp....  103 us
    reduce_scatter x1, waiting for transfers between devices, shards(): lax.psum_scatter(key_terms[0].reshape(group_len, model_width).astype(jnp....  76 us
    reduce_scatter x1, waiting for transfers between devices, shards(): lax.psum_scatter(value_term.astype(jnp.bfloat16), ('expert', 'shard'), sc...  62.2 us
    reduce_scatter x1, waiting for transfers between devices, shards(): lax.psum_scatter(key_term.astype(jnp.bfloat16), ('expert', 'shard'), scat...  61.3 us
    reduce_scatter x1, waiting for transfers between devices, shards(): lax.psum_scatter(query_term.astype(jnp.bfloat16), ('expert', 'shard'), sc...  61.2 us
    reduce_scatter x1, waiting for transfers between devices, shards(): lax.psum_scatter(out_proj_term.astype(jnp.bfloat16), ('expert', 'shard'),...  58.2 us
    psum x1, blocking collectives, shards(): lax.psum((attn_gain_grad, moe_gain_grad, router_grad, mix_grad, vec_grad)...  42 us
    reduce_scatter x1, waiting for transfers between devices, shards(): lax.psum_scatter(up_term.astype(jnp.bfloat16), 'shard', scatter_dimension...  40.5 us
  transfers between devices with their start and end apart: 20, of which 16 were waited for; matrix products, arithmetic and copies ran while one was open for 17% of the time, Pallas kernels for 0%

commit v1 on v0

--- a/solution.py
+++ b/solution.py
@@ -1,15 +1,33 @@
+import functools
+
 import jax
 import jax.numpy as jnp
 from jax import lax
+from jax.experimental import pallas as pl
+from jax.experimental.pallas import tpu as pltpu
 from jax.sharding import PartitionSpec as P
 
 HEADS = 12
 HEAD_DIM = 64
 CAP = 48
+KEY_BLK = 256
+EX, SH, GR = ("expert", "shard", "group")
+GATHER, GATHER_SUM, SWAP, SWAP_SUM = range(4)
 
 
 neg_fill = -1e30
 norm_eps = 1e-05
+bf16 = jnp.bfloat16
+f32 = jnp.float32
+VM = pl.BlockSpec(memory_space=pltpu.VMEM)
+SM = pl.BlockSpec(memory_space=pltpu.SMEM)
+HIGH = lax.Precision.HIGHEST
+
+
+def contract(a, b, da, db, precision=None):
+    return lax.dot_general(
+        a, b, (((da,), (db,)), ((), ())), preferred_element_type=f32, precision=precision
+    )
 
 
 def dense32(left_side, right_side):
@@ -63,7 +81,7 @@
 ):
     tok_rows, model_width = hidden_in.shape
     score_scale = HEAD_DIM ** (-0.5)
-    inner_rank = lax.axis_index(("expert", "shard"))
+    inner_rank = lax.axis_index((EX, SH))
     seg_group = segment_ids[0]
     group_len = seg_group.shape[0]
     key_block = min(512, group_len)
@@ -72,10 +90,10 @@
     own_pos = row_start + jnp.arange(tok_rows, dtype=jnp.int32)
     own_seg = lax.dynamic_slice_in_dim(seg_group, row_start, tok_rows)
     wq_full, wk_full, wv_full, wo_full = (
-        lax.all_gather(w_query, "shard", axis=0, tiled=True),
-        lax.all_gather(w_key, "shard", axis=0, tiled=True),
-        lax.all_gather(w_value, "shard", axis=0, tiled=True),
-        lax.all_gather(w_out, "shard", axis=0, tiled=True),
+        lax.all_gather(w_query, SH, axis=0, tiled=True),
+        lax.all_gather(w_key, SH, axis=0, tiled=True),
+        lax.all_gather(w_value, SH, axis=0, tiled=True),
+        lax.all_gather(w_out, SH, axis=0, tiled=True),
     )
     inputs = hidden_in.astype(jnp.float32)
     inv_one = lax.rsqrt(jnp.mean(inputs * inputs, axis=1, keepdims=True) + norm_eps)
@@ -85,8 +103,8 @@
     keys_own = jnp.dot(attn_in, wk_full, preferred_element_type=jnp.float32).astype(jnp.bfloat16)
     values_own = jnp.dot(attn_in, wv_full, preferred_element_type=jnp.float32).astype(jnp.bfloat16)
     keys_all, values_all = (
-        lax.all_gather(keys_own, ("expert", "shard"), axis=0, tiled=True),
-        lax.all_gather(values_own, ("expert", "shard"), axis=0, tiled=True),
+        lax.all_gather(keys_own, (EX, SH), axis=0, tiled=True),
+        lax.all_gather(values_own, (EX, SH), axis=0, tiled=True),
     )
     query_heads = queries.reshape(tok_rows, HEADS, HEAD_DIM)
 
@@ -155,7 +173,7 @@
     moe_low = moe_in.astype(jnp.bfloat16)
     n_ids = w_router.shape[1]
     local_experts = w_gate.shape[0]
-    owners = lax.axis_size("expert")
+    owners = lax.axis_size(EX)
     ffn_count = local_experts * owners
     id_table = jnp.arange(n_ids, dtype=jnp.int32)
     route_hot = (routes[:, :, None] == id_table).astype(jnp.float32)
@@ -190,7 +208,7 @@
     )
     recv_rows = lax.all_to_all(
         send_rows.reshape(owners, local_experts * CAP, model_width),
-        "expert",
+        EX,
         split_axis=0,
         concat_axis=0,
         tiled=True,
@@ -205,7 +223,7 @@
     ).astype(jnp.bfloat16)
     returned = lax.all_to_all(
         expert_out.reshape(owners, local_experts * CAP, model_width),
-        "expert",
+        EX,
         split_axis=0,
         concat_axis=0,
         tiled=True,
@@ -253,7 +271,7 @@
     grad_send = jnp.where(slot_used[:, None], grad_send, jnp.zeros((), jnp.bfloat16))
     grad_recv = lax.all_to_all(
         grad_send.reshape(owners, local_experts * CAP, model_width),
-        "expert",
+        EX,
         split_axis=0,
         concat_axis=0,
         tiled=True,
@@ -279,7 +297,7 @@
     ).astype(jnp.bfloat16)
     input_ret = lax.all_to_all(
         input_back.reshape(owners, local_experts * CAP, model_width),
-        "expert",
+        EX,
         split_axis=0,
         concat_axis=0,
         tiled=True,
@@ -360,13 +378,13 @@
     key_grad32, value_grad32 = (
         lax.psum_scatter(
             key_terms[0].reshape(group_len, model_width).astype(jnp.bfloat16),
-            ("expert", "shard"),
+            (EX, SH),
             scatter_dimension=0,
             tiled=True,
         ).astype(jnp.float32),
         lax.psum_scatter(
             key_terms[1].reshape(group_len, model_width).astype(jnp.bfloat16),
-            ("expert", "shard"),
+            (EX, SH),
             scatter_dimension=0,
             tiled=True,
         ).astype(jnp.float32),
@@ -386,41 +404,41 @@
     input_grad = resid_grad + rms_back(inputs, inv_one, attn_gain, attn_in_grad)
     query_part, key_part_w, value_part_w, out_part = (
         lax.psum_scatter(
-            query_term.astype(jnp.bfloat16), ("expert", "shard"), scatter_dimension=0, tiled=True
+            query_term.astype(jnp.bfloat16), (EX, SH), scatter_dimension=0, tiled=True
         ).astype(jnp.float32),
         lax.psum_scatter(
-            key_term.astype(jnp.bfloat16), ("expert", "shard"), scatter_dimension=0, tiled=True
+            key_term.astype(jnp.bfloat16), (EX, SH), scatter_dimension=0, tiled=True
         ).astype(jnp.float32),
         lax.psum_scatter(
-            value_term.astype(jnp.bfloat16), ("expert", "shard"), scatter_dimension=0, tiled=True
+            value_term.astype(jnp.bfloat16), (EX, SH), scatter_dimension=0, tiled=True
         ).astype(jnp.float32),
         lax.psum_scatter(
-            out_proj_term.astype(jnp.bfloat16), ("expert", "shard"), scatter_dimension=0, tiled=True
+            out_proj_term.astype(jnp.bfloat16), (EX, SH), scatter_dimension=0, tiled=True
         ).astype(jnp.float32),
     )
     gate_part, up_part, down_part = (
         lax.psum_scatter(
-            gate_term.astype(jnp.bfloat16), "shard", scatter_dimension=1, tiled=True
+            gate_term.astype(jnp.bfloat16), SH, scatter_dimension=1, tiled=True
         ).astype(jnp.float32),
         lax.psum_scatter(
-            up_term.astype(jnp.bfloat16), "shard", scatter_dimension=1, tiled=True
+            up_term.astype(jnp.bfloat16), SH, scatter_dimension=1, tiled=True
         ).astype(jnp.float32),
         lax.psum_scatter(
-            down_term.astype(jnp.bfloat16), "shard", scatter_dimension=1, tiled=True
+            down_term.astype(jnp.bfloat16), SH, scatter_dimension=1, tiled=True
         ).astype(jnp.float32),
     )
     summed = (
-        lax.psum(query_part.astype(jnp.bfloat16), "group").astype(jnp.float32),
-        lax.psum(key_part_w.astype(jnp.bfloat16), "group").astype(jnp.float32),
-        lax.psum(value_part_w.astype(jnp.bfloat16), "group").astype(jnp.float32),
-        lax.psum(out_part.astype(jnp.bfloat16), "group").astype(jnp.float32),
-        lax.psum(gate_part.astype(jnp.bfloat16), "group").astype(jnp.float32),
-        lax.psum(up_part.astype(jnp.bfloat16), "group").astype(jnp.float32),
-        lax.psum(down_part.astype(jnp.bfloat16), "group").astype(jnp.float32),
+        lax.psum(query_part.astype(jnp.bfloat16), GR).astype(jnp.float32),
+        lax.psum(key_part_w.astype(jnp.bfloat16), GR).astype(jnp.float32),
+        lax.psum(value_part_w.astype(jnp.bfloat16), GR).astype(jnp.float32),
+        lax.psum(out_part.astype(jnp.bfloat16), GR).astype(jnp.float32),
+        lax.psum(gate_part.astype(jnp.bfloat16), GR).astype(jnp.float32),
+        lax.psum(up_part.astype(jnp.bfloat16), GR).astype(jnp.float32),
+        lax.psum(down_part.astype(jnp.bfloat16), GR).astype(jnp.float32),
     )
     small_sums = lax.psum(
         (attn_gain_grad, moe_gain_grad, router_grad, mix_grad, vec_grad),
-        ("group", "expert", "shard"),
+        (GR, EX, SH),
     )
     return (
         layer_out,
@@ -440,44 +458,669 @@
     )
 
 
+def greet(peers):
+    barrier = pltpu.get_barrier_semaphore()
+    for axis, peer in peers:
+        pl.semaphore_signal(
+            barrier, inc=1, device_id={axis: peer}, device_id_type=pl.DeviceIdType.MESH
+        )
+    pl.semaphore_wait(barrier, len(peers))
+
+
+def send(src, dst, sems, index, axis, peer):
+    copy = pltpu.make_async_remote_copy(
+        src_ref=src,
+        dst_ref=dst,
+        send_sem=sems.at[0, index],
+        recv_sem=sems.at[1, index],
+        device_id={axis: peer},
+        device_id_type=pl.DeviceIdType.MESH,
+    )
+    copy.start()
+    return copy
+
+
+def comm_call(body, name, collective_id, out_shapes, scratch, copies, operands):
+    return pl.pallas_call(
+        body,
+        out_shape=out_shapes,
+        in_specs=[VM] * len(operands),
+        out_specs=[VM] * len(out_shapes),
+        scratch_shapes=list(scratch) + [pltpu.SemaphoreType.DMA((2, copies))],
+        compiler_params=pltpu.CompilerParams(collective_id=collective_id, has_side_effects=True),
+        name=name,
+    )(*operands)
+
+
+def exchange(parts, collective_id, name):
+    sizes = [lax.axis_size(axis) for axis, _, _ in parts]
+    count = len(parts)
+    out_shapes, scratch = [], []
+    for (axis, kind, x), n in zip(parts, sizes):
+        piece = x.shape if kind in (GATHER, GATHER_SUM) else x.shape[1:]
+        if kind in (GATHER_SUM, SWAP_SUM):
+            out_shapes.append(jax.ShapeDtypeStruct(piece, f32))
+            scratch.append(pltpu.VMEM((n,) + piece, x.dtype))
+        else:
+            out_shapes.append(jax.ShapeDtypeStruct((n,) + piece, x.dtype))
+    copies = sum(n - 1 for n in sizes)
+
+    def body(*refs):
+        ins, outs = refs[:count], refs[count : 2 * count]
+        lands, sems = list(refs[2 * count : -1]), refs[-1]
+        peers, seen = [], set()
+        for (axis, _, _), n in zip(parts, sizes):
+            if axis not in seen:
+                seen.add(axis)
+                me = lax.axis_index(axis)
+                peers += [(axis, lax.rem(me + d, n)) for d in range(1, n)]
+        greet(peers)
+        started, index, slots = [], 0, []
+        for k, ((axis, kind, _), n) in enumerate(zip(parts, sizes)):
+            land = lands.pop(0) if kind in (GATHER_SUM, SWAP_SUM) else outs[k]
+            slots.append(land)
+            me = lax.axis_index(axis)
+            for d in range(1, n):
+                peer = lax.rem(me + d, n)
+                src = ins[k] if kind in (GATHER, GATHER_SUM) else ins[k].at[peer]
+                started.append(send(src, land.at[me], sems, index, axis, peer))
+                index += 1
+        for k, ((axis, kind, _), n) in enumerate(zip(parts, sizes)):
+            me = lax.axis_index(axis)
+            own = ins[k][...] if kind in (GATHER, GATHER_SUM) else ins[k][me]
+            slots[k][me] = own
+        index = 0
+        for k, ((axis, kind, _), n) in enumerate(zip(parts, sizes)):
+            for d in range(1, n):
+                started[index].wait()
+                index += 1
+            if kind in (GATHER_SUM, SWAP_SUM):
+                total = slots[k][0].astype(f32)
+                for j in range(1, n):
+                    total = total + slots[k][j].astype(f32)
+                outs[k][...] = total
+
+    return comm_call(
+        body, name, collective_id, out_shapes, scratch, copies, [x for _, _, x in parts]
+    )
+
+
+def tree_gather(x, collective_id, name):
+    lines = x.shape[0]
+    half = lines // 2
+
+    def body(x_ref, out_ref, sems):
+        me = lax.axis_index(SH)
+        near, far = lax.rem(me + 1, 2) + 2 * (me // 2), lax.rem(me + 2, 4)
+        greet([(SH, near), (SH, far)])
+        lo, hi = pl.ds(0, half), pl.ds(half, half)
+        far_lo = send(x_ref.at[lo], out_ref.at[lo, me], sems, 0, SH, far)
+        far_hi = send(x_ref.at[hi], out_ref.at[hi, me], sems, 1, SH, far)
+        own = send(x_ref, out_ref.at[:, me], sems, 2, SH, near)
+        out_ref[:, me] = x_ref[...]
+        far_lo.wait_recv()
+        pass_lo = send(out_ref.at[lo, far], out_ref.at[lo, far], sems, 3, SH, near)
+        far_hi.wait_recv()
+        pass_hi = send(out_ref.at[hi, far], out_ref.at[hi, far], sems, 4, SH, near)
+        far_lo.wait_send()
+        far_hi.wait_send()
+        own.wait()
+        pass_lo.wait()
+        pass_hi.wait()
+
+    shape = (lines, 4) + x.shape[1:]
+    return comm_call(
+        body, name, collective_id, [jax.ShapeDtypeStruct(shape, x.dtype)], [], 5, [x]
+    )[0]
+
+
+def tree_reduce(arrays, collective_id, name):
+    count = len(arrays)
+    scratch = []
+    for x in arrays:
+        scratch += [pltpu.VMEM((2,) + x.shape[1:], bf16)] + [pltpu.VMEM(x.shape[1:], bf16)] * 2
+
+    def body(*refs):
+        ins, outs = refs[:count], refs[count : 2 * count]
+        sems = refs[-1]
+        me = lax.axis_index(SH)
+        side, core = me // 2, lax.rem(me, 2)
+        near, far = 2 * side + 1 - core, 2 * (1 - side) + core
+        other = 1 - side
+        greet([(SH, near), (SH, far)])
+        first = []
+        for k in range(count):
+            land = refs[2 * count + 3 * k]
+            first.append(
+                (
+                    send(
+                        ins[k].at[2 * other + 1 - core], land.at[0], sems, 3 * k, SH, near
+                    ),
+                    send(
+                        ins[k].at[2 * side + 1 - core], land.at[1], sems, 3 * k + 1, SH, near
+                    ),
+                )
+            )
+        second = []
+        for k in range(count):
+            land, mine, got = refs[2 * count + 3 * k : 2 * count + 3 * k + 3]
+            first[k][0].wait_recv()
+            mine[...] = (ins[k][far].astype(f32) + land[0].astype(f32)).astype(bf16)
+            second.append(send(mine, got, sems, 3 * k + 2, SH, far))
+        for k in range(count):
+            land, mine, got = refs[2 * count + 3 * k : 2 * count + 3 * k + 3]
+            first[k][1].wait_recv()
+            outs[k][...] = ins[k][me].astype(f32) + land[1].astype(f32)
+        for k in range(count):
+            got = refs[2 * count + 3 * k + 2]
+            second[k].wait_recv()
+            outs[k][...] += got[...].astype(f32)
+            first[k][0].wait_send()
+            first[k][1].wait_send()
+            second[k].wait_send()
+
+    return comm_call(
+        body,
+        name,
+        collective_id,
+        [jax.ShapeDtypeStruct(x.shape[1:], f32) for x in arrays],
+        scratch,
+        3 * count,
+        arrays,
+    )
+
+
+def head_columns(h, shape, axis):
+    return lax.broadcasted_iota(jnp.int32, shape, axis) // HEAD_DIM == h
+
+
+def allowed(block, key_blk, qpos, qstart, prompt):
+    kpos = block * key_blk + lax.broadcasted_iota(jnp.int32, (key_blk, qpos.shape[1]), 0)
+    return (kpos <= qpos) & ((kpos >= qstart) | (kpos < prompt))
+
+
+def attend_body(lines, heads, info_ref, q_ref, kv_ref, qinfo_ref, o_ref, low_ref, lse_ref, k_s, vt_s, acc_s, ml_s, qm_s):
+    shard = lax.axis_index(SH)
+    rows, width = q_ref.shape[1:]
+    blocks = vt_s.shape[0]
+    key_blk = vt_s.shape[2]
+    prompt = info_ref[0]
+
+    @pl.loop(0, blocks)
+    def _(j):
+        at = pl.ds(pl.multiple_of(j * key_blk, key_blk), key_blk)
+        k_s[at, :] = kv_ref[at, :width]
+        vt_s[j] = jnp.transpose(kv_ref[at, width:].astype(f32)).astype(bf16)
+
+    @pl.loop(0, lines)
+    def _(line):
+        start = (line * 4 + shard) * rows
+        queries = q_ref[line].astype(f32) * HEAD_DIM**-0.5
+        qpos = start + lax.broadcasted_iota(jnp.int32, (1, rows), 1)
+        qstart = qinfo_ref[line, 0:1, :]
+        first = info_ref[1 + line]
+        for h in range(heads):
+            qm_s[h] = jnp.where(head_columns(h, queries.shape, 1), queries, 0.0).astype(bf16)
+        acc_s[...] = jnp.zeros_like(acc_s)
+        for h in range(heads):
+            ml_s[h, 0:1, :] = jnp.full((1, rows), neg_fill, f32)
+            ml_s[h, 1:2, :] = jnp.zeros((1, rows), f32)
+
+        @pl.loop(0, (start + rows + key_blk - 1) // key_blk)
+        def _(j):
+            @pl.when((j * key_blk < prompt) | ((j + 1) * key_blk > first))
+            def _():
+                keys = k_s[pl.ds(pl.multiple_of(j * key_blk, key_blk), key_blk), :]
+                ok = allowed(j, key_blk, qpos, qstart, prompt)
+                for h in range(heads):
+                    scores = jnp.where(ok, contract(keys, qm_s[h], 1, 1), neg_fill)
+                    old = ml_s[h, 0:1, :]
+                    new = jnp.maximum(old, jnp.max(scores, axis=0, keepdims=True))
+                    probs = jnp.exp(scores - new)
+                    scale = jnp.exp(old - new)
+                    ml_s[h, 0:1, :] = new
+                    ml_s[h, 1:2, :] = ml_s[h, 1:2, :] * scale + jnp.sum(
+                        probs, axis=0, keepdims=True
+                    )
+                    part = slice(h * HEAD_DIM, (h + 1) * HEAD_DIM)
+                    acc_s[part, :] = acc_s[part, :] * scale + jnp.dot(
+                        vt_s[j, part, :], probs.astype(bf16), preferred_element_type=f32
+                    )
+
+        for h in range(heads):
+            part = slice(h * HEAD_DIM, (h + 1) * HEAD_DIM)
+            total = ml_s[h, 1:2, :]
+            acc_s[part, :] = acc_s[part, :] / total
+            lse_ref[line, h : h + 1, :] = ml_s[h, 0:1, :] + jnp.log(total)
+        result = jnp.transpose(acc_s[...])
+        o_ref[line] = result
+        low_ref[line] = result.astype(bf16)
+
+
+def attend(info, q, kv, qinfo):
+    lines, rows, width = q.shape
+    heads = width // HEAD_DIM
+    length = kv.shape[0]
+    key_blk = KEY_BLK
+    shape = jax.ShapeDtypeStruct
+    return pl.pallas_call(
+        functools.partial(attend_body, lines, heads),
+        out_shape=[
+            shape((lines, rows, width), f32),
+            shape((lines, rows, width), bf16),
+            shape((lines, 8, rows), f32),
+        ],
+        in_specs=[SM, VM, VM, VM],
+        out_specs=[VM] * 3,
+        scratch_shapes=[
+            pltpu.VMEM((length, width), bf16),
+            pltpu.VMEM((length // key_blk, width, key_blk), bf16),
+            pltpu.VMEM((width, rows), f32),
+            pltpu.VMEM((heads, 8, rows), f32),
+            pltpu.VMEM((heads, rows, width), bf16),
+        ],
+        cost_estimate=pl.CostEstimate(flops=2 * 10**9, bytes_accessed=8 * 10**6, transcendentals=4 * 10**6),
+        name="attend",
+    )(info, q, kv, qinfo)
+
+
+def attend_back_body(lines, heads, info_ref, q_ref, kv_ref, qinfo_ref, o_ref, lse_ref, back_ref, dq_ref, dkv_ref, k_s, v_s, dk_s, dv_s, dq_s, qm_s, bm_s, delta_s):
+    shard = lax.axis_index(SH)
+    rows, width = q_ref.shape[1:]
+    key_blk = KEY_BLK
+    blocks = k_s.shape[0] // key_blk
+    prompt = info_ref[0]
+
+    @pl.loop(0, blocks)
+    def _(j):
+        at = pl.ds(pl.multiple_of(j * key_blk, key_blk), key_blk)
+        k_s[at, :] = kv_ref[at, :width]
+        v_s[at, :] = kv_ref[at, width:]
+        dk_s[at, :] = jnp.zeros((key_blk, width), f32)
+        dv_s[at, :] = jnp.zeros((key_blk, width), f32)
+
+    @pl.loop(0, lines)
+    def _(line):
+        start = (line * 4 + shard) * rows
+        queries = q_ref[line].astype(f32) * HEAD_DIM**-0.5
+        back = back_ref[line].astype(f32)
+        qpos = start + lax.broadcasted_iota(jnp.int32, (1, rows), 1)
+        qstart = qinfo_ref[line, 0:1, :]
+        first = info_ref[1 + line]
+        picks = (
+            lax.broadcasted_iota(jnp.int32, (8, width), 1) // HEAD_DIM
+            == lax.broadcasted_iota(jnp.int32, (8, width), 0)
+        ).astype(f32)
+        delta_s[...] = contract(picks, back * o_ref[line], 1, 1, HIGH)
+        for h in range(heads):
+            mine = head_columns(h, queries.shape, 1)
+            qm_s[h] = jnp.where(mine, queries, 0.0).astype(bf16)
+            bm_s[h] = jnp.where(mine, back, 0.0).astype(bf16)
+        dq_s[...] = jnp.zeros_like(dq_s)
+
+        @pl.loop(0, (start + rows + key_blk - 1) // key_blk)
+        def _(j):
+            @pl.when((j * key_blk < prompt) | ((j + 1) * key_blk > first))
+            def _():
+                at = pl.ds(pl.multiple_of(j * key_blk, key_blk), key_blk)
+                keys, values = k_s[at, :], v_s[at, :]
+                ok = allowed(j, key_blk, qpos, qstart, prompt)
+                dk = jnp.zeros((key_blk, width), f32)
+                dv = jnp.zeros((key_blk, width), f32)
+                for h in range(heads):
+                    scores = contract(keys, qm_s[h], 1, 1)
+                    probs = jnp.where(ok, jnp.exp(scores - lse_ref[line, h : h + 1, :]), 0.0)
+                    grads = contract(values, bm_s[h], 1, 1)
+                    slow = (probs * (grads - delta_s[h : h + 1, :])).astype(bf16)
+                    dv = dv + jnp.dot(probs.astype(bf16), bm_s[h], preferred_element_type=f32)
+                    dk = dk + jnp.dot(slow, qm_s[h], preferred_element_type=f32)
+                    dq_s[h] += contract(slow, keys, 0, 0)
+                dk_s[at, :] += dk
+                dv_s[at, :] += dv
+
+        total = jnp.zeros(queries.shape, f32)
+        for h in range(heads):
+            total = jnp.where(head_columns(h, queries.shape, 1), dq_s[h], total)
+        dq_ref[line] = (total * HEAD_DIM**-0.5).astype(bf16)
+
+    @pl.loop(0, lines)
+    def _(line):
+        for piece in range(4):
+            at = pl.ds(pl.multiple_of((line * 4 + piece) * rows, rows), rows)
+            dkv_ref[piece, line, :, :width] = dk_s[at, :].astype(bf16)
+            dkv_ref[piece, line, :, width:] = dv_s[at, :].astype(bf16)
+
+
+def attend_back(info, q, kv, qinfo, o, lse, back):
+    lines, rows, width = q.shape
+    heads = width // HEAD_DIM
+    length = kv.shape[0]
+    shape = jax.ShapeDtypeStruct
+    return pl.pallas_call(
+        functools.partial(attend_back_body, lines, heads),
+        out_shape=[
+            shape((lines, rows, width), bf16),
+            shape((4, lines, rows, 2 * width), bf16),
+        ],
+        in_specs=[SM] + [VM] * 6,
+        out_specs=[VM] * 2,
+        scratch_shapes=[
+            pltpu.VMEM((length, width), bf16),
+            pltpu.VMEM((length, width), bf16),
+            pltpu.VMEM((length, width), f32),
+            pltpu.VMEM((length, width), f32),
+            pltpu.VMEM((heads, rows, width), f32),
+            pltpu.VMEM((heads, rows, width), bf16),
+            pltpu.VMEM((heads, rows, width), bf16),
+            pltpu.VMEM((8, rows), f32),
+        ],
+        cost_estimate=pl.CostEstimate(flops=5 * 10**9, bytes_accessed=12 * 10**6, transcendentals=4 * 10**6),
+        name="attend_back",
+    )(info, q, kv, qinfo, o, lse, back)
+
+
+def swap(x, axis, partner):
+    n = lax.axis_size(axis)
+    return lax.ppermute(x, axis, [(i, partner(i)) for i in range(n)])
+
+
+def pick(x, index):
+    return lax.dynamic_index_in_dim(x, index, axis=0, keepdims=False)
+
+
+def reduce_expert(term):
+    me = lax.axis_index(SH)
+    side, core = me // 2, lax.rem(me, 2)
+    rows, cols = term.shape
+    parts = term.reshape(2, 2, rows // 4, cols).swapaxes(0, 1)
+    kept, sent = pick(parts, core), pick(parts, 1 - core).astype(bf16)
+    both = kept + swap(sent, SH, lambda i: i ^ 1).astype(f32)
+    kept, sent = pick(both, side), pick(both, 1 - side).astype(bf16)
+    mine = (kept + swap(sent, SH, lambda i: i ^ 2).astype(f32)).astype(bf16)
+    n = lax.axis_size(GR)
+    if n == 2:
+        return mine.astype(f32) + swap(mine, GR, lambda i: 1 - i).astype(f32)
+    return jnp.sum(lax.all_gather(mine, GR).astype(f32), axis=0)
+
+
+def fast_shards(
+    hidden_in,
+    segment_ids,
+    routes,
+    attn_gain,
+    w_query,
+    w_key,
+    w_value,
+    w_out,
+    moe_gain,
+    w_router,
+    const_mix,
+    const_vec,
+    w_gate,
+    w_up,
+    w_down,
+    out_grad,
+):
+    rows, model = hidden_in.shape
+    lines = lax.axis_size(EX)
+    line, shard = lax.axis_index(EX), lax.axis_index(SH)
+    width = model // lines
+    seg = segment_ids[0]
+    length = seg.shape[0]
+
+    w_mine = lax.dynamic_slice_in_dim(
+        jnp.stack([w_query, w_key, w_value]), line * width, width, axis=2
+    )
+    hidden_all, w_cols, w_out_all = exchange(
+        [(EX, GATHER, hidden_in), (SH, GATHER, w_mine), (SH, GATHER, w_out)],
+        0,
+        "gather_in",
+    )
+    w_heads = w_cols.swapaxes(0, 1).reshape(3, model, width)
+    wo_full = w_out_all.reshape(model, model)
+    inputs_all = hidden_all.reshape(lines * rows, model).astype(f32)
+    inv_all = lax.rsqrt(jnp.mean(inputs_all * inputs_all, axis=1, keepdims=True) + norm_eps)
+    attn_in = (inputs_all * inv_all * attn_gain).astype(bf16)
+    q = jnp.dot(attn_in, w_heads[0], preferred_element_type=f32).astype(bf16)
+    w_kv = jnp.concatenate([w_heads[1], w_heads[2]], axis=1)
+    kv = jnp.dot(attn_in, w_kv, preferred_element_type=f32).astype(bf16)
+    q = q.reshape(lines, rows, width)
+    kv_all = tree_gather(kv.reshape(lines, rows, 2 * width), 1, "gather_kv")
+    kv_all = kv_all.reshape(length, 2 * width)
+
+    own_seg = jnp.take(seg.reshape(lines, 4, rows), shard, axis=1)
+    qstart = jnp.sum(
+        (seg[None, None, :] < own_seg[:, :, None]).astype(jnp.int32), axis=2, dtype=jnp.int32
+    )
+    prompt = jnp.sum((seg == 0).astype(jnp.int32), dtype=jnp.int32)
+    info = jnp.concatenate([prompt[None], qstart[:, 0]])
+    qinfo = jnp.broadcast_to(qstart[:, None, :], (lines, 8, rows))
+    attn_vec, attn_low_heads, lse = attend(info, q, kv_all, qinfo)
+    (attn_parts,) = exchange([(EX, SWAP, attn_low_heads)], 2, "heads_out")
+    attn_low = attn_parts.swapaxes(0, 1).reshape(rows, model)
+
+    inputs = hidden_in.astype(f32)
+    inv_one = lax.rsqrt(jnp.mean(inputs * inputs, axis=1, keepdims=True) + norm_eps)
+    resid_one = inputs + jnp.dot(attn_low, wo_full, preferred_element_type=f32)
+    inv_two = lax.rsqrt(jnp.mean(resid_one * resid_one, axis=1, keepdims=True) + norm_eps)
+    normed_two = resid_one * inv_two
+    moe_in = normed_two * moe_gain
+    moe_low = moe_in.astype(bf16)
+    n_ids = w_router.shape[1]
+    ids = jnp.arange(n_ids, dtype=jnp.int32)
+    hot = (routes[:, :, None] == ids).astype(f32)
+    small_w = jnp.concatenate([w_router, const_mix], axis=1)
+    small = dense32(moe_in, small_w)
+    chosen = jnp.sum(hot * small[:, None, :n_ids], axis=2)
+    gate_probs = jax.nn.softmax(chosen, axis=1)
+    mix_alpha = jax.nn.softmax(small[:, n_ids:].reshape(rows, 2, 2), axis=2)
+    ffn_mask = (routes < lines).astype(f32)
+    copy_mask = (routes == lines + 1).astype(f32)
+    const_mask = hot[:, :, lines + 2 : lines + 4]
+    copy_gate = jnp.sum(gate_probs * copy_mask, axis=1)
+    const_gate = jnp.sum(gate_probs[:, :, None] * const_mask, axis=1)
+    ffn_gate = gate_probs * ffn_mask
+    before = (jnp.arange(rows)[:, None] > jnp.arange(rows)[None, :]).astype(bf16)
+    earlier = jnp.dot(before, jnp.sum(hot, axis=1).astype(bf16), preferred_element_type=f32)
+    slot_num = jnp.sum(hot * earlier[:, None, :], axis=2).astype(jnp.int32)
+    slot = jnp.where(routes < lines, routes * CAP + slot_num, -1)
+    slots = lines * CAP
+    sits = slot[:, :, None] == jnp.arange(slots, dtype=jnp.int32)
+    sit_gate = jnp.sum(jnp.where(sits, ffn_gate[:, :, None], 0.0), axis=(0, 1))
+    place = [sits[:, k].astype(bf16) for k in range(2)]
+    either = place[0] + place[1]
+    send_rows = contract(either, moe_low, 0, 0).astype(bf16)
+    grad_send = (contract(either, out_grad, 0, 0) * sit_gate[:, None]).astype(bf16)
+    recv_rows, recv_grads = exchange(
+        [
+            (EX, SWAP, send_rows.reshape(lines, CAP, model)),
+            (EX, SWAP, grad_send.reshape(lines, CAP, model)),
+        ],
+        3,
+        "dispatch",
+    )
+
+    expert_in = recv_rows.reshape(slots, model)
+    out_back = recv_grads.reshape(slots, model)
+    wg, wu, wd = w_gate[0], w_up[0], w_down[0]
+    gate_pre = jnp.dot(expert_in, wg, preferred_element_type=f32)
+    up_pre = jnp.dot(expert_in, wu, preferred_element_type=f32)
+    gate_sigmoid = jax.nn.sigmoid(gate_pre)
+    hidden_act = (gate_pre * gate_sigmoid * up_pre).astype(bf16)
+    expert_out = jnp.dot(hidden_act, wd, preferred_element_type=f32).astype(bf16)
+    hidden_grad = contract(out_back, wd, 1, 1)
+    gate_back = (
+        hidden_grad * up_pre * gate_sigmoid * (1.0 + gate_pre * (1.0 - gate_sigmoid))
+    ).astype(bf16)
+    up_back = (hidden_grad * gate_pre * gate_sigmoid).astype(bf16)
+    input_back = (contract(gate_back, wg, 1, 1) + contract(up_back, wu, 1, 1)).astype(bf16)
+    returned, input_ret = exchange(
+        [
+            (EX, SWAP, expert_out.reshape(lines, CAP, model)),
+            (EX, SWAP, input_back.reshape(lines, CAP, model)),
+        ],
+        4,
+        "combine",
+    )
+    down_part = reduce_expert(contract(hidden_act, out_back, 0, 0))
+    gate_part = reduce_expert(contract(expert_in, gate_back, 0, 0))
+    up_part = reduce_expert(contract(expert_in, up_back, 0, 0))
+
+    returned = returned.reshape(slots, model)
+    route_out = jnp.stack(
+        [jnp.dot(place[k], returned, preferred_element_type=f32) for k in range(2)], axis=1
+    )
+    ffn_in_grad = jnp.dot(either, input_ret.reshape(slots, model), preferred_element_type=f32)
+    const_rows = mix_alpha[:, :, 0:1] * moe_in[:, None, :] + mix_alpha[:, :, 1:2] * const_vec[None]
+    moe_sum = (
+        jnp.sum(ffn_gate[:, :, None] * route_out, axis=1)
+        + copy_gate[:, None] * moe_in
+        + jnp.sum(const_gate[:, :, None] * const_rows, axis=1)
+    )
+    layer_out = (resid_one + moe_sum).astype(bf16)
+    upstream = out_grad.astype(f32)
+    route_dot = jnp.sum(upstream[:, None, :] * route_out, axis=2)
+    copy_dot = jnp.sum(upstream * moe_in, axis=1)
+    const_dot = jnp.sum(upstream[:, None, :] * const_rows, axis=2)
+    gate_back_r = (
+        ffn_mask * route_dot
+        + copy_mask * copy_dot[:, None]
+        + jnp.sum(const_mask * const_dot[:, None, :], axis=2)
+    )
+    chosen_grad = gate_probs * (
+        gate_back_r - jnp.sum(gate_probs * gate_back_r, axis=1, keepdims=True)
+    )
+    logit_grad = jnp.sum(chosen_grad[:, :, None] * hot, axis=1)
+    up_dot_vec = jnp.sum(upstream[:, None, :] * const_vec[None], axis=2)
+    alpha_grad = jnp.stack(
+        [const_gate * copy_dot[:, None], const_gate * up_dot_vec], axis=2
+    )
+    mix_back = (
+        mix_alpha * (alpha_grad - jnp.sum(mix_alpha * alpha_grad, axis=2, keepdims=True))
+    ).reshape(rows, 4)
+    vec_scale = mix_alpha[:, :, 1] * const_gate
+    small_back = jnp.concatenate([logit_grad, mix_back], axis=1)
+    moe_in_grad = (
+        ffn_in_grad
+        + (copy_gate + jnp.sum(mix_alpha[:, :, 0] * const_gate, axis=1))[:, None] * upstream
+        + dense32(small_back, small_w.T)
+    )
+    moe_gain_grad = jnp.sum(moe_in_grad * normed_two, axis=0)
+    small_grad = contract(small_back, moe_in, 0, 0, HIGH)
+    vec_grad = contract(vec_scale, upstream, 0, 0, HIGH)
+    resid_grad = upstream + rms_back(resid_one, inv_two, moe_gain, moe_in_grad)
+    branch_low = resid_grad.astype(bf16)
+    attn_back = contract(branch_low, wo_full, 1, 1).astype(bf16)
+    attn_back = attn_back.reshape(rows, lines, width).swapaxes(0, 1)
+    (back_heads,) = exchange([(EX, SWAP, attn_back)], 5, "heads_back")
+    out_proj_term = contract(attn_low, branch_low, 0, 0).astype(bf16)
+
+    dq, dkv = attend_back(info, q, kv_all, qinfo, attn_vec, lse, back_heads)
+    (dkv_own,) = tree_reduce([dkv], 6, "reduce_kv")
+    dkv_own = dkv_own.reshape(lines * rows, 2 * width).astype(bf16)
+    dq = dq.reshape(lines * rows, width)
+    back_in = (
+        contract(dq, w_heads[0], 1, 1) + contract(dkv_own, w_kv, 1, 1)
+    ).astype(bf16)
+    own = rows // lines
+    q_term = contract(attn_in, dq, 0, 0)
+    kv_term = contract(attn_in, dkv_own, 0, 0)
+    qkv_term = jnp.concatenate([q_term, kv_term], axis=1).astype(bf16)
+    qkv_term = qkv_term.reshape(lines, 4, own, 3 * width).swapaxes(0, 1)
+    out_term = out_proj_term.reshape(lines, 4, own, model).swapaxes(0, 1)
+    (attn_in_grad,) = exchange(
+        [(EX, SWAP_SUM, back_in.reshape(lines, rows, model))], 7, "input_back"
+    )
+    qkv_sum, out_sum = tree_reduce([qkv_term, out_term], 8, "reduce_w")
+    qkv_part, out_part = exchange(
+        [
+            (EX, SWAP, qkv_sum.astype(bf16)),
+            (EX, SWAP_SUM, out_sum.astype(bf16)),
+        ],
+        9,
+        "lines_w",
+    )
+    normed_one = inputs * inv_one
+    attn_gain_grad = jnp.sum(attn_in_grad * normed_one, axis=0)
+    input_grad = resid_grad + rms_back(inputs, inv_one, attn_gain, attn_in_grad)
+
+    packed = jnp.concatenate(
+        [attn_gain_grad[None], moe_gain_grad[None], vec_grad, small_grad], axis=0
+    )
+    packed, qkv_part, out_part = exchange(
+        [
+            (GR, GATHER_SUM, packed),
+            (GR, GATHER_SUM, qkv_part),
+            (GR, GATHER_SUM, out_part.astype(bf16)),
+        ],
+        10,
+        "group_sum",
+    )
+    (packed,) = exchange([(EX, GATHER_SUM, packed)], 11, "small_lines")
+    (packed,) = exchange([(SH, GATHER_SUM, packed)], 12, "small_shards")
+    grads = [
+        qkv_part[:, :, k * width : (k + 1) * width].swapaxes(0, 1).reshape(own, model)
+        for k in range(3)
+    ]
+    return (
+        layer_out,
+        input_grad,
+        packed[0],
+        grads[0],
+        grads[1],
+        grads[2],
+        out_part,
+        packed[1],
+        packed[4 : 4 + n_ids].T,
+        packed[4 + n_ids :].T,
+        packed[2:4],
+        gate_part[None],
+        up_part[None],
+        down_part[None],
+    )
+
+
 def solution(mesh):
     placed = (
-        P(("group", "expert", "shard"), None),
-        P("group", None),
-        P(("group", "expert", "shard"), None),
+        P((GR, EX, SH), None),
+        P(GR, None),
+        P((GR, EX, SH), None),
         P(),
-        P("shard", None),
-        P("shard", None),
-        P("shard", None),
-        P("shard", None),
+        P(SH, None),
+        P(SH, None),
+        P(SH, None),
+        P(SH, None),
         P(),
         P(),
         P(),
         P(),
-        P("expert", None, None),
-        P("expert", None, None),
-        P("expert", None, None),
-        P(("group", "expert", "shard"), None),
-    )
+        P(EX, None, None),
+        P(EX, None, None),
+        P(EX, None, None),
+        P((GR, EX, SH), None),
+    )
+    sizes = dict(mesh.shape)
+    lines = sizes[EX]
+    fast = sizes[SH] == 4 and lines == 4 and HEADS % lines == 0
     return jax.shard_map(
-        shards,
+        fast_shards if fast else shards,
         mesh=mesh,
         in_specs=placed,
         out_specs=(
-            P(("group", "expert", "shard"), None),
-            P(("group", "expert", "shard"), None),
+            P((GR, EX, SH), None),
+            P((GR, EX, SH), None),
             P(),
-            P(("expert", "shard"), None),
-            P(("expert", "shard"), None),
-            P(("expert", "shard"), None),
-            P(("expert", "shard"), None),
+            P((EX, SH), None),
+            P((EX, SH), None),
+            P((EX, SH), None),
+            P((EX, SH), None),
             P(),
             P(),
             P(),
             P(),
-            P("expert", "shard", None),
-            P("expert", "shard", None),
-            P("expert", "shard", None),
+            P(EX, SH, None),
+            P(EX, SH, None),
+            P(EX, SH, None),
         ),
         check_vma=False,
     )

time: 1080 us -> 469 us (0.43)
  waiting for transfers between devices: 660 us -> 44.7 us
  Pallas kernels: 0 us -> 270 us
  other arithmetic: 102 us -> 49.9 us
  local copies, waits for them, and re-layouts: 101 us -> 50.8 us
  starting transfers between devices: 52.9 us -> 6.6 us
  blocking collectives: 42 us -> 0 us
  matrix products: 70.3 us -> 41.5 us
  loops' own time: 26.4 us -> 0 us
  between operations: 15.1 us -> 1.73 us
    reduce_scatter x9 -> x0, waiting for transfers between devices: 542 us -> none  [the longest x1 103 us: shards(): lax.psum_scatter(key_terms[1].reshape(group_len, model_width).astype(jnp....]
    pallas_call x0 -> x15, Pallas kernels: none -> 270 us  [the longest x13 229 us: comm_call(): pl.pallas_call(body, out_shape=out_shapes, in_specs=[VM] * len(operands),...]
    all_gather x6 -> x0, waiting for transfers between devices: 81.6 us -> none  [the longest x1 40.4 us: shards(): lax.all_gather(keys_own, ('expert', 'shard'), axis=0, tiled=True)]
    all_to_all x4 -> x0, starting transfers between devices: 52 us -> none  [the longest x1 38.5 us: shards(): lax.all_to_all(send_rows.reshape(owners, local_experts * CAP, model_width...]
    ppermute x0 -> x9, waiting for transfers between devices: none -> 44.7 us  [swap(): return lax.ppermute(x, axis, [(i, partner(i)) for i in range(n)])]
    psum x1 -> x0, blocking collectives: 42 us -> none  [shards(): lax.psum((attn_gain_grad, moe_gain_grad, router_grad, mix_grad, vec_grad)...]
    reduce_or x18 -> x0, other arithmetic: 30.3 us -> none  [the longest x6 12.8 us: stats_step(): jnp.any(key_mask)]
    psum x1 -> x0, waiting for transfers between devices: 30.1 us -> none  [shards(): lax.psum(query_part.astype(jnp.bfloat16), 'group').astype(jnp.float32)]
  transfers between devices with their start and end apart: 20 -> 9, of which waited for: 16 -> 5; matrix products, arithmetic and copies ran while one was open for 17% -> 18% of each run, Pallas kernels for 0% -> 36%
where the time goes in v1:
time: 469 us; the launch traced here: 465 us
  Pallas kernels  270 us (58%)
  local copies, waits for them, and re-layouts  50.8 us (11%)
  other arithmetic  49.9 us (11%)
  waiting for transfers between devices  44.7 us (10%)
  matrix products  41.5 us (9%)
  starting transfers between devices  6.6 us (1%)
    pallas_call x13, Pallas kernels, comm_call(): pl.pallas_call(body, out_shape=out_shapes, in_specs=[VM] * len(operands),...  229 us
    ppermute x9, waiting for transfers between devices, swap(): return lax.ppermute(x, axis, [(i, partner(i)) for i in range(n)])  44.7 us
    pallas_call x1, Pallas kernels, attend_back(): pl.pallas_call(functools.partial(attend_back_body, lines, heads), out_sha...  24.8 us
    dot_general x16, matrix products, contract(): lax.dot_general(a, b, (((da,), (db,)), ((), ())), preferred_element_type=...  21.9 us
    pallas_call x1, Pallas kernels, attend(): pl.pallas_call(functools.partial(attend_body, lines, heads), out_shape=[s...  16 us
    unnamed x154, local copies, waits for them, and re-layouts  11.1 us
  transfers between devices with their start and end apart: 9, of which 5 were waited for; matrix products, arithmetic and copies ran while one was open for 18% of the time, Pallas kernels for 36%

profile of v1, /device:TPU:0, one launch (start us, length us, event | category | flops | bytes accessed | tf_op | source)
XLA Modules:
  0.0 465.0 jit_solution(1751953287870888239)
XLA Ops:
  0.7 1.5 convert_reduce_fusion.1
  4.1 1.4 reduce.10
  5.6 1.8 convert_reduce_fusion
  9.4 1.9 fusion.56.refs_1_
  11.3 33.5 %gather_in.1 = (bf16[4,192,768]{2,1,0:T(8,128)(2,1)}, bf16[4,3,192,192]{3,2,1,0:T(8,128)(2,1)}, bf16[4,192,768]{2,1,0:T(8,128)(2,1)}) custom-call(bf16[192,768]{1,0:T(8,128)(2,1)} %refs_0_.1, bf16[3,192,192]{2,1,0:T(8,128)(2,1)} %fusion.56.refs_1_, bf16[192,768]{1,0:T(8,128)(2,1)} %refs_2_.1), custom_call_target="tpu_custom_call" | custom-call | tf_op jit(solution)/shard_map/gather_in/pallas_call | solution.py:484
  44.8 2.3 fusion.90
  47.6 1.7 multiply_convert_fusion
  49.3 1.4 fusion.13
  52.0 1.9 copy.109
  53.9 3.1 convolution_convert_fusion.1
  57.0 19.9 %gather_kv.1 = bf16[4,4,192,384]{3,2,1,0:T(8,128)(2,1)} custom-call(bf16[4,192,384]{2,1,0:T(8,128)(2,1)} %bitcast.278), custom_call_target="tpu_custom_call" | custom-call | tf_op jit(solution)/shard_map/gather_kv/pallas_call | solution.py:484
  78.8 16.0 %attend.1 = (f32[4,192,192]{2,1,0:T(8,128)}, bf16[4,192,192]{2,1,0:T(8,128)(2,1)}, f32[4,8,192]{2,1,0:T(8,128)}) custom-call(s32[5]{0:T(128)} %pad_add_fusion.info_ref, bf16[4,192,192]{2,1,0:T(8,128)(2,1)} %bitcast.279, bf16[3072,384]{1,0:T(8,128)(2,1)} %bitcast.258, s32[4,8,192]{2,1,0:T(8,128)} %broadcast_in_dim.46.qinfo_ref), custom_call_target="tpu_custom_call" | custom-call | flops 2000000000 | bytes 8000000 | tf_op jit(solution)/shard_map/attend/pallas_call | solution.py:706
  94.8 12.2 %heads_out.1 = bf16[4,192,192]{2,1,0:T(8,128)(2,1)} custom-call(bf16[4,192,192]{2,1,0:T(8,128)(2,1)} %get-tuple-element.35.refs_0_), custom_call_target="tpu_custom_call" | custom-call | tf_op jit(solution)/shard_map/heads_out/pallas_call | solution.py:484
  107.0 2.0 multiply_reduce_fusion.9
  113.5 2.1 convolution_convert_fusion.3
  116.7 18.8 %dispatch.1 = (bf16[4,48,768]{2,1,0:T(8,128)(2,1)}, bf16[4,48,768]{2,1,0:T(8,128)(2,1)}) custom-call(bf16[4,48,768]{2,1,0:T(8,128)(2,1)} %bitcast.276, bf16[4,48,768]{2,1,0:T(8,128)(2,1)} %bitcast.283), custom_call_target="tpu_custom_call" | custom-call | tf_op jit(solution)/shard_map/dispatch/pallas_call | solution.py:484
  135.5 2.9 fusion.6
  139.6 2.6 multiply_convert_fusion.2
  144.7 3.3 dot_general.125
  147.9 2.2 fusion.45
  150.2 2.6 copy-done.7
  154.6 1.9 copy.124
  156.4 2.2 fusion.43
  158.7 1.4 fusion.14
  160.2 1.5 copy-done.6
  162.8 1.4 fusion.15
  166.5 1.6 multiply_reduce_fusion.8
  168.6 1.7 fusion.30
  171.7 1.9 fusion.33
  173.6 18.0 %combine.1 = (bf16[4,48,768]{2,1,0:T(8,128)(2,1)}, bf16[4,48,768]{2,1,0:T(8,128)(2,1)}) custom-call(bf16[4,48,768]{2,1,0:T(8,128)(2,1)} %bitcast.282, bf16[4,48,768]{2,1,0:T(8,128)(2,1)} %bitcast.269), custom_call_target="tpu_custom_call" | custom-call | tf_op jit(solution)/shard_map/combine/pallas_call | solution.py:484
  195.3 2.0 reshape.342
  197.8 1.8 multiply_reduce_fusion.3
  200.5 1.4 multiply_reduce_fusion.6
  204.9 12.3 %heads_back.1.back_ref = bf16[4,192,192]{2,1,0:T(8,128)(2,1)} custom-call(bf16[4,192,192]{2,1,0:T(8,128)(2,1)} %bitcast.265), custom_call_target="tpu_custom_call" | custom-call | tf_op jit(solution)/shard_map/heads_back/pallas_call | solution.py:484
  217.3 24.8 %attend_back.1 = (bf16[4,192,192]{2,1,0:T(8,128)(2,1)}, bf16[4,4,192,384]{3,2,1,0:T(8,128)(2,1)}) custom-call(s32[5]{0:T(128)} %pad_add_fusion.info_ref, bf16[4,192,192]{2,1,0:T(8,128)(2,1)} %bitcast.280, bf16[3072,384]{1,0:T(8,128)(2,1)} %bitcast.259, s32[4,8,192]{2,1,0:T(8,128)} %broadcast_in_dim.46.qinfo_ref, f32[4,192,192]{2,1,0:T(8,128)} %get-tuple-element.41.o_ref, ...), custom_call_target="tpu_custom_call" | custom-call | flops 5000000000 | bytes 12000000 | tf_op jit(solution)/shard_map/attend_back/pallas_call | solution.py:799
  242.1 21.5 %reduce_kv.1 = f32[4,192,384]{2,1,0:T(8,128)} custom-call(bf16[4,4,192,384]{3,2,1,0:T(8,128)(2,1)} %get-tuple-element.44.refs_0_), custom_call_target="tpu_custom_call" | custom-call | tf_op jit(solution)/shard_map/reduce_kv/pallas_call | solution.py:484
  263.6 1.5 convert_element_type.235
  266.4 1.6 fusion.24
  268.0 1.9 copy.116
  270.0 2.5 convolution_convert_fusion
  273.8 1.9 add_convert_fusion
  275.7 25.9 %input_back.1 = f32[192,768]{1,0:T(8,128)} custom-call(bf16[4,192,768]{2,1,0:T(8,128)(2,1)} %bitcast.251), custom_call_target="tpu_custom_call" | custom-call | tf_op jit(solution)/shard_map/input_back/pallas_call | solution.py:484
  303.1 1.4 copy_bitcast_fusion.1.refs_0_
  305.6 19.3 %reduce_w.1 = (f32[4,48,576]{2,1,0:T(8,128)}, f32[4,48,768]{2,1,0:T(8,128)}) custom-call(bf16[4,4,48,576]{3,2,1,0:T(8,128)(2,1)} %copy_bitcast_fusion.1.refs_0_, bf16[4,4,48,768]{3,2,1,0:T(8,128)(2,1)} %bitcast.248), custom_call_target="tpu_custom_call" | custom-call | tf_op jit(solution)/shard_map/reduce_w/pallas_call | solution.py:484
  324.9 1.8 convert_element_type.239.refs_0_
  326.7 1.8 convert_element_type.240.refs_1_
  328.5 21.1 %lines_w.1 = (bf16[4,48,576]{2,1,0:T(8,128)(2,1)}, f32[48,768]{1,0:T(8,128)}) custom-call(bf16[4,48,576]{2,1,0:T(8,128)(2,1)} %convert_element_type.239.refs_0_, bf16[4,48,768]{2,1,0:T(8,128)(2,1)} %convert_element_type.240.refs_1_), custom_call_target="tpu_custom_call" | custom-call | tf_op jit(solution)/shard_map/lines_w/pallas_call | solution.py:484
  349.6 1.6 convert_element_type.241.refs_2_
  352.3 12.1 %group_sum.1 = (f32[16,768]{1,0:T(8,128)}, f32[4,48,576]{2,1,0:T(8,128)}, f32[48,768]{1,0:T(8,128)}) custom-call(f32[16,768]{1,0:T(8,128)} %pad_maximum_fusion.5.refs_0_, bf16[4,48,576]{2,1,0:T(8,128)(2,1)} %get-tuple-element.47.refs_1_, bf16[48,768]{1,0:T(8,128)(2,1)} %convert_element_type.241.refs_2_), custom_call_target="tpu_custom_call" | custom-call | tf_op jit(solution)/shard_map/group_sum/pallas_call | solution.py:484
  364.4 8.2 %small_lines.1.refs_0_ = f32[16,768]{1,0:T(8,128)} custom-call(f32[16,768]{1,0:T(8,128)} %get-tuple-element.49.refs_0_), custom_call_target="tpu_custom_call" | custom-call | tf_op jit(solution)/shard_map/small_lines/pallas_call | solution.py:484
  372.6 6.1 %small_shards.1 = f32[16,768]{1,0:T(8,128)} custom-call(f32[16,768]{1,0:T(8,128)} %small_lines.1.refs_0_), custom_call_target="tpu_custom_call" | custom-call | tf_op jit(solution)/shard_map/small_shards/pallas_call | solution.py:484
  380.0 1.4 slice_bitcast_fusion.3
  381.4 1.9 slice_bitcast_fusion
  384.4 3.1 bitcast_add_fusion
  389.9 2.0 bitcast_add_fusion.2
  393.7 2.0 bitcast_add_fusion.1
  399.0 1.4 slice_reduce_fusion
  401.8 1.7 copy.123
  403.5 1.7 reshape.346
  406.1 1.7 reshape.345
  409.2 1.5 fusion.17
  411.6 14.5 %collective-permute-done.1 = bf16[192,2048]{1,0:T(8,128)(2,1)} collective-permute-done((bf16[192,2048]{1,0:T(8,128)(2,1)}, bf16[192,2048]{1,0:T(8,128)(2,1)}, u32[]{:S(2)}, u32[]{:S(2)}) %collective-permute-start.1) | collective-permute-done | bytes 786464 | tf_op jit(solution)/shard_map/ppermute | solution.py:824
  428.3 14.0 %collective-permute-done.4 = bf16[192,2048]{1,0:T(8,128)(2,1)} collective-permute-done((bf16[192,2048]{1,0:T(8,128)(2,1)}, bf16[192,2048]{1,0:T(8,128)(2,1)}, u32[]{:S(2)}, u32[]{:S(2)}) %collective-permute-start.4) | collective-permute-done | bytes 786464 | tf_op jit(solution)/shard_map/ppermute | solution.py:824
  447.7 15.2 %collective-permute-done.5 = bf16[192,2048]{1,0:T(8,128)(2,1)S(1)} collective-permute-done((bf16[192,2048]{1,0:T(8,128)(2,1)S(1)}, bf16[192,2048]{1,0:T(8,128)(2,1)S(1)}, u32[]{:S(2)}, u32[]{:S(2)}) %collective-permute-start.5) | collective-permute-done | bytes 786464 | tf_op jit(solution)/shard_map/ppermute | solution.py:824
  (257 shorter events, 61.7 us)
Async XLA Ops:
  0.6 138.9 %copy-start = (bf16[1,768,2048]{2,1,0:T(8,128)(2,1)S(1)}, bf16[1,768,2048]{2,1,0:T(8,128)(2,1)}, u32[]{:S(2)}) copy-start(bf16[1,768,2048]{2,1,0:T(8,128)(2,1)} %param.28) | copy-start | bytes 9437188
  44.8 2.3 copy-start.11
  44.8 2.7 copy-start.57
  47.1 3.5 copy-start.28
  57.0 19.9 %copy-start.70 = (s32[4]{0:T(128)S(1)}, s32[4]{0:T(128)}, u32[]{:S(2)}) copy-start(s32[4]{0:T(128)} %slice_reduce_fusion.2) | copy-start | bytes 52
  94.8 14.9 %copy-start.51 = (f32[768,12]{0,1:T(8,128)S(1)}, f32[768,12]{0,1:T(8,128)}, u32[]{:S(2)}) copy-start(f32[768,12]{0,1:T(8,128)} %constant_dynamic-update-slice_fusion.1) | copy-start | bytes 110596
  94.8 14.9 %copy-start.64 = (f32[768,4]{0,1:T(4,128)S(1)}, f32[768,4]{0,1:T(4,128)}, u32[]{:S(2)}) copy-start(f32[768,4]{0,1:T(4,128)} %param.26) | copy-start | bytes 36868
  94.8 15.1 %copy-start.54 = (f32[768]{0:T(1024)S(1)}, f32[768]{0:T(1024)}, u32[]{:S(2)}) copy-start(f32[768]{0:T(1024)} %param.24) | copy-start | bytes 9220
  107.0 3.6 copy-start.56
  107.0 3.6 copy-start.66
  107.0 8.6 %copy-start.19 = (bf16[192,768]{1,0:T(8,128)(2,1)S(1)}, bf16[192,768]{1,0:T(8,128)(2,1)}, u32[]{:S(2)}) copy-start(bf16[192,768]{1,0:T(8,128)(2,1)} %param.31) | copy-start | bytes 884740
  135.4 3.0 copy-start.32
  135.4 3.0 copy-start.48
  138.4 3.8 copy-start.22
  150.2 2.6 copy-start.7
  154.2 230.2 %collective-permute-start.6 = (bf16[2,512,768]{2,1,0:T(8,128)(2,1)}, bf16[2,512,768]{2,1,0:T(8,128)(2,1)}, u32[]{:S(2)}, u32[]{:S(2)}) collective-permute-start(bf16[2,512,768]{2,1,0:T(8,128)(2,1)} %fusion.16), channel_id=1, source_target_pairs={{0,1},{1,0},{2,3},{3,2},{4,5},{5,4},{6,7},{7,6},{8,9},{9,8},{10,11... | collective-permute-start | bytes 4718600 | tf_op jit(solution)/shard_map/ppermute | solution.py:824
  158.7 3.1 copy-start.6
  158.7 3.0 copy-start.27
  158.7 3.0 copy-start.34
  160.1 229.8 %collective-permute-start = (bf16[2,192,2048]{2,1,0:T(8,128)(2,1)}, bf16[2,192,2048]{2,1,0:T(8,128)(2,1)}, u32[]{:S(2)}, u32[]{:S(2)}) collective-permute-start(bf16[2,192,2048]{2,1,0:T(8,128)(2,1)} %fusion.14), channel_id=1, source_target_pairs={{0,1},{1,0},{2,3},{3,2},{4,5},{5,4},{6,7},{7,6},{8,9},{9,8},{10,11... | collective-permute-start | bytes 4718600 | tf_op jit(solution)/shard_map/ppermute | solution.py:824
  161.7 6.3 %copy-start.46 = (f32[192,2048]{1,0:T(8,128)S(1)}, f32[192,2048]{1,0:T(8,128)}, u32[]{:S(2)}) copy-start(f32[192,2048]{1,0:T(8,128)} %copy-done.45) | copy-start | bytes 4718596
  162.7 7.6 %copy-start.5 = (f32[2,2,192,2048]{3,2,1,0:T(8,128)}, f32[2,2,192,2048]{3,2,1,0:T(8,128)S(1)}, u32[]{:S(2)}) copy-start(f32[2,2,192,2048]{3,2,1,0:T(8,128)S(1)} %fusion.41) | copy-start | bytes 18874372
  162.7 3.7 copy-start.3
  162.8 5.3 %copy-start.33 = (bf16[1,2048,768]{2,1,0:T(8,128)(2,1)S(1)}, bf16[1,2048,768]{2,1,0:T(8,128)(2,1)}, u32[]{:S(2)}) copy-start(bf16[1,2048,768]{2,1,0:T(8,128)(2,1)} %param.30) | copy-start | bytes 9437188
  164.2 4.4 copy-start.23
  164.2 229.5 %collective-permute-start.3 = (bf16[2,192,2048]{2,1,0:T(8,128)(2,1)}, bf16[2,192,2048]{2,1,0:T(8,128)(2,1)}, u32[]{:S(2)}, u32[]{:S(2)}) collective-permute-start(bf16[2,192,2048]{2,1,0:T(8,128)(2,1)} %fusion.15), channel_id=1, source_target_pairs={{0,1},{1,0},{2,3},{3,2},{4,5},{5,4},{6,7},{7,6},{8,9},{9,8},{10,11... | collective-permute-start | bytes 4718600 | tf_op jit(solution)/shard_map/ppermute | solution.py:824
  173.6 20.6 %copy-start.69 = (f32[192]{0:T(256)S(1)}, f32[192]{0:T(256)}, u32[]{:S(2)}) copy-start(f32[192]{0:T(256)} %fusion.48) | copy-start | bytes 2308
  173.6 20.6 %copy-start.30 = (bf16[4,192,192]{2,1,0:T(8,128)(2,1)S(1)}, bf16[4,192,192]{2,1,0:T(8,128)(2,1)}, u32[]{:S(2)}) copy-start(bf16[4,192,192]{2,1,0:T(8,128)(2,1)} %heads_out.1) | copy-start | bytes 884740
  191.6 5.7 %slice-start.4 = ((f32[192,12]{0,1:T(8,128)}), f32[192,4]{0,1:T(4,128)S(1)}, s32[]{:S(2)}) async-start(f32[192,12]{0,1:T(8,128)} %copy-done.58), calls=%async_computation.4 | async-start | bytes 8192 | tf_op jit(solution)/shard_map/slice | solution.py:916
  191.6 5.8 %copy-start.60 = (f32[192,2,8]{0,2,1:T(8,128)S(1)}, f32[192,2,8]{0,2,1:T(8,128)}, u32[]{:S(2)}) copy-start(f32[192,2,8]{0,2,1:T(8,128)} %fusion.71) | copy-start | bytes 36868
  191.6 5.8 %copy-start.61 = (f32[192,2]{0,1:T(2,128)S(1)}, f32[192,2]{0,1:T(2,128)}, u32[]{:S(2)}) copy-start(f32[192,2]{0,1:T(2,128)} %get-tuple-element.83) | copy-start | bytes 4612
  192.8 4.9 %copy-start.39 = (f32[192,768]{1,0:T(8,128)S(1)}, f32[192,768]{1,0:T(8,128)}, u32[]{:S(2)}) copy-start(f32[192,768]{1,0:T(8,128)} %convert_element_type.230) | copy-start | bytes 1769476
  192.8 4.9 %copy-start.40 = (f32[192,768]{1,0:T(8,128)S(1)}, f32[192,768]{1,0:T(8,128)}, u32[]{:S(2)}) copy-start(f32[192,768]{1,0:T(8,128)} %get-tuple-element.92) | copy-start | bytes 1769476
  192.9 4.9 %copy-start.63 = (f32[192,2]{0,1:T(2,128)S(1)}, f32[192,2]{0,1:T(2,128)}, u32[]{:S(2)}) copy-start(f32[192,2]{0,1:T(2,128)} %copy-done.62) | copy-start | bytes 4612
  192.9 4.9 %copy-start.67 = (f32[2,768]{1,0:T(2,128)S(1)}, f32[2,768]{1,0:T(2,128)}, u32[]{:S(2)}) copy-start(f32[2,768]{1,0:T(2,128)} %param.27) | copy-start | bytes 18436
  197.8 2.7 copy-start.4
  199.7 2.2 copy-start.37
  199.7 2.2 copy-start.38
  199.7 2.2 copy-start.68
  203.0 66.9 %copy-start.17 = (f32[192,768]{1,0:T(8,128)}, f32[192,768]{1,0:T(8,128)S(1)}, u32[]{:S(2)}) copy-start(f32[192,768]{1,0:T(8,128)S(1)} %get-tuple-element.89) | copy-start | bytes 1769476
  265.0 3.0 copy-start.35
  268.0 4.5 copy-start.29
  270.0 2.6 copy-start.44
  275.7 26.0 %copy-start.21 = (bf16[192,768]{1,0:T(8,128)(2,1)S(1)}, bf16[192,768]{1,0:T(8,128)(2,1)}, u32[]{:S(2)}) copy-start(bf16[192,768]{1,0:T(8,128)(2,1)} %refs_0_.1) | copy-start | bytes 884740
  275.7 27.4 %copy-start.47 = (bf16[768,192]{1,0:T(8,128)(2,1)S(1)}, bf16[768,192]{1,0:T(8,128)(2,1)}, u32[]{:S(2)}) copy-start(bf16[768,192]{1,0:T(8,128)(2,1)} %copy.116) | copy-start | bytes 884740
  275.7 27.4 %copy-start.50 = (bf16[768,384]{1,0:T(8,128)(2,1)S(1)}, bf16[768,384]{1,0:T(8,128)(2,1)}, u32[]{:S(2)}) copy-start(bf16[768,384]{1,0:T(8,128)(2,1)} %fusion.24) | copy-start | bytes 1769476
  301.7 2.8 copy-start.26
  328.5 54.8 %copy-start.18 = (f32[192,768]{1,0:T(8,128)S(1)}, f32[192,768]{1,0:T(8,128)}, u32[]{:S(2)}) copy-start(f32[192,768]{1,0:T(8,128)} %copy-done.17) | copy-start | bytes 1769476
  328.5 54.8 %copy-start.24 = (f32[192,768]{1,0:T(8,128)S(1)}, f32[192,768]{1,0:T(8,128)}, u32[]{:S(2)}) copy-start(f32[192,768]{1,0:T(8,128)} %input_back.1) | copy-start | bytes 1769476
  383.3 6.6 %slice-start.2 = ((s8[6291456]{0:T(1024)(128)(4,1)}), s8[4194304]{0:T(1024)(128)(4,1)S(1)}, s32[]{:S(2)}) async-start(s8[6291456]{0:T(1024)(128)(4,1)} %bitcast.245), calls=%async_computation.2 | async-start | bytes 8388608
  384.4 5.5 %slice-start.3 = ((s8[6291456]{0:T(1024)(128)(4,1)}), s8[2097152]{0:T(1024)(128)(4,1)S(1)}, s32[]{:S(2)}) async-start(s8[6291456]{0:T(1024)(128)(4,1)} %bitcast.245), calls=%async_computation.3 | async-start | bytes 4194304
  384.4 9.3 %slice-start = ((s8[6291456]{0:T(1024)(128)(4,1)}), s8[4194304]{0:T(1024)(128)(4,1)S(1)}, s32[]{:S(2)}) async-start(s8[6291456]{0:T(1024)(128)(4,1)} %bitcast.243), calls=%async_computation | async-start | bytes 8388608
  388.5 5.2 %slice-start.1 = ((s8[6291456]{0:T(1024)(128)(4,1)}), s8[2097152]{0:T(1024)(128)(4,1)S(1)}, s32[]{:S(2)}) async-start(s8[6291456]{0:T(1024)(128)(4,1)} %bitcast.243), calls=%async_computation.1 | async-start | bytes 4194304
  388.5 20.7 %collective-permute-start.7 = (bf16[512,768]{1,0:T(8,128)(2,1)}, bf16[512,768]{1,0:T(8,128)(2,1)}, u32[]{:S(2)}, u32[]{:S(2)}) collective-permute-start(bf16[512,768]{1,0:T(8,128)(2,1)} %fusion.40), channel_id=1, source_target_pairs={{0,2},{1,3},{2,0},{3,1},{4,6},{5,7},{6,4},{7,5},{8,10},{9,11},{10,... | collective-permute-start | bytes 2359304 | tf_op jit(solution)/shard_map/ppermute | solution.py:824
  391.9 3.8 copy-start.13
  393.0 33.0 %collective-permute-start.1 = (bf16[192,2048]{1,0:T(8,128)(2,1)}, bf16[192,2048]{1,0:T(8,128)(2,1)}, u32[]{:S(2)}, u32[]{:S(2)}) collective-permute-start(bf16[192,2048]{1,0:T(8,128)(2,1)} %fusion.38), channel_id=1, source_target_pairs={{0,2},{1,3},{2,0},{3,1},{4,6},{5,7},{6,4},{7,5},{8,10},{9,11},{10,... | collective-permute-start | bytes 2359304 | tf_op jit(solution)/shard_map/ppermute | solution.py:824
  397.7 44.6 %collective-permute-start.4 = (bf16[192,2048]{1,0:T(8,128)(2,1)}, bf16[192,2048]{1,0:T(8,128)(2,1)}, u32[]{:S(2)}, u32[]{:S(2)}) collective-permute-start(bf16[192,2048]{1,0:T(8,128)(2,1)} %fusion.39), channel_id=1, source_target_pairs={{0,2},{1,3},{2,0},{3,1},{4,6},{5,7},{6,4},{7,5},{8,10},{9,11},{10,... | collective-permute-start | bytes 2359304 | tf_op jit(solution)/shard_map/ppermute | solution.py:824
  408.7 17.3 %copy-start.14 = (f32[2,192,2048]{2,1,0:T(8,128)S(1)}, f32[2,192,2048]{2,1,0:T(8,128)}, u32[]{:S(2)}) copy-start(f32[2,192,2048]{2,1,0:T(8,128)} %copy-done.13) | copy-start | bytes 9437188
  410.8 31.6 %copy-start.16 = (f32[2,192,2048]{2,1,0:T(8,128)S(1)}, f32[2,192,2048]{2,1,0:T(8,128)}, u32[]{:S(2)}) copy-start(f32[2,192,2048]{2,1,0:T(8,128)} %copy-done.15) | copy-start | bytes 9437188
  410.8 33.7 %collective-permute-start.8 = (bf16[512,768]{1,0:T(8,128)(2,1)S(1)}, bf16[512,768]{1,0:T(8,128)(2,1)S(1)}, u32[]{:S(2)}, u32[]{:S(2)}) collective-permute-start(bf16[512,768]{1,0:T(8,128)(2,1)S(1)} %fusion.17), channel_id=1, source_target_pairs={{0,16},{16,0},{1,17},{17,1},{2,18},{18,2},{3,19},{19,3},{4,20},{20... | collective-permute-start | bytes 2359304 | tf_op jit(solution)/shard_map/ppermute | solution.py:824
  427.4 18.9 %collective-permute-start.2 = (bf16[192,2048]{1,0:T(8,128)(2,1)S(1)}, bf16[192,2048]{1,0:T(8,128)(2,1)S(1)}, u32[]{:S(2)}, u32[]{:S(2)}) collective-permute-start(bf16[192,2048]{1,0:T(8,128)(2,1)S(1)} %fusion.23), channel_id=1, source_target_pairs={{0,16},{16,0},{1,17},{17,1},{2,18},{18,2},{3,19},{19,3},{4,20},{20... | collective-permute-start | bytes 2359304 | tf_op jit(solution)/shard_map/ppermute | solution.py:824
  443.6 19.3 %collective-permute-start.5 = (bf16[192,2048]{1,0:T(8,128)(2,1)S(1)}, bf16[192,2048]{1,0:T(8,128)(2,1)S(1)}, u32[]{:S(2)}, u32[]{:S(2)}) collective-permute-start(bf16[192,2048]{1,0:T(8,128)(2,1)S(1)} %fusion.22), channel_id=1, source_target_pairs={{0,16},{16,0},{1,17},{17,1},{2,18},{18,2},{3,19},{19,3},{4,20},{20... | collective-permute-start | bytes 2359304 | tf_op jit(solution)/shard_map/ppermute | solution.py:824
  446.4 18.6 %copy-start.1 = (bf16[1,768,2048]{2,1,0:T(8,128)(2,1)S(1)}, bf16[1,768,2048]{2,1,0:T(8,128)(2,1)}, u32[]{:S(2)}) copy-start(bf16[1,768,2048]{2,1,0:T(8,128)(2,1)} %param.28) | copy-start | bytes 9437188
  447.7 16.6 %copy-start.55 = (f32[48,768]{1,0:T(8,128)S(1)}, f32[48,768]{1,0:T(8,128)}, u32[]{:S(2)}) copy-start(f32[48,768]{1,0:T(8,128)} %get-tuple-element.129) | copy-start | bytes 442372
  (21 other events, 29.9 us)

commit v2 on v1

--- a/solution.py
+++ b/solution.py
@@ -480,154 +480,419 @@
     return copy
 
 
-def comm_call(body, name, collective_id, out_shapes, scratch, copies, operands):
+def shard_peers():
+    me = lax.axis_index(SH)
+    side, core = me // 2, lax.rem(me, 2)
+    return me, side, core, 2 * side + 1 - core, 2 * (1 - side) + core
+
+
+class Part:
+    def __init__(self, axes, ins, outs, scratch, copies, phases, specs=None):
+        self.axes, self.ins, self.outs, self.scratch = axes, ins, outs, scratch
+        self.copies, self.phases = copies, phases
+        self.specs = specs or [VM] * len(ins)
+
+
+def run_parts(parts, collective_id, name=None, cost=None):
+    ins = sum([p.ins for p in parts], [])
+    outs = sum([p.outs for p in parts], [])
+    scratch = sum([p.scratch for p in parts], [])
+    copies = sum(p.copies for p in parts)
+    axes = sorted(set(sum([list(p.axes) for p in parts], [])))
+
+    def body(*refs):
+        sems = refs[-1]
+        in_refs, out_refs = list(refs[: len(ins)]), list(refs[len(ins) : len(ins) + len(outs)])
+        scr = list(refs[len(ins) + len(outs) : -1])
+        peers = []
+        for axis in axes:
+            me, n = lax.axis_index(axis), lax.axis_size(axis)
+            peers += [(axis, lax.rem(me + d, n)) for d in range(1, n)]
+        greet(peers)
+        base, running = 0, []
+        for p in parts:
+            take = lambda pool, k: [pool.pop(0) for _ in range(k)]
+            refs_p = (take(in_refs, len(p.ins)), take(out_refs, len(p.outs)), take(scr, len(p.scratch)))
+            counter = [base]
+
+            def go(src, dst, axis, peer, counter=counter):
+                counter[0] += 1
+                return send(src, dst, sems, counter[0] - 1, axis, peer)
+
+            running.append(p.phases(*refs_p, go))
+            base += p.copies
+        while running:
+            running = [r for r in running if next(r, True) is None]
+
     return pl.pallas_call(
         body,
-        out_shape=out_shapes,
-        in_specs=[VM] * len(operands),
-        out_specs=[VM] * len(out_shapes),
-        scratch_shapes=list(scratch) + [pltpu.SemaphoreType.DMA((2, copies))],
+        out_shape=outs,
+        in_specs=sum([p.specs for p in parts], []),
+        out_specs=[VM] * len(outs),
+        scratch_shapes=scratch + [pltpu.SemaphoreType.DMA((2, copies))],
         compiler_params=pltpu.CompilerParams(collective_id=collective_id, has_side_effects=True),
+        cost_estimate=cost,
         name=name,
-    )(*operands)
-
-
-def exchange(parts, collective_id, name):
-    sizes = [lax.axis_size(axis) for axis, _, _ in parts]
-    count = len(parts)
-    out_shapes, scratch = [], []
-    for (axis, kind, x), n in zip(parts, sizes):
-        piece = x.shape if kind in (GATHER, GATHER_SUM) else x.shape[1:]
-        if kind in (GATHER_SUM, SWAP_SUM):
-            out_shapes.append(jax.ShapeDtypeStruct(piece, f32))
-            scratch.append(pltpu.VMEM((n,) + piece, x.dtype))
-        else:
-            out_shapes.append(jax.ShapeDtypeStruct((n,) + piece, x.dtype))
-    copies = sum(n - 1 for n in sizes)
-
-    def body(*refs):
-        ins, outs = refs[:count], refs[count : 2 * count]
-        lands, sems = list(refs[2 * count : -1]), refs[-1]
-        peers, seen = [], set()
-        for (axis, _, _), n in zip(parts, sizes):
-            if axis not in seen:
-                seen.add(axis)
-                me = lax.axis_index(axis)
-                peers += [(axis, lax.rem(me + d, n)) for d in range(1, n)]
-        greet(peers)
-        started, index, slots = [], 0, []
-        for k, ((axis, kind, _), n) in enumerate(zip(parts, sizes)):
-            land = lands.pop(0) if kind in (GATHER_SUM, SWAP_SUM) else outs[k]
-            slots.append(land)
-            me = lax.axis_index(axis)
-            for d in range(1, n):
-                peer = lax.rem(me + d, n)
-                src = ins[k] if kind in (GATHER, GATHER_SUM) else ins[k].at[peer]
-                started.append(send(src, land.at[me], sems, index, axis, peer))
-                index += 1
-        for k, ((axis, kind, _), n) in enumerate(zip(parts, sizes)):
-            me = lax.axis_index(axis)
-            own = ins[k][...] if kind in (GATHER, GATHER_SUM) else ins[k][me]
-            slots[k][me] = own
-        index = 0
-        for k, ((axis, kind, _), n) in enumerate(zip(parts, sizes)):
-            for d in range(1, n):
-                started[index].wait()
-                index += 1
-            if kind in (GATHER_SUM, SWAP_SUM):
-                total = slots[k][0].astype(f32)
-                for j in range(1, n):
-                    total = total + slots[k][j].astype(f32)
-                outs[k][...] = total
-
-    return comm_call(
-        body, name, collective_id, out_shapes, scratch, copies, [x for _, _, x in parts]
-    )
-
-
-def tree_gather(x, collective_id, name):
+    )(*ins)
+
+
+def start_swap(go, src, land, axis, gather):
+    me, n = lax.axis_index(axis), lax.axis_size(axis)
+    started = []
+    for d in range(1, n):
+        peer = lax.rem(me + d, n)
+        started.append(go(src if gather else src.at[peer], land.at[me], axis, peer))
+    land[me] = src[...] if gather else src[me]
+    return started
+
+
+def total_of(land, n):
+    total = land[0].astype(f32)
+    for j in range(1, n):
+        total = total + land[j].astype(f32)
+    return total
+
+
+def exchange(axis, kind, x):
+    n = lax.axis_size(axis)
+    gather, summed = kind in (GATHER, GATHER_SUM), kind in (GATHER_SUM, SWAP_SUM)
+    piece = x.shape if gather else x.shape[1:]
+    shape = jax.ShapeDtypeStruct
+    outs = [shape(piece, f32) if summed else shape((n,) + piece, x.dtype)]
+    scratch = [pltpu.VMEM((n,) + piece, x.dtype)] if summed else []
+
+    def phases(ins, outs, scr, go):
+        land = scr[0] if summed else outs[0]
+        started = start_swap(go, ins[0], land, axis, gather)
+        yield
+        for copy in started:
+            copy.wait()
+        if summed:
+            outs[0][...] = total_of(land, n)
+
+    return Part([axis], [x], outs, scratch, n - 1, phases)
+
+
+def tree_gather(x):
     lines = x.shape[0]
-    half = lines // 2
-
-    def body(x_ref, out_ref, sems):
+    cuts = [(0, lines // 2), (lines // 2, lines)] if lines > 1 else [(0, 1)]
+    cuts = [pl.ds(lo, hi - lo) for lo, hi in cuts]
+
+    def phases(ins, outs, scr, go):
+        x_ref, out_ref = ins[0], outs[0]
+        me, _, _, near, far = shard_peers()
+        across = [go(x_ref.at[c], out_ref.at[c, me], SH, far) for c in cuts]
+        own = go(x_ref, out_ref.at[:, me], SH, near)
+        out_ref[:, me] = x_ref[...]
+        yield
+        handed = []
+        for c, copy in zip(cuts, across):
+            copy.wait_recv()
+            handed.append(go(out_ref.at[c, far], out_ref.at[c, far], SH, near))
+        yield
+        for copy in across:
+            copy.wait_send()
+        own.wait()
+        for copy in handed:
+            copy.wait()
+
+    shape = (lines, 4) + x.shape[1:]
+    return Part([SH], [x], [jax.ShapeDtypeStruct(shape, x.dtype)], [], 2 * len(cuts) + 1, phases)
+
+
+def core_sum(x):
+    piece = x.shape[1:]
+    shape = jax.ShapeDtypeStruct
+
+    def phases(ins, outs, scr, go):
+        x_ref, (here, there), (land, kept, sems) = ins[0], outs, scr
+        near = shard_peers()[3]
+        sent = [go(x_ref.at[3], land.at[1], SH, near), go(x_ref.at[2], land.at[0], SH, near)]
+        local = [pltpu.make_async_copy(x_ref.at[k], kept.at[k], sems.at[k]) for k in range(2)]
+        for copy in local:
+            copy.start()
+        yield
+        for k, out in ((1, there), (0, here)):
+            sent[1 - k].wait()
+            local[k].wait()
+            out[...] = (kept[k].astype(f32) + land[k].astype(f32)).astype(bf16)
+
+    return Part(
+        [SH],
+        [x],
+        [shape(piece, bf16)] * 2,
+        [pltpu.VMEM((2,) + piece, bf16)] * 2 + [pltpu.SemaphoreType.DMA((2,))],
+        2,
+        phases,
+        [pl.BlockSpec(memory_space=pl.ANY)],
+    )
+
+
+class Tree:
+    copies = 3
+
+    @staticmethod
+    def scratch(piece):
+        return [pltpu.VMEM((2,) + piece, bf16)] + [pltpu.VMEM(piece, bf16)] * 2
+
+    def __init__(self, x, scr, go):
+        self.x, (self.land, self.mine, self.got), self.go = x, scr, go
+        self.me, self.side, self.core, self.near, self.far = shard_peers()
+        other = 2 * (1 - self.side) + 1 - self.core
+        self.first = [
+            go(x.at[other], self.land.at[0], SH, self.near),
+            go(x.at[self.near], self.land.at[1], SH, self.near),
+        ]
+
+    def across(self):
+        self.first[0].wait_recv()
+        self.mine[...] = (self.x[self.far].astype(f32) + self.land[0].astype(f32)).astype(bf16)
+        self.second = self.go(self.mine, self.got, SH, self.far)
+
+    def result(self):
+        self.first[1].wait_recv()
+        total = self.x[self.me].astype(f32) + self.land[1].astype(f32)
+        self.second.wait_recv()
+        return total + self.got[...].astype(f32)
+
+    def close(self):
+        for copy in (*self.first, self.second):
+            copy.wait_send()
+
+
+def tail(dkv, dq, attn_in, weights, out_term, packed, hidden, resid_grad, gain):
+    lines, rows, width = dq.shape
+    model = lines * width
+    own = rows // lines
+    groups = lax.axis_size(GR)
+    shape = jax.ShapeDtypeStruct
+    vmem = pltpu.VMEM
+    tok = lines * rows
+    dkv_piece, q_piece = (lines, rows, 2 * width), (lines, own, width)
+    kv_piece, o_piece = (lines, own, 2 * width), (lines, own, model)
+    part_dims = (width, 2 * width, model)
+
+    def phases(ins, outs, scr, go):
+        dkv_ref, dq_ref, attn_ref, w_ref, o_ref, packed_ref, hid_ref, resid_ref, gain_ref = ins
+        input_ref, qkv_out, out_out, packed_out, gain_out = outs
+        scr = list(scr)
+        take = lambda k: [scr.pop(0) for _ in range(k)]
+        kv_scr, q_scr, kvw_scr, o_scr = take(3), take(3), take(3), take(3)
+        own_kv, q_t, kv_t, dq_all, dkv_all, dq_full = take(6)
+        sums, lands, halves, gots = take(3), take(3), take(3), take(3)
+        pk_l, pk_s, pk_g = take(3)
+        mid_l, mid_s = take(2)
+        gn_l, gn_s, gn_g, gn_0, gn_1, gn_2 = take(6)
         me = lax.axis_index(SH)
-        near, far = lax.rem(me + 1, 2) + 2 * (me // 2), lax.rem(me + 2, 4)
-        greet([(SH, near), (SH, far)])
-        lo, hi = pl.ds(0, half), pl.ds(half, half)
-        far_lo = send(x_ref.at[lo], out_ref.at[lo, me], sems, 0, SH, far)
-        far_hi = send(x_ref.at[hi], out_ref.at[hi, me], sems, 1, SH, far)
-        own = send(x_ref, out_ref.at[:, me], sems, 2, SH, near)
-        out_ref[:, me] = x_ref[...]
-        far_lo.wait_recv()
-        pass_lo = send(out_ref.at[lo, far], out_ref.at[lo, far], sems, 3, SH, near)
-        far_hi.wait_recv()
-        pass_hi = send(out_ref.at[hi, far], out_ref.at[hi, far], sems, 4, SH, near)
-        far_lo.wait_send()
-        far_hi.wait_send()
-        own.wait()
-        pass_lo.wait()
-        pass_hi.wait()
-
-    shape = (lines, 4) + x.shape[1:]
-    return comm_call(
-        body, name, collective_id, [jax.ShapeDtypeStruct(shape, x.dtype)], [], 5, [x]
-    )[0]
-
-
-def tree_reduce(arrays, collective_id, name):
-    count = len(arrays)
-    scratch = []
-    for x in arrays:
-        scratch += [pltpu.VMEM((2,) + x.shape[1:], bf16)] + [pltpu.VMEM(x.shape[1:], bf16)] * 2
-
-    def body(*refs):
-        ins, outs = refs[:count], refs[count : 2 * count]
-        sems = refs[-1]
-        me = lax.axis_index(SH)
-        side, core = me // 2, lax.rem(me, 2)
-        near, far = 2 * side + 1 - core, 2 * (1 - side) + core
-        other = 1 - side
-        greet([(SH, near), (SH, far)])
-        first = []
-        for k in range(count):
-            land = refs[2 * count + 3 * k]
-            first.append(
-                (
-                    send(
-                        ins[k].at[2 * other + 1 - core], land.at[0], sems, 3 * k, SH, near
-                    ),
-                    send(
-                        ins[k].at[2 * side + 1 - core], land.at[1], sems, 3 * k + 1, SH, near
-                    ),
-                )
-            )
-        second = []
-        for k in range(count):
-            land, mine, got = refs[2 * count + 3 * k : 2 * count + 3 * k + 3]
-            first[k][0].wait_recv()
-            mine[...] = (ins[k][far].astype(f32) + land[0].astype(f32)).astype(bf16)
-            second.append(send(mine, got, sems, 3 * k + 2, SH, far))
-        for k in range(count):
-            land, mine, got = refs[2 * count + 3 * k : 2 * count + 3 * k + 3]
-            first[k][1].wait_recv()
-            outs[k][...] = ins[k][me].astype(f32) + land[1].astype(f32)
-        for k in range(count):
-            got = refs[2 * count + 3 * k + 2]
-            second[k].wait_recv()
-            outs[k][...] += got[...].astype(f32)
-            first[k][0].wait_send()
-            first[k][1].wait_send()
-            second[k].wait_send()
-
-    return comm_call(
-        body,
-        name,
-        collective_id,
-        [jax.ShapeDtypeStruct(x.shape[1:], f32) for x in arrays],
-        scratch,
-        3 * count,
-        arrays,
-    )
+
+        kv_tree = Tree(dkv_ref, kv_scr, go)
+        dq_swap = start_swap(go, dq_ref, dq_all, EX, False)
+        o_tree = Tree(o_ref, o_scr, go)
+        pk1 = start_swap(go, packed_ref, pk_l, EX, True)
+
+        def term(rows_ref, out):
+            value = contract(attn_ref[...], rows_ref[...].reshape(tok, rows_ref.shape[-1]), 0, 0)
+            value = value.astype(bf16)
+            for line in range(lines):
+                for piece in range(4):
+                    at = (line * 4 + piece) * own
+                    out[piece, line] = value[at : at + own]
+
+        kv_tree.across()
+        term(dq_ref, q_t)
+        o_tree.across()
+        q_tree = Tree(q_t, q_scr, go)
+        trees = [q_tree, None, o_tree]
+
+        def lines_out(k):
+            sums[k][...] = trees[k].result().astype(bf16)
+            return start_swap(go, sums[k], lands[k], EX, False)
+
+        own_kv[...] = kv_tree.result().astype(bf16)
+        dkv_swap = start_swap(go, own_kv, dkv_all, EX, False)
+        o_lines = lines_out(2)
+        q_tree.across()
+        term(own_kv, kv_t)
+        kvw_tree = Tree(kv_t, kvw_scr, go)
+        trees[1] = kvw_tree
+        for copy in pk1:
+            copy.wait()
+        mid_l[...] = total_of(pk_l, lines)
+        pk2 = start_swap(go, mid_l, pk_s, SH, True)
+        kvw_tree.across()
+        q_lines = lines_out(0)
+        for copy in dq_swap:
+            copy.wait()
+        for line in range(lines):
+            dq_full[:, line * width : (line + 1) * width] = dq_all[line]
+        grad = contract(dq_full[...], w_ref[0], 1, 1)
+        for copy in pk2:
+            copy.wait()
+        mid_s[...] = total_of(pk_s, 4)
+        pk3 = start_swap(go, mid_s, pk_g, GR, True)
+        kv_lines = lines_out(1)
+        for copy in dkv_swap:
+            copy.wait()
+        for half in range(2):
+            for line in range(lines):
+                dq_full[:, line * width : (line + 1) * width] = dkv_all[
+                    line, :, half * width : (half + 1) * width
+                ]
+            grad = grad + contract(dq_full[...], w_ref[1 + half], 1, 1)
+        inputs = hid_ref[...].astype(f32)
+        inv = lax.rsqrt(jnp.mean(inputs * inputs, axis=1, keepdims=True) + norm_eps)
+        normed = inputs * inv
+        gn_0[...] = jnp.sum((grad * normed).reshape(rows // 8, 8, model), axis=0)
+        gn1 = start_swap(go, gn_0, gn_l, EX, True)
+        input_ref[...] = resid_ref[...] + rms_back(inputs, inv, gain_ref[...], grad)
+        swaps = [None] * 3
+        for k, copies in ((2, o_lines), (0, q_lines)):
+            for copy in copies:
+                copy.wait()
+            if k == 2:
+                halves[k][...] = total_of(lands[k], lines).astype(bf16)
+            else:
+                halves[k][...] = lands[k][...]
+            swaps[k] = start_swap(go, halves[k], gots[k], GR, True)
+        for copy in gn1:
+            copy.wait()
+        gn_1[...] = total_of(gn_l, lines)
+        gn2 = start_swap(go, gn_1, gn_s, SH, True)
+        for copy in kv_lines:
+            copy.wait()
+        halves[1][...] = lands[1][...]
+        swaps[1] = start_swap(go, halves[1], gots[1], GR, True)
+        for copy in gn2:
+            copy.wait()
+        gn_2[...] = total_of(gn_s, 4)
+        gn3 = start_swap(go, gn_2, gn_g, GR, True)
+        for copy in pk3:
+            copy.wait()
+        packed_out[...] = total_of(pk_g, groups)
+        for k in (2, 0, 1):
+            for copy in swaps[k]:
+                copy.wait()
+            value = total_of(gots[k], groups)
+            if k == 2:
+                out_out[...] = value
+            elif k == 0:
+                for line in range(lines):
+                    qkv_out[0, :, line * width : (line + 1) * width] = value[line]
+            else:
+                for half in range(2):
+                    for line in range(lines):
+                        qkv_out[1 + half, :, line * width : (line + 1) * width] = value[
+                            line, :, half * width : (half + 1) * width
+                        ]
+        for copy in gn3:
+            copy.wait()
+        gain_out[...] = jnp.sum(total_of(gn_g, groups), axis=0, keepdims=True)
+        for tree in (kv_tree, o_tree, q_tree, kvw_tree):
+            tree.close()
+        yield
+
+    pieces = [(lines, own, d) for d in part_dims]
+    got_pieces = pieces[:2] + [(own, model)]
+    scratch = Tree.scratch(dkv_piece) + Tree.scratch(q_piece) + Tree.scratch(kv_piece)
+    scratch += Tree.scratch(o_piece)
+    scratch += [
+        vmem(dkv_piece, bf16),
+        vmem((4,) + q_piece, bf16),
+        vmem((4,) + kv_piece, bf16),
+        vmem((lines, rows, width), bf16),
+        vmem((lines, rows, 2 * width), bf16),
+        vmem((rows, model), bf16),
+    ]
+    scratch += [vmem(p, bf16) for p in pieces] + [vmem(p, bf16) for p in pieces]
+    scratch += [vmem(p, bf16) for p in got_pieces] + [vmem((groups,) + p, bf16) for p in got_pieces]
+    scratch += [vmem((n,) + packed.shape, f32) for n in (lines, 4, groups)]
+    scratch += [vmem(packed.shape, f32)] * 2
+    scratch += [vmem((n, 8, model), f32) for n in (lines, 4, groups)] + [vmem((8, model), f32)] * 3
+    copies = 4 * Tree.copies + 7 * (lines - 1) + 2 * 3 + 5 * (groups - 1)
+    outs = [
+        shape((rows, model), f32),
+        shape((3, own, model), f32),
+        shape((own, model), f32),
+        shape(packed.shape, f32),
+        shape((1, model), f32),
+    ]
+    ins = [dkv, dq, attn_in, weights, out_term, packed, hidden, resid_grad, gain]
+    return Part([EX, SH, GR], ins, outs, scratch, copies, phases)
+
+
+def expert_body(steps, x_ref, g_ref, wg_ref, wu_ref, wd_ref, eo_ref, ib_ref, gu_ref, d_ref, eo_s, ib_s):
+    i = pl.program_id(0)
+    me, side, core, _, _ = shard_peers()
+
+    @pl.when(i == 0)
+    def _():
+        eo_s[...] = jnp.zeros_like(eo_s)
+        ib_s[...] = jnp.zeros_like(ib_s)
+
+    x, g = x_ref[...], g_ref[...]
+    wg, wu, wd = wg_ref[...], wu_ref[...], wd_ref[...]
+    gate_pre = jnp.dot(x, wg, preferred_element_type=f32)
+    up_pre = jnp.dot(x, wu, preferred_element_type=f32)
+    hidden_grad = contract(g, wd, 1, 1)
+    gate_sigmoid = jax.nn.sigmoid(gate_pre)
+    act = (gate_pre * gate_sigmoid * up_pre).astype(bf16)
+    gate_back = (
+        hidden_grad * up_pre * gate_sigmoid * (1.0 + gate_pre * (1.0 - gate_sigmoid))
+    ).astype(bf16)
+    up_back = (hidden_grad * gate_pre * gate_sigmoid).astype(bf16)
+    eo_s[...] += jnp.dot(act, wd, preferred_element_type=f32)
+    ib_s[...] += contract(gate_back, wg, 1, 1) + contract(up_back, wu, 1, 1)
+
+    def place(quarter):
+        return 2 * lax.rem(lax.rem(quarter, 2) + core, 2) + lax.rem(quarter // 2 + side, 2)
+
+    rows = gu_ref.shape[2]
+    for k, back in enumerate((gate_back, up_back)):
+        term = contract(x, back, 0, 0).astype(bf16)
+        for quarter in range(4):
+            gu_ref[place(jnp.int32(quarter)), k] = term[quarter * rows : (quarter + 1) * rows]
+    d_ref[place(i)] = contract(act, g, 0, 0).astype(bf16)
+
+    @pl.when(i == steps - 1)
+    def _():
+        eo_ref[...] = eo_s[...].astype(bf16)
+        ib_ref[...] = ib_s[...].astype(bf16)
+
+
+def expert(x, g, wg, wu, wd):
+    slots, model = x.shape
+    inner = wg.shape[1]
+    steps = 4
+    tile = inner // steps
+    quarter = model // 4
+    shape = jax.ShapeDtypeStruct
+    whole = lambda dims: pl.BlockSpec(dims, lambda i: (0,) * len(dims))
+    return pl.pallas_call(
+        functools.partial(expert_body, steps),
+        grid=(steps,),
+        out_shape=[
+            shape((slots, model), bf16),
+            shape((slots, model), bf16),
+            shape((4, 2, quarter, inner), bf16),
+            shape((4, tile, model), bf16),
+        ],
+        in_specs=[
+            whole((slots, model)),
+            whole((slots, model)),
+            pl.BlockSpec((model, tile), lambda i: (0, i)),
+            pl.BlockSpec((model, tile), lambda i: (0, i)),
+            pl.BlockSpec((tile, model), lambda i: (i, 0)),
+        ],
+        out_specs=[
+            whole((slots, model)),
+            whole((slots, model)),
+            pl.BlockSpec((4, 2, quarter, tile), lambda i: (0, 0, 0, i)),
+            whole((4, tile, model)),
+        ],
+        scratch_shapes=[pltpu.VMEM((slots, model), f32)] * 2,
+        cost_estimate=pl.CostEstimate(flops=6 * 10**9, bytes_accessed=2 * 10**7, transcendentals=4 * 10**5),
+        name="ffn",
+    )(x, g, wg, wu, wd)
 
 
 def head_columns(h, shape, axis):
@@ -820,23 +1085,10 @@
 
 
 def swap(x, axis, partner):
-    n = lax.axis_size(axis)
-    return lax.ppermute(x, axis, [(i, partner(i)) for i in range(n)])
-
-
-def pick(x, index):
-    return lax.dynamic_index_in_dim(x, index, axis=0, keepdims=False)
-
-
-def reduce_expert(term):
-    me = lax.axis_index(SH)
-    side, core = me // 2, lax.rem(me, 2)
-    rows, cols = term.shape
-    parts = term.reshape(2, 2, rows // 4, cols).swapaxes(0, 1)
-    kept, sent = pick(parts, core), pick(parts, 1 - core).astype(bf16)
-    both = kept + swap(sent, SH, lambda i: i ^ 1).astype(f32)
-    kept, sent = pick(both, side), pick(both, 1 - side).astype(bf16)
-    mine = (kept + swap(sent, SH, lambda i: i ^ 2).astype(f32)).astype(bf16)
+    return lax.ppermute(x, axis, [(i, partner(i)) for i in range(lax.axis_size(axis))])
+
+
+def over_group(mine):
     n = lax.axis_size(GR)
     if n == 2:
         return mine.astype(f32) + swap(mine, GR, lambda i: 1 - i).astype(f32)
@@ -871,13 +1123,10 @@
     w_mine = lax.dynamic_slice_in_dim(
         jnp.stack([w_query, w_key, w_value]), line * width, width, axis=2
     )
-    hidden_all, w_cols, w_out_all = exchange(
-        [(EX, GATHER, hidden_in), (SH, GATHER, w_mine), (SH, GATHER, w_out)],
-        0,
-        "gather_in",
+    hidden_all, w_cols = run_parts(
+        [exchange(EX, GATHER, hidden_in), exchange(SH, GATHER, w_mine)], 0, "gather_in"
     )
     w_heads = w_cols.swapaxes(0, 1).reshape(3, model, width)
-    wo_full = w_out_all.reshape(model, model)
     inputs_all = hidden_all.reshape(lines * rows, model).astype(f32)
     inv_all = lax.rsqrt(jnp.mean(inputs_all * inputs_all, axis=1, keepdims=True) + norm_eps)
     attn_in = (inputs_all * inv_all * attn_gain).astype(bf16)
@@ -885,7 +1134,7 @@
     w_kv = jnp.concatenate([w_heads[1], w_heads[2]], axis=1)
     kv = jnp.dot(attn_in, w_kv, preferred_element_type=f32).astype(bf16)
     q = q.reshape(lines, rows, width)
-    kv_all = tree_gather(kv.reshape(lines, rows, 2 * width), 1, "gather_kv")
+    (kv_all,) = run_parts([tree_gather(kv.reshape(lines, rows, 2 * width))], 1, "gather_kv")
     kv_all = kv_all.reshape(length, 2 * width)
 
     own_seg = jnp.take(seg.reshape(lines, 4, rows), shard, axis=1)
@@ -896,11 +1145,13 @@
     info = jnp.concatenate([prompt[None], qstart[:, 0]])
     qinfo = jnp.broadcast_to(qstart[:, None, :], (lines, 8, rows))
     attn_vec, attn_low_heads, lse = attend(info, q, kv_all, qinfo)
-    (attn_parts,) = exchange([(EX, SWAP, attn_low_heads)], 2, "heads_out")
+    attn_parts, wo_full = run_parts(
+        [exchange(EX, SWAP, attn_low_heads), tree_gather(w_out[None])], 2, "heads_out"
+    )
+    wo_full = wo_full.reshape(model, model)
     attn_low = attn_parts.swapaxes(0, 1).reshape(rows, model)
 
     inputs = hidden_in.astype(f32)
-    inv_one = lax.rsqrt(jnp.mean(inputs * inputs, axis=1, keepdims=True) + norm_eps)
     resid_one = inputs + jnp.dot(attn_low, wo_full, preferred_element_type=f32)
     inv_two = lax.rsqrt(jnp.mean(resid_one * resid_one, axis=1, keepdims=True) + norm_eps)
     normed_two = resid_one * inv_two
@@ -931,40 +1182,32 @@
     either = place[0] + place[1]
     send_rows = contract(either, moe_low, 0, 0).astype(bf16)
     grad_send = (contract(either, out_grad, 0, 0) * sit_gate[:, None]).astype(bf16)
-    recv_rows, recv_grads = exchange(
+    recv_rows, recv_grads, weights = run_parts(
         [
-            (EX, SWAP, send_rows.reshape(lines, CAP, model)),
-            (EX, SWAP, grad_send.reshape(lines, CAP, model)),
+            exchange(EX, SWAP, send_rows.reshape(lines, CAP, model)),
+            exchange(EX, SWAP, grad_send.reshape(lines, CAP, model)),
+            tree_gather(jnp.stack([w_query, w_key, w_value])),
         ],
         3,
         "dispatch",
     )
-
-    expert_in = recv_rows.reshape(slots, model)
-    out_back = recv_grads.reshape(slots, model)
-    wg, wu, wd = w_gate[0], w_up[0], w_down[0]
-    gate_pre = jnp.dot(expert_in, wg, preferred_element_type=f32)
-    up_pre = jnp.dot(expert_in, wu, preferred_element_type=f32)
-    gate_sigmoid = jax.nn.sigmoid(gate_pre)
-    hidden_act = (gate_pre * gate_sigmoid * up_pre).astype(bf16)
-    expert_out = jnp.dot(hidden_act, wd, preferred_element_type=f32).astype(bf16)
-    hidden_grad = contract(out_back, wd, 1, 1)
-    gate_back = (
-        hidden_grad * up_pre * gate_sigmoid * (1.0 + gate_pre * (1.0 - gate_sigmoid))
-    ).astype(bf16)
-    up_back = (hidden_grad * gate_pre * gate_sigmoid).astype(bf16)
-    input_back = (contract(gate_back, wg, 1, 1) + contract(up_back, wu, 1, 1)).astype(bf16)
-    returned, input_ret = exchange(
+    weights = weights.reshape(3, model, model)
+
+    expert_out, input_back, gate_up, down = expert(
+        recv_rows.reshape(slots, model), recv_grads.reshape(slots, model), w_gate[0], w_up[0], w_down[0]
+    )
+    returned, input_ret, gu_here, gu_there, d_here, d_there = run_parts(
         [
-            (EX, SWAP, expert_out.reshape(lines, CAP, model)),
-            (EX, SWAP, input_back.reshape(lines, CAP, model)),
+            exchange(EX, SWAP, expert_out.reshape(lines, CAP, model)),
+            exchange(EX, SWAP, input_back.reshape(lines, CAP, model)),
+            core_sum(gate_up),
+            core_sum(down),
         ],
         4,
         "combine",
     )
-    down_part = reduce_expert(contract(hidden_act, out_back, 0, 0))
-    gate_part = reduce_expert(contract(expert_in, gate_back, 0, 0))
-    up_part = reduce_expert(contract(expert_in, up_back, 0, 0))
+    gu_far = swap(gu_there, SH, lambda i: i ^ 2)
+    d_far = swap(d_there, SH, lambda i: i ^ 2)
 
     returned = returned.reshape(slots, model)
     route_out = jnp.stack(
@@ -1012,70 +1255,42 @@
     branch_low = resid_grad.astype(bf16)
     attn_back = contract(branch_low, wo_full, 1, 1).astype(bf16)
     attn_back = attn_back.reshape(rows, lines, width).swapaxes(0, 1)
-    (back_heads,) = exchange([(EX, SWAP, attn_back)], 5, "heads_back")
-    out_proj_term = contract(attn_low, branch_low, 0, 0).astype(bf16)
+    (back_heads,) = run_parts([exchange(EX, SWAP, attn_back)], 5, "heads_back")
+    own = rows // lines
+    out_term = contract(attn_low, branch_low, 0, 0).astype(bf16)
+    out_term = out_term.reshape(lines, 4, own, model).swapaxes(0, 1)
+    packed = jnp.concatenate([moe_gain_grad[None], vec_grad, small_grad], axis=0)
+    packed = jnp.pad(packed, ((0, -packed.shape[0] % 8), (0, 0)))
 
     dq, dkv = attend_back(info, q, kv_all, qinfo, attn_vec, lse, back_heads)
-    (dkv_own,) = tree_reduce([dkv], 6, "reduce_kv")
-    dkv_own = dkv_own.reshape(lines * rows, 2 * width).astype(bf16)
-    dq = dq.reshape(lines * rows, width)
-    back_in = (
-        contract(dq, w_heads[0], 1, 1) + contract(dkv_own, w_kv, 1, 1)
-    ).astype(bf16)
-    own = rows // lines
-    q_term = contract(attn_in, dq, 0, 0)
-    kv_term = contract(attn_in, dkv_own, 0, 0)
-    qkv_term = jnp.concatenate([q_term, kv_term], axis=1).astype(bf16)
-    qkv_term = qkv_term.reshape(lines, 4, own, 3 * width).swapaxes(0, 1)
-    out_term = out_proj_term.reshape(lines, 4, own, model).swapaxes(0, 1)
-    (attn_in_grad,) = exchange(
-        [(EX, SWAP_SUM, back_in.reshape(lines, rows, model))], 7, "input_back"
-    )
-    qkv_sum, out_sum = tree_reduce([qkv_term, out_term], 8, "reduce_w")
-    qkv_part, out_part = exchange(
+    gu_mine = (gu_here.astype(f32) + gu_far.astype(f32)).astype(bf16)
+    d_mine = (d_here.astype(f32) + d_far.astype(f32)).astype(bf16)
+    dkv, gu_mine, d_mine = lax.optimization_barrier((dkv, gu_mine, d_mine))
+    gate_up_part, down_part = over_group(gu_mine), over_group(d_mine)
+    input_grad, qkv_part, out_part, packed, gain_sum = run_parts(
         [
-            (EX, SWAP, qkv_sum.astype(bf16)),
-            (EX, SWAP_SUM, out_sum.astype(bf16)),
+            tail(
+                dkv, dq, attn_in, weights, out_term, packed, hidden_in, resid_grad, attn_gain[None]
+            )
         ],
-        9,
-        "lines_w",
-    )
-    normed_one = inputs * inv_one
-    attn_gain_grad = jnp.sum(attn_in_grad * normed_one, axis=0)
-    input_grad = resid_grad + rms_back(inputs, inv_one, attn_gain, attn_in_grad)
-
-    packed = jnp.concatenate(
-        [attn_gain_grad[None], moe_gain_grad[None], vec_grad, small_grad], axis=0
-    )
-    packed, qkv_part, out_part = exchange(
-        [
-            (GR, GATHER_SUM, packed),
-            (GR, GATHER_SUM, qkv_part),
-            (GR, GATHER_SUM, out_part.astype(bf16)),
-        ],
-        10,
-        "group_sum",
-    )
-    (packed,) = exchange([(EX, GATHER_SUM, packed)], 11, "small_lines")
-    (packed,) = exchange([(SH, GATHER_SUM, packed)], 12, "small_shards")
-    grads = [
-        qkv_part[:, :, k * width : (k + 1) * width].swapaxes(0, 1).reshape(own, model)
-        for k in range(3)
-    ]
+        6,
+        "tail",
+        pl.CostEstimate(flops=2 * 10**10, bytes_accessed=10**8, transcendentals=0),
+    )
     return (
         layer_out,
         input_grad,
+        gain_sum[0],
+        qkv_part[0],
+        qkv_part[1],
+        qkv_part[2],
+        out_part,
         packed[0],
-        grads[0],
-        grads[1],
-        grads[2],
-        out_part,
-        packed[1],
-        packed[4 : 4 + n_ids].T,
-        packed[4 + n_ids :].T,
-        packed[2:4],
-        gate_part[None],
-        up_part[None],
+        packed[3 : 3 + n_ids].T,
+        packed[3 + n_ids : 7 + n_ids].T,
+        packed[1:3],
+        gate_up_part[0][None],
+        gate_up_part[1][None],
         down_part[None],
     )
 

time: 469 us -> 322 us (0.69); the launches traced: 465 us -> 326 us
  waiting for transfers between devices: 44.7 us -> 0.01 us
  local copies, waits for them, and re-layouts: 50.8 us -> 22.3 us
  matrix products: 41.5 us -> 14.2 us
  other arithmetic: 49.9 us -> 26.2 us
  Pallas kernels: 270 us -> 258 us
    ppermute x9 -> x4, waiting for transfers between devices: 44.7 us -> 0.01 us  [swap(): lax.ppermute(x, axis, [(i, partner(i)) for i in range(lax.axis_size(axis))])]
    pallas_call x13 -> x8, Pallas kernels: 229 us -> 210 us  [the longest x7 197 us: run_parts(): pl.pallas_call(body, out_shape=outs, in_specs=sum([p.specs for p in parts...]
    dot_general x16 -> x6, matrix products: 21.9 us -> 3.85 us  [contract(): lax.dot_general(a, b, (((da,), (db,)), ((), ())), preferred_element_type=...]
    convert_element_type x8 -> x2, other arithmetic: 12.1 us -> 3.43 us  [the longest x1 2 us: fast_shards(): gu_mine = (gu_here.astype(f32) + gu_far.astype(f32)).astype(bf16)]
    convert_element_type x6 -> x0, local copies, waits for them, and re-layouts: 7.34 us -> none  [the longest x3 4.14 us: reduce_expert(): kept, sent = (pick(parts, core), pick(parts, 1 - core).astype(bf16))]
    dot_general x3 -> x0, matrix products: 7.22 us -> none  [the longest x1 2.91 us: fast_shards(): up_pre = jnp.dot(expert_in, wu, preferred_element_type=f32)]
    unnamed x154 -> x81, local copies, waits for them, and re-layouts: 11.1 us -> 4.34 us
    add x4 -> x1, other arithmetic: 8.22 us -> 1.96 us  [over_group(): return mine.astype(f32) + swap(mine, GR, lambda i: 1 - i).astype(f32)]
  transfers between devices with their start and end apart: 9 -> 4, of which waited for: 5 -> 0; matrix products, arithmetic and copies ran while one was open for 18% -> 10% of each run, Pallas kernels for 36% -> 32%
where the time goes in v2:
time: 322 us; the launch traced here: 326 us
  Pallas kernels  258 us (80%)
  other arithmetic  26.2 us (8%)
  local copies, waits for them, and re-layouts  22.3 us (7%)
  matrix products  14.2 us (4%)
  starting transfers between devices  4.17 us (1%)
    pallas_call x7, Pallas kernels, run_parts(): pl.pallas_call(body, out_shape=outs, in_specs=sum([p.specs for p in parts...  197 us
    pallas_call x1, Pallas kernels, attend_back(): pl.pallas_call(functools.partial(attend_back_body, lines, heads), out_sha...  29.1 us
    pallas_call x1, Pallas kernels, attend(): pl.pallas_call(functools.partial(attend_body, lines, heads), out_shape=[s...  18.4 us
    pallas_call x1, Pallas kernels, expert(): pl.pallas_call(functools.partial(expert_body, steps), grid=(steps,), out_...  13.1 us
  transfers between devices with their start and end apart: 4, of which 0 were waited for; matrix products, arithmetic and copies ran while one was open for 10% of the time, Pallas kernels for 32%

profile of v2, /device:TPU:0, one launch (start us, length us, event | category | flops | bytes accessed | tf_op | source)
XLA Modules:
  0.0 326.1 jit_solution(16568267419377140015)
XLA Ops:
  0.7 1.2 pad_maximum_fusion.1.refs_2_
  1.9 1.0 constant_dynamic-slice_fusion.refs_1_
  2.9 28.8 %gather_in.1 = (bf16[4,192,768]{2,1,0:T(8,128)(2,1)}, bf16[4,3,192,192]{3,2,1,0:T(8,128)(2,1)}) custom-call(bf16[192,768]{1,0:T(8,128)(2,1)} %refs_6_.1, bf16[3,192,192]{2,1,0:T(8,128)(2,1)} %constant_dynamic-slice_fusion.refs_1_), custom_call_target="tpu_custom_call" | custom-call | tf_op jit(solution)/shard_map/gather_in/pallas_call | solution.py:527
  31.7 1.7 multiply_reduce_fusion
  34.2 0.9 copy-done.7
  35.2 1.7 convolution_convert_fusion.1
  36.8 19.4 %gather_kv.1 = bf16[4,4,192,384]{3,2,1,0:T(8,128)(2,1)} custom-call(bf16[4,192,384]{2,1,0:T(8,128)(2,1)} %bitcast.131), custom_call_target="tpu_custom_call" | custom-call | tf_op jit(solution)/shard_map/gather_kv/pallas_call | solution.py:527
  56.3 0.6 convolution_convert_fusion.4
  56.8 0.9 copy.79
  57.7 0.5 broadcast.206
  58.2 0.7 reduce.9
  59.0 0.6 convert_reduce_fusion.1
  59.7 1.1 convert_reduce_fusion
  60.9 1.3 pad_add_fusion.info_ref
  62.1 0.6 broadcast_in_dim.44.qinfo_ref
  62.8 18.4 %attend.1 = (f32[4,192,192]{2,1,0:T(8,128)}, bf16[4,192,192]{2,1,0:T(8,128)(2,1)}, f32[4,8,192]{2,1,0:T(8,128)}) custom-call(s32[5]{0:T(128)} %pad_add_fusion.info_ref, bf16[4,192,192]{2,1,0:T(8,128)(2,1)} %bitcast.135, bf16[3072,384]{1,0:T(8,128)(2,1)} %bitcast.122, s32[4,8,192]{2,1,0:T(8,128)} %broadcast_in_dim.44.qinfo_ref), custom_call_target="tpu_custom_call" | custom-call | flops 2000000000 | bytes 8000000 | tf_op jit(solution)/shard_map/attend/pallas_call | solution.py:971
  81.2 23.6 %heads_out.1 = (bf16[4,192,192]{2,1,0:T(8,128)(2,1)}, bf16[1,4,192,768]{3,2,1,0:T(8,128)(2,1)}) custom-call(bf16[4,192,192]{2,1,0:T(8,128)(2,1)} %get-tuple-element.46.refs_0_, bf16[1,192,768]{2,1,0:T(8,128)(2,1)} %bitcast.143), custom_call_target="tpu_custom_call" | custom-call | tf_op jit(solution)/shard_map/heads_out/pallas_call | solution.py:527
  104.8 1.4 copy.80
  106.7 0.5 multiply_reduce_fusion.9
  107.2 0.6 multiply_multiply_fusion.1
  107.8 0.6 copy-done.12
  108.4 0.7 fusion.35
  109.7 1.0 convolution_convert_fusion.3
  110.8 1.0 fusion.3
  111.8 30.1 %dispatch.1 = (bf16[4,48,768]{2,1,0:T(8,128)(2,1)}, bf16[4,48,768]{2,1,0:T(8,128)(2,1)}, bf16[3,4,192,768]{3,2,1,0:T(8,128)(2,1)}) custom-call(bf16[4,48,768]{2,1,0:T(8,128)(2,1)} %bitcast.130, bf16[4,48,768]{2,1,0:T(8,128)(2,1)} %bitcast.144, bf16[3,192,768]{2,1,0:T(8,128)(2,1)} %copy-done.3), custom_call_target="tpu_custom_call" | custom-call | tf_op jit(solution)/shard_map/dispatch/pallas_call | solution.py:527
  141.9 13.1 %ffn.1 = (bf16[192,768]{1,0:T(8,128)(2,1)}, bf16[192,768]{1,0:T(8,128)(2,1)}, bf16[4,2,192,2048]{3,2,1,0:T(8,128)(2,1)}, bf16[4,512,768]{2,1,0:T(8,128)(2,1)}) custom-call(bf16[192,768]{1,0:T(8,128)(2,1)} %bitcast.152, bf16[192,768]{1,0:T(8,128)(2,1)} %bitcast.153, bf16[768,2048]{1,0:T(8,128)(2,1)} %bitcast.149, bf16[768,2048]{1,0:T(8,128)(2,1)} %bitcast.150, ...), custom_call_target="tpu_custom_call" | custom-call | flops 6000000000 | bytes 20000000 | tf_op jit(solution)/shard_map/ffn/pallas_call | solution.py:870
  155.1 20.0 %combine.1 = (bf16[4,48,768]{2,1,0:T(8,128)(2,1)}, bf16[4,48,768]{2,1,0:T(8,128)(2,1)}, bf16[2,192,2048]{2,1,0:T(8,128)(2,1)}, bf16[2,192,2048]{2,1,0:T(8,128)(2...) custom-call(bf16[4,48,768]{2,1,0:T(8,128)(2,1)} %bitcast.138, bf16[4,48,768]{2,1,0:T(8,128)(2,1)} %bitcast.139, ...), custom_call_target="tpu_custom_call" | custom-call | tf_op jit(solution)/shard_map/combine/pallas_call | solution.py:527
  175.2 2.0 collective-permute-start
  177.2 1.2 convolution_bitcast_fusion.1
  178.5 2.0 convolution_bitcast_fusion
  180.5 1.5 multiply_reduce_fusion.8
  182.0 0.9 convert_element_type.132
  182.9 0.6 broadcast_in_dim.50.refs_8_
  184.1 3.2 multiply_reduce_fusion.3
  187.3 0.7 multiply_reduce_fusion.11
  188.3 0.6 div.42.clone
  188.9 0.7 sub.50.clone
  189.6 0.7 divide_multiply_fusion
  190.3 1.5 fusion.23
  191.8 2.1 multiply_reduce_fusion.6
  193.9 2.1 subtract_add_fusion
  196.1 0.6 convolution_convert_fusion.2
  197.0 0.8 copy.103
  197.8 11.7 %heads_back.1.back_ref = bf16[4,192,192]{2,1,0:T(8,128)(2,1)} custom-call(bf16[4,192,192]{2,1,0:T(8,128)(2,1)} %bitcast.125), custom_call_target="tpu_custom_call" | custom-call | tf_op jit(solution)/shard_map/heads_back/pallas_call | solution.py:527
  209.5 0.5 convolution_convert_fusion
  210.0 1.1 copy.102
  211.1 0.5 fusion.22
  211.9 0.7 select_maximum_fusion.refs_5_
  212.5 29.1 %attend_back.1 = (bf16[4,192,192]{2,1,0:T(8,128)(2,1)}, bf16[4,4,192,384]{3,2,1,0:T(8,128)(2,1)}) custom-call(s32[5]{0:T(128)} %pad_add_fusion.info_ref, bf16[4,192,192]{2,1,0:T(8,128)(2,1)} %bitcast.136, bf16[3072,384]{1,0:T(8,128)(2,1)} %bitcast.123, s32[4,8,192]{2,1,0:T(8,128)} %broadcast_in_dim.44.qinfo_ref, f32[4,192,192]{2,1,0:T(8,128)} %get-tuple-element.56.o_ref, ...), custom_call_target="tpu_custom_call" | custom-call | flops 5000000000 | bytes 12000000 | tf_op jit(solution)/shard_map/attend_back/pallas_call | solution.py:1064
  241.6 1.4 add_convert_fusion.1
  243.2 2.0 add_convert_fusion
  245.3 2.0 collective-permute-start.2
  247.3 63.6 %tail.1 = (f32[192,768]{1,0:T(8,128)}, f32[3,48,768]{2,1,0:T(8,128)}, f32[48,768]{1,0:T(8,128)}, f32[16,768]{1,0:T(8,128)}, f32[1,768]{1,0:T(1,128)}) custom-call(bf16[4,4,192,384]{3,2,1,0:T(8,128)(2,1)} %get-tuple-element.64.refs_0_, bf16[4,192,192]{2,1,0:T(8,128)(2,1)} %get-tuple-element.65.refs_1_, bf16[768,768]{1,0:T(8,128)(2,1)} %copy-done.6, ...), custom_call_target="tpu_custom_call" | custom-call | flops 20000000000 | bytes 100000000 | tf_op jit(solution)/shard_map/tail/pallas_call | solution.py:527
  310.9 1.3 slice.82
  312.2 1.3 reduce.3
  313.5 1.3 slice_reduce_fusion
  314.9 1.3 slice_bitcast_fusion.4
  316.2 1.4 slice_bitcast_fusion.3
  317.6 1.8 slice_bitcast_fusion
  319.4 1.3 add_bitcast_fusion
  320.7 2.0 convert_add_fusion
  322.7 1.9 fusion.37
  324.6 0.8 copy.109
  325.4 0.7 copy.110
  (126 shorter events, 3.8 us)
Async XLA Ops:
  1.9 31.9 %copy-start.3 = (bf16[3,192,768]{2,1,0:T(8,128)(2,1)}, bf16[3,192,768]{2,1,0:T(8,128)(2,1)S(1)}, u32[]{:S(2)}) copy-start(bf16[3,192,768]{2,1,0:T(8,128)(2,1)S(1)} %pad_maximum_fusion.1.refs_2_) | copy-start | bytes 2654212
  1.9 31.5 %copy-start.24 = (f32[768]{0:T(1024)S(1)}, f32[768]{0:T(1024)}, u32[]{:S(2)}) copy-start(f32[768]{0:T(1024)} %param.19) | copy-start | bytes 9220
  31.7 1.8 copy-start
  33.8 1.3 copy-start.7
  34.2 2.7 copy-start.6
  56.2 2.0 copy-start.23
  81.2 25.5 %copy-start.8 = (bf16[192,768]{1,0:T(8,128)(2,1)S(1)}, bf16[192,768]{1,0:T(8,128)(2,1)}, u32[]{:S(2)}) copy-start(bf16[192,768]{1,0:T(8,128)(2,1)} %refs_6_.1) | copy-start | bytes 884740
  104.8 1.8 copy-start.4
  106.2 1.5 copy-start.32
  106.2 1.5 copy-start.35
  106.3 2.2 copy-start.13
  106.6 2.5 copy-start.15
  106.6 4.1 %copy-start.1 = (bf16[192,768]{1,0:T(8,128)(2,1)S(1)}, bf16[192,768]{1,0:T(8,128)(2,1)}, u32[]{:S(2)}) copy-start(bf16[192,768]{1,0:T(8,128)(2,1)} %param.31) | copy-start | bytes 884740
  107.8 72.7 %copy-start.21 = (f32[192]{0:T(256)}, f32[192]{0:T(256)S(1)}, u32[]{:S(2)}) copy-start(f32[192]{0:T(256)S(1)} %get-tuple-element.119) | copy-start | bytes 2308
  107.8 0.6 copy-start.12
  109.1 68.1 %copy-start.18 = (f32[192,12]{0,1:T(8,128)}, f32[192,12]{0,1:T(8,128)S(1)}, u32[]{:S(2)}) copy-start(f32[192,12]{0,1:T(8,128)S(1)} %fusion.35) | copy-start | bytes 27652
  109.4 32.6 %copy-start.33 = (f32[192,2]{0,1:T(2,128)}, f32[192,2]{0,1:T(2,128)S(1)}, u32[]{:S(2)}) copy-start(f32[192,2]{0,1:T(2,128)S(1)} %get-tuple-element.100) | copy-start | bytes 4612
  109.4 74.2 %copy-start.29 = (f32[192,2]{0,1:T(2,128)}, f32[192,2]{0,1:T(2,128)S(1)}, u32[]{:S(2)}) copy-start(f32[192,2]{0,1:T(2,128)S(1)} %get-tuple-element.101) | copy-start | bytes 4612
  109.6 68.9 %copy-start.9 = (pred[192,2,192]{2,0,1:T(32,128)(4,1)}, pred[192,2,192]{2,0,1:T(32,128)(4,1)S(1)}, u32[]{:S(2)}) copy-start(pred[192,2,192]{2,0,1:T(32,128)(4,1)S(1)} %iota_compare_fusion) | copy-start | bytes 221188
  175.1 66.5 %collective-permute-start.1 = (bf16[512,768]{1,0:T(8,128)(2,1)}, bf16[512,768]{1,0:T(8,128)(2,1)}, u32[]{:S(2)}, u32[]{:S(2)}) collective-permute-start(bf16[512,768]{1,0:T(8,128)(2,1)} %get-tuple-element.63), channel_id=1, source_target_pairs={{0,2},{1,3},{2,0},{3,1},{4,6},{5,7},{6,4},{7,5},{8,10},{9,11},{10,... | collective-permute-start | bytes 2359304 | tf_op jit(solution)/shard_map/ppermute | solution.py:1088
  175.2 67.9 %collective-permute-start = (bf16[2,192,2048]{2,1,0:T(8,128)(2,1)}, bf16[2,192,2048]{2,1,0:T(8,128)(2,1)}, u32[]{:S(2)}, u32[]{:S(2)}) collective-permute-start(bf16[2,192,2048]{2,1,0:T(8,128)(2,1)} %get-tuple-element.61), channel_id=1, source_target_pairs={{0,2},{1,3},{2,0},{3,1},{4,6},{5,7},{6,4},{7,5},{8,10},{9,11},{10,... | collective-permute-start | bytes 4718600 | tf_op jit(solution)/shard_map/ppermute | solution.py:1088
  178.4 4.5 %copy-start.25 = (f32[768]{0:T(1024)S(1)}, f32[768]{0:T(1024)}, u32[]{:S(2)}) copy-start(f32[768]{0:T(1024)} %param.19) | copy-start | bytes 9220
  178.4 5.1 %slice-start = ((f32[192,12]{0,1:T(8,128)}), f32[192,4]{0,1:T(4,128)S(1)}, s32[]{:S(2)}) async-start(f32[192,12]{0,1:T(8,128)} %copy-done.18), calls=%async_computation | async-start | bytes 8192 | tf_op jit(solution)/shard_map/slice | solution.py:1167
  182.0 1.6 copy-start.28
  183.5 0.6 copy-start.19
  183.6 4.6 %copy-start.31 = (f32[192,2]{0,1:T(2,128)}, f32[192,2]{0,1:T(2,128)S(1)}, u32[]{:S(2)}) copy-start(f32[192,2]{0,1:T(2,128)S(1)} %fusion.31) | copy-start | bytes 4612
  183.6 4.4 %copy-start.26 = (f32[192,2,2]{0,1,2:T(2,128)}, f32[192,2,2]{0,1,2:T(2,128)S(1)}, u32[]{:S(2)}) copy-start(f32[192,2,2]{0,1,2:T(2,128)S(1)} %broadcast_divide_fusion) | copy-start | bytes 9220
  184.1 3.9 %copy-start.30 = (f32[192,2]{0,1:T(2,128)S(1)}, f32[192,2]{0,1:T(2,128)}, u32[]{:S(2)}) copy-start(f32[192,2]{0,1:T(2,128)} %copy-done.29) | copy-start | bytes 4612
  184.1 3.9 %copy-start.37 = (f32[192]{0:T(256)S(1)}, f32[192]{0:T(256)}, u32[]{:S(2)}) copy-start(f32[192]{0:T(256)} %get-tuple-element.109) | copy-start | bytes 2308
  184.1 4.0 %copy-start.20 = (f32[192,2]{0,1:T(2,128)S(1)}, f32[192,2]{0,1:T(2,128)}, u32[]{:S(2)}) copy-start(f32[192,2]{0,1:T(2,128)} %copy-done.19) | copy-start | bytes 4612
  188.1 5.8 %copy-start.36 = (f32[192]{0:T(256)}, f32[192]{0:T(256)S(1)}, u32[]{:S(2)}) copy-start(f32[192]{0:T(256)S(1)} %get-tuple-element.96) | copy-start | bytes 2308
  188.1 5.8 %copy-start.16 = (f32[192,8]{0,1:T(8,128)}, f32[192,8]{0,1:T(8,128)S(1)}, u32[]{:S(2)}) copy-start(f32[192,8]{0,1:T(8,128)S(1)} %select_reduce_fusion.1) | copy-start | bytes 18436
  188.2 5.7 %copy-start.22 = (f32[192]{0:T(256)S(1)}, f32[192]{0:T(256)}, u32[]{:S(2)}) copy-start(f32[192]{0:T(256)} %copy-done.21) | copy-start | bytes 2308
  196.1 13.4 %copy-start.2 = (f32[192,768]{1,0:T(8,128)}, f32[192,768]{1,0:T(8,128)S(1)}, u32[]{:S(2)}) copy-start(f32[192,768]{1,0:T(8,128)S(1)} %get-tuple-element.107.refs_7_) | copy-start | bytes 1769476
  196.6 12.8 %copy-start.34 = (f32[768]{0:T(1024)S(1)}, f32[768]{0:T(1024)}, u32[]{:S(2)}) copy-start(f32[768]{0:T(1024)} %get-tuple-element.85) | copy-start | bytes 9220
  210.0 1.1 copy-start.17
  210.0 1.6 copy-start.27
  212.5 29.1 %copy-start.10 = (bf16[512,768]{1,0:T(8,128)(2,1)S(1)}, bf16[512,768]{1,0:T(8,128)(2,1)}, u32[]{:S(2)}) copy-start(bf16[512,768]{1,0:T(8,128)(2,1)} %get-tuple-element.62) | copy-start | bytes 2359300
  241.6 1.6 copy-start.5
  245.2 74.2 %collective-permute-start.3 = (bf16[512,768]{1,0:T(8,128)(2,1)S(1)}, bf16[512,768]{1,0:T(8,128)(2,1)S(1)}, u32[]{:S(2)}, u32[]{:S(2)}) collective-permute-start(bf16[512,768]{1,0:T(8,128)(2,1)S(1)} %add_convert_fusion.1), channel_id=1, source_target_pairs={{0,16},{16,0},{1,17},{17,1},{2,18},{18,2},{3,19},{19,3},{4,20},{20... | collective-permute-start | bytes 2359304 | tf_op jit(solution)/shard_map/ppermute | solution.py:1088
  245.3 75.4 %collective-permute-start.2 = (bf16[2,192,2048]{2,1,0:T(8,128)(2,1)S(1)}, bf16[2,192,2048]{2,1,0:T(8,128)(2,1)}, u32[]{:S(2)}, u32[]{:S(2)}) collective-permute-start(bf16[2,192,2048]{2,1,0:T(8,128)(2,1)S(1)} %add_convert_fusion), channel_id=1, source_target_pairs={{0,16},{16,0},{1,17},{17,1},{2,18},{18,2},{3,19},{19,3},{4,20},{20... | collective-permute-start | bytes 4718600 | tf_op jit(solution)/shard_map/ppermute | solution.py:1088
  322.7 1.9 copy-start.11
  322.7 2.7 copy-start.14

commit v3 on v2

--- a/solution.py
+++ b/solution.py
@@ -660,7 +660,208 @@
             copy.wait_send()
 
 
-def tail(dkv, dq, attn_in, weights, out_term, packed, hidden, resid_grad, gain):
+def column(x, k):
+    return x[:, k : k + 1]
+
+
+def core_share(go, own, far, out):
+    me, _, _, near, other = shard_peers()
+    sent = [go(own, out.at[:, me], SH, near), go(far, out.at[:, other], SH, near)]
+    out[:, me] = own[...]
+    out[:, other] = far[...]
+    return sent
+
+
+def route(heads, hidden, gain, small_w, routes, out_grad, wo, wo_far, w3, w3_far, n_ids):
+    lines, rows, width = heads.shape
+    model = lines * width
+    slots = lines * CAP
+    shape = jax.ShapeDtypeStruct
+
+    def phases(ins, outs, scr, go):
+        heads_ref, hid_ref, gain_ref, small_ref, routes_ref, up_ref, wo_ref, wof_ref, w3_ref, w3f_ref = ins
+        rows_out, grads_out, w3_all, wo_all, resid_ref, table_ref, place_ref, low_ref = outs
+        land, rows_s, grads_s = scr
+        swaps = start_swap(go, heads_ref, land, EX, False)
+        swaps += core_share(go, wo_ref, wof_ref, wo_all)
+        shares = core_share(go, w3_ref, w3f_ref, w3_all)
+        ids = routes_ref[...]
+        lane = lax.broadcasted_iota(jnp.int32, (rows, 128), 1)
+        hot = [lane == column(ids, k) for k in range(2)]
+        before = (
+            lax.broadcasted_iota(jnp.int32, (rows, rows), 0)
+            > lax.broadcasted_iota(jnp.int32, (rows, rows), 1)
+        ).astype(bf16)
+        named = jnp.where(hot[0] | hot[1], 1.0, 0.0).astype(bf16)
+        earlier = jnp.dot(before, named, preferred_element_type=f32)
+        slot_at = lax.broadcasted_iota(jnp.int32, (rows, slots), 1).astype(f32)
+        place = []
+        for k in range(2):
+            number = jnp.sum(jnp.where(hot[k], earlier, 0.0), axis=1, keepdims=True)
+            wanted = column(ids, k).astype(f32) * CAP + number
+            wanted = jnp.where(column(ids, k) < lines, wanted, -1.0)
+            place.append(jnp.where(slot_at == wanted, 1.0, 0.0))
+            place_ref[k] = place[k].astype(bf16)
+        either = (place[0] + place[1]).astype(bf16)
+        up_rows = contract(either, up_ref[...], 0, 0)
+        for copy in swaps:
+            copy.wait()
+        for line in range(lines):
+            low_ref[:, line * width : (line + 1) * width] = land[line]
+        w_out = wo_all[...].reshape(model, model)
+        resid = hid_ref[...].astype(f32) + jnp.dot(
+            low_ref[...], w_out, preferred_element_type=f32
+        )
+        resid_ref[...] = resid
+        inv = lax.rsqrt(jnp.mean(resid * resid, axis=1, keepdims=True) + norm_eps)
+        moe_in = resid * inv * gain_ref[...]
+        rows_s[...] = contract(either, moe_in.astype(bf16), 0, 0).astype(bf16).reshape(
+            lines, CAP, model
+        )
+        row_swap = start_swap(go, rows_s, rows_out, EX, False)
+        small = jnp.dot(moe_in, small_ref[...], preferred_element_type=f32, precision=HIGH)
+        chosen = [jnp.sum(jnp.where(h, small, 0.0), axis=1, keepdims=True) for h in hot]
+        top = jnp.maximum(chosen[0], chosen[1])
+        powers = [jnp.exp(c - top) for c in chosen]
+        gates = [p / (powers[0] + powers[1]) for p in powers]
+        weight = place[0] * gates[0] + place[1] * gates[1]
+        weight = contract(weight, jnp.ones((rows, 128), f32), 0, 0, HIGH)[:, 0:1]
+        grads_s[...] = (up_rows * weight).astype(bf16).reshape(lines, CAP, model)
+        grad_swap = start_swap(go, grads_s, grads_out, EX, False)
+        table = jnp.zeros((rows, 128), f32)
+        entries = list(gates)
+        for j in range(2):
+            pair = [column(small, n_ids + 2 * j + k) for k in range(2)]
+            top = jnp.maximum(pair[0], pair[1])
+            powers = [jnp.exp(c - top) for c in pair]
+            entries += [p / (powers[0] + powers[1]) for p in powers]
+        entries += [column(ids, k).astype(f32) for k in range(2)]
+        for k, entry in enumerate(entries):
+            table = jnp.where(lane == k, entry, table)
+        table_ref[...] = table
+        for copy in row_swap + grad_swap + shares:
+            copy.wait()
+        yield
+
+    ins = [heads, hidden, gain, small_w, routes, out_grad, wo, wo_far, w3, w3_far]
+    outs = [
+        shape((lines, CAP, model), bf16),
+        shape((lines, CAP, model), bf16),
+        shape((3, 4, model // 4, model), bf16),
+        shape((1, 4, model // 4, model), bf16),
+        shape((rows, model), f32),
+        shape((rows, 128), f32),
+        shape((2, rows, slots), bf16),
+        shape((rows, model), bf16),
+    ]
+    scratch = [pltpu.VMEM((lines, rows, width), bf16)] + [pltpu.VMEM((lines, CAP, model), bf16)] * 2
+    return Part([EX, SH], ins, outs, scratch, 3 * (lines - 1) + 4, phases)
+
+
+def to_heads(returned, input_ret, place, table, resid, low, out_grad, gain, small_t, const_vec, wo, n_ids):
+    rows, model = resid.shape
+    lines = returned.shape[0]
+    width = model // lines
+    own = rows // lines
+    slots = lines * CAP
+    shape = jax.ShapeDtypeStruct
+
+    def phases(ins, outs, scr, go):
+        ret_ref, iret_ref, place_ref, table_ref, resid_ref, low_ref, up_ref, gain_ref, st_ref, vec_ref, wo_ref = ins
+        heads_out, layer_ref, rgrad_ref, term_ref, packed_ref = outs
+        (back_s,) = scr
+        table = table_ref[...]
+        gates = [column(table, k) for k in range(2)]
+        alpha = [[column(table, 2 + 2 * j + k) for k in range(2)] for j in range(2)]
+        ids = [column(table, 6 + k) for k in range(2)]
+        vecs = [vec_ref[j : j + 1, :] for j in range(2)]
+        resid = resid_ref[...]
+        upstream = up_ref[...].astype(f32)
+        inv = lax.rsqrt(jnp.mean(resid * resid, axis=1, keepdims=True) + norm_eps)
+        normed = resid * inv
+        moe_in = normed * gain_ref[...]
+        returned = ret_ref[...].reshape(slots, model)
+        total = lambda x: jnp.sum(x, axis=1, keepdims=True)
+        flag = lambda x: jnp.where(x, 1.0, 0.0)
+        copy_dot = total(upstream * moe_in)
+        vec_dot = [total(upstream * v) for v in vecs]
+        const_dot = [alpha[j][0] * copy_dot + alpha[j][1] * vec_dot[j] for j in range(2)]
+        output = resid
+        backs = []
+        copy_gate = jnp.zeros((rows, 1), f32)
+        const_gate = [jnp.zeros((rows, 1), f32) for _ in range(2)]
+        for k in range(2):
+            rows_k = jnp.dot(place_ref[k], returned, preferred_element_type=f32)
+            is_ffn, is_copy = flag(ids[k] < lines), flag(ids[k] == lines + 1)
+            is_const = [flag(ids[k] == lines + 2 + j) for j in range(2)]
+            output = output + (gates[k] * is_ffn) * rows_k
+            backs.append(
+                is_ffn * total(upstream * rows_k)
+                + is_copy * copy_dot
+                + is_const[0] * const_dot[0]
+                + is_const[1] * const_dot[1]
+            )
+            copy_gate = copy_gate + gates[k] * is_copy
+            const_gate = [const_gate[j] + gates[k] * is_const[j] for j in range(2)]
+        through = copy_gate + const_gate[0] * alpha[0][0] + const_gate[1] * alpha[1][0]
+        output = output + through * moe_in
+        for j in range(2):
+            output = output + (const_gate[j] * alpha[j][1]) * vecs[j]
+        layer_ref[...] = output.astype(bf16)
+        mean_back = gates[0] * backs[0] + gates[1] * backs[1]
+        lane = lax.broadcasted_iota(jnp.int32, (rows, 128), 1)
+        lane_f = lane.astype(f32)
+        small = jnp.zeros((rows, 128), f32)
+        for k in range(2):
+            small = jnp.where(lane_f == ids[k], gates[k] * (backs[k] - mean_back), small)
+        for j in range(2):
+            grads = [const_gate[j] * copy_dot, const_gate[j] * vec_dot[j]]
+            mean = alpha[j][0] * grads[0] + alpha[j][1] * grads[1]
+            for k in range(2):
+                small = jnp.where(
+                    lane == n_ids + 2 * j + k, alpha[j][k] * (grads[k] - mean), small
+                )
+            small = jnp.where(lane == n_ids + 4 + j, alpha[j][1] * const_gate[j], small)
+        either = place_ref[0] + place_ref[1]
+        moe_grad = (
+            jnp.dot(either, iret_ref[...].reshape(slots, model), preferred_element_type=f32)
+            + through * upstream
+            + jnp.dot(small, st_ref[...], preferred_element_type=f32, precision=HIGH)
+        )
+        resid_grad = upstream + rms_back(resid, inv, gain_ref[...], moe_grad)
+        branch = resid_grad.astype(bf16)
+        back = contract(branch, wo_ref[...], 1, 1).astype(bf16)
+        for line in range(lines):
+            back_s[line] = back[:, line * width : (line + 1) * width]
+        swaps = start_swap(go, back_s, heads_out, EX, False)
+        rgrad_ref[...] = resid_grad
+        packed_ref[...] = jnp.zeros_like(packed_ref)
+        packed_ref[0:1] = jnp.sum(moe_grad * normed, axis=0, keepdims=True)
+        small_grad = contract(small, moe_in, 0, 0, HIGH)
+        vec_grad = contract(small, upstream, 0, 0, HIGH)
+        packed_ref[1:3] = vec_grad[n_ids + 4 : n_ids + 6]
+        packed_ref[3 : 7 + n_ids] = small_grad[: n_ids + 4]
+        term = contract(low_ref[...], branch, 0, 0).astype(bf16)
+        for line in range(lines):
+            for piece in range(4):
+                at = (line * 4 + piece) * own
+                term_ref[piece, line] = term[at : at + own]
+        for copy in swaps:
+            copy.wait()
+        yield
+
+    ins = [returned, input_ret, place, table, resid, low, out_grad, gain, small_t, const_vec, wo]
+    outs = [
+        shape((lines, rows, width), bf16),
+        shape((rows, model), bf16),
+        shape((rows, model), f32),
+        shape((4, lines, own, model), bf16),
+        shape((-(-(7 + n_ids) // 8) * 8, model), f32),
+    ]
+    return Part([EX], ins, outs, [pltpu.VMEM((lines, rows, width), bf16)], lines - 1, phases)
+
+
+def tail(dkv, dq, attn_in, weights, out_term, packed, hidden, resid_grad, gain, n_ids):
     lines, rows, width = dq.shape
     model = lines * width
     own = rows // lines
@@ -674,7 +875,7 @@
 
     def phases(ins, outs, scr, go):
         dkv_ref, dq_ref, attn_ref, w_ref, o_ref, packed_ref, hid_ref, resid_ref, gain_ref = ins
-        input_ref, qkv_out, out_out, packed_out, gain_out = outs
+        input_ref, q_out, k_out, v_out, out_out, gain_out, mgain_out, vec_out, rout_out, mix_out = outs
         scr = list(scr)
         take = lambda k: [scr.pop(0) for _ in range(k)]
         kv_scr, q_scr, kvw_scr, o_scr = take(3), take(3), take(3), take(3)
@@ -768,7 +969,12 @@
         gn3 = start_swap(go, gn_2, gn_g, GR, True)
         for copy in pk3:
             copy.wait()
-        packed_out[...] = total_of(pk_g, groups)
+        small = total_of(pk_g, groups)
+        mgain_out[...] = small[0:1]
+        vec_out[...] = small[1:3]
+        turned = jnp.transpose(small)
+        rout_out[...] = turned[:, 3 : 3 + n_ids]
+        mix_out[...] = turned[:, 3 + n_ids : 7 + n_ids]
         for k in (2, 0, 1):
             for copy in swaps[k]:
                 copy.wait()
@@ -777,11 +983,11 @@
                 out_out[...] = value
             elif k == 0:
                 for line in range(lines):
-                    qkv_out[0, :, line * width : (line + 1) * width] = value[line]
+                    q_out[:, line * width : (line + 1) * width] = value[line]
             else:
-                for half in range(2):
+                for half, out in ((0, k_out), (1, v_out)):
                     for line in range(lines):
-                        qkv_out[1 + half, :, line * width : (line + 1) * width] = value[
+                        out[:, line * width : (line + 1) * width] = value[
                             line, :, half * width : (half + 1) * width
                         ]
         for copy in gn3:
@@ -811,16 +1017,21 @@
     copies = 4 * Tree.copies + 7 * (lines - 1) + 2 * 3 + 5 * (groups - 1)
     outs = [
         shape((rows, model), f32),
-        shape((3, own, model), f32),
         shape((own, model), f32),
-        shape(packed.shape, f32),
+        shape((own, model), f32),
+        shape((own, model), f32),
+        shape((own, model), f32),
         shape((1, model), f32),
+        shape((1, model), f32),
+        shape((2, model), f32),
+        shape((model, n_ids), f32),
+        shape((model, 4), f32),
     ]
     ins = [dkv, dq, attn_in, weights, out_term, packed, hidden, resid_grad, gain]
     return Part([EX, SH, GR], ins, outs, scratch, copies, phases)
 
 
-def expert_body(steps, x_ref, g_ref, wg_ref, wu_ref, wd_ref, eo_ref, ib_ref, gu_ref, d_ref, eo_s, ib_s):
+def expert_body(steps, x_ref, g_ref, wg_ref, wu_ref, wd_ref, eo_ref, ib_ref, ga_ref, up_ref, d_ref, eo_s, ib_s):
     i = pl.program_id(0)
     me, side, core, _, _ = shard_peers()
 
@@ -846,11 +1057,11 @@
     def place(quarter):
         return 2 * lax.rem(lax.rem(quarter, 2) + core, 2) + lax.rem(quarter // 2 + side, 2)
 
-    rows = gu_ref.shape[2]
-    for k, back in enumerate((gate_back, up_back)):
+    rows = ga_ref.shape[1]
+    for ref, back in ((ga_ref, gate_back), (up_ref, up_back)):
         term = contract(x, back, 0, 0).astype(bf16)
         for quarter in range(4):
-            gu_ref[place(jnp.int32(quarter)), k] = term[quarter * rows : (quarter + 1) * rows]
+            ref[place(jnp.int32(quarter))] = term[quarter * rows : (quarter + 1) * rows]
     d_ref[place(i)] = contract(act, g, 0, 0).astype(bf16)
 
     @pl.when(i == steps - 1)
@@ -873,7 +1084,8 @@
         out_shape=[
             shape((slots, model), bf16),
             shape((slots, model), bf16),
-            shape((4, 2, quarter, inner), bf16),
+            shape((4, quarter, inner), bf16),
+            shape((4, quarter, inner), bf16),
             shape((4, tile, model), bf16),
         ],
         in_specs=[
@@ -886,7 +1098,8 @@
         out_specs=[
             whole((slots, model)),
             whole((slots, model)),
-            pl.BlockSpec((4, 2, quarter, tile), lambda i: (0, 0, 0, i)),
+            pl.BlockSpec((4, quarter, tile), lambda i: (0, 0, i)),
+            pl.BlockSpec((4, quarter, tile), lambda i: (0, 0, i)),
             whole((4, tile, model)),
         ],
         scratch_shapes=[pltpu.VMEM((slots, model), f32)] * 2,
@@ -1120,9 +1333,10 @@
     seg = segment_ids[0]
     length = seg.shape[0]
 
-    w_mine = lax.dynamic_slice_in_dim(
-        jnp.stack([w_query, w_key, w_value]), line * width, width, axis=2
-    )
+    w_qkv = jnp.stack([w_query, w_key, w_value])
+    w_mine = lax.dynamic_slice_in_dim(w_qkv, line * width, width, axis=2)
+    wo_far = swap(w_out, SH, lambda i: i ^ 2)
+    w_far = swap(w_qkv, SH, lambda i: i ^ 2)
     hidden_all, w_cols = run_parts(
         [exchange(EX, GATHER, hidden_in), exchange(SH, GATHER, w_mine)], 0, "gather_in"
     )
@@ -1144,133 +1358,58 @@
     prompt = jnp.sum((seg == 0).astype(jnp.int32), dtype=jnp.int32)
     info = jnp.concatenate([prompt[None], qstart[:, 0]])
     qinfo = jnp.broadcast_to(qstart[:, None, :], (lines, 8, rows))
-    attn_vec, attn_low_heads, lse = attend(info, q, kv_all, qinfo)
-    attn_parts, wo_full = run_parts(
-        [exchange(EX, SWAP, attn_low_heads), tree_gather(w_out[None])], 2, "heads_out"
-    )
+    attn_vec, attn_heads, lse = attend(info, q, kv_all, qinfo)
+    n_ids = w_router.shape[1]
+    small_w = jnp.pad(
+        jnp.concatenate([w_router, const_mix], axis=1), ((0, 0), (0, 124 - n_ids))
+    )
+    gain_two = moe_gain[None]
+    recv_rows, recv_grads, weights, wo_full, resid_one, table, place, attn_low = run_parts(
+        [
+            route(
+                attn_heads, hidden_in, gain_two, small_w, routes, out_grad, w_out[None], wo_far[None], w_qkv, w_far, n_ids
+            )
+        ],
+        2,
+        "route",
+    )
+    weights = weights.reshape(3, model, model)
     wo_full = wo_full.reshape(model, model)
-    attn_low = attn_parts.swapaxes(0, 1).reshape(rows, model)
-
-    inputs = hidden_in.astype(f32)
-    resid_one = inputs + jnp.dot(attn_low, wo_full, preferred_element_type=f32)
-    inv_two = lax.rsqrt(jnp.mean(resid_one * resid_one, axis=1, keepdims=True) + norm_eps)
-    normed_two = resid_one * inv_two
-    moe_in = normed_two * moe_gain
-    moe_low = moe_in.astype(bf16)
-    n_ids = w_router.shape[1]
-    ids = jnp.arange(n_ids, dtype=jnp.int32)
-    hot = (routes[:, :, None] == ids).astype(f32)
-    small_w = jnp.concatenate([w_router, const_mix], axis=1)
-    small = dense32(moe_in, small_w)
-    chosen = jnp.sum(hot * small[:, None, :n_ids], axis=2)
-    gate_probs = jax.nn.softmax(chosen, axis=1)
-    mix_alpha = jax.nn.softmax(small[:, n_ids:].reshape(rows, 2, 2), axis=2)
-    ffn_mask = (routes < lines).astype(f32)
-    copy_mask = (routes == lines + 1).astype(f32)
-    const_mask = hot[:, :, lines + 2 : lines + 4]
-    copy_gate = jnp.sum(gate_probs * copy_mask, axis=1)
-    const_gate = jnp.sum(gate_probs[:, :, None] * const_mask, axis=1)
-    ffn_gate = gate_probs * ffn_mask
-    before = (jnp.arange(rows)[:, None] > jnp.arange(rows)[None, :]).astype(bf16)
-    earlier = jnp.dot(before, jnp.sum(hot, axis=1).astype(bf16), preferred_element_type=f32)
-    slot_num = jnp.sum(hot * earlier[:, None, :], axis=2).astype(jnp.int32)
-    slot = jnp.where(routes < lines, routes * CAP + slot_num, -1)
     slots = lines * CAP
-    sits = slot[:, :, None] == jnp.arange(slots, dtype=jnp.int32)
-    sit_gate = jnp.sum(jnp.where(sits, ffn_gate[:, :, None], 0.0), axis=(0, 1))
-    place = [sits[:, k].astype(bf16) for k in range(2)]
-    either = place[0] + place[1]
-    send_rows = contract(either, moe_low, 0, 0).astype(bf16)
-    grad_send = (contract(either, out_grad, 0, 0) * sit_gate[:, None]).astype(bf16)
-    recv_rows, recv_grads, weights = run_parts(
-        [
-            exchange(EX, SWAP, send_rows.reshape(lines, CAP, model)),
-            exchange(EX, SWAP, grad_send.reshape(lines, CAP, model)),
-            tree_gather(jnp.stack([w_query, w_key, w_value])),
-        ],
-        3,
-        "dispatch",
-    )
-    weights = weights.reshape(3, model, model)
-
-    expert_out, input_back, gate_up, down = expert(
+
+    expert_out, input_back, *terms = expert(
         recv_rows.reshape(slots, model), recv_grads.reshape(slots, model), w_gate[0], w_up[0], w_down[0]
     )
-    returned, input_ret, gu_here, gu_there, d_here, d_there = run_parts(
+    returned, input_ret, *sums = run_parts(
         [
             exchange(EX, SWAP, expert_out.reshape(lines, CAP, model)),
             exchange(EX, SWAP, input_back.reshape(lines, CAP, model)),
-            core_sum(gate_up),
-            core_sum(down),
-        ],
+        ]
+        + [core_sum(term) for term in terms],
         4,
         "combine",
     )
-    gu_far = swap(gu_there, SH, lambda i: i ^ 2)
-    d_far = swap(d_there, SH, lambda i: i ^ 2)
-
-    returned = returned.reshape(slots, model)
-    route_out = jnp.stack(
-        [jnp.dot(place[k], returned, preferred_element_type=f32) for k in range(2)], axis=1
-    )
-    ffn_in_grad = jnp.dot(either, input_ret.reshape(slots, model), preferred_element_type=f32)
-    const_rows = mix_alpha[:, :, 0:1] * moe_in[:, None, :] + mix_alpha[:, :, 1:2] * const_vec[None]
-    moe_sum = (
-        jnp.sum(ffn_gate[:, :, None] * route_out, axis=1)
-        + copy_gate[:, None] * moe_in
-        + jnp.sum(const_gate[:, :, None] * const_rows, axis=1)
-    )
-    layer_out = (resid_one + moe_sum).astype(bf16)
-    upstream = out_grad.astype(f32)
-    route_dot = jnp.sum(upstream[:, None, :] * route_out, axis=2)
-    copy_dot = jnp.sum(upstream * moe_in, axis=1)
-    const_dot = jnp.sum(upstream[:, None, :] * const_rows, axis=2)
-    gate_back_r = (
-        ffn_mask * route_dot
-        + copy_mask * copy_dot[:, None]
-        + jnp.sum(const_mask * const_dot[:, None, :], axis=2)
-    )
-    chosen_grad = gate_probs * (
-        gate_back_r - jnp.sum(gate_probs * gate_back_r, axis=1, keepdims=True)
-    )
-    logit_grad = jnp.sum(chosen_grad[:, :, None] * hot, axis=1)
-    up_dot_vec = jnp.sum(upstream[:, None, :] * const_vec[None], axis=2)
-    alpha_grad = jnp.stack(
-        [const_gate * copy_dot[:, None], const_gate * up_dot_vec], axis=2
-    )
-    mix_back = (
-        mix_alpha * (alpha_grad - jnp.sum(mix_alpha * alpha_grad, axis=2, keepdims=True))
-    ).reshape(rows, 4)
-    vec_scale = mix_alpha[:, :, 1] * const_gate
-    small_back = jnp.concatenate([logit_grad, mix_back], axis=1)
-    moe_in_grad = (
-        ffn_in_grad
-        + (copy_gate + jnp.sum(mix_alpha[:, :, 0] * const_gate, axis=1))[:, None] * upstream
-        + dense32(small_back, small_w.T)
-    )
-    moe_gain_grad = jnp.sum(moe_in_grad * normed_two, axis=0)
-    small_grad = contract(small_back, moe_in, 0, 0, HIGH)
-    vec_grad = contract(vec_scale, upstream, 0, 0, HIGH)
-    resid_grad = upstream + rms_back(resid_one, inv_two, moe_gain, moe_in_grad)
-    branch_low = resid_grad.astype(bf16)
-    attn_back = contract(branch_low, wo_full, 1, 1).astype(bf16)
-    attn_back = attn_back.reshape(rows, lines, width).swapaxes(0, 1)
-    (back_heads,) = run_parts([exchange(EX, SWAP, attn_back)], 5, "heads_back")
-    own = rows // lines
-    out_term = contract(attn_low, branch_low, 0, 0).astype(bf16)
-    out_term = out_term.reshape(lines, 4, own, model).swapaxes(0, 1)
-    packed = jnp.concatenate([moe_gain_grad[None], vec_grad, small_grad], axis=0)
-    packed = jnp.pad(packed, ((0, -packed.shape[0] % 8), (0, 0)))
-
+    far = [swap(there, SH, lambda i: i ^ 2) for there in sums[1::2]]
+    mine = [(x.astype(f32) + y.astype(f32)).astype(bf16) for x, y in zip(sums[0::2], far)]
+
+    back_heads, layer_out, resid_grad, out_term, packed = run_parts(
+        [
+            to_heads(
+                returned, input_ret, place, table, resid_one, attn_low, out_grad, gain_two, small_w.T, const_vec, wo_full, n_ids
+            )
+        ],
+        5,
+        "to_heads",
+    )
+    back_heads, mine[2] = lax.optimization_barrier((back_heads, mine[2]))
+    down_part = over_group(mine[2])
     dq, dkv = attend_back(info, q, kv_all, qinfo, attn_vec, lse, back_heads)
-    gu_mine = (gu_here.astype(f32) + gu_far.astype(f32)).astype(bf16)
-    d_mine = (d_here.astype(f32) + d_far.astype(f32)).astype(bf16)
-    dkv, gu_mine, d_mine = lax.optimization_barrier((dkv, gu_mine, d_mine))
-    gate_up_part, down_part = over_group(gu_mine), over_group(d_mine)
-    input_grad, qkv_part, out_part, packed, gain_sum = run_parts(
+    dkv, *mine[:2] = lax.optimization_barrier((dkv, *mine[:2]))
+    gate_part, up_part = over_group(mine[0]), over_group(mine[1])
+    input_grad, *grads, gain_sum, moe_gain_sum, vec_sum, router_sum, mix_sum = run_parts(
         [
             tail(
-                dkv, dq, attn_in, weights, out_term, packed, hidden_in, resid_grad, attn_gain[None]
+                dkv, dq, attn_in, weights, out_term, packed, hidden_in, resid_grad, attn_gain[None], n_ids
             )
         ],
         6,
@@ -1281,16 +1420,13 @@
         layer_out,
         input_grad,
         gain_sum[0],
-        qkv_part[0],
-        qkv_part[1],
-        qkv_part[2],
-        out_part,
-        packed[0],
-        packed[3 : 3 + n_ids].T,
-        packed[3 + n_ids : 7 + n_ids].T,
-        packed[1:3],
-        gate_up_part[0][None],
-        gate_up_part[1][None],
+        *grads,
+        moe_gain_sum[0],
+        router_sum,
+        mix_sum,
+        vec_sum,
+        gate_part[None],
+        up_part[None],
         down_part[None],
     )
 

time: 322 us -> 301 us (0.935); the launches traced: 326 us -> 301 us
  Pallas kernels: 258 us -> 245 us
  matrix products: 14.2 us -> 3.49 us
  local copies, waits for them, and re-layouts: 22.3 us -> 16 us
  waiting for transfers between devices: 0.01 us -> 5.32 us
  starting transfers between devices: 4.17 us -> 9.3 us
  other arithmetic: 26.2 us -> 21.7 us
    dot_general x13 -> x0, matrix products: 12 us -> none  [the longest x6 3.85 us: contract(): lax.dot_general(a, b, (((da,), (db,)), ((), ())), preferred_element_type=...]
    pallas_call x1, Pallas kernels: 29.1 us -> 22.8 us  [attend_back(): pl.pallas_call(functools.partial(attend_back_body, lines, heads), out_sha...]
    unnamed x81 -> x52, local copies, waits for them, and re-layouts: 4.34 us -> 10.6 us
    reduce_sum x12 -> x0, other arithmetic: 5.78 us -> none  [the longest x1 3.16 us: fast_shards(): route_dot = jnp.sum(upstream[:, None, :] * route_out, axis=2)]
    ppermute x4 -> x8, waiting for transfers between devices: 0.01 us -> 5.32 us  [swap(): lax.ppermute(x, axis, [(i, partner(i)) for i in range(lax.axis_size(axis))])]
    ppermute x4 -> x8, starting transfers between devices: 4.17 us -> 9.3 us  [swap(): lax.ppermute(x, axis, [(i, partner(i)) for i in range(lax.axis_size(axis))])]
    broadcast_in_dim x0 -> x2, other arithmetic: none -> 5.06 us  [the longest x1 2.57 us: fast_shards(): gate_part[None]]
    slice x6 -> x0, local copies, waits for them, and re-layouts: 4.56 us -> none  [the longest x1 1.86 us: fast_shards(): gate_up_part[1][None]]
  transfers between devices with their start and end apart: 4 -> 8, of which waited for: 0 -> 1; matrix products, arithmetic and copies ran while one was open for 10% -> 10% of each run, Pallas kernels for 32% -> 58%
where the time goes in v3:
time: 301 us
  Pallas kernels  245 us (81%)
  other arithmetic  21.7 us (7%)
  local copies, waits for them, and re-layouts  16 us (5%)
  starting transfers between devices  9.3 us (3%)
  waiting for transfers between devices  5.32 us (2%)
  matrix products  3.49 us (1%)
    pallas_call x6, Pallas kernels, run_parts(): pl.pallas_call(body, out_shape=outs, in_specs=sum([p.specs for p in parts...  194 us
    pallas_call x1, Pallas kernels, attend_back(): pl.pallas_call(functools.partial(attend_back_body, lines, heads), out_sha...  22.8 us
    pallas_call x1, Pallas kernels, attend(): pl.pallas_call(functools.partial(attend_body, lines, heads), out_shape=[s...  14.9 us
    pallas_call x1, Pallas kernels, expert(): pl.pallas_call(functools.partial(expert_body, steps), grid=(steps,), out_...  13.1 us
    unnamed x52, local copies, waits for them, and re-layouts  10.6 us
    ppermute x8, starting transfers between devices, swap(): lax.ppermute(x, axis, [(i, partner(i)) for i in range(lax.axis_size(axis))])  9.3 us
  transfers between devices with their start and end apart: 8, of which 1 were waited for; matrix products, arithmetic and copies ran while one was open for 10% of the time, Pallas kernels for 58%

profile of v3, /device:TPU:0, one launch (start us, length us, event | category | flops | bytes accessed | tf_op | source)
XLA Modules:
  0.0 301.4 jit_solution(4812074362121585409)
XLA Ops:
  0.6 1.2 pad_maximum_fusion.refs_8_
  1.9 0.0 copy-start.1
  1.9 0.0 copy-start.14
  1.9 3.1 %collective-permute-start.1 = (bf16[3,192,768]{2,1,0:T(8,128)(2,1)S(1)}, bf16[3,192,768]{2,1,0:T(8,128)(2,1)}, u32[]{:S(2)}, u32[]{:S(2)}) collective-permute-start(bf16[3,192,768]{2,1,0:T(8,128)(2,1)S(1)} %pad_maximum_fusion.refs_8_), channel_id=1, source_target_pairs={{0,2},{1,3},{2,0},{3,1},{4,6},{5,7},{6,4},{7,5},{8,10},{9,11},{10,... | collective-permute-start | bytes 2654216 | tf_op jit(solution)/shard_map/ppermute | solution.py:1301
  5.0 0.1 collective-permute-start
  5.1 0.9 constant_dynamic-slice_fusion.refs_1_
  5.9 38.5 %gather_in.1 = (bf16[4,192,768]{2,1,0:T(8,128)(2,1)}, bf16[4,3,192,192]{3,2,1,0:T(8,128)(2,1)}) custom-call(bf16[192,768]{1,0:T(8,128)(2,1)} %refs_6_.3, bf16[3,192,192]{2,1,0:T(8,128)(2,1)} %constant_dynamic-slice_fusion.refs_1_), custom_call_target="tpu_custom_call" | custom-call | tf_op jit(solution)/shard_map/gather_in/pallas_call | solution.py:527
  44.4 1.7 multiply_reduce_fusion
  46.1 0.1 rsqrt.13
  46.2 0.3 multiply_convert_fusion
  46.5 1.3 fusion.1.refs_2_
  47.9 0.1 fusion.7
  48.0 0.5 broadcast.76
  48.5 0.1 copy-done.13
  48.6 0.7 reduce.8
  49.3 0.7 reshape_squeeze.3
  50.0 0.6 convolution_convert_fusion.1
  50.5 2.9 convolution_convert_fusion
  53.5 0.7 broadcast_select_fusion
  54.2 19.6 %gather_kv.1 = bf16[4,4,192,384]{3,2,1,0:T(8,128)(2,1)} custom-call(bf16[4,192,384]{2,1,0:T(8,128)(2,1)} %bitcast.50), custom_call_target="tpu_custom_call" | custom-call | tf_op jit(solution)/shard_map/gather_kv/pallas_call | solution.py:527
  73.8 0.0 copy-start.18
  73.8 0.9 copy.41
  74.7 0.8 fusion.5
  75.5 0.9 copy.42.refs_3_
  76.5 0.6 broadcast_in_dim.50.refs_2_.refs_7_
  77.0 0.8 copy.43.refs_4_
  77.8 1.1 convert_reduce_fusion
  78.9 0.1 slice_reduce_fusion
  79.0 0.6 convert_reduce_fusion.1
  79.7 1.2 pad_add_fusion.info_ref
  80.9 0.6 broadcast_in_dim.49.qinfo_ref
  81.5 14.9 %attend.1 = (f32[4,192,192]{2,1,0:T(8,128)}, bf16[4,192,192]{2,1,0:T(8,128)(2,1)}, f32[4,8,192]{2,1,0:T(8,128)}) custom-call(s32[5]{0:T(128)} %pad_add_fusion.info_ref, bf16[4,192,192]{2,1,0:T(8,128)(2,1)} %bitcast.53, bf16[3072,384]{1,0:T(8,128)(2,1)} %bitcast.45, s32[4,8,192]{2,1,0:T(8,128)} %broadcast_in_dim.49.qinfo_ref), custom_call_target="tpu_custom_call" | custom-call | flops 2000000000 | bytes 8000000 | tf_op jit(solution)/shard_map/attend/pallas_call | solution.py:1184
  96.4 35.9 %route.1 = (bf16[4,48,768]{2,1,0:T(8,128)(2,1)}, bf16[4,48,768]{2,1,0:T(8,128)(2,1)}, bf16[3,4,192,768]{3,2,1,0:T(8,128)(2,1)}, bf16[1,4,192,768]{3,2,1,0:T(8,12...) custom-call(bf16[4,192,192]{2,1,0:T(8,128)(2,1)} %get-tuple-element., ...), custom_call_target="tpu_custom_call" | custom-call | tf_op jit(solution)/shard_map/route/pallas_call | solution.py:527
  132.4 13.1 %ffn.1 = (bf16[192,768]{1,0:T(8,128)(2,1)}, bf16[192,768]{1,0:T(8,128)(2,1)}, bf16[4,192,2048]{2,1,0:T(8,128)(2,1)}, bf16[4,192,2048]{2,1,0:T(8,128)(2,1)}, bf16[4,512,768]{2,1,0:T(8,128)(2,1)}) custom-call(bf16[192,768]{1,0:T(8,128)(2,1)} %bitcast.67, bf16[192,768]{1,0:T(8,128)(2,1)} %bitcast.68, bf16[768,2048]{1,0:T(8,128)(2,1)} %bitcast.64, ...), custom_call_target="tpu_custom_call" | custom-call | flops 6000000000 | bytes 20000000 | tf_op jit(solution)/shard_map/ffn/pallas_call | solution.py:1081
  145.5 21.1 %combine.1 = (bf16[4,48,768]{2,1,0:T(8,128)(2,1)}, bf16[4,48,768]{2,1,0:T(8,128)(2,1)}, bf16[192,2048]{1,0:T(8,128)(2,1)}, bf16[192,2048]{1,0:T(8,128)(2,1)}, bf...) custom-call(bf16[4,48,768]{2,1,0:T(8,128)(2,1)} %bitcast.55, ...), custom_call_target="tpu_custom_call" | custom-call | tf_op jit(solution)/shard_map/combine/pallas_call | solution.py:527
  166.6 2.0 collective-permute-start.2
  168.6 0.1 collective-permute-start.4
  168.7 0.6 broadcast_in_dim.53.refs_8_
  169.3 1.9 collective-permute-start.3
  171.2 17.6 %to_heads.1 = (bf16[4,192,192]{2,1,0:T(8,128)(2,1)}, bf16[192,768]{1,0:T(8,128)(2,1)}, f32[192,768]{1,0:T(8,128)}, bf16[4,4,48,768]{3,2,1,0:T(8,128)(2,1)}, f32[16,768]{1,0:T(8,128)}) custom-call(bf16[4,48,768]{2,1,0:T(8,128)(2,1)} %get-tuple-element.72.refs_0_, bf16[4,48,768]{2,1,0:T(8,128)(2,1)} %get-tuple-element.73.refs_1_, ...), custom_call_target="tpu_custom_call" | custom-call | tf_op jit(solution)/shard_map/to_heads/pallas_call | solution.py:527
  188.8 0.2 add_convert_fusion.2
  189.0 0.1 collective-permute-start.7
  189.1 22.8 %attend_back.1 = (bf16[4,192,192]{2,1,0:T(8,128)(2,1)}, bf16[4,4,192,384]{3,2,1,0:T(8,128)(2,1)}) custom-call(s32[5]{0:T(128)} %pad_add_fusion.info_ref, bf16[4,192,192]{2,1,0:T(8,128)(2,1)} %bitcast.54, bf16[3072,384]{1,0:T(8,128)(2,1)} %bitcast.46, s32[4,8,192]{2,1,0:T(8,128)} %broadcast_in_dim.49.qinfo_ref, f32[4,192,192]{2,1,0:T(8,128)} %get-tuple-element.80.o_ref, ...), custom_call_target="tpu_custom_call" | custom-call | flops 5000000000 | bytes 12000000 | tf_op jit(solution)/shard_map/attend_back/pallas_call | solution.py:1277
  211.9 0.9 copy-done.5
  212.7 1.4 add_convert_fusion
  214.1 5.3 %collective-permute-done.3 = bf16[192,2048]{1,0:T(8,128)(2,1)} collective-permute-done((bf16[192,2048]{1,0:T(8,128)(2,1)}, bf16[192,2048]{1,0:T(8,128)(2,1)}, u32[]{:S(2)}, u32[]{:S(2)}) %collective-permute-start.3) | collective-permute-done | bytes 786464 | tf_op jit(solution)/shard_map/ppermute | solution.py:1301
  219.4 1.4 add_convert_fusion.1
  220.8 1.0 collective-permute-start.6
  221.9 1.1 collective-permute-start.5
  222.9 61.2 %tail.1 = (f32[192,768]{1,0:T(8,128)}, f32[48,768]{1,0:T(8,128)}, f32[48,768]{1,0:T(8,128)}, f32[48,768]{1,0:T(8,128)}, f32[48,768]{1,0:T(8,128)}, /*index=5*/f3...) custom-call(bf16[4,4,192,384]{3,2,1,0:T(8,128)(2,1)} %get-tuple-element.91.refs_0_, ...), custom_call_target="tpu_custom_call" | custom-call | flops 20000000000 | bytes 100000000 | tf_op jit(solution)/shard_map/tail/pallas_call | solution.py:527
  284.2 1.7 copy.44
  285.9 1.7 copy.45
  287.6 1.3 reduce.3
  288.9 1.3 reduce.4
  290.2 1.3 add_bitcast_fusion
  291.5 2.5 add_bitcast_fusion.1
  294.0 2.6 add_bitcast_fusion.2
  296.6 0.7 copy.56
  297.3 0.8 copy.57
  298.2 0.7 copy.58
  298.8 0.7 copy.59
  299.5 0.7 copy.60
  300.1 0.7 copy.61
  300.8 0.6 copy.62
  (44 shorter events, 0.1 us)
Async XLA Ops:
  1.9 44.6 %copy-start.1 = (bf16[3,192,768]{2,1,0:T(8,128)(2,1)}, bf16[3,192,768]{2,1,0:T(8,128)(2,1)S(1)}, u32[]{:S(2)}) copy-start(bf16[3,192,768]{2,1,0:T(8,128)(2,1)S(1)} %pad_maximum_fusion.refs_8_) | copy-start | bytes 2654212
  1.9 44.3 %copy-start.14 = (f32[768]{0:T(1024)S(1)}, f32[768]{0:T(1024)}, u32[]{:S(2)}) copy-start(f32[768]{0:T(1024)} %param.19) | copy-start | bytes 9220
  1.9 94.5 %collective-permute-start.1 = (bf16[3,192,768]{2,1,0:T(8,128)(2,1)S(1)}, bf16[3,192,768]{2,1,0:T(8,128)(2,1)}, u32[]{:S(2)}, u32[]{:S(2)}) collective-permute-start(bf16[3,192,768]{2,1,0:T(8,128)(2,1)S(1)} %pad_maximum_fusion.refs_8_), channel_id=1, source_target_pairs={{0,2},{1,3},{2,0},{3,1},{4,6},{5,7},{6,4},{7,5},{8,10},{9,11},{10,... | collective-permute-start | bytes 2654216 | tf_op jit(solution)/shard_map/ppermute | solution.py:1301
  5.0 91.5 %collective-permute-start = (bf16[192,768]{1,0:T(8,128)(2,1)}, bf16[192,768]{1,0:T(8,128)(2,1)}, u32[]{:S(2)}, u32[]{:S(2)}) collective-permute-start(bf16[192,768]{1,0:T(8,128)(2,1)} %param.23), channel_id=1, source_target_pairs={{0,2},{1,3},{2,0},{3,1},{4,6},{5,7},{6,4},{7,5},{8,10},{9,11},{10,... | collective-permute-start | bytes 884744 | tf_op jit(solution)/shard_map/ppermute | solution.py:1301
  44.4 1.8 copy-start
  46.5 1.4 copy-start.2
  47.9 0.7 copy-start.13
  54.2 20.5 %copy-start.15 = (f32[768,8]{0,1:T(8,128)S(1)}, f32[768,8]{0,1:T(8,128)}, u32[]{:S(2)}) copy-start(f32[768,8]{0,1:T(8,128)} %param.25) | copy-start | bytes 73732
  54.2 20.5 %copy-start.16 = (f32[768,4]{0,1:T(4,128)S(1)}, f32[768,4]{0,1:T(4,128)}, u32[]{:S(2)}) copy-start(f32[768,4]{0,1:T(4,128)} %param.26) | copy-start | bytes 36868
  73.8 2.7 copy-start.18
  73.8 3.3 %copy-start.19 = (s32[192,2]{0,1:T(2,128)S(1)}, s32[192,2]{0,1:T(2,128)}, u32[]{:S(2)}) copy-start(s32[192,2]{0,1:T(2,128)} %param.18) | copy-start | bytes 4612
  166.6 22.1 %collective-permute-start.2 = (bf16[512,768]{1,0:T(8,128)(2,1)}, bf16[512,768]{1,0:T(8,128)(2,1)S(1)}, u32[]{:S(2)}, u32[]{:S(2)}) collective-permute-start(bf16[512,768]{1,0:T(8,128)(2,1)} %get-tuple-element.84), channel_id=1, source_target_pairs={{0,2},{1,3},{2,0},{3,1},{4,6},{5,7},{6,4},{7,5},{8,10},{9,11},{10,... | collective-permute-start | bytes 2359304 | tf_op jit(solution)/shard_map/ppermute | solution.py:1301
  168.6 43.2 %collective-permute-start.4 = (bf16[192,2048]{1,0:T(8,128)(2,1)}, bf16[192,2048]{1,0:T(8,128)(2,1)S(1)}, u32[]{:S(2)}, u32[]{:S(2)}) collective-permute-start(bf16[192,2048]{1,0:T(8,128)(2,1)} %get-tuple-element.90), channel_id=1, source_target_pairs={{0,2},{1,3},{2,0},{3,1},{4,6},{5,7},{6,4},{7,5},{8,10},{9,11},{10,... | collective-permute-start | bytes 2359304 | tf_op jit(solution)/shard_map/ppermute | solution.py:1301
  169.3 50.1 %collective-permute-start.3 = (bf16[192,2048]{1,0:T(8,128)(2,1)}, bf16[192,2048]{1,0:T(8,128)(2,1)}, u32[]{:S(2)}, u32[]{:S(2)}) collective-permute-start(bf16[192,2048]{1,0:T(8,128)(2,1)} %get-tuple-element.88), channel_id=1, source_target_pairs={{0,2},{1,3},{2,0},{3,1},{4,6},{5,7},{6,4},{7,5},{8,10},{9,11},{10,... | collective-permute-start | bytes 2359304 | tf_op jit(solution)/shard_map/ppermute | solution.py:1301
  171.2 17.6 %copy-start.6 = (bf16[512,768]{1,0:T(8,128)(2,1)S(1)}, bf16[512,768]{1,0:T(8,128)(2,1)}, u32[]{:S(2)}) copy-start(bf16[512,768]{1,0:T(8,128)(2,1)} %get-tuple-element.83) | copy-start | bytes 2359300
  189.0 101.2 %collective-permute-start.7 = (bf16[512,768]{1,0:T(8,128)(2,1)S(1)}, bf16[512,768]{1,0:T(8,128)(2,1)S(1)}, u32[]{:S(2)}, u32[]{:S(2)}) collective-permute-start(bf16[512,768]{1,0:T(8,128)(2,1)S(1)} %add_convert_fusion.2), channel_id=1, source_target_pairs={{0,16},{16,0},{1,17},{17,1},{2,18},{18,2},{3,19},{19,3},{4,20},{20... | collective-permute-start | bytes 2359304 | tf_op jit(solution)/shard_map/ppermute | solution.py:1301
  189.1 23.7 %copy-start.4 = (bf16[192,2048]{1,0:T(8,128)(2,1)S(1)}, bf16[192,2048]{1,0:T(8,128)(2,1)}, u32[]{:S(2)}) copy-start(bf16[192,2048]{1,0:T(8,128)(2,1)} %get-tuple-element.89) | copy-start | bytes 2359300
  211.8 7.6 %copy-start.3 = (bf16[192,2048]{1,0:T(8,128)(2,1)S(1)}, bf16[192,2048]{1,0:T(8,128)(2,1)}, u32[]{:S(2)}) copy-start(bf16[192,2048]{1,0:T(8,128)(2,1)} %get-tuple-element.87) | copy-start | bytes 2359300
  211.9 0.9 copy-start.5
  220.8 70.7 %collective-permute-start.6 = (bf16[192,2048]{1,0:T(8,128)(2,1)S(1)}, bf16[192,2048]{1,0:T(8,128)(2,1)}, u32[]{:S(2)}, u32[]{:S(2)}) collective-permute-start(bf16[192,2048]{1,0:T(8,128)(2,1)S(1)} %add_convert_fusion), channel_id=1, source_target_pairs={{0,16},{16,0},{1,17},{17,1},{2,18},{18,2},{3,19},{19,3},{4,20},{20... | collective-permute-start | bytes 2359304 | tf_op jit(solution)/shard_map/ppermute | solution.py:1301
  221.9 72.2 %collective-permute-start.5 = (bf16[192,2048]{1,0:T(8,128)(2,1)S(1)}, bf16[192,2048]{1,0:T(8,128)(2,1)}, u32[]{:S(2)}, u32[]{:S(2)}) collective-permute-start(bf16[192,2048]{1,0:T(8,128)(2,1)S(1)} %add_convert_fusion.1), channel_id=1, source_target_pairs={{0,16},{16,0},{1,17},{17,1},{2,18},{18,2},{3,19},{19,3},{4,20},{20... | collective-permute-start | bytes 2359304 | tf_op jit(solution)/shard_map/ppermute | solution.py:1301
  294.0 2.6 copy-start.8
  294.0 3.3 %copy-start.7 = (f32[192,768]{1,0:T(8,128)S(1)}, f32[192,768]{1,0:T(8,128)}, u32[]{:S(2)}) copy-start(f32[192,768]{1,0:T(8,128)} %get-tuple-element.183) | copy-start | bytes 1769476
  296.6 1.6 copy-start.12
  296.6 2.2 copy-start.11
  296.6 2.9 copy-start.10
  296.6 3.5 %copy-start.9 = (f32[48,768]{1,0:T(8,128)S(1)}, f32[48,768]{1,0:T(8,128)}, u32[]{:S(2)}) copy-start(f32[48,768]{1,0:T(8,128)} %get-tuple-element.188) | copy-start | bytes 442372
  296.6 4.2 %copy-start.17 = (f32[2,768]{1,0:T(2,128)S(1)}, f32[2,768]{1,0:T(2,128)}, u32[]{:S(2)}) copy-start(f32[2,768]{1,0:T(2,128)} %get-tuple-element.192) | copy-start | bytes 18436

commit v4 on v3

--- a/solution.py
+++ b/solution.py
@@ -10,6 +10,7 @@
 HEADS = 12
 HEAD_DIM = 64
 CAP = 48
+DOCS = 9
 KEY_BLK = 256
 EX, SH, GR = ("expert", "shard", "group")
 GATHER, GATHER_SUM, SWAP, SWAP_SUM = range(4)
@@ -658,6 +659,169 @@
     def close(self):
         for copy in (*self.first, self.second):
             copy.wait_send()
+
+
+def front(hidden, w_mine, gain):
+    rows, model = hidden.shape
+    lines = lax.axis_size(EX)
+    width = model // lines
+    shape = jax.ShapeDtypeStruct
+    last = lines - 1
+
+    def body(hid_ref, w_ref, gain_ref, attn_ref, q_ref, kv_ref, land, w_all, kv_own, sems):
+        line_me = lax.axis_index(EX)
+        me, _, _, near, far = shard_peers()
+        left, right = jnp.maximum(line_me - 1, 0), jnp.minimum(line_me + 1, last)
+        greet(
+            [(EX, lax.rem(line_me + d, lines)) for d in range(1, lines)]
+            + [(SH, lax.rem(me + d, 4)) for d in range(1, 4)]
+        )
+
+        def copy(src, dst, index, axis, peer):
+            return pltpu.make_async_remote_copy(
+                src_ref=src,
+                dst_ref=dst,
+                send_sem=sems.at[0, index],
+                recv_sem=sems.at[1, index],
+                device_id={axis: peer},
+                device_id_type=pl.DeviceIdType.MESH,
+            )
+
+        def relay(step, way):
+            block = line_me - step if way == 0 else line_me + step
+            block = jnp.clip(block, 0, last)
+            src = hid_ref if step == 0 else land.at[block]
+            return copy(src, land.at[block], last * way + step, EX, right if way == 0 else left)
+
+        def sends(step, way):
+            if way == 0:
+                return (line_me < last) & (line_me - step >= 0)
+            return (line_me > 0) & (line_me + step <= last)
+
+        def comes(step, way):
+            return line_me - 1 - step >= 0 if way == 0 else line_me + 1 + step <= last
+
+        def source(step, way):
+            line = line_me - 1 - step if way == 0 else line_me + 1 + step
+            return jnp.clip(line, 0, last)
+
+        def arrival(step, way):
+            line = source(step, way)
+            return copy(land.at[line], land.at[line], last * way + step, EX, right if way == 0 else left)
+
+        base = 2 * last
+        for way in range(2):
+
+            @pl.when(sends(0, way))
+            def _():
+                relay(0, way).start()
+
+        w_far = copy(w_ref, w_all.at[me], base, SH, far)
+        w_near = copy(w_ref, w_all.at[me], base + 1, SH, near)
+        w_pass = copy(w_all.at[far], w_all.at[far], base + 2, SH, near)
+        w_far.start()
+        w_near.start()
+        w_all[me] = w_ref[...]
+        base += 3
+        kv_far = lambda line: copy(kv_own.at[line], kv_ref.at[line, me], base + line, SH, far)
+        kv_near = lambda line: copy(
+            kv_own.at[line], kv_ref.at[line, me], base + lines + line, SH, near
+        )
+        kv_pass = lambda line: copy(
+            kv_ref.at[line, far], kv_ref.at[line, far], base + 2 * lines + line, SH, near
+        )
+
+        def project(line, x):
+            inputs = x.astype(f32)
+            inv = lax.rsqrt(jnp.mean(inputs * inputs, axis=1, keepdims=True) + norm_eps)
+            attn_in = (inputs * inv * gain_ref[...]).astype(bf16)
+            attn_ref[line] = attn_in
+            value = jnp.dot(
+                attn_in, w_all[...].reshape(model, 3 * width), preferred_element_type=f32
+            ).astype(bf16)
+            kv_own[line] = value[:, : 2 * width]
+            kv_far(line).start()
+            kv_near(line).start()
+            kv_ref[line, me] = value[:, : 2 * width]
+            q_ref[line] = value[:, 2 * width :]
+
+        def hand(line):
+            kv_far(line).wait_recv()
+            kv_pass(line).start()
+
+        w_far.wait_recv()
+        w_pass.start()
+        w_near.wait_recv()
+        w_pass.wait_recv()
+        project(line_me, hid_ref[...])
+        for step in range(last):
+            for way in range(2):
+
+                @pl.when(comes(step, way))
+                def _():
+                    arrival(step, way).wait_recv()
+
+                if step + 1 < last:
+
+                    @pl.when(sends(step + 1, way))
+                    def _():
+                        relay(step + 1, way).start()
+
+            for way in range(2):
+
+                @pl.when(comes(step, way))
+                def _():
+                    line = source(step, way)
+                    project(line, land[line])
+
+            if step == 0:
+                hand(line_me)
+            else:
+                for way in range(2):
+
+                    @pl.when(comes(step - 1, way))
+                    def _():
+                        hand(source(step - 1, way))
+
+        for way in range(2):
+
+            @pl.when(comes(last - 1, way))
+            def _():
+                hand(source(last - 1, way))
+
+        for way in range(2):
+            for step in range(last):
+
+                @pl.when(sends(step, way))
+                def _():
+                    relay(step, way).wait_send()
+
+        w_far.wait_send()
+        w_near.wait_send()
+        w_pass.wait_send()
+        for line in range(lines):
+            kv_far(line).wait_send()
+            kv_near(line).wait()
+            kv_pass(line).wait()
+
+    return pl.pallas_call(
+        body,
+        out_shape=[
+            shape((lines, rows, model), bf16),
+            shape((lines, rows, width), bf16),
+            shape((lines, 4, rows, 2 * width), bf16),
+        ],
+        in_specs=[VM] * 3,
+        out_specs=[VM] * 3,
+        scratch_shapes=[
+            pltpu.VMEM((lines, rows, model), bf16),
+            pltpu.VMEM((4, rows, 3 * width), bf16),
+            pltpu.VMEM((lines, rows, 2 * width), bf16),
+            pltpu.SemaphoreType.DMA((2, 2 * last + 3 + 3 * lines)),
+        ],
+        compiler_params=pltpu.CompilerParams(collective_id=0, has_side_effects=True),
+        name="front",
+    )(hidden, w_mine, gain)
 
 
 def column(x, k):
@@ -861,7 +1025,7 @@
     return Part([EX], ins, outs, [pltpu.VMEM((lines, rows, width), bf16)], lines - 1, phases)
 
 
-def tail(dkv, dq, attn_in, weights, out_term, packed, hidden, resid_grad, gain, n_ids):
+def tail(dkv, dq, attn_in, weights, out_term, packed, hidden, resid_grad, gain):
     lines, rows, width = dq.shape
     model = lines * width
     own = rows // lines
@@ -875,7 +1039,7 @@
 
     def phases(ins, outs, scr, go):
         dkv_ref, dq_ref, attn_ref, w_ref, o_ref, packed_ref, hid_ref, resid_ref, gain_ref = ins
-        input_ref, q_out, k_out, v_out, out_out, gain_out, mgain_out, vec_out, rout_out, mix_out = outs
+        input_ref, q_out, kv_out, out_out, packed_out, gain_out = outs
         scr = list(scr)
         take = lambda k: [scr.pop(0) for _ in range(k)]
         kv_scr, q_scr, kvw_scr, o_scr = take(3), take(3), take(3), take(3)
@@ -969,30 +1133,14 @@
         gn3 = start_swap(go, gn_2, gn_g, GR, True)
         for copy in pk3:
             copy.wait()
-        small = total_of(pk_g, groups)
-        mgain_out[...] = small[0:1]
-        vec_out[...] = small[1:3]
-        turned = jnp.transpose(small)
-        rout_out[...] = turned[:, 3 : 3 + n_ids]
-        mix_out[...] = turned[:, 3 + n_ids : 7 + n_ids]
-        for k in (2, 0, 1):
+        packed_out[...] = total_of(pk_g, groups)
+        for k, out in ((2, out_out), (0, q_out), (1, kv_out)):
             for copy in swaps[k]:
                 copy.wait()
-            value = total_of(gots[k], groups)
-            if k == 2:
-                out_out[...] = value
-            elif k == 0:
-                for line in range(lines):
-                    q_out[:, line * width : (line + 1) * width] = value[line]
-            else:
-                for half, out in ((0, k_out), (1, v_out)):
-                    for line in range(lines):
-                        out[:, line * width : (line + 1) * width] = value[
-                            line, :, half * width : (half + 1) * width
-                        ]
+            out[...] = total_of(gots[k], groups)
         for copy in gn3:
             copy.wait()
-        gain_out[...] = jnp.sum(total_of(gn_g, groups), axis=0, keepdims=True)
+        gain_out[...] = total_of(gn_g, groups)
         for tree in (kv_tree, o_tree, q_tree, kvw_tree):
             tree.close()
         yield
@@ -1017,15 +1165,11 @@
     copies = 4 * Tree.copies + 7 * (lines - 1) + 2 * 3 + 5 * (groups - 1)
     outs = [
         shape((rows, model), f32),
+        shape((lines, own, width), f32),
+        shape((lines, own, 2 * width), f32),
         shape((own, model), f32),
-        shape((own, model), f32),
-        shape((own, model), f32),
-        shape((own, model), f32),
-        shape((1, model), f32),
-        shape((1, model), f32),
-        shape((2, model), f32),
-        shape((model, n_ids), f32),
-        shape((model, 4), f32),
+        shape(packed.shape, f32),
+        shape((8, model), f32),
     ]
     ins = [dkv, dq, attn_in, weights, out_term, packed, hidden, resid_grad, gain]
     return Part([EX, SH, GR], ins, outs, scratch, copies, phases)
@@ -1117,12 +1261,20 @@
     return (kpos <= qpos) & ((kpos >= qstart) | (kpos < prompt))
 
 
+def doc_start(block, info_ref, qinfo_ref):
+    docs = qinfo_ref[pl.ds(block, 1), :]
+    starts = jnp.zeros(docs.shape, jnp.int32)
+    for doc in range(1, DOCS):
+        starts = jnp.where(docs == doc, info_ref[doc], starts)
+    return starts, info_ref[info_ref[DOCS + block]]
+
+
 def attend_body(lines, heads, info_ref, q_ref, kv_ref, qinfo_ref, o_ref, low_ref, lse_ref, k_s, vt_s, acc_s, ml_s, qm_s):
     shard = lax.axis_index(SH)
     rows, width = q_ref.shape[1:]
     blocks = vt_s.shape[0]
     key_blk = vt_s.shape[2]
-    prompt = info_ref[0]
+    prompt = info_ref[1]
 
     @pl.loop(0, blocks)
     def _(j):
@@ -1135,8 +1287,7 @@
         start = (line * 4 + shard) * rows
         queries = q_ref[line].astype(f32) * HEAD_DIM**-0.5
         qpos = start + lax.broadcasted_iota(jnp.int32, (1, rows), 1)
-        qstart = qinfo_ref[line, 0:1, :]
-        first = info_ref[1 + line]
+        qstart, first = doc_start(line * 4 + shard, info_ref, qinfo_ref)
         for h in range(heads):
             qm_s[h] = jnp.where(head_columns(h, queries.shape, 1), queries, 0.0).astype(bf16)
         acc_s[...] = jnp.zeros_like(acc_s)
@@ -1207,7 +1358,7 @@
     rows, width = q_ref.shape[1:]
     key_blk = KEY_BLK
     blocks = k_s.shape[0] // key_blk
-    prompt = info_ref[0]
+    prompt = info_ref[1]
 
     @pl.loop(0, blocks)
     def _(j):
@@ -1223,8 +1374,7 @@
         queries = q_ref[line].astype(f32) * HEAD_DIM**-0.5
         back = back_ref[line].astype(f32)
         qpos = start + lax.broadcasted_iota(jnp.int32, (1, rows), 1)
-        qstart = qinfo_ref[line, 0:1, :]
-        first = info_ref[1 + line]
+        qstart, first = doc_start(line * 4 + shard, info_ref, qinfo_ref)
         picks = (
             lax.broadcasted_iota(jnp.int32, (8, width), 1) // HEAD_DIM
             == lax.broadcasted_iota(jnp.int32, (8, width), 0)
@@ -1297,15 +1447,64 @@
     )(info, q, kv, qinfo, o, lse, back)
 
 
+def finale_body(lines, n_ids, *refs):
+    ins, outs = refs[:13], refs[13:]
+    for k in range(3):
+        outs[k][...] = ins[k][...].astype(f32) + ins[3 + k][...].astype(f32)
+    for k in range(2):
+        outs[3 + k][...] = ins[6 + k][...]
+
+    @pl.when(pl.program_id(0) == 0)
+    def _():
+        q_sum, kv_sum, out_sum, small_ref, gain_ref = ins[8:]
+        q_out, k_out, v_out, out_out, gain_out, mgain_out, vec_out, rout_out, mix_out = outs[5:]
+        width = q_sum.shape[2]
+        for line in range(lines):
+            at = slice(line * width, (line + 1) * width)
+            q_out[:, at] = q_sum[line]
+            k_out[:, at] = kv_sum[line, :, :width]
+            v_out[:, at] = kv_sum[line, :, width:]
+        out_out[...] = out_sum[...]
+        gain_out[...] = jnp.sum(gain_ref[...], axis=0)
+        small = small_ref[...]
+        mgain_out[...] = jnp.sum(small[0:1], axis=0)
+        vec_out[...] = small[1:3]
+        turned = jnp.transpose(small)
+        rout_out[...] = turned[:, 3 : 3 + n_ids]
+        mix_out[...] = turned[:, 3 + n_ids : 7 + n_ids]
+
+
+def finale(mine, far, input_grad, layer_out, sums, n_ids):
+    steps = 4
+    shape = jax.ShapeDtypeStruct
+    own, model = sums[2].shape
+    lines = sums[0].shape[0]
+
+    def tiled(dims, dim):
+        block = tuple(d // steps if k == dim else d for k, d in enumerate(dims))
+        return pl.BlockSpec(block, lambda i: tuple(i if k == dim else 0 for k in range(2)))
+
+    def whole(dims):
+        return pl.BlockSpec(dims, lambda i: (0,) * len(dims))
+
+    wide = [tiled(mine[0].shape, 1), tiled(mine[1].shape, 1), tiled(mine[2].shape, 0)]
+    rows = [tiled(input_grad.shape, 0), tiled(layer_out.shape, 0)]
+    small = [(own, model)] * 4 + [(model,), (model,), (2, model), (model, n_ids), (model, 4)]
+    return pl.pallas_call(
+        functools.partial(finale_body, lines, n_ids),
+        grid=(steps,),
+        out_shape=[shape(m.shape, f32) for m in mine]
+        + [shape(input_grad.shape, f32), shape(layer_out.shape, bf16)]
+        + [shape(d, f32) for d in small],
+        in_specs=wide + wide + rows + [whole(x.shape) for x in sums],
+        out_specs=wide + rows + [whole(d) for d in small],
+        cost_estimate=pl.CostEstimate(flops=10**7, bytes_accessed=10**7, transcendentals=0),
+        name="finale",
+    )(*mine, *far, input_grad, layer_out, *sums)
+
+
 def swap(x, axis, partner):
     return lax.ppermute(x, axis, [(i, partner(i)) for i in range(lax.axis_size(axis))])
-
-
-def over_group(mine):
-    n = lax.axis_size(GR)
-    if n == 2:
-        return mine.astype(f32) + swap(mine, GR, lambda i: 1 - i).astype(f32)
-    return jnp.sum(lax.all_gather(mine, GR).astype(f32), axis=0)
 
 
 def fast_shards(
@@ -1335,29 +1534,20 @@
 
     w_qkv = jnp.stack([w_query, w_key, w_value])
     w_mine = lax.dynamic_slice_in_dim(w_qkv, line * width, width, axis=2)
-    wo_far = swap(w_out, SH, lambda i: i ^ 2)
+    w_mine = jnp.concatenate([w_mine[1], w_mine[2], w_mine[0]], axis=1)
+    attn_in, q, kv_all = front(hidden_in, w_mine, attn_gain[None])
+    attn_in = attn_in.reshape(lines * rows, model)
+    kv_all, w_out_b, w_qkv = lax.optimization_barrier((kv_all, w_out, w_qkv))
+    wo_far = swap(w_out_b, SH, lambda i: i ^ 2)
     w_far = swap(w_qkv, SH, lambda i: i ^ 2)
-    hidden_all, w_cols = run_parts(
-        [exchange(EX, GATHER, hidden_in), exchange(SH, GATHER, w_mine)], 0, "gather_in"
-    )
-    w_heads = w_cols.swapaxes(0, 1).reshape(3, model, width)
-    inputs_all = hidden_all.reshape(lines * rows, model).astype(f32)
-    inv_all = lax.rsqrt(jnp.mean(inputs_all * inputs_all, axis=1, keepdims=True) + norm_eps)
-    attn_in = (inputs_all * inv_all * attn_gain).astype(bf16)
-    q = jnp.dot(attn_in, w_heads[0], preferred_element_type=f32).astype(bf16)
-    w_kv = jnp.concatenate([w_heads[1], w_heads[2]], axis=1)
-    kv = jnp.dot(attn_in, w_kv, preferred_element_type=f32).astype(bf16)
-    q = q.reshape(lines, rows, width)
-    (kv_all,) = run_parts([tree_gather(kv.reshape(lines, rows, 2 * width))], 1, "gather_kv")
     kv_all = kv_all.reshape(length, 2 * width)
-
-    own_seg = jnp.take(seg.reshape(lines, 4, rows), shard, axis=1)
-    qstart = jnp.sum(
-        (seg[None, None, :] < own_seg[:, :, None]).astype(jnp.int32), axis=2, dtype=jnp.int32
-    )
-    prompt = jnp.sum((seg == 0).astype(jnp.int32), dtype=jnp.int32)
-    info = jnp.concatenate([prompt[None], qstart[:, 0]])
-    qinfo = jnp.broadcast_to(qstart[:, None, :], (lines, 8, rows))
+    starts = jnp.sum(
+        (seg[None, :] < jnp.arange(DOCS, dtype=jnp.int32)[:, None]).astype(jnp.int32),
+        axis=1,
+        dtype=jnp.int32,
+    )
+    qinfo = seg.reshape(length // rows, rows)
+    info = jnp.concatenate([starts, qinfo[:, 0]])
     attn_vec, attn_heads, lse = attend(info, q, kv_all, qinfo)
     n_ids = w_router.shape[1]
     small_w = jnp.pad(
@@ -1402,32 +1592,36 @@
         "to_heads",
     )
     back_heads, mine[2] = lax.optimization_barrier((back_heads, mine[2]))
-    down_part = over_group(mine[2])
+    cross = lambda x: swap(x, GR, lambda i: 1 - i)
+    down_far = cross(mine[2])
     dq, dkv = attend_back(info, q, kv_all, qinfo, attn_vec, lse, back_heads)
     dkv, *mine[:2] = lax.optimization_barrier((dkv, *mine[:2]))
-    gate_part, up_part = over_group(mine[0]), over_group(mine[1])
-    input_grad, *grads, gain_sum, moe_gain_sum, vec_sum, router_sum, mix_sum = run_parts(
+    group_far = [cross(mine[0]), cross(mine[1]), down_far]
+    input_grad, *sums = run_parts(
         [
             tail(
-                dkv, dq, attn_in, weights, out_term, packed, hidden_in, resid_grad, attn_gain[None], n_ids
+                dkv, dq, attn_in, weights, out_term, packed, hidden_in, resid_grad, attn_gain[None]
             )
         ],
         6,
         "tail",
         pl.CostEstimate(flops=2 * 10**10, bytes_accessed=10**8, transcendentals=0),
     )
+    gate, up, down, input_grad, layer_out, *grads, gain, gain_two, vecs, router, mix = finale(
+        mine, group_far, input_grad, layer_out, sums, n_ids
+    )
     return (
         layer_out,
         input_grad,
-        gain_sum[0],
+        gain,
         *grads,
-        moe_gain_sum[0],
-        router_sum,
-        mix_sum,
-        vec_sum,
-        gate_part[None],
-        up_part[None],
-        down_part[None],
+        gain_two,
+        router,
+        mix,
+        vecs,
+        gate[None],
+        up[None],
+        down[None],
     )
 
 
@@ -1452,7 +1646,7 @@
     )
     sizes = dict(mesh.shape)
     lines = sizes[EX]
-    fast = sizes[SH] == 4 and lines == 4 and HEADS % lines == 0
+    fast = (sizes[GR], sizes[SH], lines) == (2, 4, 4)
     return jax.shard_map(
         fast_shards if fast else shards,
         mesh=mesh,

time: 301 us -> 268 us (0.89); the launches traced: 301 us -> 272 us
  other arithmetic: 21.7 us -> 7.39 us
  Pallas kernels: 245 us -> 233 us
  local copies, waits for them, and re-layouts: 16 us -> 9.83 us
  starting transfers between devices: 9.3 us -> 13.1 us
  matrix products: 3.49 us -> 0 us
    pallas_call x6 -> x4, Pallas kernels: 194 us -> 135 us  [run_parts(): pl.pallas_call(body, out_shape=outs, in_specs=sum([p.specs for p in parts...]
    pallas_call x0 -> x2, Pallas kernels: none -> 45.8 us  [the longest x1 38.7 us: front(): pl.pallas_call(body, out_shape=[shape((lines, rows, model), bf16), shape(...]
    broadcast_in_dim x3 -> x0, other arithmetic: 6.36 us -> none  [the longest x1 2.57 us: fast_shards(): gate_part[None]]
    unnamed x52 -> x38, local copies, waits for them, and re-layouts: 10.6 us -> 6.69 us
    ppermute x8, starting transfers between devices: 9.3 us -> 13.1 us  [swap(): lax.ppermute(x, axis, [(i, partner(i)) for i in range(lax.axis_size(axis))])]
    dot_general x2 -> x0, matrix products: 3.49 us -> none  [the longest x1 2.94 us: fast_shards(): kv = jnp.dot(attn_in, w_kv, preferred_element_type=f32).astype(bf16)]
    reduce_sum x3 -> x1, other arithmetic: 3.42 us -> 0.14 us  [fast_shards(): jnp.sum((seg[None, :] < jnp.arange(DOCS, dtype=jnp.int32)[:, None]).astyp...]
  transfers between devices with their start and end apart: 8 -> 8, of which waited for: 1 -> 2; matrix products, arithmetic and copies ran while one was open for 10% -> 3% of each run, Pallas kernels for 58% -> 46%
where the time goes in v4:
time: 268 us; the launch traced here: 272 us
  Pallas kernels  233 us (87%)
  starting transfers between devices  13.1 us (5%)
  local copies, waits for them, and re-layouts  9.83 us (4%)
  waiting for transfers between devices  7.8 us (3%)
  other arithmetic  7.39 us (3%)
    pallas_call x4, Pallas kernels, run_parts(): pl.pallas_call(body, out_shape=outs, in_specs=sum([p.specs for p in parts...  135 us
    pallas_call x1, Pallas kernels, front(): pl.pallas_call(body, out_shape=[shape((lines, rows, model), bf16), shape(...  38.7 us
    pallas_call x1, Pallas kernels, attend_back(): pl.pallas_call(functools.partial(attend_back_body, lines, heads), out_sha...  23.8 us
    pallas_call x1, Pallas kernels, attend(): pl.pallas_call(functools.partial(attend_body, lines, heads), out_shape=[s...  15.5 us
    pallas_call x1, Pallas kernels, expert(): pl.pallas_call(functools.partial(expert_body, steps), grid=(steps,), out_...  13.2 us
    ppermute x8, starting transfers between devices, swap(): lax.ppermute(x, axis, [(i, partner(i)) for i in range(lax.axis_size(axis))])  13.1 us
    ppermute x8, waiting for transfers between devices, swap(): lax.ppermute(x, axis, [(i, partner(i)) for i in range(lax.axis_size(axis))])  7.8 us
    pallas_call x1, Pallas kernels, finale(): pl.pallas_call(functools.partial(finale_body, lines, n_ids), grid=(steps,...  7.02 us
  transfers between devices with their start and end apart: 8, of which 2 were waited for; matrix products, arithmetic and copies ran while one was open for 3% of the time, Pallas kernels for 46%

profile of v4, /device:TPU:0, one launch (start us, length us, event | category | flops | bytes accessed | tf_op | source)
XLA Modules:
  0.0 272.4 jit_solution(12695411728795143818)
XLA Ops:
  0.6 1.3 broadcast_in_dim.23.gain_ref.refs_8_
  1.9 0.0 copy-start.13
  1.9 0.0 copy-start.14
  2.0 1.3 pad_maximum_fusion.refs_8_
  3.2 0.0 copy-start
  3.2 0.2 dynamic-slice_bitcast_fusion.2
  3.4 0.8 pad_maximum_fusion.1.w_ref
  4.3 38.7 %front.1 = (bf16[4,192,768]{2,1,0:T(8,128)(2,1)}, bf16[4,192,192]{2,1,0:T(8,128)(2,1)}, bf16[4,4,192,384]{3,2,1,0:T(8,128)(2,1)}) custom-call(bf16[192,768]{1,0:T(8,128)(2,1)} %refs_6_.3, bf16[192,576]{1,0:T(8,128)(2,1)} %pad_maximum_fusion.1.w_ref, f32[1,768]{1,0:T(1,128)} %broadcast_in_dim.23.gain_ref.refs_8_), custom_call_target="tpu_custom_call" | custom-call | tf_op jit(solution)/shard_map/front/pallas_call | solution.py:807
  43.0 0.9 collective-permute-start.1
  43.9 0.0 copy-done.9
  43.9 1.2 collective-permute-start
  45.1 0.0 copy-done.15
  45.1 0.6 broadcast_in_dim.24.refs_2_.refs_7_
  45.7 0.5 broadcast.16
  46.2 0.0 copy-done.11
  46.2 0.7 reduce.5
  46.9 0.1 reshape_squeeze.3.qinfo_ref
  47.0 0.0 copy-done.16
  47.0 0.8 copy.39.refs_4_
  47.7 0.0 copy-done.13
  47.8 0.0 copy-done.14
  47.8 0.8 fusion
  48.6 0.9 copy.38.refs_3_
  49.5 0.0 copy-done
  49.5 0.1 slice_reduce_fusion
  49.6 0.1 convert_reduce_fusion
  49.7 0.6 pad_add_fusion.info_ref
  50.3 0.0 copy-done.12
  50.3 15.5 %attend.1 = (f32[4,192,192]{2,1,0:T(8,128)}, bf16[4,192,192]{2,1,0:T(8,128)(2,1)}, f32[4,8,192]{2,1,0:T(8,128)}) custom-call(s32[25]{0:T(128)} %pad_add_fusion.info_ref, bf16[4,192,192]{2,1,0:T(8,128)(2,1)} %get-tuple-element.76.q_ref, bf16[3072,384]{1,0:T(8,128)(2,1)} %bitcast.41, s32[16,192]{1,0:T(8,128)} %copy-done.12), custom_call_target="tpu_custom_call" | custom-call | flops 2000000000 | bytes 8000000 | tf_op jit(solution)/shard_map/attend/pallas_call | solution.py:1335
  65.9 5.5 %collective-permute-done = bf16[192,768]{1,0:T(8,128)(2,1)S(1)} collective-permute-done((bf16[192,768]{1,0:T(8,128)(2,1)S(1)}, bf16[192,768]{1,0:T(8,128)(2,1)S(1)}, u32[]{:S(2)}, u32[]{:S(2)}) %collective-permute-start) | collective-permute-done | bytes 294944 | tf_op jit(solution)/shard_map/ppermute | solution.py:1507
  71.3 0.0 collective-permute-done.1.refs_9_
  71.3 0.7 copy-done.10
  72.0 0.3 copy-done.4
  72.3 29.9 %route.1 = (bf16[4,48,768]{2,1,0:T(8,128)(2,1)}, bf16[4,48,768]{2,1,0:T(8,128)(2,1)}, bf16[3,4,192,768]{3,2,1,0:T(8,128)(2,1)}, bf16[1,4,192,768]{3,2,1,0:T(8,12...) custom-call(bf16[4,192,192]{2,1,0:T(8,128)(2,1)} %get-tuple-element., ...), custom_call_target="tpu_custom_call" | custom-call | tf_op jit(solution)/shard_map/route/pallas_call | solution.py:528
  102.2 13.2 %ffn.1 = (bf16[192,768]{1,0:T(8,128)(2,1)}, bf16[192,768]{1,0:T(8,128)(2,1)}, bf16[4,192,2048]{2,1,0:T(8,128)(2,1)}, bf16[4,192,2048]{2,1,0:T(8,128)(2,1)}, bf16[4,512,768]{2,1,0:T(8,128)(2,1)}) custom-call(bf16[192,768]{1,0:T(8,128)(2,1)} %bitcast.47, bf16[192,768]{1,0:T(8,128)(2,1)} %bitcast.48, bf16[768,2048]{1,0:T(8,128)(2,1)} %bitcast.38, ...), custom_call_target="tpu_custom_call" | custom-call | flops 6000000000 | bytes 20000000 | tf_op jit(solution)/shard_map/ffn/pallas_call | solution.py:1225
  115.4 19.5 %combine.1 = (bf16[4,48,768]{2,1,0:T(8,128)(2,1)}, bf16[4,48,768]{2,1,0:T(8,128)(2,1)}, bf16[192,2048]{1,0:T(8,128)(2,1)}, bf16[192,2048]{1,0:T(8,128)(2,1)}, bf...) custom-call(bf16[4,48,768]{2,1,0:T(8,128)(2,1)} %bitcast.29, ...), custom_call_target="tpu_custom_call" | custom-call | tf_op jit(solution)/shard_map/combine/pallas_call | solution.py:528
  134.9 2.0 collective-permute-start.2
  136.9 0.1 collective-permute-start.3
  137.0 1.9 collective-permute-start.4
  138.9 17.6 %to_heads.1 = (bf16[4,192,192]{2,1,0:T(8,128)(2,1)}, bf16[192,768]{1,0:T(8,128)(2,1)}, f32[192,768]{1,0:T(8,128)}, bf16[4,4,48,768]{3,2,1,0:T(8,128)(2,1)}, f32[16,768]{1,0:T(8,128)}) custom-call(bf16[4,48,768]{2,1,0:T(8,128)(2,1)} %get-tuple-element.91.refs_0_, bf16[4,48,768]{2,1,0:T(8,128)(2,1)} %get-tuple-element.92.refs_1_, ...), custom_call_target="tpu_custom_call" | custom-call | tf_op jit(solution)/shard_map/to_heads/pallas_call | solution.py:528
  156.5 0.0 collective-permute-done.2
  156.5 0.0 copy-done.8
  156.5 0.2 add_convert_fusion.2.refs_2_
  156.7 0.0 copy-start.1
  156.7 3.4 %collective-permute-start.7 = (bf16[512,768]{1,0:T(8,128)(2,1)S(1)}, bf16[512,768]{1,0:T(8,128)(2,1)S(1)}, u32[]{:S(2)}, u32[]{:S(2)}) collective-permute-start(bf16[512,768]{1,0:T(8,128)(2,1)S(1)} %add_convert_fusion.2.refs_2_), channel_id=1, source_target_pairs={{0,16},{16,0},{1,17},{17,1},{2,18},{18,2},{3,19},{19,3},{4,20},{20... | collective-permute-start | bytes 2359304 | tf_op jit(solution)/shard_map/ppermute | solution.py:1507
  160.1 23.8 %attend_back.1 = (bf16[4,192,192]{2,1,0:T(8,128)(2,1)}, bf16[4,4,192,384]{3,2,1,0:T(8,128)(2,1)}) custom-call(s32[25]{0:T(128)} %pad_add_fusion.info_ref, bf16[4,192,192]{2,1,0:T(8,128)(2,1)} %get-tuple-element.76.q_ref, bf16[3072,384]{1,0:T(8,128)(2,1)} %bitcast.42, s32[16,192]{1,0:T(8,128)} %copy-done.12, f32[4,192,192]{2,1,0:T(8,128)} %get-tuple-element.79.o_ref, ...), custom_call_target="tpu_custom_call" | custom-call | flops 5000000000 | bytes 12000000 | tf_op jit(solution)/shard_map/attend_back/pallas_call | solution.py:1427
  183.9 0.0 copy-done.1
  183.9 0.0 collective-permute-done.3
  183.9 0.0 copy-done.7
  184.0 1.5 add_convert_fusion.1.refs_0_
  185.4 0.0 copy-start.2
  185.4 2.3 collective-permute-done.4
  187.8 1.4 add_convert_fusion.refs_1_
  189.2 0.0 copy-start.3
  189.2 3.5 %collective-permute-start.5 = (bf16[192,2048]{1,0:T(8,128)(2,1)S(1)}, bf16[192,2048]{1,0:T(8,128)(2,1)}, u32[]{:S(2)}, u32[]{:S(2)}) collective-permute-start(bf16[192,2048]{1,0:T(8,128)(2,1)S(1)} %add_convert_fusion.1.refs_0_), channel_id=1, source_target_pairs={{0,16},{16,0},{1,17},{17,1},{2,18},{18,2},{3,19},{19,3},{4,20},{20... | collective-permute-start | bytes 2359304 | tf_op jit(solution)/shard_map/ppermute | solution.py:1507
  192.7 0.1 collective-permute-start.6
  192.8 68.1 %tail.1 = (f32[192,768]{1,0:T(8,128)}, f32[4,48,192]{2,1,0:T(8,128)}, f32[4,48,384]{2,1,0:T(8,128)}, f32[48,768]{1,0:T(8,128)}, f32[16,768]{1,0:T(8,128)}, /*index=5*/f32[8,768]{1,0:T(8,128)}) custom-call(bf16[4,4,192,384]{3,2,1,0:T(8,128)(2,1)} %get-tuple-element.110.refs_0_, bf16[4,192,192]{2,1,0:T(8,128)(2,1)} %get-tuple-element.111.refs_1_, ...), custom_call_target="tpu_custom_call" | custom-call | flops 20000000000 | bytes 100000000 | tf_op jit(solution)/shard_map/tail/pallas_call | solution.py:528
  261.0 0.0 collective-permute-done.7.refs_5_
  261.0 0.0 collective-permute-done.5.refs_3_
  261.0 0.0 collective-permute-done.6.refs_4_
  261.0 0.9 copy-done.5
  261.9 7.0 %finale.1 = (f32[192,2048]{1,0:T(8,128)}, f32[192,2048]{1,0:T(8,128)}, f32[512,768]{1,0:T(8,128)}, f32[192,768]{1,0:T(8,128)}, bf16[192,768]{1,0:T(8,128)(2,1)},...) custom-call(bf16[192,2048]{1,0:T(8,128)(2,1)} %copy-done.2, ...), custom_call_target="tpu_custom_call" | custom-call | flops 10000000 | bytes 10000000 | tf_op jit(solution)/shard_map/finale/pallas_call | solution.py:1493
  268.9 1.7 copy.41
  270.6 1.7 copy.40
  (14 shorter events, 0.0 us)
Async XLA Ops:
  1.9 42.0 %copy-start.9 = (bf16[192,768]{1,0:T(8,128)(2,1)S(1)}, bf16[192,768]{1,0:T(8,128)(2,1)}, u32[]{:S(2)}) copy-start(bf16[192,768]{1,0:T(8,128)(2,1)} %param.23) | copy-start | bytes 884740
  1.9 43.2 %copy-start.15 = (f32[768]{0:T(1024)S(1)}, f32[768]{0:T(1024)}, u32[]{:S(2)}) copy-start(f32[768]{0:T(1024)} %param.24) | copy-start | bytes 9220
  1.9 44.3 %copy-start.11 = (s32[1,3072]{1,0:T(1,128)S(1)}, s32[1,3072]{1,0:T(1,128)}, u32[]{:S(2)}) copy-start(s32[1,3072]{1,0:T(1,128)} %param.17) | copy-start | bytes 36868
  1.9 45.0 %copy-start.16 = (s32[192,2]{0,1:T(2,128)S(1)}, s32[192,2]{0,1:T(2,128)}, u32[]{:S(2)}) copy-start(s32[192,2]{0,1:T(2,128)} %param.18) | copy-start | bytes 4612
  1.9 45.8 %copy-start.13 = (f32[768,8]{0,1:T(8,128)S(1)}, f32[768,8]{0,1:T(8,128)}, u32[]{:S(2)}) copy-start(f32[768,8]{0,1:T(8,128)} %param.25) | copy-start | bytes 73732
  1.9 45.8 %copy-start.14 = (f32[768,4]{0,1:T(4,128)S(1)}, f32[768,4]{0,1:T(4,128)}, u32[]{:S(2)}) copy-start(f32[768,4]{0,1:T(4,128)} %param.26) | copy-start | bytes 36868
  3.2 46.3 %copy-start = (bf16[3,192,768]{2,1,0:T(8,128)(2,1)}, bf16[3,192,768]{2,1,0:T(8,128)(2,1)S(1)}, u32[]{:S(2)}) copy-start(bf16[3,192,768]{2,1,0:T(8,128)(2,1)S(1)} %pad_maximum_fusion.refs_8_) | copy-start | bytes 2654212
  43.0 28.3 %collective-permute-start.1 = (bf16[3,192,768]{2,1,0:T(8,128)(2,1)S(1)}, bf16[3,192,768]{2,1,0:T(8,128)(2,1)S(1)}, u32[]{:S(2)}, u32[]{:S(2)}) collective-permute-start(bf16[3,192,768]{2,1,0:T(8,128)(2,1)S(1)} %pad_maximum_fusion.refs_8_), channel_id=1, source_target_pairs={{0,2},{1,3},{2,0},{3,1},{4,6},{5,7},{6,4},{7,5},{8,10},{9,11},{10,... | collective-permute-start | bytes 2654216 | tf_op jit(solution)/shard_map/ppermute | solution.py:1507
  43.9 27.4 %collective-permute-start = (bf16[192,768]{1,0:T(8,128)(2,1)S(1)}, bf16[192,768]{1,0:T(8,128)(2,1)S(1)}, u32[]{:S(2)}, u32[]{:S(2)}) collective-permute-start(bf16[192,768]{1,0:T(8,128)(2,1)S(1)} %copy-done.9), channel_id=1, source_target_pairs={{0,2},{1,3},{2,0},{3,1},{4,6},{5,7},{6,4},{7,5},{8,10},{9,11},{10,... | collective-permute-start | bytes 884744 | tf_op jit(solution)/shard_map/ppermute | solution.py:1507
  47.0 3.4 %copy-start.12 = (s32[16,192]{1,0:T(8,128)}, s32[16,192]{1,0:T(8,128)S(1)}, u32[]{:S(2)}) copy-start(s32[16,192]{1,0:T(8,128)S(1)} %reshape_squeeze.3.qinfo_ref) | copy-start | bytes 36868
  71.3 0.7 copy-start.10
  71.3 1.0 copy-start.4
  134.9 21.6 %collective-permute-start.2 = (bf16[512,768]{1,0:T(8,128)(2,1)}, bf16[512,768]{1,0:T(8,128)(2,1)S(1)}, u32[]{:S(2)}, u32[]{:S(2)}) collective-permute-start(bf16[512,768]{1,0:T(8,128)(2,1)} %get-tuple-element.100), channel_id=1, source_target_pairs={{0,2},{1,3},{2,0},{3,1},{4,6},{5,7},{6,4},{7,5},{8,10},{9,11},{10,... | collective-permute-start | bytes 2359304 | tf_op jit(solution)/shard_map/ppermute | solution.py:1507
  136.9 47.0 %collective-permute-start.3 = (bf16[192,2048]{1,0:T(8,128)(2,1)}, bf16[192,2048]{1,0:T(8,128)(2,1)}, u32[]{:S(2)}, u32[]{:S(2)}) collective-permute-start(bf16[192,2048]{1,0:T(8,128)(2,1)} %get-tuple-element.104), channel_id=1, source_target_pairs={{0,2},{1,3},{2,0},{3,1},{4,6},{5,7},{6,4},{7,5},{8,10},{9,11},{10,... | collective-permute-start | bytes 2359304 | tf_op jit(solution)/shard_map/ppermute | solution.py:1507
  137.0 50.8 %collective-permute-start.4 = (bf16[192,2048]{1,0:T(8,128)(2,1)}, bf16[192,2048]{1,0:T(8,128)(2,1)}, u32[]{:S(2)}, u32[]{:S(2)}) collective-permute-start(bf16[192,2048]{1,0:T(8,128)(2,1)} %get-tuple-element.106), channel_id=1, source_target_pairs={{0,2},{1,3},{2,0},{3,1},{4,6},{5,7},{6,4},{7,5},{8,10},{9,11},{10,... | collective-permute-start | bytes 2359304 | tf_op jit(solution)/shard_map/ppermute | solution.py:1507
  138.9 17.6 %copy-start.8 = (bf16[512,768]{1,0:T(8,128)(2,1)S(1)}, bf16[512,768]{1,0:T(8,128)(2,1)}, u32[]{:S(2)}) copy-start(bf16[512,768]{1,0:T(8,128)(2,1)} %get-tuple-element.99) | copy-start | bytes 2359300
  156.7 27.2 %copy-start.1 = (bf16[512,768]{1,0:T(8,128)(2,1)}, bf16[512,768]{1,0:T(8,128)(2,1)S(1)}, u32[]{:S(2)}) copy-start(bf16[512,768]{1,0:T(8,128)(2,1)S(1)} %add_convert_fusion.2.refs_2_) | copy-start | bytes 2359300
  156.7 104.2 %collective-permute-start.7 = (bf16[512,768]{1,0:T(8,128)(2,1)S(1)}, bf16[512,768]{1,0:T(8,128)(2,1)S(1)}, u32[]{:S(2)}, u32[]{:S(2)}) collective-permute-start(bf16[512,768]{1,0:T(8,128)(2,1)S(1)} %add_convert_fusion.2.refs_2_), channel_id=1, source_target_pairs={{0,16},{16,0},{1,17},{17,1},{2,18},{18,2},{3,19},{19,3},{4,20},{20... | collective-permute-start | bytes 2359304 | tf_op jit(solution)/shard_map/ppermute | solution.py:1507
  160.1 23.8 %copy-start.7 = (bf16[192,2048]{1,0:T(8,128)(2,1)S(1)}, bf16[192,2048]{1,0:T(8,128)(2,1)}, u32[]{:S(2)}) copy-start(bf16[192,2048]{1,0:T(8,128)(2,1)} %get-tuple-element.103) | copy-start | bytes 2359300
  183.9 3.8 %copy-start.6 = (bf16[192,2048]{1,0:T(8,128)(2,1)S(1)}, bf16[192,2048]{1,0:T(8,128)(2,1)}, u32[]{:S(2)}) copy-start(bf16[192,2048]{1,0:T(8,128)(2,1)} %get-tuple-element.105) | copy-start | bytes 2359300
  185.4 75.5 %copy-start.2 = (bf16[192,2048]{1,0:T(8,128)(2,1)}, bf16[192,2048]{1,0:T(8,128)(2,1)S(1)}, u32[]{:S(2)}) copy-start(bf16[192,2048]{1,0:T(8,128)(2,1)S(1)} %add_convert_fusion.1.refs_0_) | copy-start | bytes 2359300
  189.2 71.8 %copy-start.3 = (bf16[192,2048]{1,0:T(8,128)(2,1)}, bf16[192,2048]{1,0:T(8,128)(2,1)S(1)}, u32[]{:S(2)}) copy-start(bf16[192,2048]{1,0:T(8,128)(2,1)S(1)} %add_convert_fusion.refs_1_) | copy-start | bytes 2359300
  189.2 71.8 %collective-permute-start.5 = (bf16[192,2048]{1,0:T(8,128)(2,1)S(1)}, bf16[192,2048]{1,0:T(8,128)(2,1)}, u32[]{:S(2)}, u32[]{:S(2)}) collective-permute-start(bf16[192,2048]{1,0:T(8,128)(2,1)S(1)} %add_convert_fusion.1.refs_0_), channel_id=1, source_target_pairs={{0,16},{16,0},{1,17},{17,1},{2,18},{18,2},{3,19},{19,3},{4,20},{20... | collective-permute-start | bytes 2359304 | tf_op jit(solution)/shard_map/ppermute | solution.py:1507
  192.7 68.3 %collective-permute-start.6 = (bf16[192,2048]{1,0:T(8,128)(2,1)S(1)}, bf16[192,2048]{1,0:T(8,128)(2,1)}, u32[]{:S(2)}, u32[]{:S(2)}) collective-permute-start(bf16[192,2048]{1,0:T(8,128)(2,1)S(1)} %add_convert_fusion.refs_1_), channel_id=1, source_target_pairs={{0,16},{16,0},{1,17},{17,1},{2,18},{18,2},{3,19},{19,3},{4,20},{20... | collective-permute-start | bytes 2359304 | tf_op jit(solution)/shard_map/ppermute | solution.py:1507
  261.0 0.9 copy-start.5

commit v5 on v4

--- a/solution.py
+++ b/solution.py
@@ -661,14 +661,36 @@
             copy.wait_send()
 
 
-def front(hidden, w_mine, gain):
+def slot_places(ids, lines, slots):
+    rows = ids.shape[0]
+    lane = lax.broadcasted_iota(jnp.int32, (rows, 128), 1)
+    hot = [lane == column(ids, k) for k in range(2)]
+    before = (
+        lax.broadcasted_iota(jnp.int32, (rows, rows), 0)
+        > lax.broadcasted_iota(jnp.int32, (rows, rows), 1)
+    ).astype(bf16)
+    named = jnp.where(hot[0] | hot[1], 1.0, 0.0).astype(bf16)
+    earlier = jnp.dot(before, named, preferred_element_type=f32)
+    slot_at = lax.broadcasted_iota(jnp.int32, (rows, slots), 1).astype(f32)
+    place = []
+    for k in range(2):
+        number = jnp.sum(jnp.where(hot[k], earlier, 0.0), axis=1, keepdims=True)
+        wanted = column(ids, k).astype(f32) * CAP + number
+        wanted = jnp.where(column(ids, k) < lines, wanted, -1.0)
+        place.append(jnp.where(slot_at == wanted, 1.0, 0.0))
+    return place
+
+
+def front(hidden, w_mine, gain, routes, out_grad):
     rows, model = hidden.shape
     lines = lax.axis_size(EX)
     width = model // lines
     shape = jax.ShapeDtypeStruct
     last = lines - 1
 
-    def body(hid_ref, w_ref, gain_ref, attn_ref, q_ref, kv_ref, land, w_all, kv_own, sems):
+    slots = lines * CAP
+
+    def body(hid_ref, w_ref, gain_ref, ids_ref, up_ref, attn_ref, q_ref, kv_ref, place_ref, rows_out, land, w_all, kv_own, rows_s, sems):
         line_me = lax.axis_index(EX)
         me, _, _, near, far = shard_peers()
         left, right = jnp.maximum(line_me - 1, 0), jnp.minimum(line_me + 1, last)
@@ -722,6 +744,12 @@
         w_far.start()
         w_near.start()
         w_all[me] = w_ref[...]
+        ids = ids_ref[...]
+        place = slot_places(ids, lines, slots)
+        for k in range(2):
+            place_ref[k] = place[k].astype(bf16)
+        either = (place[0] + place[1]).astype(bf16)
+        rows_s[...] = contract(either, up_ref[...], 0, 0).astype(bf16).reshape(lines, CAP, model)
         base += 3
         kv_far = lambda line: copy(kv_own.at[line], kv_ref.at[line, me], base + line, SH, far)
         kv_near = lambda line: copy(
@@ -774,6 +802,14 @@
                     line = source(step, way)
                     project(line, land[line])
 
+            if step == last - 2:
+                first = base + 3 * lines
+                ups = []
+                for d in range(1, lines):
+                    peer = lax.rem(line_me + d, lines)
+                    ups.append(copy(rows_s.at[peer], rows_out.at[line_me], first + d - 1, EX, peer))
+                    ups[-1].start()
+                rows_out[line_me] = rows_s[line_me]
             if step == 0:
                 hand(line_me)
             else:
@@ -803,6 +839,8 @@
             kv_far(line).wait_send()
             kv_near(line).wait()
             kv_pass(line).wait()
+        for up in ups:
+            up.wait()
 
     return pl.pallas_call(
         body,
@@ -810,18 +848,21 @@
             shape((lines, rows, model), bf16),
             shape((lines, rows, width), bf16),
             shape((lines, 4, rows, 2 * width), bf16),
+            shape((2, rows, slots), bf16),
+            shape((lines, CAP, model), bf16),
         ],
-        in_specs=[VM] * 3,
-        out_specs=[VM] * 3,
+        in_specs=[VM] * 5,
+        out_specs=[VM] * 5,
         scratch_shapes=[
             pltpu.VMEM((lines, rows, model), bf16),
             pltpu.VMEM((4, rows, 3 * width), bf16),
             pltpu.VMEM((lines, rows, 2 * width), bf16),
-            pltpu.SemaphoreType.DMA((2, 2 * last + 3 + 3 * lines)),
+            pltpu.VMEM((lines, CAP, model), bf16),
+            pltpu.SemaphoreType.DMA((2, 3 * last + 3 + 3 * lines)),
         ],
         compiler_params=pltpu.CompilerParams(collective_id=0, has_side_effects=True),
         name="front",
-    )(hidden, w_mine, gain)
+    )(hidden, w_mine, gain, routes, out_grad)
 
 
 def column(x, k):
@@ -836,38 +877,23 @@
     return sent
 
 
-def route(heads, hidden, gain, small_w, routes, out_grad, wo, wo_far, w3, w3_far, n_ids):
+def route(heads, hidden, gain, small_w, routes, place, wo, wo_far, n_ids):
     lines, rows, width = heads.shape
     model = lines * width
     slots = lines * CAP
     shape = jax.ShapeDtypeStruct
 
     def phases(ins, outs, scr, go):
-        heads_ref, hid_ref, gain_ref, small_ref, routes_ref, up_ref, wo_ref, wof_ref, w3_ref, w3f_ref = ins
-        rows_out, grads_out, w3_all, wo_all, resid_ref, table_ref, place_ref, low_ref = outs
-        land, rows_s, grads_s = scr
+        heads_ref, hid_ref, gain_ref, small_ref, routes_ref, place_ref, wo_ref, wof_ref = ins
+        rows_out, wo_all, resid_ref, table_ref, low_ref = outs
+        land, rows_s = scr
         swaps = start_swap(go, heads_ref, land, EX, False)
         swaps += core_share(go, wo_ref, wof_ref, wo_all)
-        shares = core_share(go, w3_ref, w3f_ref, w3_all)
         ids = routes_ref[...]
         lane = lax.broadcasted_iota(jnp.int32, (rows, 128), 1)
         hot = [lane == column(ids, k) for k in range(2)]
-        before = (
-            lax.broadcasted_iota(jnp.int32, (rows, rows), 0)
-            > lax.broadcasted_iota(jnp.int32, (rows, rows), 1)
-        ).astype(bf16)
-        named = jnp.where(hot[0] | hot[1], 1.0, 0.0).astype(bf16)
-        earlier = jnp.dot(before, named, preferred_element_type=f32)
-        slot_at = lax.broadcasted_iota(jnp.int32, (rows, slots), 1).astype(f32)
-        place = []
-        for k in range(2):
-            number = jnp.sum(jnp.where(hot[k], earlier, 0.0), axis=1, keepdims=True)
-            wanted = column(ids, k).astype(f32) * CAP + number
-            wanted = jnp.where(column(ids, k) < lines, wanted, -1.0)
-            place.append(jnp.where(slot_at == wanted, 1.0, 0.0))
-            place_ref[k] = place[k].astype(bf16)
-        either = (place[0] + place[1]).astype(bf16)
-        up_rows = contract(either, up_ref[...], 0, 0)
+        place = [place_ref[k].astype(f32) for k in range(2)]
+        either = place_ref[0] + place_ref[1]
         for copy in swaps:
             copy.wait()
         for line in range(lines):
@@ -879,10 +905,6 @@
         resid_ref[...] = resid
         inv = lax.rsqrt(jnp.mean(resid * resid, axis=1, keepdims=True) + norm_eps)
         moe_in = resid * inv * gain_ref[...]
-        rows_s[...] = contract(either, moe_in.astype(bf16), 0, 0).astype(bf16).reshape(
-            lines, CAP, model
-        )
-        row_swap = start_swap(go, rows_s, rows_out, EX, False)
         small = jnp.dot(moe_in, small_ref[...], preferred_element_type=f32, precision=HIGH)
         chosen = [jnp.sum(jnp.where(h, small, 0.0), axis=1, keepdims=True) for h in hot]
         top = jnp.maximum(chosen[0], chosen[1])
@@ -890,8 +912,15 @@
         gates = [p / (powers[0] + powers[1]) for p in powers]
         weight = place[0] * gates[0] + place[1] * gates[1]
         weight = contract(weight, jnp.ones((rows, 128), f32), 0, 0, HIGH)[:, 0:1]
-        grads_s[...] = (up_rows * weight).astype(bf16).reshape(lines, CAP, model)
-        grad_swap = start_swap(go, grads_s, grads_out, EX, False)
+        high = weight.astype(bf16)
+        low = (weight - high.astype(f32)).astype(bf16)
+        slot_lane = lax.broadcasted_iota(jnp.int32, (slots, 128), 1)
+        extra = jnp.where(slot_lane == 0, high, jnp.where(slot_lane == 1, low, jnp.zeros_like(low)))
+        rows_s[:, :, :model] = (
+            contract(either, moe_in.astype(bf16), 0, 0).astype(bf16).reshape(lines, CAP, model)
+        )
+        rows_s[:, :, model:] = extra.reshape(lines, CAP, 128)
+        row_swap = start_swap(go, rows_s, rows_out, EX, False)
         table = jnp.zeros((rows, 128), f32)
         entries = list(gates)
         for j in range(2):
@@ -903,23 +932,34 @@
         for k, entry in enumerate(entries):
             table = jnp.where(lane == k, entry, table)
         table_ref[...] = table
-        for copy in row_swap + grad_swap + shares:
+        for copy in row_swap:
             copy.wait()
         yield
 
-    ins = [heads, hidden, gain, small_w, routes, out_grad, wo, wo_far, w3, w3_far]
+    ins = [heads, hidden, gain, small_w, routes, place, wo, wo_far]
     outs = [
-        shape((lines, CAP, model), bf16),
-        shape((lines, CAP, model), bf16),
-        shape((3, 4, model // 4, model), bf16),
+        shape((lines, CAP, model + 128), bf16),
         shape((1, 4, model // 4, model), bf16),
         shape((rows, model), f32),
         shape((rows, 128), f32),
-        shape((2, rows, slots), bf16),
         shape((rows, model), bf16),
     ]
-    scratch = [pltpu.VMEM((lines, rows, width), bf16)] + [pltpu.VMEM((lines, CAP, model), bf16)] * 2
-    return Part([EX, SH], ins, outs, scratch, 3 * (lines - 1) + 4, phases)
+    scratch = [
+        pltpu.VMEM((lines, rows, width), bf16),
+        pltpu.VMEM((lines, CAP, model + 128), bf16),
+    ]
+    return Part([EX, SH], ins, outs, scratch, 2 * (lines - 1) + 2, phases)
+
+
+def share_weights(own, far):
+    def phases(ins, outs, scr, go):
+        copies = core_share(go, ins[0], ins[1], outs[0])
+        yield
+        for copy in copies:
+            copy.wait()
+
+    dims = (own.shape[0], 4) + own.shape[1:]
+    return Part([SH], [own, far], [jax.ShapeDtypeStruct(dims, bf16)], [], 2, phases)
 
 
 def to_heads(returned, input_ret, place, table, resid, low, out_grad, gain, small_t, const_vec, wo, n_ids):
@@ -1033,24 +1073,50 @@
     shape = jax.ShapeDtypeStruct
     vmem = pltpu.VMEM
     tok = lines * rows
-    dkv_piece, q_piece = (lines, rows, 2 * width), (lines, own, width)
+    few = lines // 2
+    dkv_piece, q_piece = (few, rows, 2 * width), (lines, own, width)
     kv_piece, o_piece = (lines, own, 2 * width), (lines, own, model)
     part_dims = (width, 2 * width, model)
 
     def phases(ins, outs, scr, go):
-        dkv_ref, dq_ref, attn_ref, w_ref, o_ref, packed_ref, hid_ref, resid_ref, gain_ref = ins
+        lo_ref, hi_ref, dq_ref, attn_ref, w_ref, o_ref, packed_ref, hid_ref, resid_ref, gain_ref = ins
         input_ref, q_out, kv_out, out_out, packed_out, gain_out = outs
         scr = list(scr)
         take = lambda k: [scr.pop(0) for _ in range(k)]
-        kv_scr, q_scr, kvw_scr, o_scr = take(3), take(3), take(3), take(3)
+        lo_scr, hi_scr, q_scr, kvw_scr, o_scr = take(3), take(3), take(3), take(3), take(3)
         own_kv, q_t, kv_t, dq_all, dkv_all, dq_full = take(6)
+        kv_sems = take(1)[0]
         sums, lands, halves, gots = take(3), take(3), take(3), take(3)
         pk_l, pk_s, pk_g = take(3)
         mid_l, mid_s = take(2)
         gn_l, gn_s, gn_g, gn_0, gn_1, gn_2 = take(6)
         me = lax.axis_index(SH)
 
-        kv_tree = Tree(dkv_ref, kv_scr, go)
+        line_me = lax.axis_index(EX)
+        kv_trees = [Tree(lo_ref, lo_scr, go), Tree(hi_ref, hi_scr, go)]
+
+        def kv_copy(sender, target):
+            return pltpu.make_async_remote_copy(
+                src_ref=own_kv.at[target],
+                dst_ref=dkv_all.at[sender],
+                send_sem=kv_sems.at[0, target],
+                recv_sem=kv_sems.at[1, sender],
+                device_id={EX: target},
+                device_id_type=pl.DeviceIdType.MESH,
+            )
+
+        def push_kv(k):
+            own_kv[k * few : (k + 1) * few] = kv_trees[k].result().astype(bf16)
+            for target in range(k * few, (k + 1) * few):
+
+                @pl.when(line_me != target)
+                def _():
+                    kv_copy(line_me, jnp.int32(target)).start()
+
+                @pl.when(line_me == target)
+                def _():
+                    dkv_all[target] = own_kv[target]
+
         dq_swap = start_swap(go, dq_ref, dq_all, EX, False)
         o_tree = Tree(o_ref, o_scr, go)
         pk1 = start_swap(go, packed_ref, pk_l, EX, True)
@@ -1063,7 +1129,8 @@
                     at = (line * 4 + piece) * own
                     out[piece, line] = value[at : at + own]
 
-        kv_tree.across()
+        for tree in kv_trees:
+            tree.across()
         term(dq_ref, q_t)
         o_tree.across()
         q_tree = Tree(q_t, q_scr, go)
@@ -1073,8 +1140,8 @@
             sums[k][...] = trees[k].result().astype(bf16)
             return start_swap(go, sums[k], lands[k], EX, False)
 
-        own_kv[...] = kv_tree.result().astype(bf16)
-        dkv_swap = start_swap(go, own_kv, dkv_all, EX, False)
+        push_kv(0)
+        push_kv(1)
         o_lines = lines_out(2)
         q_tree.across()
         term(own_kv, kv_t)
@@ -1096,8 +1163,13 @@
         mid_s[...] = total_of(pk_s, 4)
         pk3 = start_swap(go, mid_s, pk_g, GR, True)
         kv_lines = lines_out(1)
-        for copy in dkv_swap:
-            copy.wait()
+        for other in range(lines):
+
+            @pl.when(line_me != other)
+            def _():
+                kv_copy(jnp.int32(other), line_me).wait_recv()
+                kv_copy(line_me, jnp.int32(other)).wait_send()
+
         for half in range(2):
             for line in range(lines):
                 dq_full[:, line * width : (line + 1) * width] = dkv_all[
@@ -1107,7 +1179,7 @@
         inputs = hid_ref[...].astype(f32)
         inv = lax.rsqrt(jnp.mean(inputs * inputs, axis=1, keepdims=True) + norm_eps)
         normed = inputs * inv
-        gn_0[...] = jnp.sum((grad * normed).reshape(rows // 8, 8, model), axis=0)
+        gn_0[...] = jnp.sum(grad * normed, axis=0, keepdims=True)
         gn1 = start_swap(go, gn_0, gn_l, EX, True)
         input_ref[...] = resid_ref[...] + rms_back(inputs, inv, gain_ref[...], grad)
         swaps = [None] * 3
@@ -1141,41 +1213,42 @@
         for copy in gn3:
             copy.wait()
         gain_out[...] = total_of(gn_g, groups)
-        for tree in (kv_tree, o_tree, q_tree, kvw_tree):
+        for tree in (*kv_trees, o_tree, q_tree, kvw_tree):
             tree.close()
         yield
 
     pieces = [(lines, own, d) for d in part_dims]
     got_pieces = pieces[:2] + [(own, model)]
-    scratch = Tree.scratch(dkv_piece) + Tree.scratch(q_piece) + Tree.scratch(kv_piece)
+    scratch = Tree.scratch(dkv_piece) * 2 + Tree.scratch(q_piece) + Tree.scratch(kv_piece)
     scratch += Tree.scratch(o_piece)
     scratch += [
-        vmem(dkv_piece, bf16),
+        vmem((lines, rows, 2 * width), bf16),
         vmem((4,) + q_piece, bf16),
         vmem((4,) + kv_piece, bf16),
         vmem((lines, rows, width), bf16),
         vmem((lines, rows, 2 * width), bf16),
         vmem((rows, model), bf16),
+        pltpu.SemaphoreType.DMA((2, lines)),
     ]
     scratch += [vmem(p, bf16) for p in pieces] + [vmem(p, bf16) for p in pieces]
     scratch += [vmem(p, bf16) for p in got_pieces] + [vmem((groups,) + p, bf16) for p in got_pieces]
     scratch += [vmem((n,) + packed.shape, f32) for n in (lines, 4, groups)]
     scratch += [vmem(packed.shape, f32)] * 2
-    scratch += [vmem((n, 8, model), f32) for n in (lines, 4, groups)] + [vmem((8, model), f32)] * 3
-    copies = 4 * Tree.copies + 7 * (lines - 1) + 2 * 3 + 5 * (groups - 1)
+    scratch += [vmem((n, 1, model), f32) for n in (lines, 4, groups)] + [vmem((1, model), f32)] * 3
+    copies = 5 * Tree.copies + 6 * (lines - 1) + 2 * 3 + 5 * (groups - 1)
     outs = [
         shape((rows, model), f32),
         shape((lines, own, width), f32),
         shape((lines, own, 2 * width), f32),
         shape((own, model), f32),
         shape(packed.shape, f32),
-        shape((8, model), f32),
+        shape((1, model), f32),
     ]
-    ins = [dkv, dq, attn_in, weights, out_term, packed, hidden, resid_grad, gain]
+    ins = [*dkv, dq, attn_in, weights, out_term, packed, hidden, resid_grad, gain]
     return Part([EX, SH, GR], ins, outs, scratch, copies, phases)
 
 
-def expert_body(steps, x_ref, g_ref, wg_ref, wu_ref, wd_ref, eo_ref, ib_ref, ga_ref, up_ref, d_ref, eo_s, ib_s):
+def expert_body(steps, x_ref, g_ref, wg_ref, wu_ref, wd_ref, eo_ref, ib_ref, ga_ref, up_ref, d_ref, eo_s, ib_s, g_s):
     i = pl.program_id(0)
     me, side, core, _, _ = shard_peers()
 
@@ -1183,8 +1256,12 @@
     def _():
         eo_s[...] = jnp.zeros_like(eo_s)
         ib_s[...] = jnp.zeros_like(ib_s)
-
-    x, g = x_ref[...], g_ref[...]
+        model = g_ref.shape[1]
+        high, low = x_ref[:, model : model + 1], x_ref[:, model + 1 : model + 2]
+        gate = high.astype(f32) + low.astype(f32)
+        g_s[...] = (g_ref[...].astype(f32) * gate).astype(bf16)
+
+    x, g = x_ref[:, : g_ref.shape[1]], g_s[...]
     wg, wu, wd = wg_ref[...], wu_ref[...], wd_ref[...]
     gate_pre = jnp.dot(x, wg, preferred_element_type=f32)
     up_pre = jnp.dot(x, wu, preferred_element_type=f32)
@@ -1215,7 +1292,7 @@
 
 
 def expert(x, g, wg, wu, wd):
-    slots, model = x.shape
+    slots, model = g.shape
     inner = wg.shape[1]
     steps = 4
     tile = inner // steps
@@ -1233,7 +1310,7 @@
             shape((4, tile, model), bf16),
         ],
         in_specs=[
-            whole((slots, model)),
+            whole(x.shape),
             whole((slots, model)),
             pl.BlockSpec((model, tile), lambda i: (0, i)),
             pl.BlockSpec((model, tile), lambda i: (0, i)),
@@ -1246,7 +1323,7 @@
             pl.BlockSpec((4, quarter, tile), lambda i: (0, 0, i)),
             whole((4, tile, model)),
         ],
-        scratch_shapes=[pltpu.VMEM((slots, model), f32)] * 2,
+        scratch_shapes=[pltpu.VMEM((slots, model), f32)] * 2 + [pltpu.VMEM((slots, model), bf16)],
         cost_estimate=pl.CostEstimate(flops=6 * 10**9, bytes_accessed=2 * 10**7, transcendentals=4 * 10**5),
         name="ffn",
     )(x, g, wg, wu, wd)
@@ -1353,7 +1430,7 @@
     )(info, q, kv, qinfo)
 
 
-def attend_back_body(lines, heads, info_ref, q_ref, kv_ref, qinfo_ref, o_ref, lse_ref, back_ref, dq_ref, dkv_ref, k_s, v_s, dk_s, dv_s, dq_s, qm_s, bm_s, delta_s):
+def attend_back_body(lines, heads, info_ref, q_ref, kv_ref, qinfo_ref, o_ref, lse_ref, back_ref, dq_ref, dkv_lo, dkv_hi, k_s, v_s, dk_s, dv_s, dq_s, qm_s, bm_s, delta_s):
     shard = lax.axis_index(SH)
     rows, width = q_ref.shape[1:]
     key_blk = KEY_BLK
@@ -1411,12 +1488,16 @@
             total = jnp.where(head_columns(h, queries.shape, 1), dq_s[h], total)
         dq_ref[line] = (total * HEAD_DIM**-0.5).astype(bf16)
 
-    @pl.loop(0, lines)
-    def _(line):
-        for piece in range(4):
-            at = pl.ds(pl.multiple_of((line * 4 + piece) * rows, rows), rows)
-            dkv_ref[piece, line, :, :width] = dk_s[at, :].astype(bf16)
-            dkv_ref[piece, line, :, width:] = dv_s[at, :].astype(bf16)
+    half = lines // 2
+    for k, ref in enumerate((dkv_lo, dkv_hi)):
+
+        @pl.loop(0, half)
+        def _(line):
+            for piece in range(4):
+                at = ((k * half + line) * 4 + piece) * rows
+                at = pl.ds(pl.multiple_of(at, rows), rows)
+                ref[piece, line, :, :width] = dk_s[at, :].astype(bf16)
+                ref[piece, line, :, width:] = dv_s[at, :].astype(bf16)
 
 
 def attend_back(info, q, kv, qinfo, o, lse, back):
@@ -1428,10 +1509,11 @@
         functools.partial(attend_back_body, lines, heads),
         out_shape=[
             shape((lines, rows, width), bf16),
-            shape((4, lines, rows, 2 * width), bf16),
+            shape((4, lines // 2, rows, 2 * width), bf16),
+            shape((4, lines // 2, rows, 2 * width), bf16),
         ],
         in_specs=[SM] + [VM] * 6,
-        out_specs=[VM] * 2,
+        out_specs=[VM] * 3,
         scratch_shapes=[
             pltpu.VMEM((length, width), bf16),
             pltpu.VMEM((length, width), bf16),
@@ -1535,7 +1617,9 @@
     w_qkv = jnp.stack([w_query, w_key, w_value])
     w_mine = lax.dynamic_slice_in_dim(w_qkv, line * width, width, axis=2)
     w_mine = jnp.concatenate([w_mine[1], w_mine[2], w_mine[0]], axis=1)
-    attn_in, q, kv_all = front(hidden_in, w_mine, attn_gain[None])
+    attn_in, q, kv_all, place, recv_grads = front(
+        hidden_in, w_mine, attn_gain[None], routes, out_grad
+    )
     attn_in = attn_in.reshape(lines * rows, model)
     kv_all, w_out_b, w_qkv = lax.optimization_barrier((kv_all, w_out, w_qkv))
     wo_far = swap(w_out_b, SH, lambda i: i ^ 2)
@@ -1554,31 +1638,32 @@
         jnp.concatenate([w_router, const_mix], axis=1), ((0, 0), (0, 124 - n_ids))
     )
     gain_two = moe_gain[None]
-    recv_rows, recv_grads, weights, wo_full, resid_one, table, place, attn_low = run_parts(
+    recv_rows, wo_full, resid_one, table, attn_low = run_parts(
         [
             route(
-                attn_heads, hidden_in, gain_two, small_w, routes, out_grad, w_out[None], wo_far[None], w_qkv, w_far, n_ids
+                attn_heads, hidden_in, gain_two, small_w, routes, place, w_out[None], wo_far[None], n_ids
             )
         ],
         2,
         "route",
     )
-    weights = weights.reshape(3, model, model)
     wo_full = wo_full.reshape(model, model)
     slots = lines * CAP
 
     expert_out, input_back, *terms = expert(
-        recv_rows.reshape(slots, model), recv_grads.reshape(slots, model), w_gate[0], w_up[0], w_down[0]
-    )
-    returned, input_ret, *sums = run_parts(
+        recv_rows.reshape(slots, model + 128), recv_grads.reshape(slots, model), w_gate[0], w_up[0], w_down[0]
+    )
+    returned, input_ret, weights, *sums = run_parts(
         [
             exchange(EX, SWAP, expert_out.reshape(lines, CAP, model)),
             exchange(EX, SWAP, input_back.reshape(lines, CAP, model)),
+            share_weights(w_qkv, w_far),
         ]
         + [core_sum(term) for term in terms],
         4,
         "combine",
     )
+    weights = weights.reshape(3, model, model)
     far = [swap(there, SH, lambda i: i ^ 2) for there in sums[1::2]]
     mine = [(x.astype(f32) + y.astype(f32)).astype(bf16) for x, y in zip(sums[0::2], far)]
 
@@ -1594,8 +1679,8 @@
     back_heads, mine[2] = lax.optimization_barrier((back_heads, mine[2]))
     cross = lambda x: swap(x, GR, lambda i: 1 - i)
     down_far = cross(mine[2])
-    dq, dkv = attend_back(info, q, kv_all, qinfo, attn_vec, lse, back_heads)
-    dkv, *mine[:2] = lax.optimization_barrier((dkv, *mine[:2]))
+    dq, *dkv = attend_back(info, q, kv_all, qinfo, attn_vec, lse, back_heads)
+    *dkv, mine[0], mine[1] = lax.optimization_barrier((*dkv, *mine[:2]))
     group_far = [cross(mine[0]), cross(mine[1]), down_far]
     input_grad, *sums = run_parts(
         [

time: 268 us -> 260 us (0.970); the launches traced: 272 us -> 259 us
  Pallas kernels: 233 us -> 225 us
  waiting for transfers between devices: 7.8 us -> 3.52 us
  starting transfers between devices: 13.1 us -> 9.59 us
    pallas_call x4, Pallas kernels: 135 us -> 123 us  [run_parts(): pl.pallas_call(body, out_shape=outs, in_specs=sum([p.specs for p in parts...]
    ppermute x8, waiting for transfers between devices: 7.8 us -> 3.52 us  [swap(): lax.ppermute(x, axis, [(i, partner(i)) for i in range(lax.axis_size(axis))])]
    pallas_call x1, Pallas kernels: 38.7 us -> 42.7 us  [front(): pl.pallas_call(body, out_shape=[shape((lines, rows, model), bf16), shape(...]
    ppermute x8, starting transfers between devices: 13.1 us -> 9.59 us  [swap(): lax.ppermute(x, axis, [(i, partner(i)) for i in range(lax.axis_size(axis))])]
  transfers between devices with their start and end apart: 8 -> 8, of which waited for: 2 -> 2; matrix products, arithmetic and copies ran while one was open for 3% -> 3% of each run, Pallas kernels for 46% -> 59%
where the time goes in v5:
time: 260 us; the launch traced here: 259 us
  Pallas kernels  225 us (87%)
  local copies, waits for them, and re-layouts  12 us (5%)
  starting transfers between devices  9.59 us (4%)
  other arithmetic  7.27 us (3%)
  waiting for transfers between devices  3.52 us (1%)
    pallas_call x4, Pallas kernels, run_parts(): pl.pallas_call(body, out_shape=outs, in_specs=sum([p.specs for p in parts...  123 us
    pallas_call x1, Pallas kernels, front(): pl.pallas_call(body, out_shape=[shape((lines, rows, model), bf16), shape(...  42.7 us
    pallas_call x1, Pallas kernels, attend_back(): pl.pallas_call(functools.partial(attend_back_body, lines, heads), out_sha...  23.8 us
    pallas_call x1, Pallas kernels, attend(): pl.pallas_call(functools.partial(attend_body, lines, heads), out_shape=[s...  15.5 us
    pallas_call x1, Pallas kernels, expert(): pl.pallas_call(functools.partial(expert_body, steps), grid=(steps,), out_...  13.3 us
    ppermute x8, starting transfers between devices, swap(): lax.ppermute(x, axis, [(i, partner(i)) for i in range(lax.axis_size(axis))])  9.59 us
    unnamed x38, local copies, waits for them, and re-layouts  8.85 us
    pallas_call x1, Pallas kernels, finale(): pl.pallas_call(functools.partial(finale_body, lines, n_ids), grid=(steps,...  7.04 us
  transfers between devices with their start and end apart: 8, of which 2 were waited for; matrix products, arithmetic and copies ran while one was open for 3% of the time, Pallas kernels for 59%

profile of v5, /device:TPU:0, one launch (start us, length us, event | category | flops | bytes accessed | tf_op | source)
XLA Modules:
  0.0 258.5 jit_solution(9114442479148976362)
XLA Ops:
  0.7 1.3 broadcast_in_dim.23.gain_ref.refs_9_
  1.9 1.4 copy.40.ids_ref.refs_4_
  3.4 1.3 pad_maximum_fusion.refs_2_
  4.7 0.0 copy-start
  4.7 0.0 copy-start.16
  4.7 0.2 dynamic-slice_bitcast_fusion.2
  4.9 0.8 pad_maximum_fusion.1.w_ref
  5.7 42.7 %front.1 = (bf16[4,192,768]{2,1,0:T(8,128)(2,1)}, bf16[4,192,192]{2,1,0:T(8,128)(2,1)}, bf16[4,4,192,384]{3,2,1,0:T(8,128)(2,1)}, bf16[2,192,192]{2,1,0:T(8,128)(2,1)}, bf16[4,48,768]{2,1,0:T(8,128)(2,1)}) custom-call(bf16[192,768]{1,0:T(8,128)(2,1)} %refs_7_.1, bf16[192,576]{1,0:T(8,128)(2,1)} %pad_maximum_fusion.1.w_ref, ...), custom_call_target="tpu_custom_call" | custom-call | tf_op jit(solution)/shard_map/front/pallas_call | solution.py:845
  48.4 0.0 copy-done.10
  48.4 1.2 collective-permute-start
  49.6 0.9 collective-permute-start.1
  50.5 0.0 copy-done.12
  50.5 0.1 convert_reduce_fusion
  50.6 0.5 broadcast.16
  51.1 0.7 reduce.5
  51.8 0.1 reshape_squeeze.3.qinfo_ref
  51.9 0.0 copy-done.14
  51.9 0.0 copy-done.15
  51.9 0.8 fusion
  52.7 0.1 slice_reduce_fusion
  52.8 0.0 copy-done.16
  52.8 0.6 broadcast_in_dim.24.refs_2_.refs_7_
  53.4 0.9 copy.41.refs_3_
  54.3 0.0 copy-done
  54.3 0.6 pad_add_fusion.info_ref
  54.9 0.0 copy-done.13
  54.9 15.5 %attend.1 = (f32[4,192,192]{2,1,0:T(8,128)}, bf16[4,192,192]{2,1,0:T(8,128)(2,1)}, f32[4,8,192]{2,1,0:T(8,128)}) custom-call(s32[25]{0:T(128)} %pad_add_fusion.info_ref, bf16[4,192,192]{2,1,0:T(8,128)(2,1)} %get-tuple-element.78.q_ref, bf16[3072,384]{1,0:T(8,128)(2,1)} %bitcast.41, s32[16,192]{1,0:T(8,128)} %copy-done.13), custom_call_target="tpu_custom_call" | custom-call | flops 2000000000 | bytes 8000000 | tf_op jit(solution)/shard_map/attend/pallas_call | solution.py:1412
  70.4 0.0 collective-permute-done
  70.4 0.7 copy-done.11
  71.1 25.6 %route.1 = (bf16[4,48,896]{2,1,0:T(8,128)(2,1)}, bf16[1,4,192,768]{3,2,1,0:T(8,128)(2,1)}, f32[192,768]{1,0:T(8,128)}, f32[192,128]{1,0:T(8,128)}, bf16[192,768]{1,0:T(8,128)(2,1)}) custom-call(bf16[4,192,192]{2,1,0:T(8,128)(2,1)} %get-tuple-element.83.refs_0_, bf16[192,768]{1,0:T(8,128)(2,1)} %refs_7_.1, f32[1,768]{1,0:T(1,128)} %broadcast_in_dim.24.refs_2_.refs_7_, ...), custom_call_target="tpu_custom_call" | custom-call | tf_op jit(solution)/shard_map/route/pallas_call | solution.py:528
  96.7 13.3 %ffn.1 = (bf16[192,768]{1,0:T(8,128)(2,1)}, bf16[192,768]{1,0:T(8,128)(2,1)}, bf16[4,192,2048]{2,1,0:T(8,128)(2,1)}, bf16[4,192,2048]{2,1,0:T(8,128)(2,1)}, bf16[4,512,768]{2,1,0:T(8,128)(2,1)}) custom-call(bf16[192,896]{1,0:T(8,128)(2,1)} %bitcast.47, bf16[192,768]{1,0:T(8,128)(2,1)} %bitcast.48, bf16[768,2048]{1,0:T(8,128)(2,1)} %bitcast.38, ...), custom_call_target="tpu_custom_call" | custom-call | flops 6000000000 | bytes 20000000 | tf_op jit(solution)/shard_map/ffn/pallas_call | solution.py:1302
  110.0 0.0 collective-permute-done.1.refs_3_
  110.1 0.0 copy-start.4
  110.1 0.9 copy-done.4
  111.0 21.9 %combine.1 = (bf16[4,48,768]{2,1,0:T(8,128)(2,1)}, bf16[4,48,768]{2,1,0:T(8,128)(2,1)}, bf16[3,4,192,768]{3,2,1,0:T(8,128)(2,1)}, bf16[192,2048]{1,0:T(8,128)(2,...) custom-call(bf16[4,48,768]{2,1,0:T(8,128)(2,1)} %bitcast.29, ...), custom_call_target="tpu_custom_call" | custom-call | tf_op jit(solution)/shard_map/combine/pallas_call | solution.py:528
  132.9 0.3 collective-permute-start.2
  133.2 1.8 collective-permute-start.3
  135.0 0.3 collective-permute-start.4
  135.3 17.9 %to_heads.1 = (bf16[4,192,192]{2,1,0:T(8,128)(2,1)}, bf16[192,768]{1,0:T(8,128)(2,1)}, f32[192,768]{1,0:T(8,128)}, bf16[4,4,48,768]{3,2,1,0:T(8,128)(2,1)}, f32[16,768]{1,0:T(8,128)}) custom-call(bf16[4,48,768]{2,1,0:T(8,128)(2,1)} %get-tuple-element.94.refs_0_, bf16[4,48,768]{2,1,0:T(8,128)(2,1)} %get-tuple-element.95.refs_1_, ...), custom_call_target="tpu_custom_call" | custom-call | tf_op jit(solution)/shard_map/to_heads/pallas_call | solution.py:528
  153.2 0.4 collective-permute-done.2
  153.6 0.0 copy-done.9
  153.6 0.2 add_convert_fusion.2.refs_2_
  153.8 0.0 copy-start.1
  153.8 2.7 %collective-permute-start.7 = (bf16[512,768]{1,0:T(8,128)(2,1)S(1)}, bf16[512,768]{1,0:T(8,128)(2,1)S(1)}, u32[]{:S(2)}, u32[]{:S(2)}) collective-permute-start(bf16[512,768]{1,0:T(8,128)(2,1)S(1)} %add_convert_fusion.2.refs_2_), channel_id=1, source_target_pairs={{0,16},{16,0},{1,17},{17,1},{2,18},{18,2},{3,19},{19,3},{4,20},{20... | collective-permute-start | bytes 2359304 | tf_op jit(solution)/shard_map/ppermute | solution.py:1589
  156.5 23.8 %attend_back.1 = (bf16[4,192,192]{2,1,0:T(8,128)(2,1)}, bf16[4,2,192,384]{3,2,1,0:T(8,128)(2,1)}, bf16[4,2,192,384]{3,2,1,0:T(8,128)(2,1)}) custom-call(s32[25]{0:T(128)} %pad_add_fusion.info_ref, bf16[4,192,192]{2,1,0:T(8,128)(2,1)} %get-tuple-element.78.q_ref, bf16[3072,384]{1,0:T(8,128)(2,1)} %bitcast.42, s32[16,192]{1,0:T(8,128)} %copy-done.13, ...), custom_call_target="tpu_custom_call" | custom-call | flops 5000000000 | bytes 12000000 | tf_op jit(solution)/shard_map/attend_back/pallas_call | solution.py:1508
  180.2 0.0 copy-done.1
  180.2 0.0 collective-permute-done.3
  180.2 0.0 copy-start.8
  180.3 0.9 copy-done.8
  181.1 1.4 add_convert_fusion.1.refs_0_
  182.5 0.0 copy-start.2
  182.5 3.1 %collective-permute-done.4 = bf16[192,2048]{1,0:T(8,128)(2,1)} collective-permute-done((bf16[192,2048]{1,0:T(8,128)(2,1)}, bf16[192,2048]{1,0:T(8,128)(2,1)}, u32[]{:S(2)}, u32[]{:S(2)}) %collective-permute-start.4) | collective-permute-done | bytes 786464 | tf_op jit(solution)/shard_map/ppermute | solution.py:1589
  185.6 1.4 add_convert_fusion.refs_1_
  187.0 0.0 copy-start.3
  187.0 2.4 collective-permute-start.5
  189.4 0.1 collective-permute-start.6
  189.5 57.6 %tail.1 = (f32[192,768]{1,0:T(8,128)}, f32[4,48,192]{2,1,0:T(8,128)}, f32[4,48,384]{2,1,0:T(8,128)}, f32[48,768]{1,0:T(8,128)}, f32[16,768]{1,0:T(8,128)}, /*index=5*/f32[1,768]{1,0:T(1,128)}) custom-call(bf16[4,2,192,384]{3,2,1,0:T(8,128)(2,1)} %get-tuple-element.113.refs_0_, bf16[4,2,192,384]{3,2,1,0:T(8,128)(2,1)} %get-tuple-element.114.refs_1_, ...), custom_call_target="tpu_custom_call" | custom-call | flops 20000000000 | bytes 100000000 | tf_op jit(solution)/shard_map/tail/pallas_call | solution.py:528
  247.1 0.0 collective-permute-done.7.refs_5_
  247.1 0.0 collective-permute-done.5.refs_3_
  247.1 0.0 collective-permute-done.6.refs_4_
  247.1 0.9 copy-done.5
  248.0 7.0 %finale.1 = (f32[192,2048]{1,0:T(8,128)}, f32[192,2048]{1,0:T(8,128)}, f32[512,768]{1,0:T(8,128)}, f32[192,768]{1,0:T(8,128)}, bf16[192,768]{1,0:T(8,128)(2,1)},...) custom-call(bf16[192,2048]{1,0:T(8,128)(2,1)} %copy-done.2, ...), custom_call_target="tpu_custom_call" | custom-call | flops 10000000 | bytes 10000000 | tf_op jit(solution)/shard_map/finale/pallas_call | solution.py:1575
  255.0 1.7 copy.44
  256.8 1.7 copy.43
  (14 shorter events, 0.0 us)
Async XLA Ops:
  3.4 45.0 %copy-start.10 = (bf16[192,768]{1,0:T(8,128)(2,1)S(1)}, bf16[192,768]{1,0:T(8,128)(2,1)}, u32[]{:S(2)}) copy-start(bf16[192,768]{1,0:T(8,128)(2,1)} %param.23) | copy-start | bytes 884740
  3.4 47.1 %copy-start.12 = (s32[1,3072]{1,0:T(1,128)S(1)}, s32[1,3072]{1,0:T(1,128)}, u32[]{:S(2)}) copy-start(s32[1,3072]{1,0:T(1,128)} %param.17) | copy-start | bytes 36868
  3.4 48.5 %copy-start.14 = (f32[768,8]{0,1:T(8,128)S(1)}, f32[768,8]{0,1:T(8,128)}, u32[]{:S(2)}) copy-start(f32[768,8]{0,1:T(8,128)} %param.25) | copy-start | bytes 73732
  3.4 48.5 %copy-start.15 = (f32[768,4]{0,1:T(4,128)S(1)}, f32[768,4]{0,1:T(4,128)}, u32[]{:S(2)}) copy-start(f32[768,4]{0,1:T(4,128)} %param.26) | copy-start | bytes 36868
  4.7 49.6 %copy-start = (bf16[3,192,768]{2,1,0:T(8,128)(2,1)}, bf16[3,192,768]{2,1,0:T(8,128)(2,1)S(1)}, u32[]{:S(2)}) copy-start(bf16[3,192,768]{2,1,0:T(8,128)(2,1)S(1)} %pad_maximum_fusion.refs_2_) | copy-start | bytes 2654212
  4.7 48.1 %copy-start.16 = (f32[768]{0:T(1024)S(1)}, f32[768]{0:T(1024)}, u32[]{:S(2)}) copy-start(f32[768]{0:T(1024)} %param.24) | copy-start | bytes 9220
  48.4 22.1 %collective-permute-start = (bf16[192,768]{1,0:T(8,128)(2,1)S(1)}, bf16[192,768]{1,0:T(8,128)(2,1)S(1)}, u32[]{:S(2)}, u32[]{:S(2)}) collective-permute-start(bf16[192,768]{1,0:T(8,128)(2,1)S(1)} %copy-done.10), channel_id=1, source_target_pairs={{0,2},{1,3},{2,0},{3,1},{4,6},{5,7},{6,4},{7,5},{8,10},{9,11},{10,... | collective-permute-start | bytes 884744 | tf_op jit(solution)/shard_map/ppermute | solution.py:1589
  49.6 60.5 %collective-permute-start.1 = (bf16[3,192,768]{2,1,0:T(8,128)(2,1)S(1)}, bf16[3,192,768]{2,1,0:T(8,128)(2,1)S(1)}, u32[]{:S(2)}, u32[]{:S(2)}) collective-permute-start(bf16[3,192,768]{2,1,0:T(8,128)(2,1)S(1)} %pad_maximum_fusion.refs_2_), channel_id=1, source_target_pairs={{0,2},{1,3},{2,0},{3,1},{4,6},{5,7},{6,4},{7,5},{8,10},{9,11},{10,... | collective-permute-start | bytes 2654216 | tf_op jit(solution)/shard_map/ppermute | solution.py:1589
  51.9 3.0 %copy-start.13 = (s32[16,192]{1,0:T(8,128)}, s32[16,192]{1,0:T(8,128)S(1)}, u32[]{:S(2)}) copy-start(s32[16,192]{1,0:T(8,128)S(1)} %reshape_squeeze.3.qinfo_ref) | copy-start | bytes 36868
  70.4 0.7 copy-start.11
  110.1 0.9 copy-start.4
  132.9 20.7 %collective-permute-start.2 = (bf16[512,768]{1,0:T(8,128)(2,1)}, bf16[512,768]{1,0:T(8,128)(2,1)S(1)}, u32[]{:S(2)}, u32[]{:S(2)}) collective-permute-start(bf16[512,768]{1,0:T(8,128)(2,1)} %get-tuple-element.102), channel_id=1, source_target_pairs={{0,2},{1,3},{2,0},{3,1},{4,6},{5,7},{6,4},{7,5},{8,10},{9,11},{10,... | collective-permute-start | bytes 2359304 | tf_op jit(solution)/shard_map/ppermute | solution.py:1589
  133.2 47.0 %collective-permute-start.3 = (bf16[192,2048]{1,0:T(8,128)(2,1)}, bf16[192,2048]{1,0:T(8,128)(2,1)S(1)}, u32[]{:S(2)}, u32[]{:S(2)}) collective-permute-start(bf16[192,2048]{1,0:T(8,128)(2,1)} %get-tuple-element.107), channel_id=1, source_target_pairs={{0,2},{1,3},{2,0},{3,1},{4,6},{5,7},{6,4},{7,5},{8,10},{9,11},{10,... | collective-permute-start | bytes 2359304 | tf_op jit(solution)/shard_map/ppermute | solution.py:1589
  135.0 50.6 %collective-permute-start.4 = (bf16[192,2048]{1,0:T(8,128)(2,1)}, bf16[192,2048]{1,0:T(8,128)(2,1)}, u32[]{:S(2)}, u32[]{:S(2)}) collective-permute-start(bf16[192,2048]{1,0:T(8,128)(2,1)} %get-tuple-element.109), channel_id=1, source_target_pairs={{0,2},{1,3},{2,0},{3,1},{4,6},{5,7},{6,4},{7,5},{8,10},{9,11},{10,... | collective-permute-start | bytes 2359304 | tf_op jit(solution)/shard_map/ppermute | solution.py:1589
  135.3 18.3 %copy-start.9 = (bf16[512,768]{1,0:T(8,128)(2,1)S(1)}, bf16[512,768]{1,0:T(8,128)(2,1)}, u32[]{:S(2)}) copy-start(bf16[512,768]{1,0:T(8,128)(2,1)} %get-tuple-element.101) | copy-start | bytes 2359300
  153.8 26.5 %copy-start.1 = (bf16[512,768]{1,0:T(8,128)(2,1)}, bf16[512,768]{1,0:T(8,128)(2,1)S(1)}, u32[]{:S(2)}) copy-start(bf16[512,768]{1,0:T(8,128)(2,1)S(1)} %add_convert_fusion.2.refs_2_) | copy-start | bytes 2359300
  153.8 93.3 %collective-permute-start.7 = (bf16[512,768]{1,0:T(8,128)(2,1)S(1)}, bf16[512,768]{1,0:T(8,128)(2,1)S(1)}, u32[]{:S(2)}, u32[]{:S(2)}) collective-permute-start(bf16[512,768]{1,0:T(8,128)(2,1)S(1)} %add_convert_fusion.2.refs_2_), channel_id=1, source_target_pairs={{0,16},{16,0},{1,17},{17,1},{2,18},{18,2},{3,19},{19,3},{4,20},{20... | collective-permute-start | bytes 2359304 | tf_op jit(solution)/shard_map/ppermute | solution.py:1589
  156.5 24.7 %copy-start.7 = (bf16[192,2048]{1,0:T(8,128)(2,1)S(1)}, bf16[192,2048]{1,0:T(8,128)(2,1)}, u32[]{:S(2)}) copy-start(bf16[192,2048]{1,0:T(8,128)(2,1)} %get-tuple-element.106) | copy-start | bytes 2359300
  180.2 5.4 %copy-start.6 = (bf16[192,2048]{1,0:T(8,128)(2,1)S(1)}, bf16[192,2048]{1,0:T(8,128)(2,1)}, u32[]{:S(2)}) copy-start(bf16[192,2048]{1,0:T(8,128)(2,1)} %get-tuple-element.108) | copy-start | bytes 2359300
  180.2 0.9 copy-start.8
  182.5 64.5 %copy-start.2 = (bf16[192,2048]{1,0:T(8,128)(2,1)}, bf16[192,2048]{1,0:T(8,128)(2,1)S(1)}, u32[]{:S(2)}) copy-start(bf16[192,2048]{1,0:T(8,128)(2,1)S(1)} %add_convert_fusion.1.refs_0_) | copy-start | bytes 2359300
  187.0 60.1 %copy-start.3 = (bf16[192,2048]{1,0:T(8,128)(2,1)}, bf16[192,2048]{1,0:T(8,128)(2,1)S(1)}, u32[]{:S(2)}) copy-start(bf16[192,2048]{1,0:T(8,128)(2,1)S(1)} %add_convert_fusion.refs_1_) | copy-start | bytes 2359300
  187.0 60.1 %collective-permute-start.5 = (bf16[192,2048]{1,0:T(8,128)(2,1)S(1)}, bf16[192,2048]{1,0:T(8,128)(2,1)}, u32[]{:S(2)}, u32[]{:S(2)}) collective-permute-start(bf16[192,2048]{1,0:T(8,128)(2,1)S(1)} %add_convert_fusion.1.refs_0_), channel_id=1, source_target_pairs={{0,16},{16,0},{1,17},{17,1},{2,18},{18,2},{3,19},{19,3},{4,20},{20... | collective-permute-start | bytes 2359304 | tf_op jit(solution)/shard_map/ppermute | solution.py:1589
  189.4 57.7 %collective-permute-start.6 = (bf16[192,2048]{1,0:T(8,128)(2,1)S(1)}, bf16[192,2048]{1,0:T(8,128)(2,1)}, u32[]{:S(2)}, u32[]{:S(2)}) collective-permute-start(bf16[192,2048]{1,0:T(8,128)(2,1)S(1)} %add_convert_fusion.refs_1_), channel_id=1, source_target_pairs={{0,16},{16,0},{1,17},{17,1},{2,18},{18,2},{3,19},{19,3},{4,20},{20... | collective-permute-start | bytes 2359304 | tf_op jit(solution)/shard_map/ppermute | solution.py:1589
  247.1 0.9 copy-start.5

commit v6 on v5

--- a/solution.py
+++ b/solution.py
@@ -12,6 +12,7 @@
 CAP = 48
 DOCS = 9
 KEY_BLK = 256
+KEY_BACK = 768
 EX, SH, GR = ("expert", "shard", "group")
 GATHER, GATHER_SUM, SWAP, SWAP_SUM = range(4)
 
@@ -661,6 +662,11 @@
             copy.wait_send()
 
 
+def turned_ids(ids_ref):
+    ids = ids_ref[...].astype(f32)
+    return jnp.transpose(jnp.concatenate([ids] * 4, axis=0)).astype(jnp.int32)
+
+
 def slot_places(ids, lines, slots):
     rows = ids.shape[0]
     lane = lax.broadcasted_iota(jnp.int32, (rows, 128), 1)
@@ -744,7 +750,7 @@
         w_far.start()
         w_near.start()
         w_all[me] = w_ref[...]
-        ids = ids_ref[...]
+        ids = turned_ids(ids_ref)
         place = slot_places(ids, lines, slots)
         for k in range(2):
             place_ref[k] = place[k].astype(bf16)
@@ -762,7 +768,7 @@
         def project(line, x):
             inputs = x.astype(f32)
             inv = lax.rsqrt(jnp.mean(inputs * inputs, axis=1, keepdims=True) + norm_eps)
-            attn_in = (inputs * inv * gain_ref[...]).astype(bf16)
+            attn_in = (inputs * inv * gain_ref[...][None]).astype(bf16)
             attn_ref[line] = attn_in
             value = jnp.dot(
                 attn_in, w_all[...].reshape(model, 3 * width), preferred_element_type=f32
@@ -889,7 +895,7 @@
         land, rows_s = scr
         swaps = start_swap(go, heads_ref, land, EX, False)
         swaps += core_share(go, wo_ref, wof_ref, wo_all)
-        ids = routes_ref[...]
+        ids = turned_ids(routes_ref)
         lane = lax.broadcasted_iota(jnp.int32, (rows, 128), 1)
         hot = [lane == column(ids, k) for k in range(2)]
         place = [place_ref[k].astype(f32) for k in range(2)]
@@ -904,7 +910,7 @@
         )
         resid_ref[...] = resid
         inv = lax.rsqrt(jnp.mean(resid * resid, axis=1, keepdims=True) + norm_eps)
-        moe_in = resid * inv * gain_ref[...]
+        moe_in = resid * inv * gain_ref[...][None]
         small = jnp.dot(moe_in, small_ref[...], preferred_element_type=f32, precision=HIGH)
         chosen = [jnp.sum(jnp.where(h, small, 0.0), axis=1, keepdims=True) for h in hot]
         top = jnp.maximum(chosen[0], chosen[1])
@@ -983,7 +989,7 @@
         upstream = up_ref[...].astype(f32)
         inv = lax.rsqrt(jnp.mean(resid * resid, axis=1, keepdims=True) + norm_eps)
         normed = resid * inv
-        moe_in = normed * gain_ref[...]
+        moe_in = normed * gain_ref[...][None]
         returned = ret_ref[...].reshape(slots, model)
         total = lambda x: jnp.sum(x, axis=1, keepdims=True)
         flag = lambda x: jnp.where(x, 1.0, 0.0)
@@ -1032,7 +1038,7 @@
             + through * upstream
             + jnp.dot(small, st_ref[...], preferred_element_type=f32, precision=HIGH)
         )
-        resid_grad = upstream + rms_back(resid, inv, gain_ref[...], moe_grad)
+        resid_grad = upstream + rms_back(resid, inv, gain_ref[...][None], moe_grad)
         branch = resid_grad.astype(bf16)
         back = contract(branch, wo_ref[...], 1, 1).astype(bf16)
         for line in range(lines):
@@ -1065,7 +1071,7 @@
     return Part([EX], ins, outs, [pltpu.VMEM((lines, rows, width), bf16)], lines - 1, phases)
 
 
-def tail(dkv, dq, attn_in, weights, out_term, packed, hidden, resid_grad, gain):
+def tail(dkv, dq, attn_in, weights, out_term, packed, hidden, resid_grad, gain, pairs):
     lines, rows, width = dq.shape
     model = lines * width
     own = rows // lines
@@ -1079,8 +1085,8 @@
     part_dims = (width, 2 * width, model)
 
     def phases(ins, outs, scr, go):
-        lo_ref, hi_ref, dq_ref, attn_ref, w_ref, o_ref, packed_ref, hid_ref, resid_ref, gain_ref = ins
-        input_ref, q_out, kv_out, out_out, packed_out, gain_out = outs
+        lo_ref, hi_ref, dq_ref, attn_ref, w_ref, o_ref, packed_ref, hid_ref, resid_ref, gain_ref = ins[:10]
+        input_ref, q_out, kv_out, out_out, packed_out, gain_out = outs[:6]
         scr = list(scr)
         take = lambda k: [scr.pop(0) for _ in range(k)]
         lo_scr, hi_scr, q_scr, kvw_scr, o_scr = take(3), take(3), take(3), take(3), take(3)
@@ -1092,7 +1098,7 @@
         gn_l, gn_s, gn_g, gn_0, gn_1, gn_2 = take(6)
         me = lax.axis_index(SH)
 
-        line_me = lax.axis_index(EX)
+        line_me, group_me = lax.axis_index(EX), lax.axis_index(GR)
         kv_trees = [Tree(lo_ref, lo_scr, go), Tree(hi_ref, hi_scr, go)]
 
         def kv_copy(sender, target):
@@ -1120,6 +1126,12 @@
         dq_swap = start_swap(go, dq_ref, dq_all, EX, False)
         o_tree = Tree(o_ref, o_scr, go)
         pk1 = start_swap(go, packed_ref, pk_l, EX, True)
+        wide = []
+        for k in range(len(pairs)):
+            mine, other = outs[6 + 2 * k : 8 + 2 * k]
+            here, there = ins[10 + 2 * k : 12 + 2 * k]
+            mine[...] = (here[...].astype(f32) + there[...].astype(f32)).astype(bf16)
+            wide.append(go(mine, other, GR, lax.rem(group_me + 1, groups)))
 
         def term(rows_ref, out):
             value = contract(attn_ref[...], rows_ref[...].reshape(tok, rows_ref.shape[-1]), 0, 0)
@@ -1181,7 +1193,7 @@
         normed = inputs * inv
         gn_0[...] = jnp.sum(grad * normed, axis=0, keepdims=True)
         gn1 = start_swap(go, gn_0, gn_l, EX, True)
-        input_ref[...] = resid_ref[...] + rms_back(inputs, inv, gain_ref[...], grad)
+        input_ref[...] = resid_ref[...] + rms_back(inputs, inv, gain_ref[...][None], grad)
         swaps = [None] * 3
         for k, copies in ((2, o_lines), (0, q_lines)):
             for copy in copies:
@@ -1213,6 +1225,8 @@
         for copy in gn3:
             copy.wait()
         gain_out[...] = total_of(gn_g, groups)
+        for copy in wide:
+            copy.wait()
         for tree in (*kv_trees, o_tree, q_tree, kvw_tree):
             tree.close()
         yield
@@ -1235,7 +1249,7 @@
     scratch += [vmem((n,) + packed.shape, f32) for n in (lines, 4, groups)]
     scratch += [vmem(packed.shape, f32)] * 2
     scratch += [vmem((n, 1, model), f32) for n in (lines, 4, groups)] + [vmem((1, model), f32)] * 3
-    copies = 5 * Tree.copies + 6 * (lines - 1) + 2 * 3 + 5 * (groups - 1)
+    copies = len(pairs) + 5 * Tree.copies + 6 * (lines - 1) + 2 * 3 + 5 * (groups - 1)
     outs = [
         shape((rows, model), f32),
         shape((lines, own, width), f32),
@@ -1243,8 +1257,9 @@
         shape((own, model), f32),
         shape(packed.shape, f32),
         shape((1, model), f32),
-    ]
+    ] + [shape(x.shape, bf16) for pair in pairs for x in pair]
     ins = [*dkv, dq, attn_in, weights, out_term, packed, hidden, resid_grad, gain]
+    ins += [x for pair in pairs for x in pair]
     return Part([EX, SH, GR], ins, outs, scratch, copies, phases)
 
 
@@ -1433,7 +1448,7 @@
 def attend_back_body(lines, heads, info_ref, q_ref, kv_ref, qinfo_ref, o_ref, lse_ref, back_ref, dq_ref, dkv_lo, dkv_hi, k_s, v_s, dk_s, dv_s, dq_s, qm_s, bm_s, delta_s):
     shard = lax.axis_index(SH)
     rows, width = q_ref.shape[1:]
-    key_blk = KEY_BLK
+    key_blk = KEY_BACK
     blocks = k_s.shape[0] // key_blk
     prompt = info_ref[1]
 
@@ -1551,9 +1566,8 @@
         small = small_ref[...]
         mgain_out[...] = jnp.sum(small[0:1], axis=0)
         vec_out[...] = small[1:3]
-        turned = jnp.transpose(small)
-        rout_out[...] = turned[:, 3 : 3 + n_ids]
-        mix_out[...] = turned[:, 3 + n_ids : 7 + n_ids]
+        rout_out[...] = small[3 : 3 + n_ids]
+        mix_out[...] = small[3 + n_ids : 7 + n_ids]
 
 
 def finale(mine, far, input_grad, layer_out, sums, n_ids):
@@ -1571,7 +1585,7 @@
 
     wide = [tiled(mine[0].shape, 1), tiled(mine[1].shape, 1), tiled(mine[2].shape, 0)]
     rows = [tiled(input_grad.shape, 0), tiled(layer_out.shape, 0)]
-    small = [(own, model)] * 4 + [(model,), (model,), (2, model), (model, n_ids), (model, 4)]
+    small = [(own, model)] * 4 + [(model,), (model,), (2, model), (n_ids, model), (4, model)]
     return pl.pallas_call(
         functools.partial(finale_body, lines, n_ids),
         grid=(steps,),
@@ -1618,7 +1632,7 @@
     w_mine = lax.dynamic_slice_in_dim(w_qkv, line * width, width, axis=2)
     w_mine = jnp.concatenate([w_mine[1], w_mine[2], w_mine[0]], axis=1)
     attn_in, q, kv_all, place, recv_grads = front(
-        hidden_in, w_mine, attn_gain[None], routes, out_grad
+        hidden_in, w_mine, attn_gain, routes.T, out_grad
     )
     attn_in = attn_in.reshape(lines * rows, model)
     kv_all, w_out_b, w_qkv = lax.optimization_barrier((kv_all, w_out, w_qkv))
@@ -1637,11 +1651,11 @@
     small_w = jnp.pad(
         jnp.concatenate([w_router, const_mix], axis=1), ((0, 0), (0, 124 - n_ids))
     )
-    gain_two = moe_gain[None]
+    gain_two = moe_gain
     recv_rows, wo_full, resid_one, table, attn_low = run_parts(
         [
             route(
-                attn_heads, hidden_in, gain_two, small_w, routes, place, w_out[None], wo_far[None], n_ids
+                attn_heads, hidden_in, gain_two, small_w, routes.T, place, w_out[None], wo_far[None], n_ids
             )
         ],
         2,
@@ -1665,7 +1679,7 @@
     )
     weights = weights.reshape(3, model, model)
     far = [swap(there, SH, lambda i: i ^ 2) for there in sums[1::2]]
-    mine = [(x.astype(f32) + y.astype(f32)).astype(bf16) for x, y in zip(sums[0::2], far)]
+    down = (sums[4].astype(f32) + far[2].astype(f32)).astype(bf16)
 
     back_heads, layer_out, resid_grad, out_term, packed = run_parts(
         [
@@ -1676,16 +1690,15 @@
         5,
         "to_heads",
     )
-    back_heads, mine[2] = lax.optimization_barrier((back_heads, mine[2]))
+    back_heads, down = lax.optimization_barrier((back_heads, down))
     cross = lambda x: swap(x, GR, lambda i: 1 - i)
-    down_far = cross(mine[2])
+    down_far = cross(down)
     dq, *dkv = attend_back(info, q, kv_all, qinfo, attn_vec, lse, back_heads)
-    *dkv, mine[0], mine[1] = lax.optimization_barrier((*dkv, *mine[:2]))
-    group_far = [cross(mine[0]), cross(mine[1]), down_far]
-    input_grad, *sums = run_parts(
+    pairs = [(sums[0], far[0]), (sums[2], far[1])]
+    input_grad, *parts = run_parts(
         [
             tail(
-                dkv, dq, attn_in, weights, out_term, packed, hidden_in, resid_grad, attn_gain[None]
+                dkv, dq, attn_in, weights, out_term, packed, hidden_in, resid_grad, attn_gain, pairs
             )
         ],
         6,
@@ -1693,7 +1706,12 @@
         pl.CostEstimate(flops=2 * 10**10, bytes_accessed=10**8, transcendentals=0),
     )
     gate, up, down, input_grad, layer_out, *grads, gain, gain_two, vecs, router, mix = finale(
-        mine, group_far, input_grad, layer_out, sums, n_ids
+        [parts[5], parts[7], down],
+        [parts[6], parts[8], down_far],
+        input_grad,
+        layer_out,
+        parts[:5],
+        n_ids,
     )
     return (
         layer_out,
@@ -1701,8 +1719,8 @@
         gain,
         *grads,
         gain_two,
-        router,
-        mix,
+        router.T,
+        mix.T,
         vecs,
         gate[None],
         up[None],

time: 260 us -> 250 us (0.962)
  local copies, waits for them, and re-layouts: 12 us -> 4.32 us
  other arithmetic: 7.27 us -> 4.52 us
    unnamed x38 -> x25, local copies, waits for them, and re-layouts: 8.85 us -> 3.05 us
    convert_element_type x3 -> x1, other arithmetic: 2.97 us -> 0.18 us  [fast_shards(): down = (sums[4].astype(f32) + far[2].astype(f32)).astype(bf16)]
    ppermute x8 -> x6, starting transfers between devices: 9.59 us -> 8.24 us  [swap(): lax.ppermute(x, axis, [(i, partner(i)) for i in range(lax.axis_size(axis))])]
  transfers between devices with their start and end apart: 8 -> 6, of which waited for: 2 -> 1; matrix products, arithmetic and copies ran while one was open for 3% -> 2% of each run, Pallas kernels for 59% -> 63%
where the time goes in v6:
time: 250 us; the launch traced here: 248 us
  Pallas kernels  227 us (91%)
  starting transfers between devices  8.24 us (3%)
  other arithmetic  4.52 us (2%)
  local copies, waits for them, and re-layouts  4.32 us (2%)
  waiting for transfers between devices  2.7 us (1%)
    pallas_call x4, Pallas kernels, run_parts(): pl.pallas_call(body, out_shape=outs, in_specs=sum([p.specs for p in parts...  124 us
    pallas_call x1, Pallas kernels, front(): pl.pallas_call(body, out_shape=[shape((lines, rows, model), bf16), shape(...  42.6 us
    pallas_call x1, Pallas kernels, attend_back(): pl.pallas_call(functools.partial(attend_back_body, lines, heads), out_sha...  24.6 us
    pallas_call x1, Pallas kernels, attend(): pl.pallas_call(functools.partial(attend_body, lines, heads), out_shape=[s...  15.5 us
    pallas_call x1, Pallas kernels, expert(): pl.pallas_call(functools.partial(expert_body, steps), grid=(steps,), out_...  13.3 us
    ppermute x6, starting transfers between devices, swap(): lax.ppermute(x, axis, [(i, partner(i)) for i in range(lax.axis_size(axis))])  8.24 us
    pallas_call x1, Pallas kernels, finale(): pl.pallas_call(functools.partial(finale_body, lines, n_ids), grid=(steps,...  6.48 us
  transfers between devices with their start and end apart: 6, of which 1 were waited for; matrix products, arithmetic and copies ran while one was open for 2% of the time, Pallas kernels for 63%

profile of v6, /device:TPU:0, one launch (start us, length us, event | category | flops | bytes accessed | tf_op | source)
XLA Modules:
  0.0 247.5 jit_solution(14900765617996563352)
XLA Ops:
  0.7 0.0 copy-start.5
  0.7 0.0 copy-start.7
  0.7 0.0 copy-start.9
  0.7 0.0 copy-start.10
  0.7 1.3 pad_maximum_fusion.refs_2_
  2.0 0.0 copy-start
  2.0 0.2 dynamic-slice_bitcast_fusion.2
  2.2 0.8 pad_maximum_fusion.1.w_ref
  3.0 42.6 %front.1 = (bf16[4,192,768]{2,1,0:T(8,128)(2,1)}, bf16[4,192,192]{2,1,0:T(8,128)(2,1)}, bf16[4,4,192,384]{3,2,1,0:T(8,128)(2,1)}, bf16[2,192,192]{2,1,0:T(8,128)(2,1)}, bf16[4,48,768]{2,1,0:T(8,128)(2,1)}) custom-call(bf16[192,768]{1,0:T(8,128)(2,1)} %refs_7_.3, bf16[192,576]{1,0:T(8,128)(2,1)} %pad_maximum_fusion.1.w_ref, f32[768]{0:T(1024)} %refs_9_.3, ...), custom_call_target="tpu_custom_call" | custom-call | tf_op jit(solution)/shard_map/front/pallas_call | solution.py:851
  45.6 0.0 copy-done.5
  45.7 1.2 collective-permute-start
  46.9 0.9 collective-permute-start.1
  47.7 0.0 copy-done.7
  47.7 0.1 convert_reduce_fusion
  47.9 0.5 broadcast.16
  48.4 0.7 reduce.5
  49.1 0.1 reshape_squeeze.3.qinfo_ref
  49.2 0.0 copy-done.9
  49.2 0.0 copy-done.10
  49.2 0.0 copy-start.8
  49.2 0.8 fusion
  50.0 0.1 slice_reduce_fusion
  50.1 0.9 copy.32.refs_3_
  51.0 0.0 copy-done
  51.0 0.6 pad_add_fusion.info_ref
  51.6 0.0 copy-done.8
  51.6 15.5 %attend.1 = (f32[4,192,192]{2,1,0:T(8,128)}, bf16[4,192,192]{2,1,0:T(8,128)(2,1)}, f32[4,8,192]{2,1,0:T(8,128)}) custom-call(s32[25]{0:T(128)} %pad_add_fusion.info_ref, bf16[4,192,192]{2,1,0:T(8,128)(2,1)} %get-tuple-element.78.q_ref, bf16[3072,384]{1,0:T(8,128)(2,1)} %bitcast.46, s32[16,192]{1,0:T(8,128)} %copy-done.8), custom_call_target="tpu_custom_call" | custom-call | flops 2000000000 | bytes 8000000 | tf_op jit(solution)/shard_map/attend/pallas_call | solution.py:1427
  67.1 0.0 collective-permute-done
  67.1 0.0 copy-start.6
  67.1 0.7 copy-done.6
  67.9 25.1 %route.1 = (bf16[4,48,896]{2,1,0:T(8,128)(2,1)}, bf16[1,4,192,768]{3,2,1,0:T(8,128)(2,1)}, f32[192,768]{1,0:T(8,128)}, f32[192,128]{1,0:T(8,128)}, bf16[192,768]{1,0:T(8,128)(2,1)}) custom-call(bf16[4,192,192]{2,1,0:T(8,128)(2,1)} %get-tuple-element.83.refs_0_, bf16[192,768]{1,0:T(8,128)(2,1)} %refs_7_.3, f32[768]{0:T(1024)} %refs_7_.2, ...), custom_call_target="tpu_custom_call" | custom-call | tf_op jit(solution)/shard_map/route/pallas_call | solution.py:529
  93.0 13.3 %ffn.1 = (bf16[192,768]{1,0:T(8,128)(2,1)}, bf16[192,768]{1,0:T(8,128)(2,1)}, bf16[4,192,2048]{2,1,0:T(8,128)(2,1)}, bf16[4,192,2048]{2,1,0:T(8,128)(2,1)}, bf16[4,512,768]{2,1,0:T(8,128)(2,1)}) custom-call(bf16[192,896]{1,0:T(8,128)(2,1)} %bitcast.52, bf16[192,768]{1,0:T(8,128)(2,1)} %bitcast.53, bf16[768,2048]{1,0:T(8,128)(2,1)} %bitcast.43, ...), custom_call_target="tpu_custom_call" | custom-call | flops 6000000000 | bytes 20000000 | tf_op jit(solution)/shard_map/ffn/pallas_call | solution.py:1317
  106.3 0.0 collective-permute-done.1.refs_3_
  106.3 0.0 copy-start.2
  106.3 0.9 copy-done.2
  107.2 20.5 %combine.1 = (bf16[4,48,768]{2,1,0:T(8,128)(2,1)}, bf16[4,48,768]{2,1,0:T(8,128)(2,1)}, bf16[3,4,192,768]{3,2,1,0:T(8,128)(2,1)}, bf16[192,2048]{1,0:T(8,128)(2,...) custom-call(bf16[4,48,768]{2,1,0:T(8,128)(2,1)} %bitcast.32, ...), custom_call_target="tpu_custom_call" | custom-call | tf_op jit(solution)/shard_map/combine/pallas_call | solution.py:529
  127.7 1.1 collective-permute-start.2
  128.8 1.0 collective-permute-start.3
  129.8 1.1 collective-permute-start.4
  130.8 0.0 copy-start.4
  130.8 18.1 %to_heads.1 = (bf16[4,192,192]{2,1,0:T(8,128)(2,1)}, bf16[192,768]{1,0:T(8,128)(2,1)}, f32[192,768]{1,0:T(8,128)}, bf16[4,4,48,768]{3,2,1,0:T(8,128)(2,1)}, f32[16,768]{1,0:T(8,128)}) custom-call(bf16[4,48,768]{2,1,0:T(8,128)(2,1)} %get-tuple-element.94.refs_0_, bf16[4,48,768]{2,1,0:T(8,128)(2,1)} %get-tuple-element.95.refs_1_, ...), custom_call_target="tpu_custom_call" | custom-call | tf_op jit(solution)/shard_map/to_heads/pallas_call | solution.py:529
  149.0 0.0 collective-permute-done.2
  149.0 0.0 copy-done.4
  149.0 0.2 add_convert_fusion.refs_2_
  149.2 0.0 copy-start.1
  149.2 3.0 %collective-permute-start.5 = (bf16[512,768]{1,0:T(8,128)(2,1)S(1)}, bf16[512,768]{1,0:T(8,128)(2,1)S(1)}, u32[]{:S(2)}, u32[]{:S(2)}) collective-permute-start(bf16[512,768]{1,0:T(8,128)(2,1)S(1)} %add_convert_fusion.refs_2_), channel_id=1, source_target_pairs={{0,16},{16,0},{1,17},{17,1},{2,18},{18,2},{3,19},{19,3},{4,20},{20... | collective-permute-start | bytes 2359304 | tf_op jit(solution)/shard_map/ppermute | solution.py:1603
  152.2 24.6 %attend_back.1 = (bf16[4,192,192]{2,1,0:T(8,128)(2,1)}, bf16[4,2,192,384]{3,2,1,0:T(8,128)(2,1)}, bf16[4,2,192,384]{3,2,1,0:T(8,128)(2,1)}) custom-call(s32[25]{0:T(128)} %pad_add_fusion.info_ref, bf16[4,192,192]{2,1,0:T(8,128)(2,1)} %get-tuple-element.78.q_ref, bf16[3072,384]{1,0:T(8,128)(2,1)} %bitcast.47, s32[16,192]{1,0:T(8,128)} %copy-done.8, ...), custom_call_target="tpu_custom_call" | custom-call | flops 5000000000 | bytes 12000000 | tf_op jit(solution)/shard_map/attend_back/pallas_call | solution.py:1523
  176.8 0.0 copy-done.1
  176.8 0.0 collective-permute-done.3.refs_11_
  176.8 0.0 copy-start.11
  176.8 2.7 %collective-permute-done.4.refs_13_ = bf16[192,2048]{1,0:T(8,128)(2,1)} collective-permute-done((bf16[192,2048]{1,0:T(8,128)(2,1)}, bf16[192,2048]{1,0:T(8,128)(2,1)}, u32[]{:S(2)}, u32[]{:S(2)}) %collective-permute-start.4) | collective-permute-done | bytes 786464 | tf_op jit(solution)/shard_map/ppermute | solution.py:1603
  179.5 0.0 copy-done.11
  179.5 60.5 %tail.1 = (f32[192,768]{1,0:T(8,128)}, f32[4,48,192]{2,1,0:T(8,128)}, f32[4,48,384]{2,1,0:T(8,128)}, f32[48,768]{1,0:T(8,128)}, f32[16,768]{1,0:T(8,128)}, /*ind...) custom-call(bf16[4,2,192,384]{3,2,1,0:T(8,128)(2,1)} %get-tuple-elem, ...), custom_call_target="tpu_custom_call" | custom-call | flops 20000000000 | bytes 100000000 | tf_op jit(solution)/shard_map/tail/pallas_call | solution.py:529
  240.0 0.0 collective-permute-done.5.refs_5_
  240.0 0.0 copy-start.3
  240.0 0.9 copy-done.3
  240.9 6.5 %finale.1 = (f32[192,2048]{1,0:T(8,128)}, f32[192,2048]{1,0:T(8,128)}, f32[512,768]{1,0:T(8,128)}, f32[192,768]{1,0:T(8,128)}, bf16[192,768]{1,0:T(8,128)(2,1)},...) custom-call(bf16[192,2048]{1,0:T(8,128)(2,1)} %get-tuple-element.116, ...), custom_call_target="tpu_custom_call" | custom-call | flops 10000000 | bytes 10000000 | tf_op jit(solution)/shard_map/finale/pallas_call | solution.py:1589
Async XLA Ops:
  0.7 45.0 %copy-start.5 = (bf16[192,768]{1,0:T(8,128)(2,1)S(1)}, bf16[192,768]{1,0:T(8,128)(2,1)}, u32[]{:S(2)}) copy-start(bf16[192,768]{1,0:T(8,128)(2,1)} %param.23) | copy-start | bytes 884740
  0.7 47.1 %copy-start.7 = (s32[1,3072]{1,0:T(1,128)S(1)}, s32[1,3072]{1,0:T(1,128)}, u32[]{:S(2)}) copy-start(s32[1,3072]{1,0:T(1,128)} %param.17) | copy-start | bytes 36868
  0.7 48.5 %copy-start.9 = (f32[768,8]{0,1:T(8,128)S(1)}, f32[768,8]{0,1:T(8,128)}, u32[]{:S(2)}) copy-start(f32[768,8]{0,1:T(8,128)} %param.25) | copy-start | bytes 73732
  0.7 48.5 %copy-start.10 = (f32[768,4]{0,1:T(4,128)S(1)}, f32[768,4]{0,1:T(4,128)}, u32[]{:S(2)}) copy-start(f32[768,4]{0,1:T(4,128)} %param.26) | copy-start | bytes 36868
  2.0 49.0 %copy-start = (bf16[3,192,768]{2,1,0:T(8,128)(2,1)}, bf16[3,192,768]{2,1,0:T(8,128)(2,1)S(1)}, u32[]{:S(2)}) copy-start(bf16[3,192,768]{2,1,0:T(8,128)(2,1)S(1)} %pad_maximum_fusion.refs_2_) | copy-start | bytes 2654212
  45.7 21.5 %collective-permute-start = (bf16[192,768]{1,0:T(8,128)(2,1)S(1)}, bf16[192,768]{1,0:T(8,128)(2,1)S(1)}, u32[]{:S(2)}, u32[]{:S(2)}) collective-permute-start(bf16[192,768]{1,0:T(8,128)(2,1)S(1)} %copy-done.5), channel_id=1, source_target_pairs={{0,2},{1,3},{2,0},{3,1},{4,6},{5,7},{6,4},{7,5},{8,10},{9,11},{10,... | collective-permute-start | bytes 884744 | tf_op jit(solution)/shard_map/ppermute | solution.py:1603
  46.9 59.4 %collective-permute-start.1 = (bf16[3,192,768]{2,1,0:T(8,128)(2,1)S(1)}, bf16[3,192,768]{2,1,0:T(8,128)(2,1)S(1)}, u32[]{:S(2)}, u32[]{:S(2)}) collective-permute-start(bf16[3,192,768]{2,1,0:T(8,128)(2,1)S(1)} %pad_maximum_fusion.refs_2_), channel_id=1, source_target_pairs={{0,2},{1,3},{2,0},{3,1},{4,6},{5,7},{6,4},{7,5},{8,10},{9,11},{10,... | collective-permute-start | bytes 2654216 | tf_op jit(solution)/shard_map/ppermute | solution.py:1603
  49.2 2.4 copy-start.8
  67.1 0.7 copy-start.6
  106.3 0.9 copy-start.2
  127.7 21.3 %collective-permute-start.2 = (bf16[512,768]{1,0:T(8,128)(2,1)}, bf16[512,768]{1,0:T(8,128)(2,1)S(1)}, u32[]{:S(2)}, u32[]{:S(2)}) collective-permute-start(bf16[512,768]{1,0:T(8,128)(2,1)} %get-tuple-element.102), channel_id=1, source_target_pairs={{0,2},{1,3},{2,0},{3,1},{4,6},{5,7},{6,4},{7,5},{8,10},{9,11},{10,... | collective-permute-start | bytes 2359304 | tf_op jit(solution)/shard_map/ppermute | solution.py:1603
  128.8 48.0 %collective-permute-start.3 = (bf16[192,2048]{1,0:T(8,128)(2,1)}, bf16[192,2048]{1,0:T(8,128)(2,1)S(1)}, u32[]{:S(2)}, u32[]{:S(2)}) collective-permute-start(bf16[192,2048]{1,0:T(8,128)(2,1)} %get-tuple-element.113), channel_id=1, source_target_pairs={{0,2},{1,3},{2,0},{3,1},{4,6},{5,7},{6,4},{7,5},{8,10},{9,11},{10,... | collective-permute-start | bytes 2359304 | tf_op jit(solution)/shard_map/ppermute | solution.py:1603
  129.8 49.7 %collective-permute-start.4 = (bf16[192,2048]{1,0:T(8,128)(2,1)}, bf16[192,2048]{1,0:T(8,128)(2,1)}, u32[]{:S(2)}, u32[]{:S(2)}) collective-permute-start(bf16[192,2048]{1,0:T(8,128)(2,1)} %get-tuple-element.115), channel_id=1, source_target_pairs={{0,2},{1,3},{2,0},{3,1},{4,6},{5,7},{6,4},{7,5},{8,10},{9,11},{10,... | collective-permute-start | bytes 2359304 | tf_op jit(solution)/shard_map/ppermute | solution.py:1603
  130.8 18.1 %copy-start.4 = (bf16[512,768]{1,0:T(8,128)(2,1)S(1)}, bf16[512,768]{1,0:T(8,128)(2,1)}, u32[]{:S(2)}) copy-start(bf16[512,768]{1,0:T(8,128)(2,1)} %get-tuple-element.101) | copy-start | bytes 2359300
  149.2 27.6 %copy-start.1 = (bf16[512,768]{1,0:T(8,128)(2,1)}, bf16[512,768]{1,0:T(8,128)(2,1)S(1)}, u32[]{:S(2)}) copy-start(bf16[512,768]{1,0:T(8,128)(2,1)S(1)} %add_convert_fusion.refs_2_) | copy-start | bytes 2359300
  149.2 90.8 %collective-permute-start.5 = (bf16[512,768]{1,0:T(8,128)(2,1)S(1)}, bf16[512,768]{1,0:T(8,128)(2,1)S(1)}, u32[]{:S(2)}, u32[]{:S(2)}) collective-permute-start(bf16[512,768]{1,0:T(8,128)(2,1)S(1)} %add_convert_fusion.refs_2_), channel_id=1, source_target_pairs={{0,16},{16,0},{1,17},{17,1},{2,18},{18,2},{3,19},{19,3},{4,20},{20... | collective-permute-start | bytes 2359304 | tf_op jit(solution)/shard_map/ppermute | solution.py:1603
  176.8 2.7 %copy-start.11 = (bf16[192,2048]{1,0:T(8,128)(2,1)}, bf16[192,2048]{1,0:T(8,128)(2,1)S(1)}, u32[]{:S(2)}) copy-start(bf16[192,2048]{1,0:T(8,128)(2,1)S(1)} %collective-permute-done.3.refs_11_) | copy-start | bytes 2359300
  240.0 0.9 copy-start.3

commit v7 on v6

--- a/solution.py
+++ b/solution.py
@@ -687,7 +687,7 @@
     return place
 
 
-def front(hidden, w_mine, gain, routes, out_grad):
+def front(hidden, w_mine, gain, routes, out_grad, docs):
     rows, model = hidden.shape
     lines = lax.axis_size(EX)
     width = model // lines
@@ -696,7 +696,7 @@
 
     slots = lines * CAP
 
-    def body(hid_ref, w_ref, gain_ref, ids_ref, up_ref, attn_ref, q_ref, kv_ref, place_ref, rows_out, land, w_all, kv_own, rows_s, sems):
+    def body(hid_ref, w_ref, gain_ref, ids_ref, up_ref, docs_ref, attn_ref, q_ref, kv_ref, place_ref, rows_out, info_ref, land, w_all, kv_own, rows_s, sems):
         line_me = lax.axis_index(EX)
         me, _, _, near, far = shard_peers()
         left, right = jnp.maximum(line_me - 1, 0), jnp.minimum(line_me + 1, last)
@@ -750,6 +750,14 @@
         w_far.start()
         w_near.start()
         w_all[me] = w_ref[...]
+        docs = docs_ref[...]
+        lane = lax.broadcasted_iota(jnp.int32, (docs.shape[0], 128), 1)
+        block = lax.broadcasted_iota(jnp.int32, (docs.shape[0], 128), 0)
+        table = jnp.where(lane == DOCS + block, jnp.broadcast_to(docs[:, 0:1], lane.shape), 0)
+        for doc in range(1, DOCS):
+            before = jnp.sum(jnp.where(docs < doc, 1, 0), axis=1, keepdims=True)
+            table = table + jnp.where(lane == doc, jnp.broadcast_to(before, lane.shape), 0)
+        info_ref[...] = jnp.sum(table, axis=0, keepdims=True)
         ids = turned_ids(ids_ref)
         place = slot_places(ids, lines, slots)
         for k in range(2):
@@ -856,9 +864,10 @@
             shape((lines, 4, rows, 2 * width), bf16),
             shape((2, rows, slots), bf16),
             shape((lines, CAP, model), bf16),
+            shape((1, 128), jnp.int32),
         ],
-        in_specs=[VM] * 5,
-        out_specs=[VM] * 5,
+        in_specs=[VM] * 6,
+        out_specs=[VM] * 6,
         scratch_shapes=[
             pltpu.VMEM((lines, rows, model), bf16),
             pltpu.VMEM((4, rows, 3 * width), bf16),
@@ -868,7 +877,7 @@
         ],
         compiler_params=pltpu.CompilerParams(collective_id=0, has_side_effects=True),
         name="front",
-    )(hidden, w_mine, gain, routes, out_grad)
+    )(hidden, w_mine, gain, routes, out_grad, docs)
 
 
 def column(x, k):
@@ -911,7 +920,7 @@
         resid_ref[...] = resid
         inv = lax.rsqrt(jnp.mean(resid * resid, axis=1, keepdims=True) + norm_eps)
         moe_in = resid * inv * gain_ref[...][None]
-        small = jnp.dot(moe_in, small_ref[...], preferred_element_type=f32, precision=HIGH)
+        small = contract(moe_in, small_ref[...], 1, 1, HIGH)
         chosen = [jnp.sum(jnp.where(h, small, 0.0), axis=1, keepdims=True) for h in hot]
         top = jnp.maximum(chosen[0], chosen[1])
         powers = [jnp.exp(c - top) for c in chosen]
@@ -1091,7 +1100,15 @@
         take = lambda k: [scr.pop(0) for _ in range(k)]
         lo_scr, hi_scr, q_scr, kvw_scr, o_scr = take(3), take(3), take(3), take(3), take(3)
         own_kv, q_t, kv_t, dq_all, dkv_all, dq_full = take(6)
-        kv_sems = take(1)[0]
+        kv_sems, w_s, w_sem = take(3)
+        held = take(2 * len(pairs))
+        w_copy = pltpu.make_async_copy(w_ref, w_s, w_sem.at[2 * len(pairs)])
+        fetch = [
+            pltpu.make_async_copy(ins[10 + k], held[k], w_sem.at[k]) for k in range(2 * len(pairs))
+        ]
+        for copy in fetch:
+            copy.start()
+        w_copy.start()
         sums, lands, halves, gots = take(3), take(3), take(3), take(3)
         pk_l, pk_s, pk_g = take(3)
         mid_l, mid_s = take(2)
@@ -1126,13 +1143,6 @@
         dq_swap = start_swap(go, dq_ref, dq_all, EX, False)
         o_tree = Tree(o_ref, o_scr, go)
         pk1 = start_swap(go, packed_ref, pk_l, EX, True)
-        wide = []
-        for k in range(len(pairs)):
-            mine, other = outs[6 + 2 * k : 8 + 2 * k]
-            here, there = ins[10 + 2 * k : 12 + 2 * k]
-            mine[...] = (here[...].astype(f32) + there[...].astype(f32)).astype(bf16)
-            wide.append(go(mine, other, GR, lax.rem(group_me + 1, groups)))
-
         def term(rows_ref, out):
             value = contract(attn_ref[...], rows_ref[...].reshape(tok, rows_ref.shape[-1]), 0, 0)
             value = value.astype(bf16)
@@ -1143,6 +1153,14 @@
 
         for tree in kv_trees:
             tree.across()
+        wide = []
+        for k in range(len(pairs)):
+            mine, other = outs[6 + 2 * k : 8 + 2 * k]
+            here, there = held[2 * k : 2 * k + 2]
+            fetch[2 * k].wait()
+            fetch[2 * k + 1].wait()
+            mine[...] = (here[...].astype(f32) + there[...].astype(f32)).astype(bf16)
+            wide.append(go(mine, other, GR, lax.rem(group_me + 1, groups)))
         term(dq_ref, q_t)
         o_tree.across()
         q_tree = Tree(q_t, q_scr, go)
@@ -1169,7 +1187,8 @@
             copy.wait()
         for line in range(lines):
             dq_full[:, line * width : (line + 1) * width] = dq_all[line]
-        grad = contract(dq_full[...], w_ref[0], 1, 1)
+        w_copy.wait()
+        grad = contract(dq_full[...], w_s[0], 1, 1)
         for copy in pk2:
             copy.wait()
         mid_s[...] = total_of(pk_s, 4)
@@ -1187,7 +1206,7 @@
                 dq_full[:, line * width : (line + 1) * width] = dkv_all[
                     line, :, half * width : (half + 1) * width
                 ]
-            grad = grad + contract(dq_full[...], w_ref[1 + half], 1, 1)
+            grad = grad + contract(dq_full[...], w_s[1 + half], 1, 1)
         inputs = hid_ref[...].astype(f32)
         inv = lax.rsqrt(jnp.mean(inputs * inputs, axis=1, keepdims=True) + norm_eps)
         normed = inputs * inv
@@ -1243,7 +1262,10 @@
         vmem((lines, rows, 2 * width), bf16),
         vmem((rows, model), bf16),
         pltpu.SemaphoreType.DMA((2, lines)),
+        vmem(weights.shape, bf16),
+        pltpu.SemaphoreType.DMA((2 * len(pairs) + 1,)),
     ]
+    scratch += [vmem(x.shape, bf16) for pair in pairs for x in pair]
     scratch += [vmem(p, bf16) for p in pieces] + [vmem(p, bf16) for p in pieces]
     scratch += [vmem(p, bf16) for p in got_pieces] + [vmem((groups,) + p, bf16) for p in got_pieces]
     scratch += [vmem((n,) + packed.shape, f32) for n in (lines, 4, groups)]
@@ -1260,10 +1282,12 @@
     ] + [shape(x.shape, bf16) for pair in pairs for x in pair]
     ins = [*dkv, dq, attn_in, weights, out_term, packed, hidden, resid_grad, gain]
     ins += [x for pair in pairs for x in pair]
-    return Part([EX, SH, GR], ins, outs, scratch, copies, phases)
-
-
-def expert_body(steps, x_ref, g_ref, wg_ref, wu_ref, wd_ref, eo_ref, ib_ref, ga_ref, up_ref, d_ref, eo_s, ib_s, g_s):
+    hbm = pl.BlockSpec(memory_space=pl.ANY)
+    specs = [hbm if x is weights or k >= 10 else VM for k, x in enumerate(ins)]
+    return Part([EX, SH, GR], ins, outs, scratch, copies, phases, specs)
+
+
+def expert_body(steps, x_ref, g_ref, wg_ref, wu_ref, wd_ref, eo_ref, ib_ref, ga_ref, up_ref, d_ref, eo_s, ib_s, g_s, xt_s):
     i = pl.program_id(0)
     me, side, core, _, _ = shard_peers()
 
@@ -1275,6 +1299,7 @@
         high, low = x_ref[:, model : model + 1], x_ref[:, model + 1 : model + 2]
         gate = high.astype(f32) + low.astype(f32)
         g_s[...] = (g_ref[...].astype(f32) * gate).astype(bf16)
+        xt_s[...] = jnp.transpose(x_ref[:, :model])
 
     x, g = x_ref[:, : g_ref.shape[1]], g_s[...]
     wg, wu, wd = wg_ref[...], wu_ref[...], wd_ref[...]
@@ -1295,7 +1320,7 @@
 
     rows = ga_ref.shape[1]
     for ref, back in ((ga_ref, gate_back), (up_ref, up_back)):
-        term = contract(x, back, 0, 0).astype(bf16)
+        term = jnp.dot(xt_s[...], back, preferred_element_type=f32).astype(bf16)
         for quarter in range(4):
             ref[place(jnp.int32(quarter))] = term[quarter * rows : (quarter + 1) * rows]
     d_ref[place(i)] = contract(act, g, 0, 0).astype(bf16)
@@ -1338,7 +1363,7 @@
             pl.BlockSpec((4, quarter, tile), lambda i: (0, 0, i)),
             whole((4, tile, model)),
         ],
-        scratch_shapes=[pltpu.VMEM((slots, model), f32)] * 2 + [pltpu.VMEM((slots, model), bf16)],
+        scratch_shapes=[pltpu.VMEM((slots, model), f32)] * 2 + [pltpu.VMEM((slots, model), bf16), pltpu.VMEM((model, slots), bf16)],
         cost_estimate=pl.CostEstimate(flops=6 * 10**9, bytes_accessed=2 * 10**7, transcendentals=4 * 10**5),
         name="ffn",
     )(x, g, wg, wu, wd)
@@ -1357,8 +1382,8 @@
     docs = qinfo_ref[pl.ds(block, 1), :]
     starts = jnp.zeros(docs.shape, jnp.int32)
     for doc in range(1, DOCS):
-        starts = jnp.where(docs == doc, info_ref[doc], starts)
-    return starts, info_ref[info_ref[DOCS + block]]
+        starts = jnp.where(docs == doc, info_ref[0, doc], starts)
+    return starts, info_ref[0, info_ref[0, DOCS + block]]
 
 
 def attend_body(lines, heads, info_ref, q_ref, kv_ref, qinfo_ref, o_ref, low_ref, lse_ref, k_s, vt_s, acc_s, ml_s, qm_s):
@@ -1366,7 +1391,7 @@
     rows, width = q_ref.shape[1:]
     blocks = vt_s.shape[0]
     key_blk = vt_s.shape[2]
-    prompt = info_ref[1]
+    prompt = info_ref[0, 1]
 
     @pl.loop(0, blocks)
     def _(j):
@@ -1450,7 +1475,7 @@
     rows, width = q_ref.shape[1:]
     key_blk = KEY_BACK
     blocks = k_s.shape[0] // key_blk
-    prompt = info_ref[1]
+    prompt = info_ref[0, 1]
 
     @pl.loop(0, blocks)
     def _(j):
@@ -1631,31 +1656,25 @@
     w_qkv = jnp.stack([w_query, w_key, w_value])
     w_mine = lax.dynamic_slice_in_dim(w_qkv, line * width, width, axis=2)
     w_mine = jnp.concatenate([w_mine[1], w_mine[2], w_mine[0]], axis=1)
-    attn_in, q, kv_all, place, recv_grads = front(
-        hidden_in, w_mine, attn_gain, routes.T, out_grad
+    qinfo = seg.reshape(length // rows, rows)
+    attn_in, q, kv_all, place, recv_grads, info = front(
+        hidden_in, w_mine, attn_gain, routes.T, out_grad, qinfo
     )
     attn_in = attn_in.reshape(lines * rows, model)
     kv_all, w_out_b, w_qkv = lax.optimization_barrier((kv_all, w_out, w_qkv))
     wo_far = swap(w_out_b, SH, lambda i: i ^ 2)
     w_far = swap(w_qkv, SH, lambda i: i ^ 2)
     kv_all = kv_all.reshape(length, 2 * width)
-    starts = jnp.sum(
-        (seg[None, :] < jnp.arange(DOCS, dtype=jnp.int32)[:, None]).astype(jnp.int32),
-        axis=1,
-        dtype=jnp.int32,
-    )
-    qinfo = seg.reshape(length // rows, rows)
-    info = jnp.concatenate([starts, qinfo[:, 0]])
     attn_vec, attn_heads, lse = attend(info, q, kv_all, qinfo)
     n_ids = w_router.shape[1]
-    small_w = jnp.pad(
-        jnp.concatenate([w_router, const_mix], axis=1), ((0, 0), (0, 124 - n_ids))
+    small_t = jnp.pad(
+        jnp.concatenate([w_router.T, const_mix.T], axis=0), ((0, 124 - n_ids), (0, 0))
     )
     gain_two = moe_gain
     recv_rows, wo_full, resid_one, table, attn_low = run_parts(
         [
             route(
-                attn_heads, hidden_in, gain_two, small_w, routes.T, place, w_out[None], wo_far[None], n_ids
+                attn_heads, hidden_in, gain_two, small_t, routes.T, place, w_out[None], wo_far[None], n_ids
             )
         ],
         2,
@@ -1667,29 +1686,29 @@
     expert_out, input_back, *terms = expert(
         recv_rows.reshape(slots, model + 128), recv_grads.reshape(slots, model), w_gate[0], w_up[0], w_down[0]
     )
-    returned, input_ret, weights, *sums = run_parts(
+    returned, input_ret, *sums = run_parts(
         [
             exchange(EX, SWAP, expert_out.reshape(lines, CAP, model)),
             exchange(EX, SWAP, input_back.reshape(lines, CAP, model)),
-            share_weights(w_qkv, w_far),
         ]
         + [core_sum(term) for term in terms],
         4,
         "combine",
     )
-    weights = weights.reshape(3, model, model)
     far = [swap(there, SH, lambda i: i ^ 2) for there in sums[1::2]]
     down = (sums[4].astype(f32) + far[2].astype(f32)).astype(bf16)
 
-    back_heads, layer_out, resid_grad, out_term, packed = run_parts(
+    weights, back_heads, layer_out, resid_grad, out_term, packed = run_parts(
         [
+            share_weights(w_qkv, w_far),
             to_heads(
-                returned, input_ret, place, table, resid_one, attn_low, out_grad, gain_two, small_w.T, const_vec, wo_full, n_ids
+                returned, input_ret, place, table, resid_one, attn_low, out_grad, gain_two, small_t, const_vec, wo_full, n_ids
             )
         ],
         5,
         "to_heads",
     )
+    weights = weights.reshape(3, model, model)
     back_heads, down = lax.optimization_barrier((back_heads, down))
     cross = lambda x: swap(x, GR, lambda i: 1 - i)
     down_far = cross(down)

time: 250 us -> 243 us (0.972); the launches traced: 248 us -> 245 us
  starting transfers between devices: 8.24 us -> 12.3 us
  Pallas kernels: 227 us -> 223 us
  waiting for transfers between devices: 2.7 us -> 0.02 us
    ppermute x6, starting transfers between devices: 8.24 us -> 12.3 us  [swap(): lax.ppermute(x, axis, [(i, partner(i)) for i in range(lax.axis_size(axis))])]
    pallas_call x4, Pallas kernels: 124 us -> 121 us  [run_parts(): pl.pallas_call(body, out_shape=outs, in_specs=sum([p.specs for p in parts...]
    ppermute x6, waiting for transfers between devices: 2.7 us -> 0.02 us  [swap(): lax.ppermute(x, axis, [(i, partner(i)) for i in range(lax.axis_size(axis))])]
  transfers between devices with their start and end apart: 6 -> 6, of which waited for: 1 -> 0; matrix products, arithmetic and copies ran while one was open for 2% -> 0% of each run, Pallas kernels for 63% -> 71%
where the time goes in v7:
time: 243 us; the launch traced here: 245 us
  Pallas kernels  223 us (92%)
  starting transfers between devices  12.3 us (5%)
  other arithmetic  4.46 us (2%)
  local copies, waits for them, and re-layouts  3.88 us (2%)
    pallas_call x4, Pallas kernels, run_parts(): pl.pallas_call(body, out_shape=outs, in_specs=sum([p.specs for p in parts...  121 us
    pallas_call x1, Pallas kernels, front(): pl.pallas_call(body, out_shape=[shape((lines, rows, model), bf16), shape(...  42.6 us
    pallas_call x1, Pallas kernels, attend_back(): pl.pallas_call(functools.partial(attend_back_body, lines, heads), out_sha...  24.6 us
    pallas_call x1, Pallas kernels, attend(): pl.pallas_call(functools.partial(attend_body, lines, heads), out_shape=[s...  15.5 us
    pallas_call x1, Pallas kernels, expert(): pl.pallas_call(functools.partial(expert_body, steps), grid=(steps,), out_...  13.4 us
    ppermute x6, starting transfers between devices, swap(): lax.ppermute(x, axis, [(i, partner(i)) for i in range(lax.axis_size(axis))])  12.3 us
    pallas_call x1, Pallas kernels, finale(): pl.pallas_call(functools.partial(finale_body, lines, n_ids), grid=(steps,...  6.48 us
  transfers between devices with their start and end apart: 6, of which 0 were waited for; matrix products, arithmetic and copies ran while one was open for 0% of the time, Pallas kernels for 71%

profile of v7, /device:TPU:0, one launch (start us, length us, event | category | flops | bytes accessed | tf_op | source)
XLA Modules:
  0.0 244.9 jit_solution(15370196775274291468)
XLA Ops:
  0.7 0.5 broadcast.11
  1.2 1.4 reduce.3
  2.5 0.7 reshape_squeeze.3.docs_ref.qinfo_ref
  3.2 0.0 copy-start.5
  3.2 0.0 copy-start.7
  3.2 0.0 copy-start.8
  3.2 1.3 pad_maximum_fusion.refs_0_
  4.5 0.0 copy-start
  4.5 0.2 dynamic-slice_bitcast_fusion.2
  4.7 0.8 pad_maximum_fusion.1.w_ref
  5.6 42.6 %front.1 = (bf16[4,192,768]{2,1,0:T(8,128)(2,1)}, bf16[4,192,192]{2,1,0:T(8,128)(2,1)}, bf16[4,4,192,384]{3,2,1,0:T(8,128)(2,1)}, bf16[2,192,192]{2,1,0:T(8,128)...) custom-call(bf16[192,768]{1,0:T(8,128)(2,1)} %refs_7_.1, bf16[192,576]{1,0:T(8,128)(2,1)} %pad_maximum_fusion.1.w_ref, ...), custom_call_target="tpu_custom_call" | custom-call | tf_op jit(solution)/shard_map/front/pallas_call | solution.py:859
  48.2 0.0 copy-done.5
  48.2 1.2 collective-permute-start.1
  49.4 0.9 collective-permute-start
  50.3 0.0 copy-done.7
  50.3 0.0 copy-done.8
  50.3 0.8 select_maximum_fusion.refs_3_.refs_10_
  51.1 15.5 %attend.1 = (f32[4,192,192]{2,1,0:T(8,128)}, bf16[4,192,192]{2,1,0:T(8,128)(2,1)}, f32[4,8,192]{2,1,0:T(8,128)}) custom-call(s32[1,128]{1,0:T(1,128)} %get-tuple-element.79.info_ref, bf16[4,192,192]{2,1,0:T(8,128)(2,1)} %get-tuple-element.80.q_ref, bf16[3072,384]{1,0:T(8,128)(2,1)} %bitcast.46, s32[16,192]{1,0:T(8,128)} %reshape_squeeze.3.docs_ref.qinfo_ref), custom_call_target="tpu_custom_call" | custom-call | flops 2000000000 | bytes 8000000 | tf_op jit(solution)/shard_map/attend/pallas_call | solution.py:1452
  66.6 0.0 copy-done
  66.6 0.0 collective-permute-done.1
  66.6 0.0 copy-start.6
  66.6 0.7 copy-done.6
  67.3 24.5 %route.1 = (bf16[4,48,896]{2,1,0:T(8,128)(2,1)}, bf16[1,4,192,768]{3,2,1,0:T(8,128)(2,1)}, f32[192,768]{1,0:T(8,128)}, f32[192,128]{1,0:T(8,128)}, bf16[192,768]{1,0:T(8,128)(2,1)}) custom-call(bf16[4,192,192]{2,1,0:T(8,128)(2,1)} %get-tuple-element.86.refs_0_, bf16[192,768]{1,0:T(8,128)(2,1)} %refs_7_.1, f32[768]{0:T(1024)} %refs_9_.2, ...), custom_call_target="tpu_custom_call" | custom-call | tf_op jit(solution)/shard_map/route/pallas_call | solution.py:529
  91.8 13.4 %ffn.1 = (bf16[192,768]{1,0:T(8,128)(2,1)}, bf16[192,768]{1,0:T(8,128)(2,1)}, bf16[4,192,2048]{2,1,0:T(8,128)(2,1)}, bf16[4,192,2048]{2,1,0:T(8,128)(2,1)}, bf16[4,512,768]{2,1,0:T(8,128)(2,1)}) custom-call(bf16[192,896]{1,0:T(8,128)(2,1)} %bitcast.52, bf16[192,768]{1,0:T(8,128)(2,1)} %bitcast.53, bf16[768,2048]{1,0:T(8,128)(2,1)} %bitcast.43, ...), custom_call_target="tpu_custom_call" | custom-call | flops 6000000000 | bytes 20000000 | tf_op jit(solution)/shard_map/ffn/pallas_call | solution.py:1342
  105.3 19.0 %combine.1 = (bf16[4,48,768]{2,1,0:T(8,128)(2,1)}, bf16[4,48,768]{2,1,0:T(8,128)(2,1)}, bf16[192,2048]{1,0:T(8,128)(2,1)}, bf16[192,2048]{1,0:T(8,128)(2,1)}, bf...) custom-call(bf16[4,48,768]{2,1,0:T(8,128)(2,1)} %bitcast.31, ...), custom_call_target="tpu_custom_call" | custom-call | tf_op jit(solution)/shard_map/combine/pallas_call | solution.py:529
  124.3 2.2 collective-permute-start.2
  126.5 0.1 collective-permute-start.3
  126.6 1.9 collective-permute-start.4
  128.5 0.0 collective-permute-done.refs_1_
  128.5 0.0 copy-start.2
  128.5 0.9 copy-done.2
  129.5 0.0 copy-start.4
  129.5 20.0 %to_heads.1 = (bf16[3,4,192,768]{3,2,1,0:T(8,128)(2,1)}, bf16[4,192,192]{2,1,0:T(8,128)(2,1)}, bf16[192,768]{1,0:T(8,128)(2,1)}, f32[192,768]{1,0:T(8,128)}, bf1...) custom-call(bf16[3,192,768]{2,1,0:T(8,128)(2,1)} %copy-done, bf16[3,192,768]{2,1,0:T(8,128)(2,1)} %copy-done.2, ...), custom_call_target="tpu_custom_call" | custom-call | tf_op jit(solution)/shard_map/to_heads/pallas_call | solution.py:529
  149.5 0.0 collective-permute-done.2
  149.5 0.0 copy-done.4
  149.5 0.2 add_convert_fusion.refs_2_
  149.7 0.0 copy-start.1
  149.7 6.0 %collective-permute-start.5 = (bf16[512,768]{1,0:T(8,128)(2,1)S(1)}, bf16[512,768]{1,0:T(8,128)(2,1)S(1)}, u32[]{:S(2)}, u32[]{:S(2)}) collective-permute-start(bf16[512,768]{1,0:T(8,128)(2,1)S(1)} %add_convert_fusion.refs_2_), channel_id=1, source_target_pairs={{0,16},{16,0},{1,17},{17,1},{2,18},{18,2},{3,19},{19,3},{4,20},{20... | collective-permute-start | bytes 2359304 | tf_op jit(solution)/shard_map/ppermute | solution.py:1628
  155.7 24.6 %attend_back.1 = (bf16[4,192,192]{2,1,0:T(8,128)(2,1)}, bf16[4,2,192,384]{3,2,1,0:T(8,128)(2,1)}, bf16[4,2,192,384]{3,2,1,0:T(8,128)(2,1)}) custom-call(s32[1,128]{1,0:T(1,128)} %get-tuple-element.79.info_ref, bf16[4,192,192]{2,1,0:T(8,128)(2,1)} %get-tuple-element.80.q_ref, bf16[3072,384]{1,0:T(8,128)(2,1)} %bitcast.47, ...), custom_call_target="tpu_custom_call" | custom-call | flops 5000000000 | bytes 12000000 | tf_op jit(solution)/shard_map/attend_back/pallas_call | solution.py:1548
  180.3 0.0 copy-done.1
  180.3 0.0 collective-permute-done.3.refs_11_
  180.3 0.0 collective-permute-done.4.refs_13_
  180.3 57.0 %tail.1 = (f32[192,768]{1,0:T(8,128)}, f32[4,48,192]{2,1,0:T(8,128)}, f32[4,48,384]{2,1,0:T(8,128)}, f32[48,768]{1,0:T(8,128)}, f32[16,768]{1,0:T(8,128)}, /*ind...) custom-call(bf16[4,2,192,384]{3,2,1,0:T(8,128)(2,1)} %get-tuple-elem, ...), custom_call_target="tpu_custom_call" | custom-call | flops 20000000000 | bytes 100000000 | tf_op jit(solution)/shard_map/tail/pallas_call | solution.py:529
  237.3 0.0 collective-permute-done.5.refs_5_
  237.3 0.0 copy-start.3
  237.3 0.9 copy-done.3
  238.2 6.5 %finale.1 = (f32[192,2048]{1,0:T(8,128)}, f32[192,2048]{1,0:T(8,128)}, f32[512,768]{1,0:T(8,128)}, f32[192,768]{1,0:T(8,128)}, bf16[192,768]{1,0:T(8,128)(2,1)},...) custom-call(bf16[192,2048]{1,0:T(8,128)(2,1)} %get-tuple-element.118, ...), custom_call_target="tpu_custom_call" | custom-call | flops 10000000 | bytes 10000000 | tf_op jit(solution)/shard_map/finale/pallas_call | solution.py:1614
Async XLA Ops:
  3.2 45.0 %copy-start.5 = (bf16[192,768]{1,0:T(8,128)(2,1)S(1)}, bf16[192,768]{1,0:T(8,128)(2,1)}, u32[]{:S(2)}) copy-start(bf16[192,768]{1,0:T(8,128)(2,1)} %param.23) | copy-start | bytes 884740
  3.2 47.1 %copy-start.7 = (f32[768,8]{0,1:T(8,128)S(1)}, f32[768,8]{0,1:T(8,128)}, u32[]{:S(2)}) copy-start(f32[768,8]{0,1:T(8,128)} %param.25) | copy-start | bytes 73732
  3.2 47.1 %copy-start.8 = (f32[768,4]{0,1:T(4,128)S(1)}, f32[768,4]{0,1:T(4,128)}, u32[]{:S(2)}) copy-start(f32[768,4]{0,1:T(4,128)} %param.26) | copy-start | bytes 36868
  4.5 62.1 %copy-start = (bf16[3,192,768]{2,1,0:T(8,128)(2,1)}, bf16[3,192,768]{2,1,0:T(8,128)(2,1)S(1)}, u32[]{:S(2)}) copy-start(bf16[3,192,768]{2,1,0:T(8,128)(2,1)S(1)} %pad_maximum_fusion.refs_0_) | copy-start | bytes 2654212
  48.2 18.4 %collective-permute-start.1 = (bf16[192,768]{1,0:T(8,128)(2,1)S(1)}, bf16[192,768]{1,0:T(8,128)(2,1)S(1)}, u32[]{:S(2)}, u32[]{:S(2)}) collective-permute-start(bf16[192,768]{1,0:T(8,128)(2,1)S(1)} %copy-done.5), channel_id=1, source_target_pairs={{0,2},{1,3},{2,0},{3,1},{4,6},{5,7},{6,4},{7,5},{8,10},{9,11},{10,... | collective-permute-start | bytes 884744 | tf_op jit(solution)/shard_map/ppermute | solution.py:1628
  49.4 79.1 %collective-permute-start = (bf16[3,192,768]{2,1,0:T(8,128)(2,1)S(1)}, bf16[3,192,768]{2,1,0:T(8,128)(2,1)S(1)}, u32[]{:S(2)}, u32[]{:S(2)}) collective-permute-start(bf16[3,192,768]{2,1,0:T(8,128)(2,1)S(1)} %pad_maximum_fusion.refs_0_), channel_id=1, source_target_pairs={{0,2},{1,3},{2,0},{3,1},{4,6},{5,7},{6,4},{7,5},{8,10},{9,11},{10,... | collective-permute-start | bytes 2654216 | tf_op jit(solution)/shard_map/ppermute | solution.py:1628
  66.6 0.7 copy-start.6
  124.3 25.2 %collective-permute-start.2 = (bf16[512,768]{1,0:T(8,128)(2,1)}, bf16[512,768]{1,0:T(8,128)(2,1)S(1)}, u32[]{:S(2)}, u32[]{:S(2)}) collective-permute-start(bf16[512,768]{1,0:T(8,128)(2,1)} %get-tuple-element.104), channel_id=1, source_target_pairs={{0,2},{1,3},{2,0},{3,1},{4,6},{5,7},{6,4},{7,5},{8,10},{9,11},{10,... | collective-permute-start | bytes 2359304 | tf_op jit(solution)/shard_map/ppermute | solution.py:1628
  126.5 53.8 %collective-permute-start.3 = (bf16[192,2048]{1,0:T(8,128)(2,1)}, bf16[192,2048]{1,0:T(8,128)(2,1)}, u32[]{:S(2)}, u32[]{:S(2)}) collective-permute-start(bf16[192,2048]{1,0:T(8,128)(2,1)} %get-tuple-element.115), channel_id=1, source_target_pairs={{0,2},{1,3},{2,0},{3,1},{4,6},{5,7},{6,4},{7,5},{8,10},{9,11},{10,... | collective-permute-start | bytes 2359304 | tf_op jit(solution)/shard_map/ppermute | solution.py:1628
  126.6 53.7 %collective-permute-start.4 = (bf16[192,2048]{1,0:T(8,128)(2,1)}, bf16[192,2048]{1,0:T(8,128)(2,1)}, u32[]{:S(2)}, u32[]{:S(2)}) collective-permute-start(bf16[192,2048]{1,0:T(8,128)(2,1)} %get-tuple-element.117), channel_id=1, source_target_pairs={{0,2},{1,3},{2,0},{3,1},{4,6},{5,7},{6,4},{7,5},{8,10},{9,11},{10,... | collective-permute-start | bytes 2359304 | tf_op jit(solution)/shard_map/ppermute | solution.py:1628
  128.5 0.9 copy-start.2
  129.5 20.0 %copy-start.4 = (bf16[512,768]{1,0:T(8,128)(2,1)S(1)}, bf16[512,768]{1,0:T(8,128)(2,1)}, u32[]{:S(2)}) copy-start(bf16[512,768]{1,0:T(8,128)(2,1)} %get-tuple-element.103) | copy-start | bytes 2359300
  149.7 30.6 %copy-start.1 = (bf16[512,768]{1,0:T(8,128)(2,1)}, bf16[512,768]{1,0:T(8,128)(2,1)S(1)}, u32[]{:S(2)}) copy-start(bf16[512,768]{1,0:T(8,128)(2,1)S(1)} %add_convert_fusion.refs_2_) | copy-start | bytes 2359300
  149.7 87.6 %collective-permute-start.5 = (bf16[512,768]{1,0:T(8,128)(2,1)S(1)}, bf16[512,768]{1,0:T(8,128)(2,1)S(1)}, u32[]{:S(2)}, u32[]{:S(2)}) collective-permute-start(bf16[512,768]{1,0:T(8,128)(2,1)S(1)} %add_convert_fusion.refs_2_), channel_id=1, source_target_pairs={{0,16},{16,0},{1,17},{17,1},{2,18},{18,2},{3,19},{19,3},{4,20},{20... | collective-permute-start | bytes 2359304 | tf_op jit(solution)/shard_map/ppermute | solution.py:1628
  237.3 0.9 copy-start.3

commit v8 on v7

--- a/solution.py
+++ b/solution.py
@@ -1094,21 +1094,26 @@
     part_dims = (width, 2 * width, model)
 
     def phases(ins, outs, scr, go):
-        lo_ref, hi_ref, dq_ref, attn_ref, w_ref, o_ref, packed_ref, hid_ref, resid_ref, gain_ref = ins[:10]
+        lo_ref, hi_ref, dq_ref, attn_ref, w_ref, wf_ref, o_ref, packed_ref, hid_ref, resid_ref, gain_ref = ins[:11]
         input_ref, q_out, kv_out, out_out, packed_out, gain_out = outs[:6]
         scr = list(scr)
         take = lambda k: [scr.pop(0) for _ in range(k)]
         lo_scr, hi_scr, q_scr, kvw_scr, o_scr = take(3), take(3), take(3), take(3), take(3)
         own_kv, q_t, kv_t, dq_all, dkv_all, dq_full = take(6)
-        kv_sems, w_s, w_sem = take(3)
+        kv_sems, w_s, w_sem, turned = take(4)
         held = take(2 * len(pairs))
-        w_copy = pltpu.make_async_copy(w_ref, w_s, w_sem.at[2 * len(pairs)])
+        me, _, _, near, far = shard_peers()
+        w_copies = [
+            pltpu.make_async_copy(ref, w_s.at[:, at], w_sem.at[2 * len(pairs) + k])
+            for k, (ref, at) in enumerate(((w_ref, me), (wf_ref, far)))
+        ]
         fetch = [
-            pltpu.make_async_copy(ins[10 + k], held[k], w_sem.at[k]) for k in range(2 * len(pairs))
+            pltpu.make_async_copy(ins[11 + k], held[k], w_sem.at[k]) for k in range(2 * len(pairs))
         ]
         for copy in fetch:
             copy.start()
-        w_copy.start()
+        for copy in w_copies:
+            copy.start()
         sums, lands, halves, gots = take(3), take(3), take(3), take(3)
         pk_l, pk_s, pk_g = take(3)
         mid_l, mid_s = take(2)
@@ -1144,8 +1149,11 @@
         o_tree = Tree(o_ref, o_scr, go)
         pk1 = start_swap(go, packed_ref, pk_l, EX, True)
         def term(rows_ref, out):
-            value = contract(attn_ref[...], rows_ref[...].reshape(tok, rows_ref.shape[-1]), 0, 0)
-            value = value.astype(bf16)
+            value = jnp.dot(
+                turned[...],
+                rows_ref[...].reshape(tok, rows_ref.shape[-1]),
+                preferred_element_type=f32,
+            ).astype(bf16)
             for line in range(lines):
                 for piece in range(4):
                     at = (line * 4 + piece) * own
@@ -1161,6 +1169,9 @@
             fetch[2 * k + 1].wait()
             mine[...] = (here[...].astype(f32) + there[...].astype(f32)).astype(bf16)
             wide.append(go(mine, other, GR, lax.rem(group_me + 1, groups)))
+        w_copies.append(go(w_ref, w_s.at[:, me], SH, near))
+        w_copies.append(go(wf_ref, w_s.at[:, far], SH, near))
+        turned[...] = jnp.transpose(attn_ref[...])
         term(dq_ref, q_t)
         o_tree.across()
         q_tree = Tree(q_t, q_scr, go)
@@ -1171,12 +1182,12 @@
             return start_swap(go, sums[k], lands[k], EX, False)
 
         push_kv(0)
+        q_tree.across()
         push_kv(1)
-        o_lines = lines_out(2)
-        q_tree.across()
         term(own_kv, kv_t)
         kvw_tree = Tree(kv_t, kvw_scr, go)
         trees[1] = kvw_tree
+        o_lines = lines_out(2)
         for copy in pk1:
             copy.wait()
         mid_l[...] = total_of(pk_l, lines)
@@ -1187,8 +1198,9 @@
             copy.wait()
         for line in range(lines):
             dq_full[:, line * width : (line + 1) * width] = dq_all[line]
-        w_copy.wait()
-        grad = contract(dq_full[...], w_s[0], 1, 1)
+        for copy in w_copies:
+            copy.wait()
+        grad = contract(dq_full[...], w_s[0].reshape(model, model), 1, 1)
         for copy in pk2:
             copy.wait()
         mid_s[...] = total_of(pk_s, 4)
@@ -1206,7 +1218,7 @@
                 dq_full[:, line * width : (line + 1) * width] = dkv_all[
                     line, :, half * width : (half + 1) * width
                 ]
-            grad = grad + contract(dq_full[...], w_s[1 + half], 1, 1)
+            grad = grad + contract(dq_full[...], w_s[1 + half].reshape(model, model), 1, 1)
         inputs = hid_ref[...].astype(f32)
         inv = lax.rsqrt(jnp.mean(inputs * inputs, axis=1, keepdims=True) + norm_eps)
         normed = inputs * inv
@@ -1262,8 +1274,9 @@
         vmem((lines, rows, 2 * width), bf16),
         vmem((rows, model), bf16),
         pltpu.SemaphoreType.DMA((2, lines)),
-        vmem(weights.shape, bf16),
-        pltpu.SemaphoreType.DMA((2 * len(pairs) + 1,)),
+        vmem((3, 4) + weights[0].shape[1:], bf16),
+        pltpu.SemaphoreType.DMA((2 * len(pairs) + 2,)),
+        vmem((model, tok), bf16),
     ]
     scratch += [vmem(x.shape, bf16) for pair in pairs for x in pair]
     scratch += [vmem(p, bf16) for p in pieces] + [vmem(p, bf16) for p in pieces]
@@ -1271,7 +1284,7 @@
     scratch += [vmem((n,) + packed.shape, f32) for n in (lines, 4, groups)]
     scratch += [vmem(packed.shape, f32)] * 2
     scratch += [vmem((n, 1, model), f32) for n in (lines, 4, groups)] + [vmem((1, model), f32)] * 3
-    copies = len(pairs) + 5 * Tree.copies + 6 * (lines - 1) + 2 * 3 + 5 * (groups - 1)
+    copies = 2 + len(pairs) + 5 * Tree.copies + 6 * (lines - 1) + 2 * 3 + 5 * (groups - 1)
     outs = [
         shape((rows, model), f32),
         shape((lines, own, width), f32),
@@ -1280,10 +1293,10 @@
         shape(packed.shape, f32),
         shape((1, model), f32),
     ] + [shape(x.shape, bf16) for pair in pairs for x in pair]
-    ins = [*dkv, dq, attn_in, weights, out_term, packed, hidden, resid_grad, gain]
+    ins = [*dkv, dq, attn_in, *weights, out_term, packed, hidden, resid_grad, gain]
     ins += [x for pair in pairs for x in pair]
     hbm = pl.BlockSpec(memory_space=pl.ANY)
-    specs = [hbm if x is weights or k >= 10 else VM for k, x in enumerate(ins)]
+    specs = [hbm if k in (4, 5) or k >= 11 else VM for k in range(len(ins))]
     return Part([EX, SH, GR], ins, outs, scratch, copies, phases, specs)
 
 
@@ -1650,22 +1663,22 @@
     lines = lax.axis_size(EX)
     line, shard = lax.axis_index(EX), lax.axis_index(SH)
     width = model // lines
-    seg = segment_ids[0]
-    length = seg.shape[0]
+    length = segment_ids.shape[1]
 
     w_qkv = jnp.stack([w_query, w_key, w_value])
     w_mine = lax.dynamic_slice_in_dim(w_qkv, line * width, width, axis=2)
     w_mine = jnp.concatenate([w_mine[1], w_mine[2], w_mine[0]], axis=1)
-    qinfo = seg.reshape(length // rows, rows)
+    qinfo = segment_ids.reshape(length // rows, rows)
     attn_in, q, kv_all, place, recv_grads, info = front(
         hidden_in, w_mine, attn_gain, routes.T, out_grad, qinfo
     )
     attn_in = attn_in.reshape(lines * rows, model)
-    kv_all, w_out_b, w_qkv = lax.optimization_barrier((kv_all, w_out, w_qkv))
+    kv_all, w_out_b = lax.optimization_barrier((kv_all, w_out))
     wo_far = swap(w_out_b, SH, lambda i: i ^ 2)
-    w_far = swap(w_qkv, SH, lambda i: i ^ 2)
     kv_all = kv_all.reshape(length, 2 * width)
     attn_vec, attn_heads, lse = attend(info, q, kv_all, qinfo)
+    attn_heads, w_qkv = lax.optimization_barrier((attn_heads, w_qkv))
+    w_far = swap(w_qkv, SH, lambda i: i ^ 2)
     n_ids = w_router.shape[1]
     small_t = jnp.pad(
         jnp.concatenate([w_router.T, const_mix.T], axis=0), ((0, 124 - n_ids), (0, 0))
@@ -1681,6 +1694,7 @@
         "route",
     )
     wo_full = wo_full.reshape(model, model)
+    recv_rows, w_far = lax.optimization_barrier((recv_rows, w_far))
     slots = lines * CAP
 
     expert_out, input_back, *terms = expert(
@@ -1698,9 +1712,8 @@
     far = [swap(there, SH, lambda i: i ^ 2) for there in sums[1::2]]
     down = (sums[4].astype(f32) + far[2].astype(f32)).astype(bf16)
 
-    weights, back_heads, layer_out, resid_grad, out_term, packed = run_parts(
+    back_heads, layer_out, resid_grad, out_term, packed = run_parts(
         [
-            share_weights(w_qkv, w_far),
             to_heads(
                 returned, input_ret, place, table, resid_one, attn_low, out_grad, gain_two, small_t, const_vec, wo_full, n_ids
             )
@@ -1708,7 +1721,6 @@
         5,
         "to_heads",
     )
-    weights = weights.reshape(3, model, model)
     back_heads, down = lax.optimization_barrier((back_heads, down))
     cross = lambda x: swap(x, GR, lambda i: 1 - i)
     down_far = cross(down)
@@ -1717,7 +1729,7 @@
     input_grad, *parts = run_parts(
         [
             tail(
-                dkv, dq, attn_in, weights, out_term, packed, hidden_in, resid_grad, attn_gain, pairs
+                dkv, dq, attn_in, (w_qkv, w_far), out_term, packed, hidden_in, resid_grad, attn_gain, pairs
             )
         ],
         6,

time: 243 us -> 269 us (1.11)
  waiting for transfers between devices: 0.02 us -> 30.3 us
  starting transfers between devices: 12.3 us -> 4.26 us
  Pallas kernels: 223 us -> 226 us
    ppermute x6, waiting for transfers between devices: 0.02 us -> 30.3 us  [swap(): lax.ppermute(x, axis, [(i, partner(i)) for i in range(lax.axis_size(axis))])]
    ppermute x6, starting transfers between devices: 12.3 us -> 4.26 us  [swap(): lax.ppermute(x, axis, [(i, partner(i)) for i in range(lax.axis_size(axis))])]
  transfers between devices with their start and end apart: 6 -> 6, of which waited for: 0 -> 3; matrix products, arithmetic and copies ran while one was open for 0% -> 0% of each run, Pallas kernels for 71% -> 46%
where the time goes in v8:
time: 269 us
  Pallas kernels  226 us (84%)
  waiting for transfers between devices  30.3 us (11%)
  other arithmetic  4.41 us (2%)
  starting transfers between devices  4.26 us (2%)
  local copies, waits for them, and re-layouts  2.97 us (1%)
    pallas_call x4, Pallas kernels, run_parts(): pl.pallas_call(body, out_shape=outs, in_specs=sum([p.specs for p in parts...  119 us
    pallas_call x1, Pallas kernels, front(): pl.pallas_call(body, out_shape=[shape((lines, rows, model), bf16), shape(...  42.6 us
    ppermute x6, waiting for transfers between devices, swap(): lax.ppermute(x, axis, [(i, partner(i)) for i in range(lax.axis_size(axis))])  30.3 us
    pallas_call x1, Pallas kernels, attend_back(): pl.pallas_call(functools.partial(attend_back_body, lines, heads), out_sha...  26.8 us
    pallas_call x1, Pallas kernels, attend(): pl.pallas_call(functools.partial(attend_body, lines, heads), out_shape=[s...  17.4 us
    pallas_call x1, Pallas kernels, expert(): pl.pallas_call(functools.partial(expert_body, steps), grid=(steps,), out_...  13.7 us
    pallas_call x1, Pallas kernels, finale(): pl.pallas_call(functools.partial(finale_body, lines, n_ids), grid=(steps,...  6.48 us
  transfers between devices with their start and end apart: 6, of which 3 were waited for; matrix products, arithmetic and copies ran while one was open for 0% of the time, Pallas kernels for 46%

profile of v8, /device:TPU:0, one launch (start us, length us, event | category | flops | bytes accessed | tf_op | source)
XLA Modules:
  0.0 268.6 jit_solution(4091452083551695747)
XLA Ops:
  0.6 0.5 broadcast.11
  1.2 1.4 reduce.3
  2.5 0.7 reshape.52.docs_ref.qinfo_ref
  3.2 1.2 pad_maximum_fusion.refs_4_
  4.5 0.0 copy-start.1
  4.5 0.2 dynamic-slice_bitcast_fusion.2
  4.7 0.8 pad_maximum_fusion.1.w_ref
  5.5 42.6 %front.1 = (bf16[4,192,768]{2,1,0:T(8,128)(2,1)}, bf16[4,192,192]{2,1,0:T(8,128)(2,1)}, bf16[4,4,192,384]{3,2,1,0:T(8,128)(2,1)}, bf16[2,192,192]{2,1,0:T(8,128)...) custom-call(bf16[192,768]{1,0:T(8,128)(2,1)} %refs_8_.1, bf16[192,576]{1,0:T(8,128)(2,1)} %pad_maximum_fusion.1.w_ref, ...), custom_call_target="tpu_custom_call" | custom-call | tf_op jit(solution)/shard_map/front/pallas_call | solution.py:859
  48.1 0.0 copy-start.4
  48.2 0.0 copy-start.6
  48.2 0.0 copy-start.7
  48.2 17.4 %attend.1 = (f32[4,192,192]{2,1,0:T(8,128)}, bf16[4,192,192]{2,1,0:T(8,128)(2,1)}, f32[4,8,192]{2,1,0:T(8,128)}) custom-call(s32[1,128]{1,0:T(1,128)} %get-tuple-element.81.info_ref, bf16[4,192,192]{2,1,0:T(8,128)(2,1)} %get-tuple-element.82.q_ref, bf16[3072,384]{1,0:T(8,128)(2,1)} %bitcast.44, s32[16,192]{1,0:T(8,128)} %reshape.52.docs_ref.qinfo_ref), custom_call_target="tpu_custom_call" | custom-call | flops 2000000000 | bytes 8000000 | tf_op jit(solution)/shard_map/attend/pallas_call | solution.py:1465
  65.6 0.0 copy-done.1
  65.6 1.3 collective-permute-start.1
  66.9 0.0 copy-done.4
  66.9 0.8 collective-permute-start
  67.6 0.0 copy-done.6
  67.6 0.0 copy-done.7
  67.6 0.8 select_maximum_fusion.refs_3_.refs_8_
  68.4 24.8 %collective-permute-done = bf16[192,768]{1,0:T(8,128)(2,1)S(1)} collective-permute-done((bf16[192,768]{1,0:T(8,128)(2,1)S(1)}, bf16[192,768]{1,0:T(8,128)(2,1)S(1)}, u32[]{:S(2)}, u32[]{:S(2)}) %collective-permute-start) | collective-permute-done | bytes 294944 | tf_op jit(solution)/shard_map/ppermute | solution.py:1641
  93.2 0.0 copy-start.5
  93.2 0.7 copy-done.5
  93.9 24.6 %route.1 = (bf16[4,48,896]{2,1,0:T(8,128)(2,1)}, bf16[1,4,192,768]{3,2,1,0:T(8,128)(2,1)}, f32[192,768]{1,0:T(8,128)}, f32[192,128]{1,0:T(8,128)}, bf16[192,768]{1,0:T(8,128)(2,1)}) custom-call(bf16[4,192,192]{2,1,0:T(8,128)(2,1)} %get-tuple-element.88.refs_0_, bf16[192,768]{1,0:T(8,128)(2,1)} %refs_8_.1, f32[768]{0:T(1024)} %refs_7_.1, ...), custom_call_target="tpu_custom_call" | custom-call | tf_op jit(solution)/shard_map/route/pallas_call | solution.py:529
  118.5 0.0 collective-permute-done.1.refs_5_
  118.5 0.0 copy-start.8
  118.5 13.7 %ffn.1 = (bf16[192,768]{1,0:T(8,128)(2,1)}, bf16[192,768]{1,0:T(8,128)(2,1)}, bf16[4,192,2048]{2,1,0:T(8,128)(2,1)}, bf16[4,192,2048]{2,1,0:T(8,128)(2,1)}, bf16[4,512,768]{2,1,0:T(8,128)(2,1)}) custom-call(bf16[192,896]{1,0:T(8,128)(2,1)} %bitcast.50, bf16[192,768]{1,0:T(8,128)(2,1)} %bitcast.51, bf16[768,2048]{1,0:T(8,128)(2,1)} %bitcast.41, ...), custom_call_target="tpu_custom_call" | custom-call | flops 6000000000 | bytes 20000000 | tf_op jit(solution)/shard_map/ffn/pallas_call | solution.py:1355
  132.3 0.0 copy-done.8
  132.3 22.1 %combine.1 = (bf16[4,48,768]{2,1,0:T(8,128)(2,1)}, bf16[4,48,768]{2,1,0:T(8,128)(2,1)}, bf16[192,2048]{1,0:T(8,128)(2,1)}, bf16[192,2048]{1,0:T(8,128)(2,1)}, bf...) custom-call(bf16[4,48,768]{2,1,0:T(8,128)(2,1)} %bitcast.30, ...), custom_call_target="tpu_custom_call" | custom-call | tf_op jit(solution)/shard_map/combine/pallas_call | solution.py:529
  154.4 0.1 collective-permute-start.2
  154.5 2.0 collective-permute-start.3
  156.5 0.1 collective-permute-start.4
  156.6 0.0 copy-start.3
  156.6 17.8 %to_heads.1 = (bf16[4,192,192]{2,1,0:T(8,128)(2,1)}, bf16[192,768]{1,0:T(8,128)(2,1)}, f32[192,768]{1,0:T(8,128)}, bf16[4,4,48,768]{3,2,1,0:T(8,128)(2,1)}, f32[16,768]{1,0:T(8,128)}) custom-call(bf16[4,48,768]{2,1,0:T(8,128)(2,1)} %get-tuple-element.100.refs_0_, bf16[4,48,768]{2,1,0:T(8,128)(2,1)} %get-tuple-element.101.refs_1_, ...), custom_call_target="tpu_custom_call" | custom-call | tf_op jit(solution)/shard_map/to_heads/pallas_call | solution.py:529
  174.3 0.8 collective-permute-done.2
  175.1 0.0 copy-done.3
  175.1 0.2 add_convert_fusion.refs_2_
  175.3 0.0 copy-start
  175.3 0.1 collective-permute-start.5
  175.4 26.8 %attend_back.1 = (bf16[4,192,192]{2,1,0:T(8,128)(2,1)}, bf16[4,2,192,384]{3,2,1,0:T(8,128)(2,1)}, bf16[4,2,192,384]{3,2,1,0:T(8,128)(2,1)}) custom-call(s32[1,128]{1,0:T(1,128)} %get-tuple-element.81.info_ref, bf16[4,192,192]{2,1,0:T(8,128)(2,1)} %get-tuple-element.82.q_ref, bf16[3072,384]{1,0:T(8,128)(2,1)} %bitcast.45, ...), custom_call_target="tpu_custom_call" | custom-call | flops 5000000000 | bytes 12000000 | tf_op jit(solution)/shard_map/attend_back/pallas_call | solution.py:1561
  202.2 0.0 copy-done
  202.2 0.0 collective-permute-done.3.refs_12_
  202.2 0.0 copy-start.9
  202.2 4.8 %collective-permute-done.4.refs_14_ = bf16[192,2048]{1,0:T(8,128)(2,1)} collective-permute-done((bf16[192,2048]{1,0:T(8,128)(2,1)}, bf16[192,2048]{1,0:T(8,128)(2,1)}, u32[]{:S(2)}, u32[]{:S(2)}) %collective-permute-start.4) | collective-permute-done | bytes 786464 | tf_op jit(solution)/shard_map/ppermute | solution.py:1641
  207.0 0.0 copy-done.9
  207.0 54.1 %tail.1 = (f32[192,768]{1,0:T(8,128)}, f32[4,48,192]{2,1,0:T(8,128)}, f32[4,48,384]{2,1,0:T(8,128)}, f32[48,768]{1,0:T(8,128)}, f32[16,768]{1,0:T(8,128)}, /*ind...) custom-call(bf16[4,2,192,384]{3,2,1,0:T(8,128)(2,1)} %get-tuple-elem, ...), custom_call_target="tpu_custom_call" | custom-call | flops 20000000000 | bytes 100000000 | tf_op jit(solution)/shard_map/tail/pallas_call | solution.py:529
  261.1 0.0 collective-permute-done.5.refs_5_
  261.1 0.0 copy-start.2
  261.1 0.9 copy-done.2
  262.0 6.5 %finale.1 = (f32[192,2048]{1,0:T(8,128)}, f32[192,2048]{1,0:T(8,128)}, f32[512,768]{1,0:T(8,128)}, f32[192,768]{1,0:T(8,128)}, bf16[192,768]{1,0:T(8,128)(2,1)},...) custom-call(bf16[192,2048]{1,0:T(8,128)(2,1)} %get-tuple-element.122, ...), custom_call_target="tpu_custom_call" | custom-call | flops 10000000 | bytes 10000000 | tf_op jit(solution)/shard_map/finale/pallas_call | solution.py:1627
Async XLA Ops:
  4.5 61.1 %copy-start.1 = (bf16[3,192,768]{2,1,0:T(8,128)(2,1)}, bf16[3,192,768]{2,1,0:T(8,128)(2,1)S(1)}, u32[]{:S(2)}) copy-start(bf16[3,192,768]{2,1,0:T(8,128)(2,1)S(1)} %pad_maximum_fusion.refs_4_) | copy-start | bytes 2654212
  48.1 18.7 %copy-start.4 = (bf16[192,768]{1,0:T(8,128)(2,1)S(1)}, bf16[192,768]{1,0:T(8,128)(2,1)}, u32[]{:S(2)}) copy-start(bf16[192,768]{1,0:T(8,128)(2,1)} %param.23) | copy-start | bytes 884740
  48.2 19.5 %copy-start.6 = (f32[768,8]{0,1:T(8,128)S(1)}, f32[768,8]{0,1:T(8,128)}, u32[]{:S(2)}) copy-start(f32[768,8]{0,1:T(8,128)} %param.25) | copy-start | bytes 73732
  48.2 19.5 %copy-start.7 = (f32[768,4]{0,1:T(4,128)S(1)}, f32[768,4]{0,1:T(4,128)}, u32[]{:S(2)}) copy-start(f32[768,4]{0,1:T(4,128)} %param.26) | copy-start | bytes 36868
  65.6 52.9 %collective-permute-start.1 = (bf16[3,192,768]{2,1,0:T(8,128)(2,1)S(1)}, bf16[3,192,768]{2,1,0:T(8,128)(2,1)S(1)}, u32[]{:S(2)}, u32[]{:S(2)}) collective-permute-start(bf16[3,192,768]{2,1,0:T(8,128)(2,1)S(1)} %pad_maximum_fusion.refs_4_), channel_id=1, source_target_pairs={{0,2},{1,3},{2,0},{3,1},{4,6},{5,7},{6,4},{7,5},{8,10},{9,11},{10,... | collective-permute-start | bytes 2654216 | tf_op jit(solution)/shard_map/ppermute | solution.py:1641
  66.9 26.3 %collective-permute-start = (bf16[192,768]{1,0:T(8,128)(2,1)S(1)}, bf16[192,768]{1,0:T(8,128)(2,1)S(1)}, u32[]{:S(2)}, u32[]{:S(2)}) collective-permute-start(bf16[192,768]{1,0:T(8,128)(2,1)S(1)} %copy-done.4), channel_id=1, source_target_pairs={{0,2},{1,3},{2,0},{3,1},{4,6},{5,7},{6,4},{7,5},{8,10},{9,11},{10,... | collective-permute-start | bytes 884744 | tf_op jit(solution)/shard_map/ppermute | solution.py:1641
  93.2 0.7 copy-start.5
  118.5 13.7 %copy-start.8 = (bf16[3,192,768]{2,1,0:T(8,128)(2,1)}, bf16[3,192,768]{2,1,0:T(8,128)(2,1)S(1)}, u32[]{:S(2)}) copy-start(bf16[3,192,768]{2,1,0:T(8,128)(2,1)S(1)} %collective-permute-done.1.refs_5_) | copy-start | bytes 2654212
  154.4 20.7 %collective-permute-start.2 = (bf16[512,768]{1,0:T(8,128)(2,1)}, bf16[512,768]{1,0:T(8,128)(2,1)S(1)}, u32[]{:S(2)}, u32[]{:S(2)}) collective-permute-start(bf16[512,768]{1,0:T(8,128)(2,1)} %get-tuple-element.108), channel_id=1, source_target_pairs={{0,2},{1,3},{2,0},{3,1},{4,6},{5,7},{6,4},{7,5},{8,10},{9,11},{10,... | collective-permute-start | bytes 2359304 | tf_op jit(solution)/shard_map/ppermute | solution.py:1641
  154.5 47.7 %collective-permute-start.3 = (bf16[192,2048]{1,0:T(8,128)(2,1)}, bf16[192,2048]{1,0:T(8,128)(2,1)S(1)}, u32[]{:S(2)}, u32[]{:S(2)}) collective-permute-start(bf16[192,2048]{1,0:T(8,128)(2,1)} %get-tuple-element.119), channel_id=1, source_target_pairs={{0,2},{1,3},{2,0},{3,1},{4,6},{5,7},{6,4},{7,5},{8,10},{9,11},{10,... | collective-permute-start | bytes 2359304 | tf_op jit(solution)/shard_map/ppermute | solution.py:1641
  156.5 50.5 %collective-permute-start.4 = (bf16[192,2048]{1,0:T(8,128)(2,1)}, bf16[192,2048]{1,0:T(8,128)(2,1)}, u32[]{:S(2)}, u32[]{:S(2)}) collective-permute-start(bf16[192,2048]{1,0:T(8,128)(2,1)} %get-tuple-element.121), channel_id=1, source_target_pairs={{0,2},{1,3},{2,0},{3,1},{4,6},{5,7},{6,4},{7,5},{8,10},{9,11},{10,... | collective-permute-start | bytes 2359304 | tf_op jit(solution)/shard_map/ppermute | solution.py:1641
  156.6 18.5 %copy-start.3 = (bf16[512,768]{1,0:T(8,128)(2,1)S(1)}, bf16[512,768]{1,0:T(8,128)(2,1)}, u32[]{:S(2)}) copy-start(bf16[512,768]{1,0:T(8,128)(2,1)} %get-tuple-element.107) | copy-start | bytes 2359300
  175.3 26.9 %copy-start = (bf16[512,768]{1,0:T(8,128)(2,1)}, bf16[512,768]{1,0:T(8,128)(2,1)S(1)}, u32[]{:S(2)}) copy-start(bf16[512,768]{1,0:T(8,128)(2,1)S(1)} %add_convert_fusion.refs_2_) | copy-start | bytes 2359300
  175.3 85.8 %collective-permute-start.5 = (bf16[512,768]{1,0:T(8,128)(2,1)S(1)}, bf16[512,768]{1,0:T(8,128)(2,1)S(1)}, u32[]{:S(2)}, u32[]{:S(2)}) collective-permute-start(bf16[512,768]{1,0:T(8,128)(2,1)S(1)} %add_convert_fusion.refs_2_), channel_id=1, source_target_pairs={{0,16},{16,0},{1,17},{17,1},{2,18},{18,2},{3,19},{19,3},{4,20},{20... | collective-permute-start | bytes 2359304 | tf_op jit(solution)/shard_map/ppermute | solution.py:1641
  202.2 4.8 %copy-start.9 = (bf16[192,2048]{1,0:T(8,128)(2,1)}, bf16[192,2048]{1,0:T(8,128)(2,1)S(1)}, u32[]{:S(2)}) copy-start(bf16[192,2048]{1,0:T(8,128)(2,1)S(1)} %collective-permute-done.3.refs_12_) | copy-start | bytes 2359300
  261.1 0.9 copy-start.2

commit v9 on v8

--- a/solution.py
+++ b/solution.py
@@ -1677,7 +1677,7 @@
     wo_far = swap(w_out_b, SH, lambda i: i ^ 2)
     kv_all = kv_all.reshape(length, 2 * width)
     attn_vec, attn_heads, lse = attend(info, q, kv_all, qinfo)
-    attn_heads, w_qkv = lax.optimization_barrier((attn_heads, w_qkv))
+    attn_heads, w_qkv, wo_far = lax.optimization_barrier((attn_heads, w_qkv, wo_far))
     w_far = swap(w_qkv, SH, lambda i: i ^ 2)
     n_ids = w_router.shape[1]
     small_t = jnp.pad(

time: 269 us -> 243 us (0.903)
  waiting for transfers between devices: 30.3 us -> 4.24 us
  starting transfers between devices: 4.26 us -> 10.7 us
  Pallas kernels: 226 us -> 221 us
    ppermute x6, waiting for transfers between devices: 30.3 us -> 4.24 us  [swap(): lax.ppermute(x, axis, [(i, partner(i)) for i in range(lax.axis_size(axis))])]
    ppermute x6, starting transfers between devices: 4.26 us -> 10.7 us  [swap(): lax.ppermute(x, axis, [(i, partner(i)) for i in range(lax.axis_size(axis))])]
    pallas_call x4, Pallas kernels: 119 us -> 116 us  [run_parts(): pl.pallas_call(body, out_shape=outs, in_specs=sum([p.specs for p in parts...]
  transfers between devices with their start and end apart: 6 -> 6, of which waited for: 3 -> 1; matrix products, arithmetic and copies ran while one was open for 0% -> 0% of each run, Pallas kernels for 46% -> 56%
where the time goes in v9:
time: 243 us; the launch traced here: 244 us
  Pallas kernels  221 us (91%)
  starting transfers between devices  10.7 us (4%)
  other arithmetic  4.46 us (2%)
  waiting for transfers between devices  4.24 us (2%)
    pallas_call x4, Pallas kernels, run_parts(): pl.pallas_call(body, out_shape=outs, in_specs=sum([p.specs for p in parts...  116 us
    pallas_call x1, Pallas kernels, front(): pl.pallas_call(body, out_shape=[shape((lines, rows, model), bf16), shape(...  42.7 us
    pallas_call x1, Pallas kernels, attend_back(): pl.pallas_call(functools.partial(attend_back_body, lines, heads), out_sha...  26.6 us
    pallas_call x1, Pallas kernels, attend(): pl.pallas_call(functools.partial(attend_body, lines, heads), out_shape=[s...  16.2 us
    pallas_call x1, Pallas kernels, expert(): pl.pallas_call(functools.partial(expert_body, steps), grid=(steps,), out_...  13.7 us
    ppermute x6, starting transfers between devices, swap(): lax.ppermute(x, axis, [(i, partner(i)) for i in range(lax.axis_size(axis))])  10.7 us
    pallas_call x1, Pallas kernels, finale(): pl.pallas_call(functools.partial(finale_body, lines, n_ids), grid=(steps,...  6.48 us
  transfers between devices with their start and end apart: 6, of which 1 were waited for; matrix products, arithmetic and copies ran while one was open for 0% of the time, Pallas kernels for 56%

profile of v9, /device:TPU:0, one launch (start us, length us, event | category | flops | bytes accessed | tf_op | source)
XLA Modules:
  0.0 243.8 jit_solution(17542689145352882744)
XLA Ops:
  0.6 0.5 broadcast.11
  1.2 1.4 reduce.3
  2.5 0.7 reshape.52.docs_ref.qinfo_ref
  3.2 0.0 copy-start.4
  3.2 1.3 pad_maximum_fusion.refs_4_
  4.5 0.0 copy-start.1
  4.5 0.2 dynamic-slice_bitcast_fusion.2
  4.7 0.8 pad_maximum_fusion.1.w_ref
  5.5 42.7 %front.1 = (bf16[4,192,768]{2,1,0:T(8,128)(2,1)}, bf16[4,192,192]{2,1,0:T(8,128)(2,1)}, bf16[4,4,192,384]{3,2,1,0:T(8,128)(2,1)}, bf16[2,192,192]{2,1,0:T(8,128)...) custom-call(bf16[192,768]{1,0:T(8,128)(2,1)} %refs_8_.1, bf16[192,576]{1,0:T(8,128)(2,1)} %pad_maximum_fusion.1.w_ref, ...), custom_call_target="tpu_custom_call" | custom-call | tf_op jit(solution)/shard_map/front/pallas_call | solution.py:859
  48.2 0.0 copy-done.4
  48.2 1.2 collective-permute-start
  49.4 0.0 copy-start.6
  49.4 0.0 copy-start.7
  49.4 16.2 %attend.1 = (f32[4,192,192]{2,1,0:T(8,128)}, bf16[4,192,192]{2,1,0:T(8,128)(2,1)}, f32[4,8,192]{2,1,0:T(8,128)}) custom-call(s32[1,128]{1,0:T(1,128)} %get-tuple-element.82.info_ref, bf16[4,192,192]{2,1,0:T(8,128)(2,1)} %get-tuple-element.83.q_ref, bf16[3072,384]{1,0:T(8,128)(2,1)} %bitcast.44, s32[16,192]{1,0:T(8,128)} %reshape.52.docs_ref.qinfo_ref), custom_call_target="tpu_custom_call" | custom-call | flops 2000000000 | bytes 8000000 | tf_op jit(solution)/shard_map/attend/pallas_call | solution.py:1465
  65.6 0.0 collective-permute-done
  65.6 0.0 copy-start.5
  65.6 0.0 copy-done.1
  65.6 5.3 %collective-permute-start.1 = (bf16[3,192,768]{2,1,0:T(8,128)(2,1)S(1)}, bf16[3,192,768]{2,1,0:T(8,128)(2,1)S(1)}, u32[]{:S(2)}, u32[]{:S(2)}) collective-permute-start(bf16[3,192,768]{2,1,0:T(8,128)(2,1)S(1)} %pad_maximum_fusion.refs_4_), channel_id=1, source_target_pairs={{0,2},{1,3},{2,0},{3,1},{4,6},{5,7},{6,4},{7,5},{8,10},{9,11},{10,... | collective-permute-start | bytes 2654216 | tf_op jit(solution)/shard_map/ppermute | solution.py:1641
  71.0 0.0 copy-done.6
  71.0 0.0 copy-done.7
  71.0 0.8 select_maximum_fusion.refs_3_.refs_8_
  71.7 0.0 copy-done.5
  71.7 21.2 %route.1 = (bf16[4,48,896]{2,1,0:T(8,128)(2,1)}, bf16[1,4,192,768]{3,2,1,0:T(8,128)(2,1)}, f32[192,768]{1,0:T(8,128)}, f32[192,128]{1,0:T(8,128)}, bf16[192,768]{1,0:T(8,128)(2,1)}) custom-call(bf16[4,192,192]{2,1,0:T(8,128)(2,1)} %get-tuple-element.90.refs_0_, bf16[192,768]{1,0:T(8,128)(2,1)} %refs_8_.1, f32[768]{0:T(1024)} %refs_7_.1, ...), custom_call_target="tpu_custom_call" | custom-call | tf_op jit(solution)/shard_map/route/pallas_call | solution.py:529
  93.0 0.0 collective-permute-done.1.refs_5_
  93.0 0.0 copy-start.8
  93.0 13.7 %ffn.1 = (bf16[192,768]{1,0:T(8,128)(2,1)}, bf16[192,768]{1,0:T(8,128)(2,1)}, bf16[4,192,2048]{2,1,0:T(8,128)(2,1)}, bf16[4,192,2048]{2,1,0:T(8,128)(2,1)}, bf16[4,512,768]{2,1,0:T(8,128)(2,1)}) custom-call(bf16[192,896]{1,0:T(8,128)(2,1)} %bitcast.50, bf16[192,768]{1,0:T(8,128)(2,1)} %bitcast.51, bf16[768,2048]{1,0:T(8,128)(2,1)} %bitcast.41, ...), custom_call_target="tpu_custom_call" | custom-call | flops 6000000000 | bytes 20000000 | tf_op jit(solution)/shard_map/ffn/pallas_call | solution.py:1355
  106.7 0.0 copy-done.8
  106.7 20.6 %combine.1 = (bf16[4,48,768]{2,1,0:T(8,128)(2,1)}, bf16[4,48,768]{2,1,0:T(8,128)(2,1)}, bf16[192,2048]{1,0:T(8,128)(2,1)}, bf16[192,2048]{1,0:T(8,128)(2,1)}, bf...) custom-call(bf16[4,48,768]{2,1,0:T(8,128)(2,1)} %bitcast.30, ...), custom_call_target="tpu_custom_call" | custom-call | tf_op jit(solution)/shard_map/combine/pallas_call | solution.py:529
  127.4 0.5 collective-permute-start.2
  127.9 1.6 collective-permute-start.3
  129.5 0.4 collective-permute-start.4
  129.9 0.0 copy-start.3
  129.9 18.4 %to_heads.1 = (bf16[4,192,192]{2,1,0:T(8,128)(2,1)}, bf16[192,768]{1,0:T(8,128)(2,1)}, f32[192,768]{1,0:T(8,128)}, bf16[4,4,48,768]{3,2,1,0:T(8,128)(2,1)}, f32[16,768]{1,0:T(8,128)}) custom-call(bf16[4,48,768]{2,1,0:T(8,128)(2,1)} %get-tuple-element.102.refs_0_, bf16[4,48,768]{2,1,0:T(8,128)(2,1)} %get-tuple-element.103.refs_1_, ...), custom_call_target="tpu_custom_call" | custom-call | tf_op jit(solution)/shard_map/to_heads/pallas_call | solution.py:529
  148.3 0.0 collective-permute-done.2
  148.3 0.0 copy-done.3
  148.3 0.2 add_convert_fusion.refs_2_
  148.5 0.0 copy-start
  148.5 1.6 collective-permute-start.5
  150.1 26.6 %attend_back.1 = (bf16[4,192,192]{2,1,0:T(8,128)(2,1)}, bf16[4,2,192,384]{3,2,1,0:T(8,128)(2,1)}, bf16[4,2,192,384]{3,2,1,0:T(8,128)(2,1)}) custom-call(s32[1,128]{1,0:T(1,128)} %get-tuple-element.82.info_ref, bf16[4,192,192]{2,1,0:T(8,128)(2,1)} %get-tuple-element.83.q_ref, bf16[3072,384]{1,0:T(8,128)(2,1)} %bitcast.45, ...), custom_call_target="tpu_custom_call" | custom-call | flops 5000000000 | bytes 12000000 | tf_op jit(solution)/shard_map/attend_back/pallas_call | solution.py:1561
  176.7 0.0 copy-done
  176.7 0.0 collective-permute-done.3.refs_12_
  176.7 0.0 copy-start.9
  176.7 4.2 %collective-permute-done.4.refs_14_ = bf16[192,2048]{1,0:T(8,128)(2,1)} collective-permute-done((bf16[192,2048]{1,0:T(8,128)(2,1)}, bf16[192,2048]{1,0:T(8,128)(2,1)}, u32[]{:S(2)}, u32[]{:S(2)}) %collective-permute-start.4) | collective-permute-done | bytes 786464 | tf_op jit(solution)/shard_map/ppermute | solution.py:1641
  180.9 0.0 copy-done.9
  180.9 55.3 %tail.1 = (f32[192,768]{1,0:T(8,128)}, f32[4,48,192]{2,1,0:T(8,128)}, f32[4,48,384]{2,1,0:T(8,128)}, f32[48,768]{1,0:T(8,128)}, f32[16,768]{1,0:T(8,128)}, /*ind...) custom-call(bf16[4,2,192,384]{3,2,1,0:T(8,128)(2,1)} %get-tuple-elem, ...), custom_call_target="tpu_custom_call" | custom-call | flops 20000000000 | bytes 100000000 | tf_op jit(solution)/shard_map/tail/pallas_call | solution.py:529
  236.3 0.0 collective-permute-done.5.refs_5_
  236.3 0.0 copy-start.2
  236.3 0.9 copy-done.2
  237.1 6.5 %finale.1 = (f32[192,2048]{1,0:T(8,128)}, f32[192,2048]{1,0:T(8,128)}, f32[512,768]{1,0:T(8,128)}, f32[192,768]{1,0:T(8,128)}, bf16[192,768]{1,0:T(8,128)(2,1)},...) custom-call(bf16[192,2048]{1,0:T(8,128)(2,1)} %get-tuple-element.124, ...), custom_call_target="tpu_custom_call" | custom-call | flops 10000000 | bytes 10000000 | tf_op jit(solution)/shard_map/finale/pallas_call | solution.py:1627
Async XLA Ops:
  3.2 45.0 %copy-start.4 = (bf16[192,768]{1,0:T(8,128)(2,1)S(1)}, bf16[192,768]{1,0:T(8,128)(2,1)}, u32[]{:S(2)}) copy-start(bf16[192,768]{1,0:T(8,128)(2,1)} %param.23) | copy-start | bytes 884740
  4.5 61.1 %copy-start.1 = (bf16[3,192,768]{2,1,0:T(8,128)(2,1)}, bf16[3,192,768]{2,1,0:T(8,128)(2,1)S(1)}, u32[]{:S(2)}) copy-start(bf16[3,192,768]{2,1,0:T(8,128)(2,1)S(1)} %pad_maximum_fusion.refs_4_) | copy-start | bytes 2654212
  48.2 17.4 %collective-permute-start = (bf16[192,768]{1,0:T(8,128)(2,1)S(1)}, bf16[192,768]{1,0:T(8,128)(2,1)S(1)}, u32[]{:S(2)}, u32[]{:S(2)}) collective-permute-start(bf16[192,768]{1,0:T(8,128)(2,1)S(1)} %copy-done.4), channel_id=1, source_target_pairs={{0,2},{1,3},{2,0},{3,1},{4,6},{5,7},{6,4},{7,5},{8,10},{9,11},{10,... | collective-permute-start | bytes 884744 | tf_op jit(solution)/shard_map/ppermute | solution.py:1641
  49.4 21.5 %copy-start.6 = (f32[768,8]{0,1:T(8,128)S(1)}, f32[768,8]{0,1:T(8,128)}, u32[]{:S(2)}) copy-start(f32[768,8]{0,1:T(8,128)} %param.25) | copy-start | bytes 73732
  49.4 21.5 %copy-start.7 = (f32[768,4]{0,1:T(4,128)S(1)}, f32[768,4]{0,1:T(4,128)}, u32[]{:S(2)}) copy-start(f32[768,4]{0,1:T(4,128)} %param.26) | copy-start | bytes 36868
  65.6 6.1 %copy-start.5 = (bf16[192,768]{1,0:T(8,128)(2,1)}, bf16[192,768]{1,0:T(8,128)(2,1)S(1)}, u32[]{:S(2)}) copy-start(bf16[192,768]{1,0:T(8,128)(2,1)S(1)} %collective-permute-done) | copy-start | bytes 884740
  65.6 27.4 %collective-permute-start.1 = (bf16[3,192,768]{2,1,0:T(8,128)(2,1)S(1)}, bf16[3,192,768]{2,1,0:T(8,128)(2,1)S(1)}, u32[]{:S(2)}, u32[]{:S(2)}) collective-permute-start(bf16[3,192,768]{2,1,0:T(8,128)(2,1)S(1)} %pad_maximum_fusion.refs_4_), channel_id=1, source_target_pairs={{0,2},{1,3},{2,0},{3,1},{4,6},{5,7},{6,4},{7,5},{8,10},{9,11},{10,... | collective-permute-start | bytes 2654216 | tf_op jit(solution)/shard_map/ppermute | solution.py:1641
  93.0 13.7 %copy-start.8 = (bf16[3,192,768]{2,1,0:T(8,128)(2,1)}, bf16[3,192,768]{2,1,0:T(8,128)(2,1)S(1)}, u32[]{:S(2)}) copy-start(bf16[3,192,768]{2,1,0:T(8,128)(2,1)S(1)} %collective-permute-done.1.refs_5_) | copy-start | bytes 2654212
  127.4 20.9 %collective-permute-start.2 = (bf16[512,768]{1,0:T(8,128)(2,1)}, bf16[512,768]{1,0:T(8,128)(2,1)S(1)}, u32[]{:S(2)}, u32[]{:S(2)}) collective-permute-start(bf16[512,768]{1,0:T(8,128)(2,1)} %get-tuple-element.110), channel_id=1, source_target_pairs={{0,2},{1,3},{2,0},{3,1},{4,6},{5,7},{6,4},{7,5},{8,10},{9,11},{10,... | collective-permute-start | bytes 2359304 | tf_op jit(solution)/shard_map/ppermute | solution.py:1641
  127.9 48.8 %collective-permute-start.3 = (bf16[192,2048]{1,0:T(8,128)(2,1)}, bf16[192,2048]{1,0:T(8,128)(2,1)S(1)}, u32[]{:S(2)}, u32[]{:S(2)}) collective-permute-start(bf16[192,2048]{1,0:T(8,128)(2,1)} %get-tuple-element.121), channel_id=1, source_target_pairs={{0,2},{1,3},{2,0},{3,1},{4,6},{5,7},{6,4},{7,5},{8,10},{9,11},{10,... | collective-permute-start | bytes 2359304 | tf_op jit(solution)/shard_map/ppermute | solution.py:1641
  129.5 51.5 %collective-permute-start.4 = (bf16[192,2048]{1,0:T(8,128)(2,1)}, bf16[192,2048]{1,0:T(8,128)(2,1)}, u32[]{:S(2)}, u32[]{:S(2)}) collective-permute-start(bf16[192,2048]{1,0:T(8,128)(2,1)} %get-tuple-element.123), channel_id=1, source_target_pairs={{0,2},{1,3},{2,0},{3,1},{4,6},{5,7},{6,4},{7,5},{8,10},{9,11},{10,... | collective-permute-start | bytes 2359304 | tf_op jit(solution)/shard_map/ppermute | solution.py:1641
  129.9 18.4 %copy-start.3 = (bf16[512,768]{1,0:T(8,128)(2,1)S(1)}, bf16[512,768]{1,0:T(8,128)(2,1)}, u32[]{:S(2)}) copy-start(bf16[512,768]{1,0:T(8,128)(2,1)} %get-tuple-element.109) | copy-start | bytes 2359300
  148.5 28.2 %copy-start = (bf16[512,768]{1,0:T(8,128)(2,1)}, bf16[512,768]{1,0:T(8,128)(2,1)S(1)}, u32[]{:S(2)}) copy-start(bf16[512,768]{1,0:T(8,128)(2,1)S(1)} %add_convert_fusion.refs_2_) | copy-start | bytes 2359300
  148.5 87.8 %collective-permute-start.5 = (bf16[512,768]{1,0:T(8,128)(2,1)S(1)}, bf16[512,768]{1,0:T(8,128)(2,1)S(1)}, u32[]{:S(2)}, u32[]{:S(2)}) collective-permute-start(bf16[512,768]{1,0:T(8,128)(2,1)S(1)} %add_convert_fusion.refs_2_), channel_id=1, source_target_pairs={{0,16},{16,0},{1,17},{17,1},{2,18},{18,2},{3,19},{19,3},{4,20},{20... | collective-permute-start | bytes 2359304 | tf_op jit(solution)/shard_map/ppermute | solution.py:1641
  176.7 4.2 %copy-start.9 = (bf16[192,2048]{1,0:T(8,128)(2,1)}, bf16[192,2048]{1,0:T(8,128)(2,1)S(1)}, u32[]{:S(2)}) copy-start(bf16[192,2048]{1,0:T(8,128)(2,1)S(1)} %collective-permute-done.3.refs_12_) | copy-start | bytes 2359300
  236.3 0.9 copy-start.2
